TPU v7x, 768 devices: a whole 4x8x12 slice. The times are simulated.
768 devices in a mesh: cluster: 96 (over y, z), sub: 8 (over x, core).
Axes of the slice: x: 4, y: 8, z: 12, core: 2. Of those that a mesh axis runs over, the one named last changes fastest.
Arguments:
- rhs: float32 [3072, 4, 384], P(('cluster', 'sub')), may hold values from -8 to 8
- operators: bfloat16 [3072, 384, 384], P(('cluster', 'sub')), may hold values from -1 to 5
- signs: int32 [3072, 384], P(('cluster', 'sub')), may hold values from -1 to 1, as said below
- links: int32 [3072, 3, 128], P(('cluster', 'sub')), may hold values from 0 to 127, as said below
- cluster_basis: float32 [3072, 24, 384], P(('cluster', 'sub')), may hold values from -0.3125 to 0.3125
- corner_basis: float32 [3072, 8, 384], P(('cluster', 'sub')), may hold values from -0.3125 to 0.3125
- corner_ids: int32 [3072, 8], P(('cluster', 'sub')), may hold values from 0 to 1535
- cluster_coarse: float32 [96, 768, 768], P('cluster', 'sub'), may hold values from -1 to 3
- global_coarse: float32 [1536, 1536], P('sub'), may hold values from -0.2 to 0.5
Outputs:
- multipliers: float32 [3072, 4, 384], P(('cluster', 'sub'))
- residual: float32 [3072, 4, 384], P(('cluster', 'sub'))
Inputs may be any that keep to these rules, and one draw needn't show every extreme that they name: `signs`: each entry is -1 or 1. Each links[s, b] is a permutation of 0 to 127; both subdomains of an interface pair hold the same permutation for it.
All inputs are finite; a program needn't handle non-finite values.
Results may differ from a plain program's by a relative error of at most 0.007.
Values sent between devices are 32-bit elements; how exact they have to be, the bound alone decides.
No kernel may reach another device: no remote copies, remote signals or barrier semaphores. Data moves between devices by JAX's collectives and lax.ppermute only.
A program may use at most 32 MiB of HBM per device.

v0:
```python
import functools

import jax
import jax.numpy as jnp
from jax import lax
from jax.sharding import Mesh
from jax.sharding import PartitionSpec as P

ITERS = 2
SUB = ("sub_0", "sub_1")
CLUSTER = ("cluster_0", "cluster_1")
CLUSTER_SUB = ("cluster_0", "cluster_1", "sub_0", "sub_1")


HIGHEST_PRECISION = lax.Precision.HIGHEST


def extended(block, sides, width):
    for axis, dim in sides:
        count = lax.axis_size(axis)
        forward = [(i, i + 1) for i in range(count - 1)]
        backward = [(target, source) for source, target in forward]
        low = lax.ppermute(
            lax.slice_in_dim(block, block.shape[dim] - width, None, axis=dim), axis, forward
        )
        high = lax.ppermute(lax.slice_in_dim(block, 0, width, axis=dim), axis, backward)
        block = jnp.concatenate([low, block, high], axis=dim)
    return block


def one_axis_at_a_time(shard, axes):
    return functools.reduce(lax.psum, axes, shard)


def cut_along(shard, dim, count):
    before, after = (shard.shape[:dim], shard.shape[dim + 1 :])
    return jnp.moveaxis(shard.reshape(*before, count, -1, *after), dim, 0)


def sum_at_owner(shard, axis, dim):
    count = lax.axis_size(axis)
    blocks = lax.all_to_all(cut_along(shard, dim, count), axis, 0, 0, tiled=True)
    return jnp.sum(blocks, axis=0)


def sent_to_all(shard, axis):
    count = lax.axis_size(axis)
    return lax.all_to_all(
        jnp.broadcast_to(shard[None], (count, *shard.shape)), axis, 0, 0, tiled=True
    )


def of_everyone(shard, axis):
    everything = sent_to_all(shard, axis)
    return jnp.sum(everything, axis=0)


def packed_total(arrays, axis):
    ravelled, at, done = (jnp.concatenate([a.reshape(-1) for a in arrays]), 0, [])
    subtotal = of_everyone(ravelled, axis)
    for a in arrays:
        done.append(subtotal[at : at + a.size].reshape(a.shape))
        at += a.size
    return tuple(done)


def invert(order):
    row_index = jnp.broadcast_to(jnp.arange(order.shape[0], dtype=jnp.int32)[:, None], order.shape)
    col_index = jnp.broadcast_to(jnp.arange(order.shape[1], dtype=jnp.int32)[None, :], order.shape)
    return jnp.zeros_like(order).at[row_index, order].set(col_index)


def permuted(blocks, order):
    return jnp.take_along_axis(blocks, order[:, None, :], axis=2)


def interface(vector, tables):
    inv_up, order_down, inv_even, order_odd = tables
    block_width = vector.shape[2] // 3
    up_part = vector[:, :, :block_width]
    down_part = vector[:, :, block_width : 2 * block_width]
    across = vector[:, :, 2 * block_width :]
    send_up = permuted(up_part, inv_up)
    send_down = permuted(down_part, order_down)
    inside_rims = extended(jnp.stack([send_down, send_up]), ((SUB, 0),), 1)
    send_even = permuted(across[0::2], inv_even)
    send_odd = permuted(across[1::2], order_odd)
    outside_rims = extended(jnp.stack([send_odd, send_even]), ((CLUSTER, 0),), 1)
    new_across = jnp.stack([outside_rims[3], outside_rims[0]], axis=1).reshape(across.shape)
    return jnp.concatenate([inside_rims[3], inside_rims[0], new_across], axis=2)


def apply(vector, sign_field, operators, tables):
    spread = sign_field * (vector + interface(vector, tables))
    product = jnp.einsum(
        "srk,skl->srl", spread.astype(jnp.bfloat16), operators, preferred_element_type=jnp.float32
    )
    signed = sign_field * product
    result = signed + interface(signed, tables)
    curvature = one_axis_at_a_time(jnp.sum(vector * result, axis=(0, 2)), CLUSTER_SUB)
    return (result, curvature)


def project(vector, coarse):
    cluster_basis, corner_basis, flat_ids, onehot, cluster_coarse, global_coarse = coarse
    load_count = vector.shape[1]
    local_subs = vector.shape[0]
    cluster_coef = jnp.einsum("srl,skl->srk", vector, cluster_basis, precision=HIGHEST_PRECISION)
    own_coef = cluster_coef.transpose(1, 0, 2).reshape(load_count, -1)
    part_cluster = jnp.dot(own_coef, cluster_coarse[0], precision=HIGHEST_PRECISION)
    corner_coef = jnp.einsum(
        "scl,srl->rsc", corner_basis, vector, precision=HIGHEST_PRECISION
    ).reshape(load_count, -1)
    corner_local = jnp.dot(corner_coef, onehot, precision=HIGHEST_PRECISION)
    squares = jnp.sum(vector * vector, axis=(0, 2))
    spread_norm = jnp.broadcast_to(squares[:, None], (load_count, lax.axis_size(SUB)))
    corner_rows, norm_piece = (
        sum_at_owner(corner_local, SUB, 1),
        sum_at_owner(spread_norm, SUB, 1),
    )
    corner_rows, norm_piece = (
        one_axis_at_a_time(corner_rows, CLUSTER),
        one_axis_at_a_time(norm_piece, CLUSTER),
    )
    total_norm = norm_piece[:, 0]
    part_global = jnp.dot(corner_rows, global_coarse, precision=HIGHEST_PRECISION)
    cluster_all, global_all = packed_total((part_cluster, part_global), SUB)
    own_width = own_coef.shape[1]
    cluster_own = lax.dynamic_slice_in_dim(
        cluster_all, lax.axis_index(SUB) * own_width, own_width, 1
    )
    cluster_own = cluster_own.reshape(load_count, local_subs, -1)
    fix_cluster = jnp.einsum(
        "rsk,skl->srl", cluster_own, cluster_basis, precision=HIGHEST_PRECISION
    )
    picked = jnp.take(global_all, flat_ids, axis=1).reshape(load_count, local_subs, -1)
    fix_corner = jnp.einsum("rsc,scl->srl", picked, corner_basis, precision=HIGHEST_PRECISION)
    return (vector - fix_cluster - fix_corner, total_norm)


def local(
    rhs,
    operators,
    signs,
    links,
    cluster_basis,
    corner_basis,
    corner_ids,
    cluster_coarse,
    global_coarse,
):
    sign_field = signs.astype(jnp.float32)[:, None, :]
    tables = (invert(links[:, 0]), links[:, 1], invert(links[0::2, 2]), links[1::2, 2])
    flat_ids = corner_ids.reshape(-1)
    onehot = (
        flat_ids[:, None] == jnp.arange(global_coarse.shape[1], dtype=jnp.int32)[None, :]
    ).astype(jnp.float32)
    coarse = (cluster_basis, corner_basis, flat_ids, onehot, cluster_coarse, global_coarse)
    residual = rhs
    projected, residual_norm = project(residual, coarse)
    direction = projected
    multipliers = jnp.zeros_like(rhs)
    for iteration in range(ITERS):
        product, curvature = apply(direction, sign_field, operators, tables)
        step_size = (residual_norm / curvature)[None, :, None]
        multipliers = multipliers + step_size * direction
        residual = residual - step_size * product
        if iteration + 1 < ITERS:
            projected, norm_next = project(residual, coarse)
            direction = projected + (norm_next / residual_norm)[None, :, None] * direction
            residual_norm = norm_next
    return (multipliers, residual)


def solution(mesh):
    torus = Mesh(mesh.devices.reshape(8, 12, 4, 2), ("cluster_0", "cluster_1", "sub_0", "sub_1"))
    in_specs = (
        P(CLUSTER_SUB, None, None),
        P(CLUSTER_SUB, None, None),
        P(CLUSTER_SUB, None),
        P(CLUSTER_SUB, None, None),
        P(CLUSTER_SUB, None, None),
        P(CLUSTER_SUB, None, None),
        P(CLUSTER_SUB, None),
        P(CLUSTER, SUB, None),
        P(SUB, None),
    )
    out_specs = (P(CLUSTER_SUB, None, None), P(CLUSTER_SUB, None, None))
    return jax.shard_map(local, mesh=torus, in_specs=in_specs, out_specs=out_specs, check_vma=False)
```

profile of v0, /device:TPU:1, one launch (start us, length us, event | category | flops | bytes accessed | tf_op | source)
XLA Modules:
  0.0 399.9 jit_solution(16681935050485757216)
XLA Ops:
  3.5 13.8 %all-to-all-start.1 = ((f32[8,4,192]{2,1,0:T(4,128)}), f32[8,4,192]{2,1,0:T(4,128)S(1)}, u32[]{:S(2)}, u32[]{:S(2)}) async-start(f32[8,4,192]{2,1,0:T(4,128)} %convolution_bitcast_fusion.1), calls=%async_computation.1 | async-start | bytes 65536 | tf_op jit(solution)/shard_map/all_to_all | solution.py:42
  19.5 11.4 %scatter_fusion.1 = s32[2,128]{1,0:T(2,128)S(1)} fusion(s32[2,128]{1,0:T(2,128)S(1)} %broadcast.138, s32[256]{0:T(256)S(1)} %fusion.49, s32[256]{0:T(256)S(1)} %iota_bitcast_fusion.1), kind=kCustom, calls=%fused_computation.19 | custom fusion | bytes 5120 | tf_op jit(solution)/shard_map/scatter | solution.py:70
  31.1 22.5 %scatter_fusion = s32[4,128]{1,0:T(4,128)S(1)} fusion(s32[4,128]{1,0:T(4,128)S(1)} %broadcast.136, s32[512]{0:T(512)S(1)} %get-tuple-element.36, s32[512]{0:T(512)S(1)} %iota_bitcast_fusion), kind=kCustom, calls=%fused_computation.18 | custom fusion | bytes 10240 | tf_op jit(solution)/shard_map/scatter | solution.py:70
  55.0 4.8 %all-to-all-start = ((f32[8,4,1]{1,2,0:T(1,128)}), f32[8,4,1]{1,2,0:T(1,128)S(1)}, u32[]{:S(2)}, u32[]{:S(2)}) async-start(f32[8,4,1]{1,2,0:T(1,128)} %transpose.39), calls=%async_computation | async-start | bytes 8192 | tf_op jit(solution)/shard_map/all_to_all | solution.py:42
  59.9 10.7 %psum.114 = f32[4,192]{1,0:T(4,128)S(1)} all-reduce(f32[4,192]{1,0:T(4,128)S(1)} %reduce_sum.97), channel_id=1, replica_groups=mesh['cluster_0'=8,'cluster_1'=12,'sub_0'=4,'sub_1'=2] {'cluster_0'}, use_global_device_ids=true, to_apply=%region_5.0 | all-reduce | flops 768 | bytes 6144 | tf_op jit(solution)/shard_map/psum | solution.py:32
  70.6 23.0 %psum.115 = f32[4,192]{1,0:T(4,128)S(1)} all-reduce(f32[4,192]{1,0:T(4,128)S(1)} %psum.114), channel_id=1, replica_groups=mesh['cluster_0'=8,'cluster_1'=12,'sub_0'=4,'sub_1'=2] {'cluster_1'}, use_global_device_ids=true, to_apply=%region_6.0 | all-reduce | flops 768 | bytes 6144 | tf_op jit(solution)/shard_map/psum | solution.py:32
  95.2 14.1 %all-to-all-start.2 = ((f32[8,1,9216]{2,1,0:T(1,128)}), f32[8,1,9216]{2,1,0:T(1,128)S(1)}, u32[]{:S(2)}, u32[]{:S(2)}) async-start(f32[8,1,9216]{2,1,0:T(1,128)} %broadcast_in_dim.30), calls=%async_computation.2 | async-start | bytes 589824 | tf_op jit(solution)/shard_map/all_to_all | solution.py:48
  109.3 6.7 %all-to-all-done.2 = f32[8,1,9216]{2,1,0:T(1,128)S(1)} async-done(((f32[8,1,9216]{2,1,0:T(1,128)}), f32[8,1,9216]{2,1,0:T(1,128)S(1)}, u32[]{:S(2)}, u32[]{:S(2)}) %all-to-all-start.2) | async-done | bytes 294944 | tf_op jit(solution)/shard_map/all_to_all | solution.py:48
  118.1 1.9 gather_fusion.3
  121.7 1.9 gather_fusion.4
  123.7 4.0 collective-permute-start.3
  127.8 3.7 gather_fusion.1
  131.6 3.6 collective-permute-start
  135.3 3.7 gather_fusion.2
  139.1 2.1 collective-permute-start.1
  142.6 1.9 gather_fusion.7
  146.2 1.9 gather_fusion.8
  148.2 4.0 collective-permute-start.7
  152.4 3.7 gather_fusion.5
  156.2 2.6 collective-permute-start.4
  158.9 3.7 gather_fusion.6
  162.7 3.8 collective-permute-start.5
  167.5 11.9 %all-reduce.3 = (f32[4,1]{0,1:T(1,128)S(1)}, f32[4]{0:T(128)S(1)}) all-reduce(f32[4,1]{0,1:T(1,128)S(1)} %bitcast.310, f32[4]{0:T(128)S(1)} %multiply_reduce_fusion.2), channel_id=1, replica_groups=mesh['cluster_0'=8,'cluster_1'=12,'sub_0'=4,'sub_1'=2] {'cluster_0'}, use_global_device_ids=true, to_apply=%region_2.0 | all-reduce | flops 8 | bytes 64 | tf_op jit(solution)/shard_map/psum | solution.py:32
  179.4 20.1 %all-reduce.1 = (f32[4]{0:T(128)S(1)}, f32[4]{0:T(128)S(1)}) all-reduce(f32[4]{0:T(128)S(1)} %bitcast.312, f32[4]{0:T(128)S(1)} %get-tuple-element.12), channel_id=1, replica_groups=mesh['cluster_0'=8,'cluster_1'=12,'sub_0'=4,'sub_1'=2] {'cluster_1'}, use_global_device_ids=true, to_apply=%region_3.0 | all-reduce | flops 8 | bytes 64 | tf_op jit(solution)/shard_map/psum | solution.py:32
  199.5 7.1 %psum.118 = f32[4]{0:T(128)S(1)} all-reduce(f32[4]{0:T(128)S(1)} %get-tuple-element.8), channel_id=1, replica_groups=mesh['cluster_0'=8,'cluster_1'=12,'sub_0'=4,'sub_1'=2] {'sub_0'}, use_global_device_ids=true, to_apply=%region_13.17 | all-reduce | flops 4 | bytes 32 | tf_op jit(solution)/shard_map/psum | solution.py:32
  206.6 14.8 %psum.119 = f32[4]{0:T(128)S(1)} all-reduce(f32[4]{0:T(128)S(1)} %psum.118), channel_id=1, replica_groups=mesh['cluster_0'=8,'cluster_1'=12,'sub_0'=4,'sub_1'=2] {'sub_1'}, use_global_device_ids=true, to_apply=%region_14.18 | all-reduce | flops 4 | bytes 32 | tf_op jit(solution)/shard_map/psum | solution.py:32
  222.7 3.6 all-to-all-start.3
  227.2 3.6 all-to-all-done.3
  230.8 3.9 all-to-all-start.4
  235.1 4.4 %all-to-all-done.4 = f32[8,4,192]{2,1,0:T(4,128)S(1)} async-done(((f32[8,4,192]{2,1,0:T(4,128)}), f32[8,4,192]{2,1,0:T(4,128)S(1)}, u32[]{:S(2)}, u32[]{:S(2)}) %all-to-all-start.4) | async-done | bytes 24608 | tf_op jit(solution)/shard_map/all_to_all | solution.py:42
  239.5 10.9 %all-reduce.2 = (f32[4,192]{1,0:T(4,128)S(1)}, f32[4,1]{0,1:T(1,128)S(1)}) all-reduce(f32[4,192]{1,0:T(4,128)S(1)} %reduce_sum.103, f32[4,1]{0,1:T(1,128)S(1)} %bitcast.309), channel_id=1, replica_groups=mesh['cluster_0'=8,'cluster_1'=12,'sub_0'=4,'sub_1'=2] {'cluster_0'}, use_global_device_ids=true, to_apply=%region_20.24 | all-reduce | flops 772 | bytes 6176 | tf_op jit(solution)/shard_map/psum | solution.py:32
  250.5 15.8 %all-reduce = (f32[4,192]{1,0:T(4,128)S(1)}, f32[4]{0:T(128)S(1)}) all-reduce(f32[4,192]{1,0:T(4,128)S(1)} %get-tuple-element.9, f32[4]{0:T(128)S(1)} %bitcast.311), channel_id=1, replica_groups=mesh['cluster_0'=8,'cluster_1'=12,'sub_0'=4,'sub_1'=2] {'cluster_1'}, use_global_device_ids=true, to_apply=%region_21.25 | all-reduce | flops 772 | bytes 6176 | tf_op jit(solution)/shard_map/psum | solution.py:32
  267.8 12.7 %all-to-all-start.5 = ((f32[8,1,9216]{2,1,0:T(1,128)}), f32[8,1,9216]{2,1,0:T(1,128)S(1)}, u32[]{:S(2)}, u32[]{:S(2)}) async-start(f32[8,1,9216]{2,1,0:T(1,128)} %broadcast_in_dim.42), calls=%async_computation.5 | async-start | bytes 589824 | tf_op jit(solution)/shard_map/all_to_all | solution.py:48
  280.5 6.8 %all-to-all-done.5 = f32[8,1,9216]{2,1,0:T(1,128)S(1)} async-done(((f32[8,1,9216]{2,1,0:T(1,128)}), f32[8,1,9216]{2,1,0:T(1,128)S(1)}, u32[]{:S(2)}, u32[]{:S(2)}) %all-to-all-start.5) | async-done | bytes 294944 | tf_op jit(solution)/shard_map/all_to_all | solution.py:48
  296.8 4.3 %collective-permute-start.11 = (f32[1,2,4,128]{3,2,1,0:T(4,128)S(1)}, f32[1,2,4,128]{3,2,1,0:T(4,128)S(1)}, u32[]{:S(2)}, u32[]{:S(2)}) collective-permute-start(f32[1,2,4,128]{3,2,1,0:T(4,128)S(1)} %select_bitcast_fusion.2), channel_id=1, source_target_pairs={{0,8},{8,16},{16,24},{24,32},{32,40},{40,48},{48,56},{56,64},{64,7... | collective-permute-start | bytes 12296 | tf_op jit(solution)/shard_map/ppermute | solution.py:23
  301.2 3.7 gather_fusion.10
  305.0 3.5 collective-permute-start.8
  308.7 3.7 gather_fusion.11
  312.5 2.3 collective-permute-start.9
  321.4 4.3 %collective-permute-start.15 = (f32[1,2,4,128]{3,2,1,0:T(4,128)S(1)}, f32[1,2,4,128]{3,2,1,0:T(4,128)S(1)}, u32[]{:S(2)}, u32[]{:S(2)}) collective-permute-start(f32[1,2,4,128]{3,2,1,0:T(4,128)S(1)} %select_bitcast_fusion), channel_id=1, source_target_pairs={{0,8},{8,16},{16,24},{24,32},{32,40},{40,48},{48,56},{56,64},{64,7... | collective-permute-start | bytes 12296 | tf_op jit(solution)/shard_map/ppermute | solution.py:23
  325.8 3.7 gather_fusion.14
  329.6 2.4 collective-permute-start.12
  332.1 3.7 gather_fusion.15
  335.9 4.0 %collective-permute-start.13 = (f32[1,4,4,128]{3,2,1,0:T(4,128)S(1)}, f32[1,4,4,128]{3,2,1,0:T(4,128)S(1)}, u32[]{:S(2)}, u32[]{:S(2)}) collective-permute-start(f32[1,4,4,128]{3,2,1,0:T(4,128)S(1)} %fusion.23), channel_id=1, source_target_pairs={{0,1},{1,2},{2,3},{3,4},{4,5},{5,6},{6,7},{8,9},{9,10},{10,11},{11... | collective-permute-start | bytes 24584 | tf_op jit(solution)/shard_map/ppermute | solution.py:23
  340.9 15.6 %psum.124 = f32[4]{0:T(128)S(1)} all-reduce(f32[4]{0:T(128)S(1)} %multiply_reduce_fusion), channel_id=1, replica_groups=mesh['cluster_0'=8,'cluster_1'=12,'sub_0'=4,'sub_1'=2] {'cluster_0'}, use_global_device_ids=true, to_apply=%region_24.28 | all-reduce | flops 4 | bytes 32 | tf_op jit(solution)/shard_map/psum | solution.py:32
  356.5 20.9 %psum.125 = f32[4]{0:T(128)S(1)} all-reduce(f32[4]{0:T(128)S(1)} %psum.124), channel_id=1, replica_groups=mesh['cluster_0'=8,'cluster_1'=12,'sub_0'=4,'sub_1'=2] {'cluster_1'}, use_global_device_ids=true, to_apply=%region_25.29 | all-reduce | flops 4 | bytes 32 | tf_op jit(solution)/shard_map/psum | solution.py:32
  377.4 6.9 %psum.126 = f32[4]{0:T(128)S(1)} all-reduce(f32[4]{0:T(128)S(1)} %psum.125), channel_id=1, replica_groups=mesh['cluster_0'=8,'cluster_1'=12,'sub_0'=4,'sub_1'=2] {'sub_0'}, use_global_device_ids=true, to_apply=%region_26.30 | all-reduce | flops 4 | bytes 32 | tf_op jit(solution)/shard_map/psum | solution.py:32
  384.3 14.9 %psum.127 = f32[4]{0:T(128)S(1)} all-reduce(f32[4]{0:T(128)S(1)} %psum.126), channel_id=1, replica_groups=mesh['cluster_0'=8,'cluster_1'=12,'sub_0'=4,'sub_1'=2] {'sub_1'}, use_global_device_ids=true, to_apply=%region_27.31 | all-reduce | flops 4 | bytes 32 | tf_op jit(solution)/shard_map/psum | solution.py:32
  (187 shorter events, 39.6 us)
Async XLA Ops:
  0.6 93.0 %copy-start = (f32[192,1536]{1,0:T(8,128)S(1)}, f32[192,1536]{1,0:T(8,128)}, u32[]{:S(2)}) copy-start(f32[192,1536]{1,0:T(8,128)} %param.23) | copy-start | bytes 3538948
  3.5 27.5 %copy-start.6 = (s32[4,3,128]{2,0,1:T(4,128)S(1)}, s32[4,3,128]{2,0,1:T(4,128)}, u32[]{:S(2)}) copy-start(s32[4,3,128]{2,0,1:T(4,128)} %param.18) | copy-start | bytes 18436
  3.5 51.0 %all-to-all-start.1 = ((f32[8,4,192]{2,1,0:T(4,128)}), f32[8,4,192]{2,1,0:T(4,128)S(1)}, u32[]{:S(2)}, u32[]{:S(2)}) async-start(f32[8,4,192]{2,1,0:T(4,128)} %convolution_bitcast_fusion.1), calls=%async_computation.1 | async-start | bytes 65536 | tf_op jit(solution)/shard_map/all_to_all | solution.py:42
  31.0 22.6 %copy-start.2 = (f32[4,24,384]{2,1,0:T(8,128)S(1)}, f32[4,24,384]{2,1,0:T(8,128)}, u32[]{:S(2)}) copy-start(f32[4,24,384]{2,1,0:T(8,128)} %param.19) | copy-start | bytes 442372
  31.0 22.6 %copy-start.5 = (f32[4,4,384]{2,1,0:T(4,128)S(1)}, f32[4,4,384]{2,1,0:T(4,128)}, u32[]{:S(2)}) copy-start(f32[4,4,384]{2,1,0:T(4,128)} %param.15) | copy-start | bytes 73732
  31.1 23.0 %copy-start.3 = (f32[1,96,768]{2,1,0:T(8,128)S(1)}, f32[1,96,768]{2,1,0:T(8,128)}, u32[]{:S(2)}) copy-start(f32[1,96,768]{2,1,0:T(8,128)} %param.22) | copy-start | bytes 884740
  54.4 54.8 %copy-start.7 = (s32[4,384]{1,0:T(4,128)S(1)}, s32[4,384]{1,0:T(4,128)}, u32[]{:S(2)}) copy-start(s32[4,384]{1,0:T(4,128)} %param.17) | copy-start | bytes 18436
  55.0 39.3 %all-to-all-start = ((f32[8,4,1]{1,2,0:T(1,128)}), f32[8,4,1]{1,2,0:T(1,128)S(1)}, u32[]{:S(2)}, u32[]{:S(2)}) async-start(f32[8,4,1]{1,2,0:T(1,128)} %transpose.39), calls=%async_computation | async-start | bytes 8192 | tf_op jit(solution)/shard_map/all_to_all | solution.py:42
  94.3 23.3 %copy-start.4 = (f32[4,8,384]{2,1,0:T(8,128)S(1)}, f32[4,8,384]{2,1,0:T(8,128)}, u32[]{:S(2)}) copy-start(f32[4,8,384]{2,1,0:T(8,128)} %param.20) | copy-start | bytes 147460
  95.2 20.8 %all-to-all-start.2 = ((f32[8,1,9216]{2,1,0:T(1,128)}), f32[8,1,9216]{2,1,0:T(1,128)S(1)}, u32[]{:S(2)}, u32[]{:S(2)}) async-start(f32[8,1,9216]{2,1,0:T(1,128)} %broadcast_in_dim.30), calls=%async_computation.2 | async-start | bytes 589824 | tf_op jit(solution)/shard_map/all_to_all | solution.py:48
  120.0 22.2 %copy-start.1 = (bf16[4,384,384]{2,1,0:T(8,128)(2,1)S(1)}, bf16[4,384,384]{2,1,0:T(8,128)(2,1)}, u32[]{:S(2)}) copy-start(bf16[4,384,384]{2,1,0:T(8,128)(2,1)} %param.16) | copy-start | bytes 3538948
  120.1 21.1 %collective-permute-start.2 = (f32[1,2,4,128]{3,2,1,0:T(4,128)S(1)}, f32[1,2,4,128]{3,2,1,0:T(4,128)S(1)}, u32[]{:S(2)}, u32[]{:S(2)}) collective-permute-start(f32[1,2,4,128]{3,2,1,0:T(4,128)S(1)} %select_bitcast_fusion.7), channel_id=1, source_target_pairs={{8,0},{16,8},{24,16},{32,24},{40,32},{48,40},{56,48},{64,56},{72,6... | collective-permute-start | bytes 12296 | tf_op jit(solution)/shard_map/ppermute | solution.py:26
  123.7 17.6 %collective-permute-start.3 = (f32[1,2,4,128]{3,2,1,0:T(4,128)S(1)}, f32[1,2,4,128]{3,2,1,0:T(4,128)S(1)}, u32[]{:S(2)}, u32[]{:S(2)}) collective-permute-start(f32[1,2,4,128]{3,2,1,0:T(4,128)S(1)} %select_bitcast_fusion.6), channel_id=1, source_target_pairs={{0,8},{8,16},{16,24},{24,32},{32,40},{40,48},{48,56},{56,64},{64,7... | collective-permute-start | bytes 12296 | tf_op jit(solution)/shard_map/ppermute | solution.py:23
  131.6 9.6 %collective-permute-start = (f32[1,4,4,128]{3,2,1,0:T(4,128)S(1)}, f32[1,4,4,128]{3,2,1,0:T(4,128)S(1)}, u32[]{:S(2)}, u32[]{:S(2)}) collective-permute-start(f32[1,4,4,128]{3,2,1,0:T(4,128)S(1)} %fusion.30), channel_id=1, source_target_pairs={{1,0},{2,1},{3,2},{4,3},{5,4},{6,5},{7,6},{9,8},{10,9},{11,10},{12... | collective-permute-start | bytes 24584 | tf_op jit(solution)/shard_map/ppermute | solution.py:26
  139.1 3.1 collective-permute-start.1
  144.6 22.0 %collective-permute-start.6 = (f32[1,2,4,128]{3,2,1,0:T(4,128)S(1)}, f32[1,2,4,128]{3,2,1,0:T(4,128)S(1)}, u32[]{:S(2)}, u32[]{:S(2)}) collective-permute-start(f32[1,2,4,128]{3,2,1,0:T(4,128)S(1)} %select_bitcast_fusion.5), channel_id=1, source_target_pairs={{8,0},{16,8},{24,16},{32,24},{40,32},{48,40},{56,48},{64,56},{72,6... | collective-permute-start | bytes 12296 | tf_op jit(solution)/shard_map/ppermute | solution.py:26
  148.2 18.4 %collective-permute-start.7 = (f32[1,2,4,128]{3,2,1,0:T(4,128)S(1)}, f32[1,2,4,128]{3,2,1,0:T(4,128)S(1)}, u32[]{:S(2)}, u32[]{:S(2)}) collective-permute-start(f32[1,2,4,128]{3,2,1,0:T(4,128)S(1)} %select_bitcast_fusion.4), channel_id=1, source_target_pairs={{0,8},{8,16},{16,24},{24,32},{32,40},{40,48},{48,56},{56,64},{64,7... | collective-permute-start | bytes 12296 | tf_op jit(solution)/shard_map/ppermute | solution.py:23
  156.2 10.5 %collective-permute-start.4 = (f32[1,4,4,128]{3,2,1,0:T(4,128)S(1)}, f32[1,4,4,128]{3,2,1,0:T(4,128)S(1)}, u32[]{:S(2)}, u32[]{:S(2)}) collective-permute-start(f32[1,4,4,128]{3,2,1,0:T(4,128)S(1)} %fusion.28), channel_id=1, source_target_pairs={{1,0},{2,1},{3,2},{4,3},{5,4},{6,5},{7,6},{9,8},{10,9},{11,10},{12... | collective-permute-start | bytes 24584 | tf_op jit(solution)/shard_map/ppermute | solution.py:26
  162.7 4.6 %collective-permute-start.5 = (f32[1,4,4,128]{3,2,1,0:T(4,128)S(1)}, f32[1,4,4,128]{3,2,1,0:T(4,128)S(1)}, u32[]{:S(2)}, u32[]{:S(2)}) collective-permute-start(f32[1,4,4,128]{3,2,1,0:T(4,128)S(1)} %fusion.27), channel_id=1, source_target_pairs={{0,1},{1,2},{2,3},{3,4},{4,5},{5,6},{6,7},{8,9},{9,10},{10,11},{11... | collective-permute-start | bytes 24584 | tf_op jit(solution)/shard_map/ppermute | solution.py:23
  222.7 8.1 %all-to-all-start.3 = ((f32[8,4,1]{1,2,0:T(1,128)}), f32[8,4,1]{1,2,0:T(1,128)S(1)}, u32[]{:S(2)}, u32[]{:S(2)}) async-start(f32[8,4,1]{1,2,0:T(1,128)} %transpose.43), calls=%async_computation.3 | async-start | bytes 8192 | tf_op jit(solution)/shard_map/all_to_all | solution.py:42
  230.8 8.7 %all-to-all-start.4 = ((f32[8,4,192]{2,1,0:T(4,128)}), f32[8,4,192]{2,1,0:T(4,128)S(1)}, u32[]{:S(2)}, u32[]{:S(2)}) async-start(f32[8,4,192]{2,1,0:T(4,128)} %convolution_bitcast_fusion), calls=%async_computation.4 | async-start | bytes 65536 | tf_op jit(solution)/shard_map/all_to_all | solution.py:42
  267.8 19.5 %all-to-all-start.5 = ((f32[8,1,9216]{2,1,0:T(1,128)}), f32[8,1,9216]{2,1,0:T(1,128)S(1)}, u32[]{:S(2)}, u32[]{:S(2)}) async-start(f32[8,1,9216]{2,1,0:T(1,128)} %broadcast_in_dim.42), calls=%async_computation.5 | async-start | bytes 589824 | tf_op jit(solution)/shard_map/all_to_all | solution.py:48
  293.4 21.4 %collective-permute-start.10 = (f32[1,2,4,128]{3,2,1,0:T(4,128)S(1)}, f32[1,2,4,128]{3,2,1,0:T(4,128)S(1)}, u32[]{:S(2)}, u32[]{:S(2)}) collective-permute-start(f32[1,2,4,128]{3,2,1,0:T(4,128)S(1)} %select_bitcast_fusion.3), channel_id=1, source_target_pairs={{8,0},{16,8},{24,16},{32,24},{40,32},{48,40},{56,48},{64,56},{72,6... | collective-permute-start | bytes 12296 | tf_op jit(solution)/shard_map/ppermute | solution.py:26
  296.8 18.0 %collective-permute-start.11 = (f32[1,2,4,128]{3,2,1,0:T(4,128)S(1)}, f32[1,2,4,128]{3,2,1,0:T(4,128)S(1)}, u32[]{:S(2)}, u32[]{:S(2)}) collective-permute-start(f32[1,2,4,128]{3,2,1,0:T(4,128)S(1)} %select_bitcast_fusion.2), channel_id=1, source_target_pairs={{0,8},{8,16},{16,24},{24,32},{32,40},{40,48},{48,56},{56,64},{64,7... | collective-permute-start | bytes 12296 | tf_op jit(solution)/shard_map/ppermute | solution.py:23
  305.0 9.8 %collective-permute-start.8 = (f32[1,4,4,128]{3,2,1,0:T(4,128)S(1)}, f32[1,4,4,128]{3,2,1,0:T(4,128)S(1)}, u32[]{:S(2)}, u32[]{:S(2)}) collective-permute-start(f32[1,4,4,128]{3,2,1,0:T(4,128)S(1)} %fusion.26), channel_id=1, source_target_pairs={{1,0},{2,1},{3,2},{4,3},{5,4},{6,5},{7,6},{9,8},{10,9},{11,10},{12... | collective-permute-start | bytes 24584 | tf_op jit(solution)/shard_map/ppermute | solution.py:26
  312.5 3.1 collective-permute-start.9
  318.0 22.0 %collective-permute-start.14 = (f32[1,2,4,128]{3,2,1,0:T(4,128)S(1)}, f32[1,2,4,128]{3,2,1,0:T(4,128)S(1)}, u32[]{:S(2)}, u32[]{:S(2)}) collective-permute-start(f32[1,2,4,128]{3,2,1,0:T(4,128)S(1)} %select_bitcast_fusion.1), channel_id=1, source_target_pairs={{8,0},{16,8},{24,16},{32,24},{40,32},{48,40},{56,48},{64,56},{72,6... | collective-permute-start | bytes 12296 | tf_op jit(solution)/shard_map/ppermute | solution.py:26
  321.4 18.6 %collective-permute-start.15 = (f32[1,2,4,128]{3,2,1,0:T(4,128)S(1)}, f32[1,2,4,128]{3,2,1,0:T(4,128)S(1)}, u32[]{:S(2)}, u32[]{:S(2)}) collective-permute-start(f32[1,2,4,128]{3,2,1,0:T(4,128)S(1)} %select_bitcast_fusion), channel_id=1, source_target_pairs={{0,8},{8,16},{16,24},{24,32},{32,40},{40,48},{48,56},{56,64},{64,7... | collective-permute-start | bytes 12296 | tf_op jit(solution)/shard_map/ppermute | solution.py:23
  329.6 10.4 %collective-permute-start.12 = (f32[1,4,4,128]{3,2,1,0:T(4,128)S(1)}, f32[1,4,4,128]{3,2,1,0:T(4,128)S(1)}, u32[]{:S(2)}, u32[]{:S(2)}) collective-permute-start(f32[1,4,4,128]{3,2,1,0:T(4,128)S(1)} %fusion.24), channel_id=1, source_target_pairs={{1,0},{2,1},{3,2},{4,3},{5,4},{6,5},{7,6},{9,8},{10,9},{11,10},{12... | collective-permute-start | bytes 24584 | tf_op jit(solution)/shard_map/ppermute | solution.py:26
  335.9 4.8 %collective-permute-start.13 = (f32[1,4,4,128]{3,2,1,0:T(4,128)S(1)}, f32[1,4,4,128]{3,2,1,0:T(4,128)S(1)}, u32[]{:S(2)}, u32[]{:S(2)}) collective-permute-start(f32[1,4,4,128]{3,2,1,0:T(4,128)S(1)} %fusion.23), channel_id=1, source_target_pairs={{0,1},{1,2},{2,3},{3,4},{4,5},{5,6},{6,7},{8,9},{9,10},{10,11},{11... | collective-permute-start | bytes 24584 | tf_op jit(solution)/shard_map/ppermute | solution.py:23
where the time goes:
time: 401 us; the launch traced here: 400 us
  blocking collectives  173 us (43%)
  starting transfers between devices  99.2 us (25%)
  local copies, waits for them, and re-layouts  92.1 us (23%)
  waiting for transfers between devices  24.7 us (6%)
  matrix products  6.99 us (2%)
    psum x12, blocking collectives, one_axis_at_a_time(): return functools.reduce(lax.psum, axes, shard)  173 us
    gather x32, local copies, waits for them, and re-layouts, permuted(): return jnp.take_along_axis(blocks, order[:, None, :], axis=2)  46 us
    scatter x2, local copies, waits for them, and re-layouts, invert(): return jnp.zeros_like(order).at[row_index, order].set(col_index)  34 us
    ppermute x8, starting transfers between devices, extended(): lax.ppermute(lax.slice_in_dim(block, block.shape[dim] - width, None, axis...  28.8 us
    all_to_all x2, starting transfers between devices, sent_to_all(): lax.all_to_all(jnp.broadcast_to(shard[None], (count, *shard.shape)), axis...  26.8 us
    all_to_all x4, starting transfers between devices, sum_at_owner(): lax.all_to_all(cut_along(shard, dim, count), axis, 0, 0, tiled=True)  26.2 us
    ppermute x8, starting transfers between devices, extended(): lax.ppermute(lax.slice_in_dim(block, 0, width, axis=dim), axis, backward)  17.5 us
    all_to_all x2, waiting for transfers between devices, sent_to_all(): lax.all_to_all(jnp.broadcast_to(shard[None], (count, *shard.shape)), axis...  13.5 us
  transfers between devices with their start and end apart: 22, of which 8 were waited for; matrix products, arithmetic and copies ran while one was open for 20% of the time, Pallas kernels for 0%

commit v1 on v0

v1 whole, which is shorter than its diff:
```python
import jax
import jax.numpy as jnp
from jax import lax
from jax.experimental import pallas as pl
from jax.experimental.pallas import tpu as pltpu
from jax.sharding import PartitionSpec as P

F32 = jnp.float32
BF16 = jnp.bfloat16
I32 = jnp.int32
R = 4
S = 4
ROWS = R * S
B = 128
D = 384
KC = 24
NB = 128
NCL = S * KC
CHUNK = 192
NSUB = 8


def iota(shape, dim):
    return lax.broadcasted_iota(I32, shape, dim)


def split(x):
    hi = x.astype(BF16)
    return hi, (x - hi.astype(F32)).astype(BF16)


def mm(a, b):
    return lax.dot_general(a, b, (((1,), (0,)), ((), ())), preferred_element_type=F32)


def mm_t(a, b):
    return lax.dot_general(a, b, (((1,), (1,)), ((), ())), preferred_element_type=F32)


def dot2(x, w, f=mm):
    n = x.shape[0]
    xh, xl = split(x)
    wh, wl = split(w)
    xs = jnp.concatenate([xh, xl], axis=0)
    both = f(xs, wh)
    return both[:n] + both[n:] + f(xh, wl)


def lanes_of_sub(shape):
    lane = iota(shape, 1)
    return jnp.where(lane < NCL, lane // KC, (lane - NCL) // 8)


def own_mask():
    return iota((ROWS, NB), 0) // R == lanes_of_sub((ROWS, NB))


def by_load(x):
    y = x[:8] + x[8:]
    y = y + pltpu.roll(y, 4, 0)
    return jnp.concatenate([y, y], axis=0)


def coefs(v, w):
    return by_load(jnp.where(own_mask(), dot2(v, w, mm_t), 0.0))


def spread_back(sol, w):
    return dot2(jnp.where(own_mask(), sol, 0.0), w)


def ids_row(ids):
    lane = iota((8, NB), 1)
    row = jnp.full((8, NB), -1, I32)
    for s in range(S):
        for c in range(8):
            row = jnp.where(lane == NCL + 8 * s + c, ids[s, c], row)
    return row


def to_column(row):
    full = jnp.broadcast_to(row[:1], (NB, NB))
    eye = iota((NB, NB), 0) == iota((NB, NB), 1)
    return jnp.sum(jnp.where(eye, full, 0.0), axis=1, keepdims=True)


def write_message(msg, coef, cc, ids, scalars):
    row = ids_row(ids).astype(F32)
    col = to_column(row).astype(I32)
    c4 = coef[:8]
    hi, lo = split(c4)
    low = (c4 - hi.astype(F32) - lo.astype(F32)).astype(BF16)
    parts = jnp.concatenate([hi[:8], lo[:8], low[:8]], axis=0)
    ccp = dot2(jnp.where(iota((8, NB), 1) < NCL, c4, 0.0)[:, :NCL], cc[...])
    lane = iota((8, B), 1)
    extra = jnp.zeros((8, B), F32)
    for j, val in enumerate(scalars):
        extra = jnp.where(lane == 64 + j, val, extra)
    for k in range(NSUB):
        n = iota((NB, 2 * B), 1)
        onehot = jnp.where((col == n + CHUNK * k) & (n < CHUNK), 1.0, 0.0).astype(BF16)
        y = mm(parts, onehot)
        y = y[:8] + y[8:16] + y[16:24]
        first = y[:, :B]
        second = y[:, B:] + extra
        at = NCL * k
        tile, off = at // B, at % B
        here = ccp[:, tile * B : (tile + 1) * B]
        if off:
            here = pltpu.roll(here, B - off, 1)
            if off + NCL > B:
                after = pltpu.roll(ccp[:, (tile + 1) * B : (tile + 2) * B], B - off, 1)
                here = jnp.where(lane < B - off, here, after)
        third = jnp.where(lane < NCL, here, row)
        msg[k, :, 0:B] = first[:R]
        msg[k, :, B : 2 * B] = second[:R]
        msg[k, :, 2 * B : 3 * B] = third[:R]


def row_dot(a, b):
    return by_load(jnp.sum(a * b, axis=1, keepdims=True))


def k_start(ids, rhs, cb, kb, cc, signs, links, msg, w_out, v_out, sg_out, idx_out):
    for s in range(S):
        v_out[R * s : R * s + R, :] = rhs[s]
        sg_out[R * s : R * s + R, :] = jnp.broadcast_to(signs[s : s + 1, :].astype(F32), (R, D))
        w_out[KC * s : KC * s + KC, :] = cb[s]
        w_out[NCL + 8 * s : NCL + 8 * s + 8, :] = kb[s]
    pos = iota((8, B), 1).astype(BF16)
    for s in range(S):
        for b in range(3):
            q = links[s, b : b + 1, :]
            if b == 0 or (b == 2 and s % 2 == 0):
                hot = jnp.where(iota((B, B), 0) == q, 1.0, 0.0).astype(BF16)
                q = mm_t(pos, hot)[:1].astype(I32)
            idx_out[b, R * s : R * s + R, :] = jnp.broadcast_to(q, (R, B))
    v = v_out[...]
    coef = coefs(v, w_out[...])
    write_message(msg, coef, cc, ids, [row_dot(v, v)[:8]])


def k_rows(recv, out, csol):
    total = recv[0]
    for k in range(1, NSUB):
        total = total + recv[k]
    x = jnp.concatenate([total[:, :B], total[:, B : 2 * B]], axis=0)
    out[...] = jnp.broadcast_to(x[None], out.shape)
    csol[...] = jnp.where(iota((R, B), 1) < NCL, total[:, 2 * B :], 0.0)


def k_picked(recv, gc, hi_out, lo_out):
    lane = iota((8, B), 1)
    cols = []
    for half in range(2):
        ids = jnp.zeros((8, B), F32)
        for j in range(4):
            row = jnp.broadcast_to(recv[4 * half + j, 0:1, 2 * B : 3 * B], (8, B))
            ids = jnp.where(lane // 32 == j, pltpu.roll(row, (32 + 32 * j) % B, 1), ids)
        cols.append(ids[:1].astype(I32))
    ids = jnp.concatenate(cols, axis=1)
    n = iota((gc.shape[1], 2 * B), 0)
    onehot = jnp.where(n == ids, 1.0, 0.0).astype(BF16)
    gh, gl = split(gc[...])
    zero = jnp.zeros((2 * B - CHUNK, 2 * B), BF16)
    hi_out[0:CHUNK, :] = mm(gh, onehot).astype(BF16)
    hi_out[CHUNK : 2 * B, :] = zero
    lo_out[0:CHUNK, :] = mm(gl, onehot).astype(BF16)
    lo_out[CHUNK : 2 * B, :] = zero


def k_global(recv, gh, gl, msg, scal):
    total = jnp.sum(recv[...], axis=0)
    first = jnp.concatenate([total[:R], total[:R]], axis=0)
    second = jnp.concatenate([total[R:], total[R:]], axis=0)
    lane = iota((8, B), 1)
    x = jnp.concatenate([first, jnp.where(lane < 64, second, 0.0)], axis=1)
    xh, xl = split(x)
    y = mm(jnp.concatenate([xh, xl], axis=0), gh[...])
    y = y[:8] + y[8:] + mm(xh, gl[...])
    for k in range(NSUB):
        tile, j = k // 4, k % 4
        here = pltpu.roll(y[:, tile * B : (tile + 1) * B], (96 - 32 * j) % B, 1)
        msg[k] = jnp.where(lane < NCL, 0.0, here)[:R]
    scal[...] = jnp.concatenate([second, second], axis=0)


def solution_of(recv, csol):
    total = recv[0]
    for k in range(1, NSUB):
        total = total + recv[k]
    sol = total + csol[...]
    sol = jnp.concatenate([sol, sol], axis=0)
    return jnp.concatenate([sol, sol], axis=0)


def write_sends(v, idx, up, down, even, odd):
    def moved(b):
        return jnp.take_along_axis(v[:, b * B : (b + 1) * B], idx[b], axis=1)

    up[...] = moved(0)
    down[...] = moved(1)
    across = moved(2)
    for h in range(2):
        even[R * h : R * h + R, :] = across[8 * h : 8 * h + 4]
        odd[R * h : R * h + R, :] = across[8 * h + 4 : 8 * h + 8]


def received(from_next, from_prev, odd_in, even_in):
    across = jnp.concatenate(
        [odd_in[0:R, :], even_in[0:R, :], odd_in[R : 2 * R, :], even_in[R : 2 * R, :]], axis=0
    )
    return jnp.concatenate([from_next[...], from_prev[...], across], axis=1)


def k_first_direction(recv, csol, w, v, idx, d_out, up, down, even, odd):
    d = v[...] - spread_back(solution_of(recv, csol), w[...])
    d_out[...] = d
    write_sends(d, idx, up, down, even, odd)


def image_of(d, pi, sg, ops):
    spread = sg * (d + pi)
    low = spread.astype(BF16)
    image = jnp.zeros((ROWS, D), F32)
    row = iota((ROWS, D), 0) // R
    for s in range(S):
        image = jnp.where(row == s, mm(low, ops[s]), image)
    return sg * image, row_dot(spread, image)


def k_image(d, fn, fp, oi, ei, sg, ops, idx, signed_out, curv, up, down, even, odd):
    signed, c = image_of(d[...], received(fn, fp, oi, ei), sg[...], ops)
    signed_out[...] = signed
    curv[...] = jnp.broadcast_to(c[:8], (8, B))
    write_sends(signed, idx, up, down, even, odd)


def k_product(ids, signed, fn, fp, oi, ei, v, w, cc, curv, ap_out, msg):
    ap = signed[...] + received(fn, fp, oi, ei)
    ap_out[...] = ap
    scalars = [curv[...][:, :1], row_dot(v[...], ap)[:8], row_dot(ap, ap)[:8]]
    write_message(msg, coefs(ap, w[...]), cc, ids, scalars)


def scalar_at(scal, j):
    return jnp.sum(jnp.where(iota((ROWS, B), 1) == 64 + j, scal, 0.0), axis=1, keepdims=True)


def k_next_direction(recv, csol, scal0, scal1, w, d, ap, v, idx, r_out, x_out, d_out, up, down, even, odd):
    rho = scalar_at(scal0[...], 0)
    s1 = scal1[...]
    step = rho / scalar_at(s1, 0)
    rho_new = rho - 2.0 * step * scalar_at(s1, 1) + step * step * scalar_at(s1, 2)
    ap_ = ap[...]
    d0 = d[...]
    r_out[...] = v[...] - step * ap_
    x_out[...] = step * d0
    projected = d0 - step * (ap_ - spread_back(solution_of(recv, csol), w[...]))
    d1 = projected + (rho_new / rho) * d0
    d_out[...] = d1
    write_sends(d1, idx, up, down, even, odd)


def k_last_image(d, r, fn, fp, oi, ei, sg, ops, idx, signed_out, msg, up, down, even, odd):
    signed, c = image_of(d[...], received(fn, fp, oi, ei), sg[...], ops)
    rho = row_dot(r[...], r[...])
    signed_out[...] = signed
    lane = iota((8, B), 1)
    row = iota((8, B), 0)
    both = jnp.where(lane == row, c[:8], jnp.where(lane == row + R, rho[:8], 0.0))
    line = jnp.sum(jnp.where(row < R, both, 0.0), axis=0, keepdims=True)
    msg[...] = jnp.broadcast_to(line[None], msg.shape)
    write_sends(signed, idx, up, down, even, odd)


def k_total(recv, out):
    out[...] = jnp.broadcast_to(jnp.sum(recv[...], axis=0, keepdims=True), out.shape)


def k_finish(recv, signed, fn, fp, oi, ei, x, r, d, x_out, r_out):
    line = jnp.broadcast_to(jnp.sum(recv[...], axis=0), (ROWS, B))
    lane = iota((ROWS, B), 1)
    row = iota((ROWS, B), 0) % R
    curv = jnp.sum(jnp.where(lane == row, line, 0.0), axis=1, keepdims=True)
    rho = jnp.sum(jnp.where(lane == row + R, line, 0.0), axis=1, keepdims=True)
    step = rho / curv
    xn = x[...] + step * d[...]
    rn = r[...] - step * (signed[...] + received(fn, fp, oi, ei))
    for s in range(S):
        x_out[s] = xn[R * s : R * s + R]
        r_out[s] = rn[R * s : R * s + R]


def call(body, outs, *args, smem=()):
    specs = [
        pl.BlockSpec(memory_space=pltpu.SMEM if i in smem else pltpu.VMEM) for i in range(len(args))
    ]
    out_shape = tuple(jax.ShapeDtypeStruct(s, t) for s, t in outs)
    return pl.pallas_call(
        body,
        out_shape=out_shape,
        in_specs=specs,
        out_specs=tuple(pl.BlockSpec(memory_space=pltpu.VMEM) for _ in outs),
        name=body.__name__,
    )(*args)


def to_owner(x, axis):
    return lax.all_to_all(x, axis, 0, 0, tiled=True)


FIELD = ((ROWS, D), F32)
SENDS = (((ROWS, B), F32), ((ROWS, B), F32), ((2 * R, B), F32), ((2 * R, B), F32))


def exchange(up, down, even, odd, n_sub, n_cl):
    def ahead(n):
        return [(i, i + 1) for i in range(n - 1)]

    def back(n):
        return [(i + 1, i) for i in range(n - 1)]

    odd_in = lax.ppermute(odd, "cluster", back(n_cl))
    even_in = lax.ppermute(even, "cluster", ahead(n_cl))
    from_prev = lax.ppermute(up, "sub", ahead(n_sub))
    from_next = lax.ppermute(down, "sub", back(n_sub))
    return from_next, from_prev, odd_in, even_in


def local(rhs, operators, signs, links, cb, kb, ids, cluster_coarse, gc):
    n_sub = lax.axis_size("sub")
    n_cl = lax.axis_size("cluster")
    cc = cluster_coarse.reshape(NCL, NSUB * NCL)
    message = ((NSUB, R, D), F32)
    spread_rows = (((n_cl, 8, B), F32), ((R, B), F32))
    picked = ((2 * B, 2 * B), BF16)
    answer = (((NSUB, R, B), F32), ((ROWS, B), F32))

    msg, w, v, sg, idx = call(
        k_start,
        (message, ((NB, D), F32), FIELD, FIELD, ((3, ROWS, B), I32)),
        ids, rhs, cb, kb, cc, signs, links, smem=(0,),
    )
    recv = to_owner(msg, "sub")
    rows, csol = call(k_rows, spread_rows, recv)
    gh, gl = call(k_picked, (picked, picked), recv, gc)
    back, scal0 = call(k_global, answer, to_owner(rows, "cluster"), gh, gl)
    d, *sends = call(
        k_first_direction, (FIELD, *SENDS), to_owner(back, "sub"), csol, w, v, idx
    )
    got = exchange(*sends, n_sub, n_cl)
    signed, curv, *sends = call(
        k_image, (FIELD, ((8, B), F32), *SENDS), d, *got, sg, operators, idx
    )
    got = exchange(*sends, n_sub, n_cl)
    ap, msg = call(k_product, (FIELD, message), ids, signed, *got, v, w, cc, curv, smem=(0,))
    rows, csol = call(k_rows, spread_rows, to_owner(msg, "sub"))
    back, scal1 = call(k_global, answer, to_owner(rows, "cluster"), gh, gl)
    r, x, d1, *sends = call(
        k_next_direction,
        (FIELD, FIELD, FIELD, *SENDS),
        to_owner(back, "sub"), csol, scal0, scal1, w, d, ap, v, idx,
    )
    got = exchange(*sends, n_sub, n_cl)
    signed, msg, *sends = call(
        k_last_image, (FIELD, ((NSUB, 1, B), F32), *SENDS), d1, r, *got, sg, operators, idx
    )
    got = exchange(*sends, n_sub, n_cl)
    (line,) = call(k_total, (((n_cl, 1, B), F32),), to_owner(msg, "sub"))
    out = ((S, R, D), F32)
    return call(k_finish, (out, out), to_owner(line, "cluster"), signed, *got, x, r, d1)


def solution(mesh):
    both = ("cluster", "sub")
    in_specs = (
        P(both, None, None),
        P(both, None, None),
        P(both, None),
        P(both, None, None),
        P(both, None, None),
        P(both, None, None),
        P(both, None),
        P("cluster", "sub", None),
        P("sub", None),
    )
    out_specs = (P(both, None, None), P(both, None, None))
    return jax.shard_map(local, mesh=mesh, in_specs=in_specs, out_specs=out_specs, check_vma=False)
```

time: 401 us -> 224 us (0.56)
  the two profiles are of different devices: /device:TPU:1 before, /device:TPU:32 now
where the time goes in v1:
time: 224 us; the launch traced here: 223 us
  blocking collectives  75.2 us (34%)
  starting transfers between devices  73 us (33%)
  waiting for transfers between devices  43.4 us (19%)
  Pallas kernels  25.7 us (11%)
  local copies, waits for them, and re-layouts  4.38 us (2%)
    all_to_all x6, blocking collectives, to_owner(): return lax.all_to_all(x, axis, 0, 0, tiled=True)  75.2 us
    all_to_all x2, starting transfers between devices, to_owner(): return lax.all_to_all(x, axis, 0, 0, tiled=True)  30 us
    ppermute x4, waiting for transfers between devices, exchange(): even_in = lax.ppermute(even, 'cluster', ahead(n_cl))  26.3 us
    pallas_call x13, Pallas kernels, call(): pl.pallas_call(body, out_shape=out_shape, in_specs=specs, out_specs=tuple...  25.7 us
    all_to_all x2, waiting for transfers between devices, to_owner(): return lax.all_to_all(x, axis, 0, 0, tiled=True)  17.1 us
    ppermute x4, starting transfers between devices, exchange(): odd_in = lax.ppermute(odd, 'cluster', back(n_cl))  16 us
    ppermute x4, starting transfers between devices, exchange(): from_prev = lax.ppermute(up, 'sub', ahead(n_sub))  12.1 us
    ppermute x4, starting transfers between devices, exchange(): even_in = lax.ppermute(even, 'cluster', ahead(n_cl))  9.68 us
  transfers between devices with their start and end apart: 18, of which 5 were waited for; matrix products, arithmetic and copies ran while one was open for 0% of the time, Pallas kernels for 1%

profile of v1, /device:TPU:32, one launch (start us, length us, event | category | flops | bytes accessed | tf_op | source)
XLA Modules:
  0.0 222.7 jit_solution(2017515741776404292)
XLA Ops:
  0.6 1.3 copy.11.links
  1.9 2.3 %k_start.1 = (f32[8,4,384]{2,1,0:T(4,128)}, f32[128,384]{1,0:T(8,128)}, f32[16,384]{1,0:T(8,128)}, f32[16,384]{1,0:T(8,128)}, s32[3,16,128]{2,1,0:T(8,128)}) custom-call(s32[4,8]{1,0:T(4,128)} %ids.3, f32[4,4,384]{2,1,0:T(4,128)} %rhs.1, f32[4,24,384]{2,1,0:T(8,128)} %cb.1, f32[4,8,384]{2,1,0:T(8,128)} %kb.1, f32[96,768]{1,0:T(8,128)} %bitcast.1, ...), custom_call_target="tpu_custom_call" | custom-call | tf_op jit(solution)/shard_map/k_start/pallas_call | solution.py:300
  4.2 9.9 %all_to_all.40.recv = f32[8,4,384]{2,1,0:T(4,128)} all-to-all(f32[8,4,384]{2,1,0:T(4,128)} %get-tuple-element.43), channel_id=1, replica_groups=mesh['cluster'=96,'sub'=8] {'sub'}, dimensions={0} | all-to-all | bytes 98304 | tf_op jit(solution)/shard_map/all_to_all | solution.py:310
  14.1 1.6 k_rows.2
  15.7 21.6 %all-to-all-start.1 = ((f32[96,8,128]{2,1,0:T(8,128)}), f32[96,8,128]{2,1,0:T(8,128)S(1)}, u32[]{:S(2)}, u32[]{:S(2)}) async-start(f32[96,8,128]{2,1,0:T(8,128)} %get-tuple-element.44), calls=%async_computation.1 | async-start | bytes 786432 | tf_op jit(solution)/shard_map/all_to_all | solution.py:310
  37.4 2.6 %k_picked.1 = (bf16[256,256]{1,0:T(8,128)(2,1)}, bf16[256,256]{1,0:T(8,128)(2,1)}) custom-call(f32[8,4,384]{2,1,0:T(4,128)} %all_to_all.40.recv, f32[192,1536]{1,0:T(8,128)} %gc.1), custom_call_target="tpu_custom_call" | custom-call | tf_op jit(solution)/shard_map/k_picked/pallas_call | solution.py:300
  40.0 17.1 %all-to-all-done.1.recv = f32[96,8,128]{2,1,0:T(8,128)S(1)} async-done(((f32[96,8,128]{2,1,0:T(8,128)}), f32[96,8,128]{2,1,0:T(8,128)S(1)}, u32[]{:S(2)}, u32[]{:S(2)}) %all-to-all-start.1) | async-done | bytes 393248 | tf_op jit(solution)/shard_map/all_to_all | solution.py:310
  57.0 0.7 copy-done
  57.8 2.0 k_global.2
  59.8 9.3 %all_to_all.41.recv = f32[8,4,128]{2,1,0:T(4,128)} all-to-all(f32[8,4,128]{2,1,0:T(4,128)} %get-tuple-element.47), channel_id=1, replica_groups=mesh['cluster'=96,'sub'=8] {'sub'}, dimensions={0} | all-to-all | bytes 32768 | tf_op jit(solution)/shard_map/all_to_all | solution.py:310
  69.0 1.8 k_first_direction.1
  70.8 1.3 collective-permute-start
  72.1 3.0 %collective-permute-start.1 = (f32[16,128]{1,0:T(8,128)}, f32[16,128]{1,0:T(8,128)S(1)}, u32[]{:S(2)}, u32[]{:S(2)}) collective-permute-start(f32[16,128]{1,0:T(8,128)} %get-tuple-element.54), channel_id=1, source_target_pairs={{0,1},{1,2},{2,3},{3,4},{4,5},{5,6},{6,7},{8,9},{9,10},{10,11},{11... | collective-permute-start | bytes 24584 | tf_op jit(solution)/shard_map/ppermute | solution.py:326
  75.2 4.8 %collective-permute-start.2 = (f32[8,128]{1,0:T(8,128)}, f32[8,128]{1,0:T(8,128)S(1)}, u32[]{:S(2)}, u32[]{:S(2)}) collective-permute-start(f32[8,128]{1,0:T(8,128)} %get-tuple-element.55), channel_id=1, source_target_pairs={{8,0},{16,8},{24,16},{32,24},{40,32},{48,40},{56,48},{64,56},{72,6... | collective-permute-start | bytes 12296 | tf_op jit(solution)/shard_map/ppermute | solution.py:324
  79.9 1.9 collective-permute-start.3
  81.9 7.1 %collective-permute-done.3.ei = f32[8,128]{1,0:T(8,128)S(1)} collective-permute-done((f32[8,128]{1,0:T(8,128)}, f32[8,128]{1,0:T(8,128)S(1)}, u32[]{:S(2)}, u32[]{:S(2)}) %collective-permute-start.3) | collective-permute-done | bytes 4128 | tf_op jit(solution)/shard_map/ppermute | solution.py:325
  89.0 0.6 copy-done.12
  89.6 2.4 %k_image.1 = (f32[16,384]{1,0:T(8,128)}, f32[8,128]{1,0:T(8,128)}, f32[16,128]{1,0:T(8,128)}, f32[16,128]{1,0:T(8,128)}, f32[8,128]{1,0:T(8,128)}, /*index=5*/f32[8,128]{1,0:T(8,128)}) custom-call(f32[16,384]{1,0:T(8,128)} %get-tuple-element.52.d, f32[16,128]{1,0:T(8,128)} %copy-done.2, f32[16,128]{1,0:T(8,128)} %copy-done.4, f32[8,128]{1,0:T(8,128)} %copy-done.10, ...), custom_call_target="tpu_custom_call" | custom-call | tf_op jit(solution)/shard_map/k_image/pallas_call | solution.py:300
  92.0 1.3 collective-permute-start.4
  93.3 3.0 %collective-permute-start.5 = (f32[16,128]{1,0:T(8,128)}, f32[16,128]{1,0:T(8,128)S(1)}, u32[]{:S(2)}, u32[]{:S(2)}) collective-permute-start(f32[16,128]{1,0:T(8,128)} %get-tuple-element.60), channel_id=1, source_target_pairs={{0,1},{1,2},{2,3},{3,4},{4,5},{5,6},{6,7},{8,9},{9,10},{10,11},{11... | collective-permute-start | bytes 24584 | tf_op jit(solution)/shard_map/ppermute | solution.py:326
  96.3 1.9 collective-permute-start.6
  98.2 3.9 %collective-permute-start.7 = (f32[8,128]{1,0:T(8,128)}, f32[8,128]{1,0:T(8,128)S(1)}, u32[]{:S(2)}, u32[]{:S(2)}) collective-permute-start(f32[8,128]{1,0:T(8,128)} %get-tuple-element.62), channel_id=1, source_target_pairs={{0,8},{8,16},{16,24},{24,32},{32,40},{40,48},{48,56},{56,64},{64,7... | collective-permute-start | bytes 12296 | tf_op jit(solution)/shard_map/ppermute | solution.py:325
  102.2 5.1 %collective-permute-done.7.ei = f32[8,128]{1,0:T(8,128)S(1)} collective-permute-done((f32[8,128]{1,0:T(8,128)}, f32[8,128]{1,0:T(8,128)S(1)}, u32[]{:S(2)}, u32[]{:S(2)}) %collective-permute-start.7) | collective-permute-done | bytes 4128 | tf_op jit(solution)/shard_map/ppermute | solution.py:325
  107.3 0.6 copy-done.15
  107.9 2.2 k_product.1
  110.1 9.5 %all_to_all.42.recv = f32[8,4,384]{2,1,0:T(4,128)} all-to-all(f32[8,4,384]{2,1,0:T(4,128)} %get-tuple-element.64), channel_id=1, replica_groups=mesh['cluster'=96,'sub'=8] {'sub'}, dimensions={0} | all-to-all | bytes 98304 | tf_op jit(solution)/shard_map/all_to_all | solution.py:310
  119.6 1.6 k_rows.3
  121.2 28.1 %all_to_all.43.recv = f32[96,8,128]{2,1,0:T(8,128)} all-to-all(f32[96,8,128]{2,1,0:T(8,128)} %get-tuple-element.65), channel_id=1, replica_groups=mesh['cluster'=96,'sub'=8] {'cluster'}, dimensions={0} | all-to-all | bytes 786432 | tf_op jit(solution)/shard_map/all_to_all | solution.py:310
  149.3 2.0 k_global.3
  151.3 9.2 %all_to_all.44.recv = f32[8,4,128]{2,1,0:T(4,128)} all-to-all(f32[8,4,128]{2,1,0:T(4,128)} %get-tuple-element.66), channel_id=1, replica_groups=mesh['cluster'=96,'sub'=8] {'sub'}, dimensions={0} | all-to-all | bytes 32768 | tf_op jit(solution)/shard_map/all_to_all | solution.py:310
  160.5 1.9 k_next_direction.1
  162.4 1.3 collective-permute-start.8
  163.7 3.0 %collective-permute-start.9 = (f32[16,128]{1,0:T(8,128)}, f32[16,128]{1,0:T(8,128)S(1)}, u32[]{:S(2)}, u32[]{:S(2)}) collective-permute-start(f32[16,128]{1,0:T(8,128)} %get-tuple-element.74), channel_id=1, source_target_pairs={{0,1},{1,2},{2,3},{3,4},{4,5},{5,6},{6,7},{8,9},{9,10},{10,11},{11... | collective-permute-start | bytes 24584 | tf_op jit(solution)/shard_map/ppermute | solution.py:326
  166.7 4.8 %collective-permute-start.10 = (f32[8,128]{1,0:T(8,128)}, f32[8,128]{1,0:T(8,128)S(1)}, u32[]{:S(2)}, u32[]{:S(2)}) collective-permute-start(f32[8,128]{1,0:T(8,128)} %get-tuple-element.75), channel_id=1, source_target_pairs={{8,0},{16,8},{24,16},{32,24},{40,32},{48,40},{56,48},{64,56},{72,6... | collective-permute-start | bytes 12296 | tf_op jit(solution)/shard_map/ppermute | solution.py:324
  171.5 1.9 collective-permute-start.11
  173.5 7.1 %collective-permute-done.11.ei = f32[8,128]{1,0:T(8,128)S(1)} collective-permute-done((f32[8,128]{1,0:T(8,128)}, f32[8,128]{1,0:T(8,128)S(1)}, u32[]{:S(2)}, u32[]{:S(2)}) %collective-permute-start.11) | collective-permute-done | bytes 4128 | tf_op jit(solution)/shard_map/ppermute | solution.py:325
  180.6 0.6 copy-done.14
  181.1 2.4 %k_last_image.1 = (f32[16,384]{1,0:T(8,128)}, f32[8,1,128]{2,1,0:T(1,128)}, f32[16,128]{1,0:T(8,128)}, f32[16,128]{1,0:T(8,128)}, f32[8,128]{1,0:T(8,128)}, /*index=5*/f32[8,128]{1,0:T(8,128)}) custom-call(f32[16,384]{1,0:T(8,128)} %get-tuple-element.71.d, f32[16,384]{1,0:T(8,128)} %get-tuple-element.72.r, f32[16,128]{1,0:T(8,128)} %copy-done.3, ...), custom_call_target="tpu_custom_call" | custom-call | tf_op jit(solution)/shard_map/k_last_image/pallas_call | solution.py:300
  183.5 9.2 %all_to_all.45.recv = f32[8,1,128]{2,1,0:T(1,128)} all-to-all(f32[8,1,128]{2,1,0:T(1,128)} %get-tuple-element.77), channel_id=1, replica_groups=mesh['cluster'=96,'sub'=8] {'sub'}, dimensions={0} | all-to-all | bytes 8192 | tf_op jit(solution)/shard_map/all_to_all | solution.py:310
  192.7 1.3 k_total.1
  194.0 8.4 %all-to-all-start.7 = ((f32[96,1,128]{2,1,0:T(1,128)}), f32[96,1,128]{2,1,0:T(1,128)S(1)}, u32[]{:S(2)}, u32[]{:S(2)}) async-start(f32[96,1,128]{2,1,0:T(1,128)} %k_total.1), calls=%async_computation.7 | async-start | bytes 98304 | tf_op jit(solution)/shard_map/all_to_all | solution.py:310
  202.4 1.3 collective-permute-start.12
  203.7 3.0 %collective-permute-start.13 = (f32[16,128]{1,0:T(8,128)}, f32[16,128]{1,0:T(8,128)S(1)}, u32[]{:S(2)}, u32[]{:S(2)}) collective-permute-start(f32[16,128]{1,0:T(8,128)} %get-tuple-element.80), channel_id=1, source_target_pairs={{0,1},{1,2},{2,3},{3,4},{4,5},{5,6},{6,7},{8,9},{9,10},{10,11},{11... | collective-permute-start | bytes 24584 | tf_op jit(solution)/shard_map/ppermute | solution.py:326
  206.7 4.6 %collective-permute-start.14 = (f32[8,128]{1,0:T(8,128)}, f32[8,128]{1,0:T(8,128)S(1)}, u32[]{:S(2)}, u32[]{:S(2)}) collective-permute-start(f32[8,128]{1,0:T(8,128)} %get-tuple-element.81), channel_id=1, source_target_pairs={{8,0},{16,8},{24,16},{32,24},{40,32},{48,40},{56,48},{64,56},{72,6... | collective-permute-start | bytes 12296 | tf_op jit(solution)/shard_map/ppermute | solution.py:324
  211.3 1.9 collective-permute-start.15
  213.3 7.1 %collective-permute-done.15.ei = f32[8,128]{1,0:T(8,128)S(1)} collective-permute-done((f32[8,128]{1,0:T(8,128)}, f32[8,128]{1,0:T(8,128)S(1)}, u32[]{:S(2)}, u32[]{:S(2)}) %collective-permute-start.15) | collective-permute-done | bytes 4128 | tf_op jit(solution)/shard_map/ppermute | solution.py:325
  220.4 0.5 copy-done.17
  221.0 1.7 k_finish.1
  (44 shorter events, 0.2 us)
Async XLA Ops:
  15.7 41.3 %all-to-all-start.1 = ((f32[96,8,128]{2,1,0:T(8,128)}), f32[96,8,128]{2,1,0:T(8,128)S(1)}, u32[]{:S(2)}, u32[]{:S(2)}) async-start(f32[96,8,128]{2,1,0:T(8,128)} %get-tuple-element.44), calls=%async_computation.1 | async-start | bytes 786432 | tf_op jit(solution)/shard_map/all_to_all | solution.py:310
  57.0 0.7 copy-start
  70.8 18.1 %collective-permute-start = (f32[16,128]{1,0:T(8,128)}, f32[16,128]{1,0:T(8,128)S(1)}, u32[]{:S(2)}, u32[]{:S(2)}) collective-permute-start(f32[16,128]{1,0:T(8,128)} %get-tuple-element.53), channel_id=1, source_target_pairs={{1,0},{2,1},{3,2},{4,3},{5,4},{6,5},{7,6},{9,8},{10,9},{11,10},{12... | collective-permute-start | bytes 24584 | tf_op jit(solution)/shard_map/ppermute | solution.py:327
  72.1 16.9 %collective-permute-start.1 = (f32[16,128]{1,0:T(8,128)}, f32[16,128]{1,0:T(8,128)S(1)}, u32[]{:S(2)}, u32[]{:S(2)}) collective-permute-start(f32[16,128]{1,0:T(8,128)} %get-tuple-element.54), channel_id=1, source_target_pairs={{0,1},{1,2},{2,3},{3,4},{4,5},{5,6},{6,7},{8,9},{9,10},{10,11},{11... | collective-permute-start | bytes 24584 | tf_op jit(solution)/shard_map/ppermute | solution.py:326
  75.2 6.7 %collective-permute-start.2 = (f32[8,128]{1,0:T(8,128)}, f32[8,128]{1,0:T(8,128)S(1)}, u32[]{:S(2)}, u32[]{:S(2)}) collective-permute-start(f32[8,128]{1,0:T(8,128)} %get-tuple-element.55), channel_id=1, source_target_pairs={{8,0},{16,8},{24,16},{32,24},{40,32},{48,40},{56,48},{64,56},{72,6... | collective-permute-start | bytes 12296 | tf_op jit(solution)/shard_map/ppermute | solution.py:324
  79.9 9.0 %collective-permute-start.3 = (f32[8,128]{1,0:T(8,128)}, f32[8,128]{1,0:T(8,128)S(1)}, u32[]{:S(2)}, u32[]{:S(2)}) collective-permute-start(f32[8,128]{1,0:T(8,128)} %get-tuple-element.56), channel_id=1, source_target_pairs={{0,8},{8,16},{16,24},{24,32},{32,40},{40,48},{48,56},{56,64},{64,7... | collective-permute-start | bytes 12296 | tf_op jit(solution)/shard_map/ppermute | solution.py:325
  81.9 7.1 %copy-start.10 = (f32[8,128]{1,0:T(8,128)}, f32[8,128]{1,0:T(8,128)S(1)}, u32[]{:S(2)}) copy-start(f32[8,128]{1,0:T(8,128)S(1)} %collective-permute-done.2.oi) | copy-start | bytes 12292
  89.0 0.6 copy-start.12
  89.0 0.6 copy-start.2
  89.0 0.6 copy-start.4
  92.0 15.3 %collective-permute-start.4 = (f32[16,128]{1,0:T(8,128)}, f32[16,128]{1,0:T(8,128)S(1)}, u32[]{:S(2)}, u32[]{:S(2)}) collective-permute-start(f32[16,128]{1,0:T(8,128)} %get-tuple-element.59), channel_id=1, source_target_pairs={{1,0},{2,1},{3,2},{4,3},{5,4},{6,5},{7,6},{9,8},{10,9},{11,10},{12... | collective-permute-start | bytes 24584 | tf_op jit(solution)/shard_map/ppermute | solution.py:327
  93.3 14.0 %collective-permute-start.5 = (f32[16,128]{1,0:T(8,128)}, f32[16,128]{1,0:T(8,128)S(1)}, u32[]{:S(2)}, u32[]{:S(2)}) collective-permute-start(f32[16,128]{1,0:T(8,128)} %get-tuple-element.60), channel_id=1, source_target_pairs={{0,1},{1,2},{2,3},{3,4},{4,5},{5,6},{6,7},{8,9},{9,10},{10,11},{11... | collective-permute-start | bytes 24584 | tf_op jit(solution)/shard_map/ppermute | solution.py:326
  96.3 5.9 %collective-permute-start.6 = (f32[8,128]{1,0:T(8,128)}, f32[8,128]{1,0:T(8,128)S(1)}, u32[]{:S(2)}, u32[]{:S(2)}) collective-permute-start(f32[8,128]{1,0:T(8,128)} %get-tuple-element.61), channel_id=1, source_target_pairs={{8,0},{16,8},{24,16},{32,24},{40,32},{48,40},{56,48},{64,56},{72,6... | collective-permute-start | bytes 12296 | tf_op jit(solution)/shard_map/ppermute | solution.py:324
  98.2 9.0 %collective-permute-start.7 = (f32[8,128]{1,0:T(8,128)}, f32[8,128]{1,0:T(8,128)S(1)}, u32[]{:S(2)}, u32[]{:S(2)}) collective-permute-start(f32[8,128]{1,0:T(8,128)} %get-tuple-element.62), channel_id=1, source_target_pairs={{0,8},{8,16},{16,24},{24,32},{32,40},{40,48},{48,56},{56,64},{64,7... | collective-permute-start | bytes 12296 | tf_op jit(solution)/shard_map/ppermute | solution.py:325
  102.2 5.1 %copy-start.13 = (f32[8,128]{1,0:T(8,128)}, f32[8,128]{1,0:T(8,128)S(1)}, u32[]{:S(2)}) copy-start(f32[8,128]{1,0:T(8,128)S(1)} %collective-permute-done.6.oi) | copy-start | bytes 12292
  107.3 0.6 copy-start.15
  107.3 0.6 copy-start.5
  107.3 0.6 copy-start.7
  162.4 18.1 %collective-permute-start.8 = (f32[16,128]{1,0:T(8,128)}, f32[16,128]{1,0:T(8,128)S(1)}, u32[]{:S(2)}, u32[]{:S(2)}) collective-permute-start(f32[16,128]{1,0:T(8,128)} %get-tuple-element.73), channel_id=1, source_target_pairs={{1,0},{2,1},{3,2},{4,3},{5,4},{6,5},{7,6},{9,8},{10,9},{11,10},{12... | collective-permute-start | bytes 24584 | tf_op jit(solution)/shard_map/ppermute | solution.py:327
  163.7 16.9 %collective-permute-start.9 = (f32[16,128]{1,0:T(8,128)}, f32[16,128]{1,0:T(8,128)S(1)}, u32[]{:S(2)}, u32[]{:S(2)}) collective-permute-start(f32[16,128]{1,0:T(8,128)} %get-tuple-element.74), channel_id=1, source_target_pairs={{0,1},{1,2},{2,3},{3,4},{4,5},{5,6},{6,7},{8,9},{9,10},{10,11},{11... | collective-permute-start | bytes 24584 | tf_op jit(solution)/shard_map/ppermute | solution.py:326
  166.7 6.7 %collective-permute-start.10 = (f32[8,128]{1,0:T(8,128)}, f32[8,128]{1,0:T(8,128)S(1)}, u32[]{:S(2)}, u32[]{:S(2)}) collective-permute-start(f32[8,128]{1,0:T(8,128)} %get-tuple-element.75), channel_id=1, source_target_pairs={{8,0},{16,8},{24,16},{32,24},{40,32},{48,40},{56,48},{64,56},{72,6... | collective-permute-start | bytes 12296 | tf_op jit(solution)/shard_map/ppermute | solution.py:324
  171.5 9.0 %collective-permute-start.11 = (f32[8,128]{1,0:T(8,128)}, f32[8,128]{1,0:T(8,128)S(1)}, u32[]{:S(2)}, u32[]{:S(2)}) collective-permute-start(f32[8,128]{1,0:T(8,128)} %get-tuple-element.76), channel_id=1, source_target_pairs={{0,8},{8,16},{16,24},{24,32},{32,40},{40,48},{48,56},{56,64},{64,7... | collective-permute-start | bytes 12296 | tf_op jit(solution)/shard_map/ppermute | solution.py:325
  173.4 7.1 %copy-start.11 = (f32[8,128]{1,0:T(8,128)}, f32[8,128]{1,0:T(8,128)S(1)}, u32[]{:S(2)}) copy-start(f32[8,128]{1,0:T(8,128)S(1)} %collective-permute-done.10.oi) | copy-start | bytes 12292
  180.5 0.6 copy-start.14
  180.5 0.6 copy-start.3
  180.5 0.6 copy-start.6
  194.0 26.3 %all-to-all-start.7 = ((f32[96,1,128]{2,1,0:T(1,128)}), f32[96,1,128]{2,1,0:T(1,128)S(1)}, u32[]{:S(2)}, u32[]{:S(2)}) async-start(f32[96,1,128]{2,1,0:T(1,128)} %k_total.1), calls=%async_computation.7 | async-start | bytes 98304 | tf_op jit(solution)/shard_map/all_to_all | solution.py:310
  202.4 18.0 %collective-permute-start.12 = (f32[16,128]{1,0:T(8,128)}, f32[16,128]{1,0:T(8,128)S(1)}, u32[]{:S(2)}, u32[]{:S(2)}) collective-permute-start(f32[16,128]{1,0:T(8,128)} %get-tuple-element.79), channel_id=1, source_target_pairs={{1,0},{2,1},{3,2},{4,3},{5,4},{6,5},{7,6},{9,8},{10,9},{11,10},{12... | collective-permute-start | bytes 24584 | tf_op jit(solution)/shard_map/ppermute | solution.py:327
  203.7 16.7 %collective-permute-start.13 = (f32[16,128]{1,0:T(8,128)}, f32[16,128]{1,0:T(8,128)S(1)}, u32[]{:S(2)}, u32[]{:S(2)}) collective-permute-start(f32[16,128]{1,0:T(8,128)} %get-tuple-element.80), channel_id=1, source_target_pairs={{0,1},{1,2},{2,3},{3,4},{4,5},{5,6},{6,7},{8,9},{9,10},{10,11},{11... | collective-permute-start | bytes 24584 | tf_op jit(solution)/shard_map/ppermute | solution.py:326
  206.7 6.5 %collective-permute-start.14 = (f32[8,128]{1,0:T(8,128)}, f32[8,128]{1,0:T(8,128)S(1)}, u32[]{:S(2)}, u32[]{:S(2)}) collective-permute-start(f32[8,128]{1,0:T(8,128)} %get-tuple-element.81), channel_id=1, source_target_pairs={{8,0},{16,8},{24,16},{32,24},{40,32},{48,40},{56,48},{64,56},{72,6... | collective-permute-start | bytes 12296 | tf_op jit(solution)/shard_map/ppermute | solution.py:324
  211.3 9.0 %collective-permute-start.15 = (f32[8,128]{1,0:T(8,128)}, f32[8,128]{1,0:T(8,128)S(1)}, u32[]{:S(2)}, u32[]{:S(2)}) collective-permute-start(f32[8,128]{1,0:T(8,128)} %get-tuple-element.82), channel_id=1, source_target_pairs={{0,8},{8,16},{16,24},{24,32},{32,40},{40,48},{48,56},{56,64},{64,7... | collective-permute-start | bytes 12296 | tf_op jit(solution)/shard_map/ppermute | solution.py:325
  213.3 7.1 %copy-start.16 = (f32[8,128]{1,0:T(8,128)}, f32[8,128]{1,0:T(8,128)S(1)}, u32[]{:S(2)}) copy-start(f32[8,128]{1,0:T(8,128)S(1)} %collective-permute-done.14.oi) | copy-start | bytes 12292
  220.3 0.6 copy-start.17
  220.3 0.6 copy-start.8
  220.4 0.6 copy-start.9
  220.4 0.6 copy-start.1

commit v2 on v1

--- a/solution.py
+++ b/solution.py
@@ -18,6 +18,7 @@
 NCL = S * KC
 CHUNK = 192
 NSUB = 8
+VMEM_LIMIT = 16 * 2**20
 
 
 def iota(shape, dim):
@@ -169,6 +170,11 @@
     lo_out[CHUNK : 2 * B, :] = zero
 
 
+def k_first_rows(recv, gc, out, csol, hi_out, lo_out):
+    k_rows(recv, out, csol)
+    k_picked(recv, gc, hi_out, lo_out)
+
+
 def k_global(recv, gh, gl, msg, scal):
     total = jnp.sum(recv[...], axis=0)
     first = jnp.concatenate([total[:R], total[:R]], axis=0)
@@ -303,6 +309,7 @@
         in_specs=specs,
         out_specs=tuple(pl.BlockSpec(memory_space=pltpu.VMEM) for _ in outs),
         name=body.__name__,
+        compiler_params=pltpu.CompilerParams(vmem_limit_bytes=VMEM_LIMIT),
     )(*args)
 
 
@@ -343,8 +350,7 @@
         ids, rhs, cb, kb, cc, signs, links, smem=(0,),
     )
     recv = to_owner(msg, "sub")
-    rows, csol = call(k_rows, spread_rows, recv)
-    gh, gl = call(k_picked, (picked, picked), recv, gc)
+    rows, csol, gh, gl = call(k_first_rows, (*spread_rows, picked, picked), recv, gc)
     back, scal0 = call(k_global, answer, to_owner(rows, "cluster"), gh, gl)
     d, *sends = call(
         k_first_direction, (FIELD, *SENDS), to_owner(back, "sub"), csol, w, v, idx

time: 224 us -> 202 us (0.902)
  blocking collectives: 75.2 us -> 110 us
  starting transfers between devices: 73 us -> 51.4 us
  Pallas kernels: 25.7 us -> 6.23 us
  waiting for transfers between devices: 43.4 us -> 25.6 us
  local copies, waits for them, and re-layouts: 4.38 us -> 6.76 us
    all_to_all x6 -> x7, blocking collectives: 75.2 us -> 110 us  [to_owner(): return lax.all_to_all(x, axis, 0, 0, tiled=True)]
    all_to_all x2 -> x1, starting transfers between devices: 30 us -> 8.36 us  [to_owner(): return lax.all_to_all(x, axis, 0, 0, tiled=True)]
    pallas_call x13 -> x12, Pallas kernels: 25.7 us -> 6.23 us  [call(): pl.pallas_call(body, out_shape=out_shape, in_specs=specs, out_specs=tuple...]
    all_to_all x2 -> x1, waiting for transfers between devices: 17.1 us -> 0.01 us  [to_owner(): return lax.all_to_all(x, axis, 0, 0, tiled=True)]
    unnamed x37 -> x21, local copies, waits for them, and re-layouts: 4.38 us -> 6.76 us
  transfers between devices with their start and end apart: 18 -> 17, of which waited for: 5 -> 4; matrix products, arithmetic and copies ran while one was open for 0% -> 0% of each run, Pallas kernels for 1% -> 0%
where the time goes in v2:
time: 202 us; the launch traced here: 201 us
  blocking collectives  110 us (54%)
  starting transfers between devices  51.4 us (25%)
  waiting for transfers between devices  25.6 us (13%)
  local copies, waits for them, and re-layouts  6.76 us (3%)
  Pallas kernels  6.23 us (3%)
    all_to_all x7, blocking collectives, to_owner(): return lax.all_to_all(x, axis, 0, 0, tiled=True)  110 us
    ppermute x4, waiting for transfers between devices, exchange(): even_in = lax.ppermute(even, 'cluster', ahead(n_cl))  25.5 us
    ppermute x4, starting transfers between devices, exchange(): odd_in = lax.ppermute(odd, 'cluster', back(n_cl))  16 us
    ppermute x4, starting transfers between devices, exchange(): from_prev = lax.ppermute(up, 'sub', ahead(n_sub))  12.1 us
    ppermute x4, starting transfers between devices, exchange(): even_in = lax.ppermute(even, 'cluster', ahead(n_cl))  9.68 us
    all_to_all x1, starting transfers between devices, to_owner(): return lax.all_to_all(x, axis, 0, 0, tiled=True)  8.36 us
    unnamed x21, local copies, waits for them, and re-layouts  6.76 us
    pallas_call x12, Pallas kernels, call(): pl.pallas_call(body, out_shape=out_shape, in_specs=specs, out_specs=tuple...  6.23 us
  transfers between devices with their start and end apart: 17, of which 4 were waited for; matrix products, arithmetic and copies ran while one was open for 0% of the time, Pallas kernels for 0%

profile of v2, /device:TPU:32, one launch (start us, length us, event | category | flops | bytes accessed | tf_op | source)
XLA Modules:
  0.0 201.0 jit_solution(1094061105364978289)
XLA Ops:
  0.6 0.7 copy.11.links
  1.3 1.0 copy-done.2
  2.3 0.9 copy-done.4
  3.2 0.8 copy-done.5
  4.0 0.7 copy-done.6
  4.7 0.7 copy-done.7
  5.4 0.7 copy-done.9
  6.1 1.2 k_start.1
  7.3 9.6 %all_to_all.40.recv = f32[8,4,384]{2,1,0:T(4,128)S(1)} all-to-all(f32[8,4,384]{2,1,0:T(4,128)S(1)} %get-tuple-element.43), channel_id=1, replica_groups=mesh['cluster'=96,'sub'=8] {'sub'}, dimensions={0} | all-to-all | bytes 98304 | tf_op jit(solution)/shard_map/all_to_all | solution.py:317
  16.9 1.3 copy-done.1
  18.2 0.6 k_first_rows.1
  18.8 0.0 copy-start
  18.8 41.2 %all_to_all.41.recv = f32[96,8,128]{2,1,0:T(8,128)S(1)} all-to-all(f32[96,8,128]{2,1,0:T(8,128)S(1)} %get-tuple-element.44), channel_id=1, replica_groups=mesh['cluster'=96,'sub'=8] {'cluster'}, dimensions={0} | all-to-all | bytes 786432 | tf_op jit(solution)/shard_map/all_to_all | solution.py:317
  60.0 0.3 k_global.2
  60.3 7.7 %all_to_all.42.recv = f32[8,4,128]{2,1,0:T(4,128)S(1)} all-to-all(f32[8,4,128]{2,1,0:T(4,128)S(1)} %get-tuple-element.47), channel_id=1, replica_groups=mesh['cluster'=96,'sub'=8] {'sub'}, dimensions={0} | all-to-all | bytes 32768 | tf_op jit(solution)/shard_map/all_to_all | solution.py:317
  68.0 0.2 k_first_direction.1
  68.2 1.3 collective-permute-start
  69.5 3.0 %collective-permute-start.1 = (f32[16,128]{1,0:T(8,128)S(1)}, f32[16,128]{1,0:T(8,128)S(1)}, u32[]{:S(2)}, u32[]{:S(2)}) collective-permute-start(f32[16,128]{1,0:T(8,128)S(1)} %get-tuple-element.54), channel_id=1, source_target_pairs={{0,1},{1,2},{2,3},{3,4},{4,5},{5,6},{6,7},{8,9},{9,10},{10,11},{11... | collective-permute-start | bytes 24584 | tf_op jit(solution)/shard_map/ppermute | solution.py:333
  72.6 4.8 %collective-permute-start.2 = (f32[8,128]{1,0:T(8,128)S(1)}, f32[8,128]{1,0:T(8,128)S(1)}, u32[]{:S(2)}, u32[]{:S(2)}) collective-permute-start(f32[8,128]{1,0:T(8,128)S(1)} %get-tuple-element.55), channel_id=1, source_target_pairs={{8,0},{16,8},{24,16},{32,24},{40,32},{48,40},{56,48},{64,56},{72,6... | collective-permute-start | bytes 12296 | tf_op jit(solution)/shard_map/ppermute | solution.py:331
  77.4 1.9 collective-permute-start.3
  79.3 6.9 %collective-permute-done.3.ei = f32[8,128]{1,0:T(8,128)S(1)} collective-permute-done((f32[8,128]{1,0:T(8,128)S(1)}, f32[8,128]{1,0:T(8,128)S(1)}, u32[]{:S(2)}, u32[]{:S(2)}) %collective-permute-start.3) | collective-permute-done | bytes 4128 | tf_op jit(solution)/shard_map/ppermute | solution.py:332
  86.2 0.4 k_image.1
  86.6 1.3 collective-permute-start.4
  87.9 3.0 %collective-permute-start.5 = (f32[16,128]{1,0:T(8,128)S(1)}, f32[16,128]{1,0:T(8,128)S(1)}, u32[]{:S(2)}, u32[]{:S(2)}) collective-permute-start(f32[16,128]{1,0:T(8,128)S(1)} %get-tuple-element.60), channel_id=1, source_target_pairs={{0,1},{1,2},{2,3},{3,4},{4,5},{5,6},{6,7},{8,9},{9,10},{10,11},{11... | collective-permute-start | bytes 24584 | tf_op jit(solution)/shard_map/ppermute | solution.py:333
  91.0 1.9 collective-permute-start.6
  92.9 3.9 %collective-permute-start.7 = (f32[8,128]{1,0:T(8,128)S(1)}, f32[8,128]{1,0:T(8,128)S(1)}, u32[]{:S(2)}, u32[]{:S(2)}) collective-permute-start(f32[8,128]{1,0:T(8,128)S(1)} %get-tuple-element.62), channel_id=1, source_target_pairs={{0,8},{8,16},{16,24},{24,32},{32,40},{40,48},{48,56},{56,64},{64,7... | collective-permute-start | bytes 12296 | tf_op jit(solution)/shard_map/ppermute | solution.py:332
  96.8 4.9 %collective-permute-done.7.ei = f32[8,128]{1,0:T(8,128)S(1)} collective-permute-done((f32[8,128]{1,0:T(8,128)S(1)}, f32[8,128]{1,0:T(8,128)S(1)}, u32[]{:S(2)}, u32[]{:S(2)}) %collective-permute-start.7) | collective-permute-done | bytes 4128 | tf_op jit(solution)/shard_map/ppermute | solution.py:332
  101.7 1.1 k_product.1
  102.8 8.2 %all_to_all.43.recv = f32[8,4,384]{2,1,0:T(4,128)S(1)} all-to-all(f32[8,4,384]{2,1,0:T(4,128)S(1)} %get-tuple-element.64), channel_id=1, replica_groups=mesh['cluster'=96,'sub'=8] {'sub'}, dimensions={0} | all-to-all | bytes 98304 | tf_op jit(solution)/shard_map/all_to_all | solution.py:317
  111.0 27.8 %all_to_all.44.recv = f32[96,8,128]{2,1,0:T(8,128)S(1)} all-to-all(f32[96,8,128]{2,1,0:T(8,128)S(1)} %get-tuple-element.65), channel_id=1, replica_groups=mesh['cluster'=96,'sub'=8] {'cluster'}, dimensions={0} | all-to-all | bytes 786432 | tf_op jit(solution)/shard_map/all_to_all | solution.py:317
  138.8 0.3 k_global.3
  139.1 7.7 %all_to_all.45.recv = f32[8,4,128]{2,1,0:T(4,128)S(1)} all-to-all(f32[8,4,128]{2,1,0:T(4,128)S(1)} %get-tuple-element.66), channel_id=1, replica_groups=mesh['cluster'=96,'sub'=8] {'sub'}, dimensions={0} | all-to-all | bytes 32768 | tf_op jit(solution)/shard_map/all_to_all | solution.py:317
  146.9 0.2 k_next_direction.1
  147.1 1.3 collective-permute-start.8
  148.4 3.0 %collective-permute-start.9 = (f32[16,128]{1,0:T(8,128)S(1)}, f32[16,128]{1,0:T(8,128)S(1)}, u32[]{:S(2)}, u32[]{:S(2)}) collective-permute-start(f32[16,128]{1,0:T(8,128)S(1)} %get-tuple-element.74), channel_id=1, source_target_pairs={{0,1},{1,2},{2,3},{3,4},{4,5},{5,6},{6,7},{8,9},{9,10},{10,11},{11... | collective-permute-start | bytes 24584 | tf_op jit(solution)/shard_map/ppermute | solution.py:333
  151.4 4.8 %collective-permute-start.10 = (f32[8,128]{1,0:T(8,128)S(1)}, f32[8,128]{1,0:T(8,128)S(1)}, u32[]{:S(2)}, u32[]{:S(2)}) collective-permute-start(f32[8,128]{1,0:T(8,128)S(1)} %get-tuple-element.75), channel_id=1, source_target_pairs={{8,0},{16,8},{24,16},{32,24},{40,32},{48,40},{56,48},{64,56},{72,6... | collective-permute-start | bytes 12296 | tf_op jit(solution)/shard_map/ppermute | solution.py:331
  156.2 1.9 collective-permute-start.11
  158.1 6.9 %collective-permute-done.11.ei = f32[8,128]{1,0:T(8,128)S(1)} collective-permute-done((f32[8,128]{1,0:T(8,128)S(1)}, f32[8,128]{1,0:T(8,128)S(1)}, u32[]{:S(2)}, u32[]{:S(2)}) %collective-permute-start.11) | collective-permute-done | bytes 4128 | tf_op jit(solution)/shard_map/ppermute | solution.py:332
  165.0 0.4 k_last_image.1
  165.5 7.9 %all_to_all.46.recv = f32[8,1,128]{2,1,0:T(1,128)S(1)} all-to-all(f32[8,1,128]{2,1,0:T(1,128)S(1)} %get-tuple-element.77), channel_id=1, replica_groups=mesh['cluster'=96,'sub'=8] {'sub'}, dimensions={0} | all-to-all | bytes 8192 | tf_op jit(solution)/shard_map/all_to_all | solution.py:317
  173.4 0.6 k_total.1
  174.1 8.4 %all-to-all-start.7 = ((f32[96,1,128]{2,1,0:T(1,128)}), f32[96,1,128]{2,1,0:T(1,128)S(1)}, u32[]{:S(2)}, u32[]{:S(2)}) async-start(f32[96,1,128]{2,1,0:T(1,128)} %k_total.1), calls=%async_computation.7 | async-start | bytes 98304 | tf_op jit(solution)/shard_map/all_to_all | solution.py:317
  182.4 1.3 collective-permute-start.12
  183.7 3.0 %collective-permute-start.13 = (f32[16,128]{1,0:T(8,128)S(1)}, f32[16,128]{1,0:T(8,128)S(1)}, u32[]{:S(2)}, u32[]{:S(2)}) collective-permute-start(f32[16,128]{1,0:T(8,128)S(1)} %get-tuple-element.80), channel_id=1, source_target_pairs={{0,1},{1,2},{2,3},{3,4},{4,5},{5,6},{6,7},{8,9},{9,10},{10,11},{11... | collective-permute-start | bytes 24584 | tf_op jit(solution)/shard_map/ppermute | solution.py:333
  186.8 4.6 %collective-permute-start.14 = (f32[8,128]{1,0:T(8,128)S(1)}, f32[8,128]{1,0:T(8,128)S(1)}, u32[]{:S(2)}, u32[]{:S(2)}) collective-permute-start(f32[8,128]{1,0:T(8,128)S(1)} %get-tuple-element.81), channel_id=1, source_target_pairs={{8,0},{16,8},{24,16},{32,24},{40,32},{48,40},{56,48},{64,56},{72,6... | collective-permute-start | bytes 12296 | tf_op jit(solution)/shard_map/ppermute | solution.py:331
  191.3 1.9 collective-permute-start.15
  193.3 6.9 %collective-permute-done.15.ei = f32[8,128]{1,0:T(8,128)S(1)} collective-permute-done((f32[8,128]{1,0:T(8,128)S(1)}, f32[8,128]{1,0:T(8,128)S(1)}, u32[]{:S(2)}, u32[]{:S(2)}) %collective-permute-start.15) | collective-permute-done | bytes 4128 | tf_op jit(solution)/shard_map/ppermute | solution.py:332
  200.2 0.8 k_finish.1
  (26 shorter events, 0.1 us)
Async XLA Ops:
  1.3 1.0 copy-start.2
  2.3 0.9 copy-start.4
  3.2 0.8 copy-start.5
  4.0 0.7 copy-start.6
  4.7 0.7 copy-start.7
  5.4 0.7 copy-start.9
  16.9 1.3 copy-start.1
  18.8 67.4 %copy-start = (bf16[4,384,384]{2,1,0:T(8,128)(2,1)S(1)}, bf16[4,384,384]{2,1,0:T(8,128)(2,1)}, u32[]{:S(2)}) copy-start(bf16[4,384,384]{2,1,0:T(8,128)(2,1)} %ops.3) | copy-start | bytes 3538948
  60.0 41.7 %copy-start.3 = (f32[1,96,768]{2,1,0:T(8,128)S(1)}, f32[1,96,768]{2,1,0:T(8,128)}, u32[]{:S(2)}) copy-start(f32[1,96,768]{2,1,0:T(8,128)} %param.16) | copy-start | bytes 884740
  60.0 41.7 %copy-start.8 = (s32[4,8]{1,0:T(4,128)S(1)}, s32[4,8]{1,0:T(4,128)}, u32[]{:S(2)}) copy-start(s32[4,8]{1,0:T(4,128)} %ids.3) | copy-start | bytes 388
  68.2 17.9 %collective-permute-start = (f32[16,128]{1,0:T(8,128)S(1)}, f32[16,128]{1,0:T(8,128)S(1)}, u32[]{:S(2)}, u32[]{:S(2)}) collective-permute-start(f32[16,128]{1,0:T(8,128)S(1)} %get-tuple-element.53), channel_id=1, source_target_pairs={{1,0},{2,1},{3,2},{4,3},{5,4},{6,5},{7,6},{9,8},{10,9},{11,10},{12... | collective-permute-start | bytes 24584 | tf_op jit(solution)/shard_map/ppermute | solution.py:334
  69.5 16.6 %collective-permute-start.1 = (f32[16,128]{1,0:T(8,128)S(1)}, f32[16,128]{1,0:T(8,128)S(1)}, u32[]{:S(2)}, u32[]{:S(2)}) collective-permute-start(f32[16,128]{1,0:T(8,128)S(1)} %get-tuple-element.54), channel_id=1, source_target_pairs={{0,1},{1,2},{2,3},{3,4},{4,5},{5,6},{6,7},{8,9},{9,10},{10,11},{11... | collective-permute-start | bytes 24584 | tf_op jit(solution)/shard_map/ppermute | solution.py:333
  72.6 6.7 %collective-permute-start.2 = (f32[8,128]{1,0:T(8,128)S(1)}, f32[8,128]{1,0:T(8,128)S(1)}, u32[]{:S(2)}, u32[]{:S(2)}) collective-permute-start(f32[8,128]{1,0:T(8,128)S(1)} %get-tuple-element.55), channel_id=1, source_target_pairs={{8,0},{16,8},{24,16},{32,24},{40,32},{48,40},{56,48},{64,56},{72,6... | collective-permute-start | bytes 12296 | tf_op jit(solution)/shard_map/ppermute | solution.py:331
  77.4 8.8 %collective-permute-start.3 = (f32[8,128]{1,0:T(8,128)S(1)}, f32[8,128]{1,0:T(8,128)S(1)}, u32[]{:S(2)}, u32[]{:S(2)}) collective-permute-start(f32[8,128]{1,0:T(8,128)S(1)} %get-tuple-element.56), channel_id=1, source_target_pairs={{0,8},{8,16},{16,24},{24,32},{32,40},{40,48},{48,56},{56,64},{64,7... | collective-permute-start | bytes 12296 | tf_op jit(solution)/shard_map/ppermute | solution.py:332
  86.6 15.1 %collective-permute-start.4 = (f32[16,128]{1,0:T(8,128)S(1)}, f32[16,128]{1,0:T(8,128)S(1)}, u32[]{:S(2)}, u32[]{:S(2)}) collective-permute-start(f32[16,128]{1,0:T(8,128)S(1)} %get-tuple-element.59), channel_id=1, source_target_pairs={{1,0},{2,1},{3,2},{4,3},{5,4},{6,5},{7,6},{9,8},{10,9},{11,10},{12... | collective-permute-start | bytes 24584 | tf_op jit(solution)/shard_map/ppermute | solution.py:334
  87.9 13.8 %collective-permute-start.5 = (f32[16,128]{1,0:T(8,128)S(1)}, f32[16,128]{1,0:T(8,128)S(1)}, u32[]{:S(2)}, u32[]{:S(2)}) collective-permute-start(f32[16,128]{1,0:T(8,128)S(1)} %get-tuple-element.60), channel_id=1, source_target_pairs={{0,1},{1,2},{2,3},{3,4},{4,5},{5,6},{6,7},{8,9},{9,10},{10,11},{11... | collective-permute-start | bytes 24584 | tf_op jit(solution)/shard_map/ppermute | solution.py:333
  91.0 5.9 %collective-permute-start.6 = (f32[8,128]{1,0:T(8,128)S(1)}, f32[8,128]{1,0:T(8,128)S(1)}, u32[]{:S(2)}, u32[]{:S(2)}) collective-permute-start(f32[8,128]{1,0:T(8,128)S(1)} %get-tuple-element.61), channel_id=1, source_target_pairs={{8,0},{16,8},{24,16},{32,24},{40,32},{48,40},{56,48},{64,56},{72,6... | collective-permute-start | bytes 12296 | tf_op jit(solution)/shard_map/ppermute | solution.py:331
  92.9 8.8 %collective-permute-start.7 = (f32[8,128]{1,0:T(8,128)S(1)}, f32[8,128]{1,0:T(8,128)S(1)}, u32[]{:S(2)}, u32[]{:S(2)}) collective-permute-start(f32[8,128]{1,0:T(8,128)S(1)} %get-tuple-element.62), channel_id=1, source_target_pairs={{0,8},{8,16},{16,24},{24,32},{32,40},{40,48},{48,56},{56,64},{64,7... | collective-permute-start | bytes 12296 | tf_op jit(solution)/shard_map/ppermute | solution.py:332
  147.1 17.9 %collective-permute-start.8 = (f32[16,128]{1,0:T(8,128)S(1)}, f32[16,128]{1,0:T(8,128)S(1)}, u32[]{:S(2)}, u32[]{:S(2)}) collective-permute-start(f32[16,128]{1,0:T(8,128)S(1)} %get-tuple-element.73), channel_id=1, source_target_pairs={{1,0},{2,1},{3,2},{4,3},{5,4},{6,5},{7,6},{9,8},{10,9},{11,10},{12... | collective-permute-start | bytes 24584 | tf_op jit(solution)/shard_map/ppermute | solution.py:334
  148.4 16.6 %collective-permute-start.9 = (f32[16,128]{1,0:T(8,128)S(1)}, f32[16,128]{1,0:T(8,128)S(1)}, u32[]{:S(2)}, u32[]{:S(2)}) collective-permute-start(f32[16,128]{1,0:T(8,128)S(1)} %get-tuple-element.74), channel_id=1, source_target_pairs={{0,1},{1,2},{2,3},{3,4},{4,5},{5,6},{6,7},{8,9},{9,10},{10,11},{11... | collective-permute-start | bytes 24584 | tf_op jit(solution)/shard_map/ppermute | solution.py:333
  151.4 6.7 %collective-permute-start.10 = (f32[8,128]{1,0:T(8,128)S(1)}, f32[8,128]{1,0:T(8,128)S(1)}, u32[]{:S(2)}, u32[]{:S(2)}) collective-permute-start(f32[8,128]{1,0:T(8,128)S(1)} %get-tuple-element.75), channel_id=1, source_target_pairs={{8,0},{16,8},{24,16},{32,24},{40,32},{48,40},{56,48},{64,56},{72,6... | collective-permute-start | bytes 12296 | tf_op jit(solution)/shard_map/ppermute | solution.py:331
  156.2 8.8 %collective-permute-start.11 = (f32[8,128]{1,0:T(8,128)S(1)}, f32[8,128]{1,0:T(8,128)S(1)}, u32[]{:S(2)}, u32[]{:S(2)}) collective-permute-start(f32[8,128]{1,0:T(8,128)S(1)} %get-tuple-element.76), channel_id=1, source_target_pairs={{0,8},{8,16},{16,24},{24,32},{32,40},{40,48},{48,56},{56,64},{64,7... | collective-permute-start | bytes 12296 | tf_op jit(solution)/shard_map/ppermute | solution.py:332
  174.1 26.1 %all-to-all-start.7 = ((f32[96,1,128]{2,1,0:T(1,128)}), f32[96,1,128]{2,1,0:T(1,128)S(1)}, u32[]{:S(2)}, u32[]{:S(2)}) async-start(f32[96,1,128]{2,1,0:T(1,128)} %k_total.1), calls=%async_computation.7 | async-start | bytes 98304 | tf_op jit(solution)/shard_map/all_to_all | solution.py:317
  182.4 17.7 %collective-permute-start.12 = (f32[16,128]{1,0:T(8,128)S(1)}, f32[16,128]{1,0:T(8,128)S(1)}, u32[]{:S(2)}, u32[]{:S(2)}) collective-permute-start(f32[16,128]{1,0:T(8,128)S(1)} %get-tuple-element.79), channel_id=1, source_target_pairs={{1,0},{2,1},{3,2},{4,3},{5,4},{6,5},{7,6},{9,8},{10,9},{11,10},{12... | collective-permute-start | bytes 24584 | tf_op jit(solution)/shard_map/ppermute | solution.py:334
  183.7 16.4 %collective-permute-start.13 = (f32[16,128]{1,0:T(8,128)S(1)}, f32[16,128]{1,0:T(8,128)S(1)}, u32[]{:S(2)}, u32[]{:S(2)}) collective-permute-start(f32[16,128]{1,0:T(8,128)S(1)} %get-tuple-element.80), channel_id=1, source_target_pairs={{0,1},{1,2},{2,3},{3,4},{4,5},{5,6},{6,7},{8,9},{9,10},{10,11},{11... | collective-permute-start | bytes 24584 | tf_op jit(solution)/shard_map/ppermute | solution.py:333
  186.8 6.5 %collective-permute-start.14 = (f32[8,128]{1,0:T(8,128)S(1)}, f32[8,128]{1,0:T(8,128)S(1)}, u32[]{:S(2)}, u32[]{:S(2)}) collective-permute-start(f32[8,128]{1,0:T(8,128)S(1)} %get-tuple-element.81), channel_id=1, source_target_pairs={{8,0},{16,8},{24,16},{32,24},{40,32},{48,40},{56,48},{64,56},{72,6... | collective-permute-start | bytes 12296 | tf_op jit(solution)/shard_map/ppermute | solution.py:331
  191.3 8.8 %collective-permute-start.15 = (f32[8,128]{1,0:T(8,128)S(1)}, f32[8,128]{1,0:T(8,128)S(1)}, u32[]{:S(2)}, u32[]{:S(2)}) collective-permute-start(f32[8,128]{1,0:T(8,128)S(1)} %get-tuple-element.82), channel_id=1, source_target_pairs={{0,8},{8,16},{16,24},{24,32},{32,40},{40,48},{48,56},{56,64},{64,7... | collective-permute-start | bytes 12296 | tf_op jit(solution)/shard_map/ppermute | solution.py:332

commit v3 on v2

v3 whole, which is shorter than its diff:
```python
import jax
import jax.numpy as jnp
from jax import lax
from jax.experimental import pallas as pl
from jax.experimental.pallas import tpu as pltpu
from jax.sharding import PartitionSpec as P

F32 = jnp.float32
BF16 = jnp.bfloat16
I32 = jnp.int32
R = 4
S = 4
ROWS = R * S
B = 128
D = 384
KC = 24
NB = 128
NCL = S * KC
CHUNK = 192
NSUB = 8
VMEM_LIMIT = 16 * 2**20


def iota(shape, dim):
    return lax.broadcasted_iota(I32, shape, dim)


def split(x):
    hi = x.astype(BF16)
    return hi, (x - hi.astype(F32)).astype(BF16)


def mm(a, b):
    return lax.dot_general(a, b, (((1,), (0,)), ((), ())), preferred_element_type=F32)


def mm_t(a, b):
    return lax.dot_general(a, b, (((1,), (1,)), ((), ())), preferred_element_type=F32)


def dot2(x, w, f=mm):
    n = x.shape[0]
    xh, xl = split(x)
    wh, wl = split(w)
    xs = jnp.concatenate([xh, xl], axis=0)
    both = f(xs, wh)
    return both[:n] + both[n:] + f(xh, wl)


def lanes_of_sub(shape):
    lane = iota(shape, 1)
    return jnp.where(lane < NCL, lane // KC, (lane - NCL) // 8)


def own_mask():
    return iota((ROWS, NB), 0) // R == lanes_of_sub((ROWS, NB))


def by_load(x):
    y = x[:8] + x[8:]
    y = y + pltpu.roll(y, 4, 0)
    return jnp.concatenate([y, y], axis=0)


def coefs(v, w):
    return by_load(jnp.where(own_mask(), dot2(v, w, mm_t), 0.0))


def spread_back(sol, w):
    return dot2(jnp.where(own_mask(), sol, 0.0), w)


def ids_row(ids):
    lane = iota((8, NB), 1)
    row = jnp.full((8, NB), -1, I32)
    for s in range(S):
        for c in range(8):
            row = jnp.where(lane == NCL + 8 * s + c, ids[s, c], row)
    return row


def to_column(row):
    full = jnp.broadcast_to(row[:1], (NB, NB))
    eye = iota((NB, NB), 0) == iota((NB, NB), 1)
    return jnp.sum(jnp.where(eye, full, 0.0), axis=1, keepdims=True)


def window(x, at, width):
    lane = iota((x.shape[0], B), 1)
    tile, off = at // B, at % B
    here = x[:, tile * B : (tile + 1) * B]
    if off:
        here = pltpu.roll(here, B - off, 1)
        if off + width > B:
            after = pltpu.roll(x[:, (tile + 1) * B : (tile + 2) * B], B - off, 1)
            here = jnp.where(lane < B - off, here, after)
    return here


MSG = 5 * B


def write_message(msg, coef, cc, ids, scalars, across_ids=None):
    row = ids_row(ids).astype(F32)
    col = to_column(row).astype(I32)
    c4 = coef[:8]
    hi, lo = split(c4)
    low = (c4 - hi.astype(F32) - lo.astype(F32)).astype(BF16)
    parts = jnp.concatenate([hi, lo, low], axis=0)
    ccp = dot2(jnp.where(iota((8, NB), 1) < NCL, c4, 0.0)[:, :NCL], cc[...])
    lane = iota((8, B), 1)
    extra = jnp.zeros((8, B), F32)
    for j, val in enumerate(scalars):
        extra = jnp.where(lane == 64 + j, val, extra)
    if across_ids is None:
        tail = jnp.zeros((8, B), F32)
    else:
        tail = jnp.where(iota((8, B), 0) == 0, row, across_ids)
    none = jnp.zeros((8, B), F32)
    cluster = [jnp.where(lane < NCL, window(ccp, NCL * k, NCL), 0.0) for k in range(NSUB)]
    for k in range(NSUB):
        n = iota((NB, 2 * B), 1)
        onehot = jnp.where((col == n + CHUNK * k) & (n < CHUNK), 1.0, 0.0).astype(BF16)
        y = mm(parts, onehot)
        y = y[:8] + y[8:16] + y[16:24]
        tiles = (
            y[:, :B],
            y[:, B:] + extra,
            jnp.where(lane < NCL, cluster[k], tail),
            cluster[k + 1] if k + 1 < NSUB else none,
            cluster[k - 1] if k > 0 else none,
        )
        for t, x in enumerate(tiles):
            msg[k, :, t * B : (t + 1) * B] = x[:R]


def row_dot(a, b):
    return by_load(jnp.sum(a * b, axis=1, keepdims=True))


STATIC = NB + ROWS
PACK = 80


def k_send_static(
    ids, rhs, cb, kb, signs, links, up, down, even, odd, w_out, v_out, sg_out, idx_out
):
    pos = iota((8, B), 1).astype(BF16)
    moves = []
    for s in range(S):
        for b in range(3):
            q = links[b, s : s + 1, :]
            if b == 0 or (b == 2 and s % 2 == 0):
                hot = jnp.where(iota((B, B), 0) == q, 1.0, 0.0).astype(BF16)
                q = mm_t(pos, hot)[:1].astype(I32)
            idx_out[b, R * s : R * s + R, :] = jnp.broadcast_to(q, (R, B))
            moves.append(q)
    for s in range(S):
        v_out[R * s : R * s + R, :] = rhs[s]
        sg_out[R * s : R * s + R, :] = jnp.broadcast_to(signs[s : s + 1, :].astype(F32), (R, D))
        w_out[KC * s : KC * s + KC, :] = cb[s]
        w_out[NCL + 8 * s : NCL + 8 * s + 8, :] = kb[s]

    def moved(x, s, b):
        q = jnp.broadcast_to(moves[3 * s + b], (x.shape[0], B))
        return jnp.take_along_axis(x[:, b * B : (b + 1) * B], q, axis=1)

    for s in range(S):
        h = s // 2
        side = odd if s % 2 else even
        for x, at, to in ((cb[s], KC * s, KC * h), (kb[s], NCL + 8 * s, 2 * KC + 8 * h)):
            n = x.shape[0]
            up[at : at + n, :] = moved(x, s, 0)
            down[at : at + n, :] = moved(x, s, 1)
            side[to : to + n, :] = moved(x, s, 2)
    write_moved(v_out[...], idx_out, up, down, even, odd, NB, 2 * KC + 16)
    row = ids_row(ids).astype(F32)
    even[72:80, :] = row
    odd[72:80, :] = row


def write_moved(v, idx, up, down, even, odd, at=0, pack_at=0):
    def moved(b):
        return jnp.take_along_axis(v[:, b * B : (b + 1) * B], idx[b], axis=1)

    up[at : at + ROWS, :] = moved(0)
    down[at : at + ROWS, :] = moved(1)
    across = moved(2)
    for h in range(2):
        even[pack_at + R * h : pack_at + R * h + R, :] = across[8 * h : 8 * h + 4]
        odd[pack_at + R * h : pack_at + R * h + R, :] = across[8 * h + 4 : 8 * h + 8]


def k_start(ids, from_next, from_prev, odd_in, even_in, w, v, cc, msg, pw_out, pv_out):
    pw_out[:, 0:B] = from_next[0:NB, :]
    pw_out[:, B : 2 * B] = from_prev[0:NB, :]
    for s in range(S):
        h = s // 2
        side = even_in if s % 2 else odd_in
        pw_out[KC * s : KC * s + KC, 2 * B :] = side[KC * h : KC * h + KC, :]
        at = 2 * KC + 8 * h
        pw_out[NCL + 8 * s : NCL + 8 * s + 8, 2 * B :] = side[at : at + 8, :]
        at = 2 * KC + 16 + R * h
        pv_out[R * s : R * s + R, 2 * B :] = side[at : at + R, :]
    pv_out[:, 0:B] = from_next[NB:STATIC, :]
    pv_out[:, B : 2 * B] = from_prev[NB:STATIC, :]
    lane_even = (iota((8, B), 1) - NCL) // 8 % 2 == 0
    after = pltpu.roll(odd_in[72:80, :], B - 8, 1)
    before = pltpu.roll(even_in[72:80, :], 8, 1)
    x = v[...]
    coef = coefs(x, w[...])
    across_ids = jnp.where(lane_even, after, before)
    write_message(msg, coef, cc, ids, [row_dot(x, x)[:8]], across_ids)


def k_rows(recv, out, csol):
    total = recv[0]
    for k in range(1, NSUB):
        total = total + recv[k]
    own = jnp.where(iota((R, B), 1) < NCL, total[:, 2 * B : 3 * B], 0.0)
    csol[0] = own
    csol[1] = total[:, 3 * B : 4 * B]
    csol[2] = total[:, 4 * B : 5 * B]
    x = jnp.concatenate([total[:, : 2 * B], own], axis=1)
    out[...] = jnp.broadcast_to(x[None], out.shape)


def k_picked(recv, gc, hi_out, lo_out):
    lane = iota((8, B), 1)
    cols = []
    for kind in range(2):
        for half in range(2):
            ids = jnp.zeros((8, B), F32)
            for j in range(4):
                row = recv[4 * half + j, kind : kind + 1, 2 * B : 3 * B]
                row = pltpu.roll(jnp.broadcast_to(row, (8, B)), (32 + 32 * j) % B, 1)
                ids = jnp.where(lane // 32 == j, row, ids)
            cols.append(ids[:1].astype(I32))
    ids = jnp.concatenate(cols, axis=1)
    n = iota((gc.shape[1], 4 * B), 0)
    onehot = jnp.where(n == ids, 1.0, 0.0).astype(BF16)
    gh, gl = split(gc[...])
    zero = jnp.zeros((2 * B - CHUNK, 4 * B), BF16)
    hi_out[0:CHUNK, :] = mm(gh, onehot).astype(BF16)
    hi_out[CHUNK : 2 * B, :] = zero
    lo_out[0:CHUNK, :] = mm(gl, onehot).astype(BF16)
    lo_out[CHUNK : 2 * B, :] = zero


def k_first_rows(recv, gc, out, csol, hi_out, lo_out):
    k_rows(recv, out, csol)
    k_picked(recv, gc, hi_out, lo_out)


def k_global(recv, gh, gl, msg, scal, cacross):
    n_cl = recv.shape[0]
    c = lax.axis_index("cluster")
    total = jnp.sum(recv[:, :, 0 : 2 * B], axis=0)
    total = jnp.concatenate([total, total], axis=0)
    second = total[:, B:]
    lane = iota((8, B), 1)
    x = jnp.concatenate([total[:, :B], jnp.where(lane < 64, second, 0.0)], axis=1)
    xh, xl = split(x)
    y = mm(jnp.concatenate([xh, xl], axis=0), gh[...])
    y = y[:8] + y[8:] + mm(xh, gl[...])

    def pick(kind, k, to):
        at = 8 * 32 * kind + 32 * k
        return pltpu.roll(y[:, at // B * B : at // B * B + B], (to - at) % B, 1)

    none = jnp.zeros((8, B), F32)
    for k in range(NSUB):
        after = pick(0, k + 1, 32) if k + 1 < NSUB else none
        before = pick(0, k - 1, 64) if k > 0 else none
        here = jnp.where(lane < 32, pick(0, k, 0), jnp.where(lane < 64, after, before))
        msg[k] = jnp.where(lane < 96, here, pick(1, k, 96))[:R]
    scal[...] = jnp.concatenate([second, second], axis=0)
    after = recv[jnp.minimum(c + 1, n_cl - 1), :, 2 * B :]
    before = recv[jnp.maximum(c - 1, 0), :, 2 * B :]
    after = pltpu.roll(jnp.concatenate([after, after], axis=0), B - KC, 1)
    before = pltpu.roll(jnp.concatenate([before, before], axis=0), KC, 1)
    both = jnp.where(lane // KC % 2 == 0, after, before)
    cacross[...] = jnp.where(lane < NCL, both, 0.0)[:R]


def four_times(x):
    x = jnp.concatenate([x, x], axis=0)
    return jnp.concatenate([x, x], axis=0)


def corrections(recv, csol, cacross, w, pw):
    total = recv[0]
    for k in range(1, NSUB):
        total = total + recv[k]
    picks = four_times(total)
    tail = iota((ROWS, B), 1) >= NCL

    def sol(cluster, turn):
        p = pltpu.roll(picks, turn, 1) if turn else picks
        return jnp.where(tail, p, four_times(cluster))

    own = spread_back(sol(csol[0], 96), w[...])
    sides = (sol(csol[1], 64), sol(csol[2], 32), sol(cacross[...], 0))
    pi = [spread_back(x, pw[:, b * B : (b + 1) * B]) for b, x in enumerate(sides)]
    return own, jnp.concatenate(pi, axis=1)


def received(from_next, from_prev, odd_in, even_in):
    across = jnp.concatenate(
        [odd_in[0:R, :], even_in[0:R, :], odd_in[R : 2 * R, :], even_in[R : 2 * R, :]], axis=0
    )
    return jnp.concatenate([from_next[...], from_prev[...], across], axis=1)


def paired(n_cl):
    c, k = lax.axis_index("cluster"), lax.axis_index("sub")
    lane = iota((ROWS, D), 1)
    is_even = iota((ROWS, D), 0) // R % 2 == 0
    yes = [
        jnp.where(x, 1.0, 0.0) for x in (k < NSUB - 1, k > 0, c < n_cl - 1, c > 0)
    ]
    across = jnp.where(is_even, yes[2], yes[3])
    return jnp.where(lane < B, yes[0], jnp.where(lane < 2 * B, yes[1], across))


def image_of(d, pd, sg, ops):
    spread = sg * (d + pd)
    low = spread.astype(BF16)
    image = jnp.zeros((ROWS, D), F32)
    row = iota((ROWS, D), 0) // R
    for s in range(S):
        image = jnp.where(row == s, mm(low, ops[s]), image)
    return sg * image, row_dot(spread, image)


def k_first_image(
    recv, csol, cacross, w, pw, v, pv, sg, ops, idx,
    d_out, pd_out, signed_out, curv, up, down, even, odd,
):
    fix, pfix = corrections(recv, csol, cacross, w, pw)
    d = v[...] - fix
    pd = pv[...] - pfix
    d_out[...] = d
    pd_out[...] = pd
    signed, c = image_of(d, pd, sg[...], ops)
    signed_out[...] = signed
    curv[...] = jnp.broadcast_to(c[:8], (8, B))
    write_moved(signed, idx, up, down, even, odd)


def make_product(n_cl):
    def k_product(ids, signed, fn, fp, oi, ei, v, w, cc, curv, ap_out, pap_out, msg):
        pi = received(fn, fp, oi, ei)
        u = signed[...]
        ap = u + pi
        ap_out[...] = ap
        pap_out[...] = pi + paired(n_cl) * u
        scalars = [curv[...][:, :1], row_dot(v[...], ap)[:8], row_dot(ap, ap)[:8]]
        write_message(msg, coefs(ap, w[...]), cc, ids, scalars)

    return k_product


def scalar_at(scal, j):
    return jnp.sum(jnp.where(iota((ROWS, B), 1) == 64 + j, scal, 0.0), axis=1, keepdims=True)


LAST = ROWS + 8


def k_last_image(
    recv, csol, cacross, scal0, scal1, w, pw, v, d, pd, ap, pap, sg, ops, idx,
    r_out, x_out, d_out, signed_out, msg, even, odd, up, down,
):
    fix, pfix = corrections(recv, csol, cacross, w, pw)
    rho = scalar_at(scal0[...], 0)
    s1 = scal1[...]
    step = rho / scalar_at(s1, 0)
    rho_new = rho - 2.0 * step * scalar_at(s1, 1) + step * step * scalar_at(s1, 2)
    beta = rho_new / rho
    ap_ = ap[...]
    d0 = d[...]
    pd0 = pd[...]
    r = v[...] - step * ap_
    r_out[...] = r
    x_out[...] = step * d0
    d1 = d0 - step * (ap_ - fix) + beta * d0
    pd1 = pd0 - step * (pap[...] - pfix) + beta * pd0
    d_out[...] = d1
    signed, c = image_of(d1, pd1, sg[...], ops)
    signed_out[...] = signed
    sq = row_dot(r, r)
    lane = iota((8, B), 1)
    row = iota((8, B), 0)
    both = jnp.where(lane == row, c[:8], jnp.where(lane == row + R, sq[:8], 0.0))
    both = jnp.where(row < R, both, 0.0)
    write_moved(signed, idx, up, down, even, odd)
    msg[...] = jnp.zeros(msg.shape, F32)
    for k in range(NSUB):
        msg[k, ROWS:LAST, :] = both
    k = lax.axis_index("sub")
    msg[jnp.minimum(k + 1, NSUB - 1), 0:ROWS, :] = up[...]
    msg[jnp.maximum(k - 1, 0), 0:ROWS, :] = down[...]


def k_total(recv, out, from_next, from_prev):
    total = recv[0, ROWS:LAST, :]
    for j in range(1, NSUB):
        total = total + recv[j, ROWS:LAST, :]
    line = jnp.sum(total, axis=0, keepdims=True)
    out[...] = jnp.broadcast_to(line[None], out.shape)
    k = lax.axis_index("sub")
    after = recv[jnp.minimum(k + 1, NSUB - 1), 0:ROWS, :]
    before = recv[jnp.maximum(k - 1, 0), 0:ROWS, :]
    from_next[...] = jnp.where(jnp.full((ROWS, B), k, I32) < NSUB - 1, after, 0.0)
    from_prev[...] = jnp.where(jnp.full((ROWS, B), k, I32) > 0, before, 0.0)


def k_finish(recv, signed, fn, fp, oi, ei, x, r, d, x_out, r_out):
    line = jnp.broadcast_to(jnp.sum(recv[...], axis=0), (ROWS, B))
    lane = iota((ROWS, B), 1)
    row = iota((ROWS, B), 0) % R
    curv = jnp.sum(jnp.where(lane == row, line, 0.0), axis=1, keepdims=True)
    rho = jnp.sum(jnp.where(lane == row + R, line, 0.0), axis=1, keepdims=True)
    step = rho / curv
    xn = x[...] + step * d[...]
    rn = r[...] - step * (signed[...] + received(fn, fp, oi, ei))
    for s in range(S):
        x_out[s] = xn[R * s : R * s + R]
        r_out[s] = rn[R * s : R * s + R]


def call(body, outs, *args, smem=(), scratch=()):
    def space(i):
        return pltpu.SMEM if i in smem else pltpu.VMEM

    specs = [pl.BlockSpec(memory_space=space(i)) for i in range(len(args))]
    out_shape = tuple(jax.ShapeDtypeStruct(s, t) for s, t in outs)
    return pl.pallas_call(
        body,
        out_shape=out_shape,
        in_specs=specs,
        out_specs=tuple(pl.BlockSpec(memory_space=pltpu.VMEM) for _ in outs),
        scratch_shapes=scratch,
        name=body.__name__,
        compiler_params=pltpu.CompilerParams(vmem_limit_bytes=VMEM_LIMIT),
    )(*args)


def to_owner(x, axis):
    return lax.all_to_all(x, axis, 0, 0, tiled=True)


def f32(*shape):
    return (shape, F32)


FIELD = f32(ROWS, D)


def sends(rows, pack):
    return (f32(rows, B), f32(rows, B), f32(pack, B), f32(pack, B))


def ahead(n):
    return [(i, i + 1) for i in range(n - 1)]


def back(n):
    return [(i + 1, i) for i in range(n - 1)]


def exchange_across(even, odd, n_cl):
    odd_in = lax.ppermute(odd, "cluster", back(n_cl))
    even_in = lax.ppermute(even, "cluster", ahead(n_cl))
    return odd_in, even_in


def exchange(up, down, even, odd, n_sub, n_cl):
    across = exchange_across(even, odd, n_cl)
    from_prev = lax.ppermute(up, "sub", ahead(n_sub))
    from_next = lax.ppermute(down, "sub", back(n_sub))
    return from_next, from_prev, *across


def local(rhs, operators, signs, links, cb, kb, ids, cluster_coarse, gc):
    n_sub = lax.axis_size("sub")
    n_cl = lax.axis_size("cluster")
    cc = cluster_coarse.reshape(NCL, NSUB * NCL)
    message = f32(NSUB, R, MSG)
    spread_rows = (f32(n_cl, R, D), f32(3, R, B))
    picked = ((2 * B, 4 * B), BF16)
    answer = (f32(NSUB, R, B), f32(ROWS, B), f32(R, B))

    *out, w, v, sg, idx = call(
        k_send_static,
        (*sends(STATIC, PACK), f32(NB, D), FIELD, FIELD, ((3, ROWS, B), I32)),
        ids, rhs, cb, kb, signs, links.transpose(1, 0, 2),
        smem=(0,),
    )
    got = exchange(*out, n_sub, n_cl)
    msg, pw, pv = call(
        k_start, (message, f32(NB, D), FIELD), ids, *got, w, v, cc, smem=(0,)
    )
    rows, csol, gh, gl = call(
        k_first_rows, (*spread_rows, picked, picked), to_owner(msg, "sub"), gc
    )
    to_all, scal0, cacross = call(
        k_global, answer, to_owner(rows, "cluster"), gh, gl
    )
    d, pd, signed, curv, *out = call(
        k_first_image,
        (FIELD, FIELD, FIELD, f32(8, B), *sends(ROWS, 2 * R)),
        to_owner(to_all, "sub"), csol, cacross, w, pw, v, pv, sg, operators, idx,
    )
    got = exchange(*out, n_sub, n_cl)
    ap, pap, msg = call(
        make_product(n_cl),
        (FIELD, FIELD, message),
        ids, signed, *got, v, w, cc, curv, smem=(0,),
    )
    rows, csol = call(k_rows, spread_rows, to_owner(msg, "sub"))
    to_all, scal1, cacross = call(
        k_global, answer, to_owner(rows, "cluster"), gh, gl
    )
    r, x, d1, signed, msg, even, odd = call(
        k_last_image,
        (FIELD, FIELD, FIELD, FIELD, f32(NSUB, LAST, B), f32(2 * R, B), f32(2 * R, B)),
        to_owner(to_all, "sub"), csol, cacross, scal0, scal1,
        w, pw, v, d, pd, ap, pap, sg, operators, idx,
        scratch=(pltpu.VMEM((ROWS, B), F32), pltpu.VMEM((ROWS, B), F32)),
    )
    line, from_next, from_prev = call(
        k_total, (f32(n_cl, 1, B), f32(ROWS, B), f32(ROWS, B)), to_owner(msg, "sub")
    )
    across = exchange_across(even, odd, n_cl)
    out = f32(S, R, D)
    return call(
        k_finish, (out, out), to_owner(line, "cluster"), signed, from_next, from_prev, *across, x, r, d1
    )


def solution(mesh):
    both = ("cluster", "sub")
    in_specs = (
        P(both, None, None),
        P(both, None, None),
        P(both, None),
        P(both, None, None),
        P(both, None, None),
        P(both, None, None),
        P(both, None),
        P("cluster", "sub", None),
        P("sub", None),
    )
    out_specs = (P(both, None, None), P(both, None, None))
    return jax.shard_map(local, mesh=mesh, in_specs=in_specs, out_specs=out_specs, check_vma=False)
```

time: 202 us -> 195 us (0.965)
  the two profiles are of different devices: /device:TPU:32 before, /device:TPU:1 now
where the time goes in v3:
time: 195 us; the launch traced here: 194 us
  blocking collectives  127 us (65%)
  starting transfers between devices  43.1 us (22%)
  waiting for transfers between devices  9.54 us (5%)
  Pallas kernels  7.55 us (4%)
  local copies, waits for them, and re-layouts  6.75 us (3%)
    all_to_all x7, blocking collectives, to_owner(): return lax.all_to_all(x, axis, 0, 0, tiled=True)  127 us
    ppermute x2, starting transfers between devices, exchange(): from_next = lax.ppermute(down, 'sub', back(n_sub))  15 us
    ppermute x3, starting transfers between devices, exchange_across(): even_in = lax.ppermute(even, 'cluster', ahead(n_cl))  12 us
    pallas_call x11, Pallas kernels, call(): pl.pallas_call(body, out_shape=out_shape, in_specs=specs, out_specs=tuple...  7.55 us
    all_to_all x1, starting transfers between devices, to_owner(): return lax.all_to_all(x, axis, 0, 0, tiled=True)  7.38 us
    all_to_all x1, waiting for transfers between devices, to_owner(): return lax.all_to_all(x, axis, 0, 0, tiled=True)  6.99 us
    unnamed x22, local copies, waits for them, and re-layouts  6.75 us
    ppermute x2, starting transfers between devices, exchange(): from_prev = lax.ppermute(up, 'sub', ahead(n_sub))  4.86 us
  transfers between devices with their start and end apart: 11, of which 4 were waited for; matrix products, arithmetic and copies ran while one was open for 0% of the time, Pallas kernels for 0%

profile of v3, /device:TPU:1, one launch (start us, length us, event | category | flops | bytes accessed | tf_op | source)
XLA Modules:
  0.0 194.5 jit_solution(14652389873631492941)
XLA Ops:
  0.6 0.9 copy-done.4
  1.5 0.8 copy-done.5
  2.3 0.7 copy-done.6
  3.1 0.7 copy-done.7
  3.8 0.7 copy-done.9
  4.5 0.7 copy-done.10
  5.1 0.9 k_send_static.1
  6.0 12.4 %collective-permute-start = (f32[144,128]{1,0:T(8,128)S(1)}, f32[144,128]{1,0:T(8,128)S(1)}, u32[]{:S(2)}, u32[]{:S(2)}) collective-permute-start(f32[144,128]{1,0:T(8,128)S(1)} %get-tuple-element.46), channel_id=1, source_target_pairs={{1,0},{2,1},{3,2},{4,3},{5,4},{6,5},{7,6},{9,8},{10,9},{11,10},{12... | collective-permute-start | bytes 221192 | tf_op jit(solution)/shard_map/ppermute | solution.py:482
  18.4 1.9 collective-permute-start.1
  20.4 1.3 collective-permute-start.2
  21.7 4.0 %collective-permute-start.3 = (f32[80,128]{1,0:T(8,128)S(1)}, f32[80,128]{1,0:T(8,128)S(1)}, u32[]{:S(2)}, u32[]{:S(2)}) collective-permute-start(f32[80,128]{1,0:T(8,128)S(1)} %get-tuple-element.49), channel_id=1, source_target_pairs={{0,8},{8,16},{16,24},{24,32},{32,40},{40,48},{48,56},{56,64},{64,7... | collective-permute-start | bytes 122888 | tf_op jit(solution)/shard_map/ppermute | solution.py:475
  25.6 0.0 collective-permute-done.2.odd_in
  25.7 1.1 collective-permute-done.3.even_in
  26.7 0.0 collective-permute-done.from_next
  26.7 0.0 collective-permute-done.1.from_prev
  26.7 1.0 copy-done.2
  27.7 1.1 k_start.1
  28.8 8.9 %all_to_all.40.recv = f32[8,4,640]{2,1,0:T(4,128)S(1)} all-to-all(f32[8,4,640]{2,1,0:T(4,128)S(1)} %get-tuple-element.52), channel_id=1, replica_groups=mesh['cluster'=96,'sub'=8] {'sub'}, dimensions={0} | all-to-all | bytes 163840 | tf_op jit(solution)/shard_map/all_to_all | solution.py:451
  37.7 1.3 copy-done.1
  39.0 1.0 k_first_rows.1
  40.0 0.0 copy-start
  40.0 42.6 %all_to_all.41.recv = f32[96,4,384]{2,1,0:T(4,128)S(1)} all-to-all(f32[96,4,384]{2,1,0:T(4,128)S(1)} %get-tuple-element.53), channel_id=1, replica_groups=mesh['cluster'=96,'sub'=8] {'cluster'}, dimensions={0} | all-to-all | bytes 1179648 | tf_op jit(solution)/shard_map/all_to_all | solution.py:451
  82.6 0.4 k_global.2
  83.0 10.7 %all_to_all.42.recv = f32[8,4,128]{2,1,0:T(4,128)S(1)} all-to-all(f32[8,4,128]{2,1,0:T(4,128)S(1)} %get-tuple-element.56), channel_id=1, replica_groups=mesh['cluster'=96,'sub'=8] {'sub'}, dimensions={0} | all-to-all | bytes 32768 | tf_op jit(solution)/shard_map/all_to_all | solution.py:451
  93.7 0.6 k_first_image.1
  94.3 2.6 %collective-permute-start.4 = (f32[16,128]{1,0:T(8,128)S(1)}, f32[16,128]{1,0:T(8,128)S(1)}, u32[]{:S(2)}, u32[]{:S(2)}) collective-permute-start(f32[16,128]{1,0:T(8,128)S(1)} %get-tuple-element.64), channel_id=1, source_target_pairs={{1,0},{2,1},{3,2},{4,3},{5,4},{6,5},{7,6},{9,8},{10,9},{11,10},{12... | collective-permute-start | bytes 24584 | tf_op jit(solution)/shard_map/ppermute | solution.py:482
  97.0 2.9 %collective-permute-start.5 = (f32[16,128]{1,0:T(8,128)S(1)}, f32[16,128]{1,0:T(8,128)S(1)}, u32[]{:S(2)}, u32[]{:S(2)}) collective-permute-start(f32[16,128]{1,0:T(8,128)S(1)} %get-tuple-element.65), channel_id=1, source_target_pairs={{0,1},{1,2},{2,3},{3,4},{4,5},{5,6},{6,7},{8,9},{9,10},{10,11},{11... | collective-permute-start | bytes 24584 | tf_op jit(solution)/shard_map/ppermute | solution.py:481
  99.9 1.3 collective-permute-start.6
  101.2 4.0 %collective-permute-start.7 = (f32[8,128]{1,0:T(8,128)S(1)}, f32[8,128]{1,0:T(8,128)S(1)}, u32[]{:S(2)}, u32[]{:S(2)}) collective-permute-start(f32[8,128]{1,0:T(8,128)S(1)} %get-tuple-element.67), channel_id=1, source_target_pairs={{0,8},{8,16},{16,24},{24,32},{32,40},{40,48},{48,56},{56,64},{64,7... | collective-permute-start | bytes 12296 | tf_op jit(solution)/shard_map/ppermute | solution.py:475
  105.2 0.7 collective-permute-done.7.ei
  106.0 0.0 collective-permute-done.4.fn
  106.0 0.0 collective-permute-done.5.fp
  106.0 1.1 k_product.1
  107.1 8.1 %all_to_all.43.recv = f32[8,4,640]{2,1,0:T(4,128)S(1)} all-to-all(f32[8,4,640]{2,1,0:T(4,128)S(1)} %get-tuple-element.69), channel_id=1, replica_groups=mesh['cluster'=96,'sub'=8] {'sub'}, dimensions={0} | all-to-all | bytes 163840 | tf_op jit(solution)/shard_map/all_to_all | solution.py:451
  115.2 0.1 k_rows.1
  115.3 37.5 %all_to_all.44.recv = f32[96,4,384]{2,1,0:T(4,128)S(1)} all-to-all(f32[96,4,384]{2,1,0:T(4,128)S(1)} %get-tuple-element.70), channel_id=1, replica_groups=mesh['cluster'=96,'sub'=8] {'cluster'}, dimensions={0} | all-to-all | bytes 1179648 | tf_op jit(solution)/shard_map/all_to_all | solution.py:451
  152.8 0.4 k_global.3
  153.1 10.7 %all_to_all.45.recv = f32[8,4,128]{2,1,0:T(4,128)S(1)} all-to-all(f32[8,4,128]{2,1,0:T(4,128)S(1)} %get-tuple-element.71), channel_id=1, replica_groups=mesh['cluster'=96,'sub'=8] {'sub'}, dimensions={0} | all-to-all | bytes 32768 | tf_op jit(solution)/shard_map/all_to_all | solution.py:451
  163.9 0.6 k_last_image.1
  164.5 8.1 %all_to_all.46.recv = f32[8,24,128]{2,1,0:T(8,128)S(1)} all-to-all(f32[8,24,128]{2,1,0:T(8,128)S(1)} %get-tuple-element.80), channel_id=1, replica_groups=mesh['cluster'=96,'sub'=8] {'sub'}, dimensions={0} | all-to-all | bytes 196608 | tf_op jit(solution)/shard_map/all_to_all | solution.py:451
  172.6 0.7 k_total.1
  173.3 7.4 %all-to-all-start.7 = ((f32[96,1,128]{2,1,0:T(1,128)}), f32[96,1,128]{2,1,0:T(1,128)S(1)}, u32[]{:S(2)}, u32[]{:S(2)}) async-start(f32[96,1,128]{2,1,0:T(1,128)} %get-tuple-element.81), calls=%async_computation.7 | async-start | bytes 98304 | tf_op jit(solution)/shard_map/all_to_all | solution.py:451
  180.6 1.3 collective-permute-start.8
  181.9 4.0 %collective-permute-start.9 = (f32[8,128]{1,0:T(8,128)S(1)}, f32[8,128]{1,0:T(8,128)S(1)}, u32[]{:S(2)}, u32[]{:S(2)}) collective-permute-start(f32[8,128]{1,0:T(8,128)S(1)} %get-tuple-element.86), channel_id=1, source_target_pairs={{0,8},{8,16},{16,24},{24,32},{32,40},{40,48},{48,56},{56,64},{64,7... | collective-permute-start | bytes 12296 | tf_op jit(solution)/shard_map/ppermute | solution.py:475
  185.9 0.0 collective-permute-done.8.oi
  186.0 0.7 collective-permute-done.9.ei
  186.7 7.0 %all-to-all-done.7.recv = f32[96,1,128]{2,1,0:T(1,128)S(1)} async-done(((f32[96,1,128]{2,1,0:T(1,128)}), f32[96,1,128]{2,1,0:T(1,128)S(1)}, u32[]{:S(2)}, u32[]{:S(2)}) %all-to-all-start.7) | async-done | bytes 49184 | tf_op jit(solution)/shard_map/all_to_all | solution.py:451
  193.7 0.8 k_finish.1
  (14 shorter events, 0.0 us)
Async XLA Ops:
  0.6 0.9 copy-start.4
  1.5 0.8 copy-start.5
  2.3 0.7 copy-start.6
  3.1 0.7 copy-start.7
  3.8 0.7 copy-start.9
  4.5 0.7 copy-start.10
  6.0 20.7 %collective-permute-start = (f32[144,128]{1,0:T(8,128)S(1)}, f32[144,128]{1,0:T(8,128)S(1)}, u32[]{:S(2)}, u32[]{:S(2)}) collective-permute-start(f32[144,128]{1,0:T(8,128)S(1)} %get-tuple-element.46), channel_id=1, source_target_pairs={{1,0},{2,1},{3,2},{4,3},{5,4},{6,5},{7,6},{9,8},{10,9},{11,10},{12... | collective-permute-start | bytes 221192 | tf_op jit(solution)/shard_map/ppermute | solution.py:482
  18.4 8.3 %collective-permute-start.1 = (f32[144,128]{1,0:T(8,128)S(1)}, f32[144,128]{1,0:T(8,128)S(1)}, u32[]{:S(2)}, u32[]{:S(2)}) collective-permute-start(f32[144,128]{1,0:T(8,128)S(1)} %get-tuple-element.47), channel_id=1, source_target_pairs={{0,1},{1,2},{2,3},{3,4},{4,5},{5,6},{6,7},{8,9},{9,10},{10,11},{11... | collective-permute-start | bytes 221192 | tf_op jit(solution)/shard_map/ppermute | solution.py:481
  20.4 5.3 %collective-permute-start.2 = (f32[80,128]{1,0:T(8,128)S(1)}, f32[80,128]{1,0:T(8,128)S(1)}, u32[]{:S(2)}, u32[]{:S(2)}) collective-permute-start(f32[80,128]{1,0:T(8,128)S(1)} %get-tuple-element.48), channel_id=1, source_target_pairs={{8,0},{16,8},{24,16},{32,24},{40,32},{48,40},{56,48},{64,56},{72,6... | collective-permute-start | bytes 122888 | tf_op jit(solution)/shard_map/ppermute | solution.py:474
  21.7 5.1 %collective-permute-start.3 = (f32[80,128]{1,0:T(8,128)S(1)}, f32[80,128]{1,0:T(8,128)S(1)}, u32[]{:S(2)}, u32[]{:S(2)}) collective-permute-start(f32[80,128]{1,0:T(8,128)S(1)} %get-tuple-element.49), channel_id=1, source_target_pairs={{0,8},{8,16},{16,24},{24,32},{32,40},{40,48},{48,56},{56,64},{64,7... | collective-permute-start | bytes 122888 | tf_op jit(solution)/shard_map/ppermute | solution.py:475
  26.7 1.0 copy-start.2
  37.7 1.3 copy-start.1
  40.0 53.7 %copy-start = (bf16[4,384,384]{2,1,0:T(8,128)(2,1)S(1)}, bf16[4,384,384]{2,1,0:T(8,128)(2,1)}, u32[]{:S(2)}) copy-start(bf16[4,384,384]{2,1,0:T(8,128)(2,1)} %ops.3) | copy-start | bytes 3538948
  82.6 23.4 %copy-start.3 = (f32[1,96,768]{2,1,0:T(8,128)S(1)}, f32[1,96,768]{2,1,0:T(8,128)}, u32[]{:S(2)}) copy-start(f32[1,96,768]{2,1,0:T(8,128)} %param.16) | copy-start | bytes 884740
  82.6 23.4 %copy-start.8 = (s32[4,8]{1,0:T(4,128)S(1)}, s32[4,8]{1,0:T(4,128)}, u32[]{:S(2)}) copy-start(s32[4,8]{1,0:T(4,128)} %ids.5) | copy-start | bytes 388
  94.3 11.6 %collective-permute-start.4 = (f32[16,128]{1,0:T(8,128)S(1)}, f32[16,128]{1,0:T(8,128)S(1)}, u32[]{:S(2)}, u32[]{:S(2)}) collective-permute-start(f32[16,128]{1,0:T(8,128)S(1)} %get-tuple-element.64), channel_id=1, source_target_pairs={{1,0},{2,1},{3,2},{4,3},{5,4},{6,5},{7,6},{9,8},{10,9},{11,10},{12... | collective-permute-start | bytes 24584 | tf_op jit(solution)/shard_map/ppermute | solution.py:482
  97.0 9.0 %collective-permute-start.5 = (f32[16,128]{1,0:T(8,128)S(1)}, f32[16,128]{1,0:T(8,128)S(1)}, u32[]{:S(2)}, u32[]{:S(2)}) collective-permute-start(f32[16,128]{1,0:T(8,128)S(1)} %get-tuple-element.65), channel_id=1, source_target_pairs={{0,1},{1,2},{2,3},{3,4},{4,5},{5,6},{6,7},{8,9},{9,10},{10,11},{11... | collective-permute-start | bytes 24584 | tf_op jit(solution)/shard_map/ppermute | solution.py:481
  99.9 5.3 %collective-permute-start.6 = (f32[8,128]{1,0:T(8,128)S(1)}, f32[8,128]{1,0:T(8,128)S(1)}, u32[]{:S(2)}, u32[]{:S(2)}) collective-permute-start(f32[8,128]{1,0:T(8,128)S(1)} %get-tuple-element.66), channel_id=1, source_target_pairs={{8,0},{16,8},{24,16},{32,24},{40,32},{48,40},{56,48},{64,56},{72,6... | collective-permute-start | bytes 12296 | tf_op jit(solution)/shard_map/ppermute | solution.py:474
  101.2 4.7 %collective-permute-start.7 = (f32[8,128]{1,0:T(8,128)S(1)}, f32[8,128]{1,0:T(8,128)S(1)}, u32[]{:S(2)}, u32[]{:S(2)}) collective-permute-start(f32[8,128]{1,0:T(8,128)S(1)} %get-tuple-element.67), channel_id=1, source_target_pairs={{0,8},{8,16},{16,24},{24,32},{32,40},{40,48},{48,56},{56,64},{64,7... | collective-permute-start | bytes 12296 | tf_op jit(solution)/shard_map/ppermute | solution.py:475
  173.3 20.4 %all-to-all-start.7 = ((f32[96,1,128]{2,1,0:T(1,128)}), f32[96,1,128]{2,1,0:T(1,128)S(1)}, u32[]{:S(2)}, u32[]{:S(2)}) async-start(f32[96,1,128]{2,1,0:T(1,128)} %get-tuple-element.81), calls=%async_computation.7 | async-start | bytes 98304 | tf_op jit(solution)/shard_map/all_to_all | solution.py:451
  180.6 5.3 %collective-permute-start.8 = (f32[8,128]{1,0:T(8,128)S(1)}, f32[8,128]{1,0:T(8,128)S(1)}, u32[]{:S(2)}, u32[]{:S(2)}) collective-permute-start(f32[8,128]{1,0:T(8,128)S(1)} %get-tuple-element.85), channel_id=1, source_target_pairs={{8,0},{16,8},{24,16},{32,24},{40,32},{48,40},{56,48},{64,56},{72,6... | collective-permute-start | bytes 12296 | tf_op jit(solution)/shard_map/ppermute | solution.py:474
  181.9 4.7 %collective-permute-start.9 = (f32[8,128]{1,0:T(8,128)S(1)}, f32[8,128]{1,0:T(8,128)S(1)}, u32[]{:S(2)}, u32[]{:S(2)}) collective-permute-start(f32[8,128]{1,0:T(8,128)S(1)} %get-tuple-element.86), channel_id=1, source_target_pairs={{0,8},{8,16},{16,24},{24,32},{32,40},{40,48},{48,56},{56,64},{64,7... | collective-permute-start | bytes 12296 | tf_op jit(solution)/shard_map/ppermute | solution.py:475

commit v4 on v3

--- a/solution.py
+++ b/solution.py
@@ -3,6 +3,7 @@
 from jax import lax
 from jax.experimental import pallas as pl
 from jax.experimental.pallas import tpu as pltpu
+from jax.sharding import Mesh
 from jax.sharding import PartitionSpec as P
 
 F32 = jnp.float32
@@ -18,6 +19,7 @@
 NCL = S * KC
 CHUNK = 192
 NSUB = 8
+CLUSTER = ("y", "z")
 VMEM_LIMIT = 16 * 2**20
 
 
@@ -100,7 +102,7 @@
 MSG = 5 * B
 
 
-def write_message(msg, coef, cc, ids, scalars, across_ids=None):
+def write_message(msg, coef, cc, ids, scalars):
     row = ids_row(ids).astype(F32)
     col = to_column(row).astype(I32)
     c4 = coef[:8]
@@ -112,10 +114,6 @@
     extra = jnp.zeros((8, B), F32)
     for j, val in enumerate(scalars):
         extra = jnp.where(lane == 64 + j, val, extra)
-    if across_ids is None:
-        tail = jnp.zeros((8, B), F32)
-    else:
-        tail = jnp.where(iota((8, B), 0) == 0, row, across_ids)
     none = jnp.zeros((8, B), F32)
     cluster = [jnp.where(lane < NCL, window(ccp, NCL * k, NCL), 0.0) for k in range(NSUB)]
     for k in range(NSUB):
@@ -126,7 +124,7 @@
         tiles = (
             y[:, :B],
             y[:, B:] + extra,
-            jnp.where(lane < NCL, cluster[k], tail),
+            jnp.where(lane < NCL, cluster[k], row),
             cluster[k + 1] if k + 1 < NSUB else none,
             cluster[k - 1] if k > 0 else none,
         )
@@ -139,15 +137,24 @@
 
 
 STATIC = NB + ROWS
-PACK = 80
-
-
-def k_send_static(
-    ids, rhs, cb, kb, signs, links, up, down, even, odd, w_out, v_out, sg_out, idx_out
-):
+PACK = 72
+
+
+def k_coefs(ids, rhs, cb, kb, cc, msg, w_out, v_out):
+    for s in range(S):
+        v_out[R * s : R * s + R, :] = rhs[s]
+        w_out[KC * s : KC * s + KC, :] = cb[s]
+        w_out[NCL + 8 * s : NCL + 8 * s + 8, :] = kb[s]
+    v = v_out[...]
+    write_message(msg, coefs(v, w_out[...]), cc, ids, [row_dot(v, v)[:8]])
+
+
+def k_send_static(after, w, v, signs, links, up, down, even, odd, sg_out, idx_out):
+    del after
     pos = iota((8, B), 1).astype(BF16)
     moves = []
     for s in range(S):
+        sg_out[R * s : R * s + R, :] = jnp.broadcast_to(signs[s : s + 1, :].astype(F32), (R, D))
         for b in range(3):
             q = links[b, s : s + 1, :]
             if b == 0 or (b == 2 and s % 2 == 0):
@@ -155,28 +162,19 @@
                 q = mm_t(pos, hot)[:1].astype(I32)
             idx_out[b, R * s : R * s + R, :] = jnp.broadcast_to(q, (R, B))
             moves.append(q)
-    for s in range(S):
-        v_out[R * s : R * s + R, :] = rhs[s]
-        sg_out[R * s : R * s + R, :] = jnp.broadcast_to(signs[s : s + 1, :].astype(F32), (R, D))
-        w_out[KC * s : KC * s + KC, :] = cb[s]
-        w_out[NCL + 8 * s : NCL + 8 * s + 8, :] = kb[s]
-
-    def moved(x, s, b):
-        q = jnp.broadcast_to(moves[3 * s + b], (x.shape[0], B))
-        return jnp.take_along_axis(x[:, b * B : (b + 1) * B], q, axis=1)
+
+    def moved(at, n, s, b):
+        q = jnp.broadcast_to(moves[3 * s + b], (n, B))
+        return jnp.take_along_axis(w[at : at + n, b * B : (b + 1) * B], q, axis=1)
 
     for s in range(S):
         h = s // 2
         side = odd if s % 2 else even
-        for x, at, to in ((cb[s], KC * s, KC * h), (kb[s], NCL + 8 * s, 2 * KC + 8 * h)):
-            n = x.shape[0]
-            up[at : at + n, :] = moved(x, s, 0)
-            down[at : at + n, :] = moved(x, s, 1)
-            side[to : to + n, :] = moved(x, s, 2)
-    write_moved(v_out[...], idx_out, up, down, even, odd, NB, 2 * KC + 16)
-    row = ids_row(ids).astype(F32)
-    even[72:80, :] = row
-    odd[72:80, :] = row
+        for at, n, to in ((KC * s, KC, KC * h), (NCL + 8 * s, 8, 2 * KC + 8 * h)):
+            up[at : at + n, :] = moved(at, n, s, 0)
+            down[at : at + n, :] = moved(at, n, s, 1)
+            side[to : to + n, :] = moved(at, n, s, 2)
+    write_moved(v[...], idx_out, up, down, even, odd, NB, 2 * KC + 16)
 
 
 def write_moved(v, idx, up, down, even, odd, at=0, pack_at=0):
@@ -191,7 +189,7 @@
         odd[pack_at + R * h : pack_at + R * h + R, :] = across[8 * h + 4 : 8 * h + 8]
 
 
-def k_start(ids, from_next, from_prev, odd_in, even_in, w, v, cc, msg, pw_out, pv_out):
+def k_take_static(from_next, from_prev, odd_in, even_in, pw_out, pv_out):
     pw_out[:, 0:B] = from_next[0:NB, :]
     pw_out[:, B : 2 * B] = from_prev[0:NB, :]
     for s in range(S):
@@ -204,69 +202,102 @@
         pv_out[R * s : R * s + R, 2 * B :] = side[at : at + R, :]
     pv_out[:, 0:B] = from_next[NB:STATIC, :]
     pv_out[:, B : 2 * B] = from_prev[NB:STATIC, :]
-    lane_even = (iota((8, B), 1) - NCL) // 8 % 2 == 0
-    after = pltpu.roll(odd_in[72:80, :], B - 8, 1)
-    before = pltpu.roll(even_in[72:80, :], 8, 1)
-    x = v[...]
-    coef = coefs(x, w[...])
-    across_ids = jnp.where(lane_even, after, before)
-    write_message(msg, coef, cc, ids, [row_dot(x, x)[:8]], across_ids)
-
-
-def k_rows(recv, out, csol):
+
+
+def member_sum(recv):
     total = recv[0]
     for k in range(1, NSUB):
         total = total + recv[k]
+    return total
+
+
+def k_rows(recv, out, csol):
+    total = member_sum(recv)
     own = jnp.where(iota((R, B), 1) < NCL, total[:, 2 * B : 3 * B], 0.0)
     csol[0] = own
     csol[1] = total[:, 3 * B : 4 * B]
     csol[2] = total[:, 4 * B : 5 * B]
     x = jnp.concatenate([total[:, : 2 * B], own], axis=1)
-    out[...] = jnp.broadcast_to(x[None], out.shape)
-
-
-def k_picked(recv, gc, hi_out, lo_out):
+    out[:, :, 0:D] = jnp.broadcast_to(x[None], (out.shape[0], R, D))
+
+
+def cluster_ids(recv):
     lane = iota((8, B), 1)
-    cols = []
-    for kind in range(2):
-        for half in range(2):
-            ids = jnp.zeros((8, B), F32)
-            for j in range(4):
-                row = recv[4 * half + j, kind : kind + 1, 2 * B : 3 * B]
-                row = pltpu.roll(jnp.broadcast_to(row, (8, B)), (32 + 32 * j) % B, 1)
-                ids = jnp.where(lane // 32 == j, row, ids)
-            cols.append(ids[:1].astype(I32))
-    ids = jnp.concatenate(cols, axis=1)
-    n = iota((gc.shape[1], 4 * B), 0)
+    rows = []
+    for half in range(2):
+        ids = jnp.zeros((8, B), F32)
+        for j in range(4):
+            row = recv[4 * half + j, 0:1, 2 * B : 3 * B]
+            row = pltpu.roll(jnp.broadcast_to(row, (8, B)), (32 + 32 * j) % B, 1)
+            ids = jnp.where(lane // 32 == j, row, ids)
+        rows.append(ids)
+    return rows
+
+
+def k_first_rows(recv, out, csol, ids_out):
+    k_rows(recv, out, csol)
+    low, high = cluster_ids(recv)
+    ids = jnp.where(iota((8, B), 0) == 0, low, high)
+    ids_out[...] = ids
+    out[:, :, D:] = jnp.broadcast_to(ids[None, :R], (out.shape[0], R, B))
+
+
+def k_pass(recv, out):
+    y, z = lax.axis_index("y"), lax.axis_index("z")
+    n_y, n_z = recv.shape[0], out.shape[0]
+    total = jnp.sum(recv[:, :, 0 : 2 * B], axis=0)
+    other = jnp.where(z == 0, jnp.minimum(y + 1, n_y - 1), jnp.maximum(y - 1, 0))
+    x = jnp.concatenate([total, recv[y, :, 2 * B :], recv[other, :, 2 * B :]], axis=1)
+    out[...] = jnp.broadcast_to(x[None], (n_z, *x.shape))
+
+
+def neighbours(recv, at, wrapped_at):
+    z = lax.axis_index("z")
+    n_z = recv.shape[0]
+    last, first = z == n_z - 1, z == 0
+    nxt = recv[jnp.where(last, 0, z + 1)]
+    prv = recv[jnp.where(first, n_z - 1, z - 1)]
+
+    def tile(x, use_wrapped):
+        plain = x[:, at : at + B]
+        wrapped = x[:, wrapped_at : wrapped_at + B]
+        x = jnp.where(jnp.full((R, B), use_wrapped.astype(I32), I32) == 1, wrapped, plain)
+        return jnp.concatenate([x, x], axis=0)
+
+    return tile(nxt, last), tile(prv, first)
+
+
+def picked_columns(gc, rows, hi_out, lo_out):
+    ids = jnp.concatenate([x[:1].astype(I32) for x in rows], axis=1)
+    n = iota((gc.shape[1], ids.shape[1]), 0)
     onehot = jnp.where(n == ids, 1.0, 0.0).astype(BF16)
     gh, gl = split(gc[...])
-    zero = jnp.zeros((2 * B - CHUNK, 4 * B), BF16)
+    zero = jnp.zeros((2 * B - CHUNK, ids.shape[1]), BF16)
     hi_out[0:CHUNK, :] = mm(gh, onehot).astype(BF16)
     hi_out[CHUNK : 2 * B, :] = zero
     lo_out[0:CHUNK, :] = mm(gl, onehot).astype(BF16)
     lo_out[CHUNK : 2 * B, :] = zero
 
 
-def k_first_rows(recv, gc, out, csol, hi_out, lo_out):
-    k_rows(recv, out, csol)
-    k_picked(recv, gc, hi_out, lo_out)
-
-
-def k_global(recv, gh, gl, msg, scal, cacross):
-    n_cl = recv.shape[0]
-    c = lax.axis_index("cluster")
+def k_own_columns(ids, gc, hi_out, lo_out):
+    picked_columns(gc, [ids[0:1, :], ids[1:2, :]], hi_out, lo_out)
+
+
+def solve(recv, parts, msg, scal, cacross, stride):
     total = jnp.sum(recv[:, :, 0 : 2 * B], axis=0)
     total = jnp.concatenate([total, total], axis=0)
     second = total[:, B:]
     lane = iota((8, B), 1)
     x = jnp.concatenate([total[:, :B], jnp.where(lane < 64, second, 0.0)], axis=1)
     xh, xl = split(x)
-    y = mm(jnp.concatenate([xh, xl], axis=0), gh[...])
-    y = y[:8] + y[8:] + mm(xh, gl[...])
+    ys = []
+    for gh, gl in parts:
+        y = mm(jnp.concatenate([xh, xl], axis=0), gh[...])
+        ys.append(y[:8] + y[8:] + mm(xh, gl[...]))
 
     def pick(kind, k, to):
-        at = 8 * 32 * kind + 32 * k
-        return pltpu.roll(y[:, at // B * B : at // B * B + B], (to - at) % B, 1)
+        at = 32 * k
+        return pltpu.roll(ys[kind][:, at // B * B : at // B * B + B], (to - at) % B, 1)
 
     none = jnp.zeros((8, B), F32)
     for k in range(NSUB):
@@ -275,12 +306,25 @@
         here = jnp.where(lane < 32, pick(0, k, 0), jnp.where(lane < 64, after, before))
         msg[k] = jnp.where(lane < 96, here, pick(1, k, 96))[:R]
     scal[...] = jnp.concatenate([second, second], axis=0)
-    after = recv[jnp.minimum(c + 1, n_cl - 1), :, 2 * B :]
-    before = recv[jnp.maximum(c - 1, 0), :, 2 * B :]
-    after = pltpu.roll(jnp.concatenate([after, after], axis=0), B - KC, 1)
-    before = pltpu.roll(jnp.concatenate([before, before], axis=0), KC, 1)
+    after, before = neighbours(recv, 2 * B, 2 * B + stride)
+    after = pltpu.roll(after, B - KC, 1)
+    before = pltpu.roll(before, KC, 1)
     both = jnp.where(lane // KC % 2 == 0, after, before)
     cacross[...] = jnp.where(lane < NCL, both, 0.0)[:R]
+
+
+def k_first_global(recv, gc, gh, gl, msg, scal, cacross, ah, al):
+    after, before = neighbours(recv, 3 * B, 5 * B)
+    lane = iota((8, B), 1)
+    after = pltpu.roll(after, B - 8, 1)
+    before = pltpu.roll(before, 8, 1)
+    ids = jnp.where(lane // 8 % 2 == 0, after, before)
+    picked_columns(gc, [ids[0:1], ids[1:2]], ah, al)
+    solve(recv, ((gh, gl), (ah, al)), msg, scal, cacross, 2 * B)
+
+
+def k_global(recv, gh, gl, ah, al, msg, scal, cacross):
+    solve(recv, ((gh, gl), (ah, al)), msg, scal, cacross, B)
 
 
 def four_times(x):
@@ -289,10 +333,7 @@
 
 
 def corrections(recv, csol, cacross, w, pw):
-    total = recv[0]
-    for k in range(1, NSUB):
-        total = total + recv[k]
-    picks = four_times(total)
+    picks = four_times(member_sum(recv))
     tail = iota((ROWS, B), 1) >= NCL
 
     def sol(cluster, turn):
@@ -313,7 +354,7 @@
 
 
 def paired(n_cl):
-    c, k = lax.axis_index("cluster"), lax.axis_index("sub")
+    c, k = lax.axis_index("y") * lax.axis_size("z") + lax.axis_index("z"), lax.axis_index("sub")
     lane = iota((ROWS, D), 1)
     is_even = iota((ROWS, D), 0) // R % 2 == 0
     yes = [
@@ -471,8 +512,8 @@
 
 
 def exchange_across(even, odd, n_cl):
-    odd_in = lax.ppermute(odd, "cluster", back(n_cl))
-    even_in = lax.ppermute(even, "cluster", ahead(n_cl))
+    odd_in = lax.ppermute(odd, CLUSTER, back(n_cl))
+    even_in = lax.ppermute(even, CLUSTER, ahead(n_cl))
     return odd_in, even_in
 
 
@@ -485,28 +526,32 @@
 
 def local(rhs, operators, signs, links, cb, kb, ids, cluster_coarse, gc):
     n_sub = lax.axis_size("sub")
-    n_cl = lax.axis_size("cluster")
+    n_y = lax.axis_size("y")
+    n_z = lax.axis_size("z")
+    n_cl = n_y * n_z
     cc = cluster_coarse.reshape(NCL, NSUB * NCL)
     message = f32(NSUB, R, MSG)
-    spread_rows = (f32(n_cl, R, D), f32(3, R, B))
-    picked = ((2 * B, 4 * B), BF16)
+    picked = ((2 * B, 2 * B), BF16)
     answer = (f32(NSUB, R, B), f32(ROWS, B), f32(R, B))
 
-    *out, w, v, sg, idx = call(
+    msg, w, v = call(
+        k_coefs, (message, f32(NB, D), FIELD), ids, rhs, cb, kb, cc, smem=(0,)
+    )
+    recv = to_owner(msg, "sub")
+    rows, csol, all_ids = call(
+        k_first_rows, (f32(n_y, R, 4 * B), f32(3, R, B), f32(8, B)), recv
+    )
+    *out, sg, idx = call(
         k_send_static,
-        (*sends(STATIC, PACK), f32(NB, D), FIELD, FIELD, ((3, ROWS, B), I32)),
-        ids, rhs, cb, kb, signs, links.transpose(1, 0, 2),
-        smem=(0,),
+        (*sends(STATIC, PACK), FIELD, ((3, ROWS, B), I32)),
+        all_ids, w, v, signs, links.transpose(1, 0, 2),
     )
     got = exchange(*out, n_sub, n_cl)
-    msg, pw, pv = call(
-        k_start, (message, f32(NB, D), FIELD), ids, *got, w, v, cc, smem=(0,)
-    )
-    rows, csol, gh, gl = call(
-        k_first_rows, (*spread_rows, picked, picked), to_owner(msg, "sub"), gc
-    )
-    to_all, scal0, cacross = call(
-        k_global, answer, to_owner(rows, "cluster"), gh, gl
+    pw, pv = call(k_take_static, (f32(NB, D), FIELD), *got)
+    gh, gl = call(k_own_columns, (picked, picked), all_ids, gc)
+    (rows,) = call(k_pass, (f32(n_z, R, 6 * B),), to_owner(rows, "y"))
+    to_all, scal0, cacross, ah, al = call(
+        k_first_global, (*answer, picked, picked), to_owner(rows, "z"), gc, gh, gl
     )
     d, pd, signed, curv, *out = call(
         k_first_image,
@@ -519,10 +564,9 @@
         (FIELD, FIELD, message),
         ids, signed, *got, v, w, cc, curv, smem=(0,),
     )
-    rows, csol = call(k_rows, spread_rows, to_owner(msg, "sub"))
-    to_all, scal1, cacross = call(
-        k_global, answer, to_owner(rows, "cluster"), gh, gl
-    )
+    rows, csol = call(k_rows, (f32(n_y, R, D), f32(3, R, B)), to_owner(msg, "sub"))
+    (rows,) = call(k_pass, (f32(n_z, R, 4 * B),), to_owner(rows, "y"))
+    to_all, scal1, cacross = call(k_global, answer, to_owner(rows, "z"), gh, gl, ah, al)
     r, x, d1, signed, msg, even, odd = call(
         k_last_image,
         (FIELD, FIELD, FIELD, FIELD, f32(NSUB, LAST, B), f32(2 * R, B), f32(2 * R, B)),
@@ -536,12 +580,14 @@
     across = exchange_across(even, odd, n_cl)
     out = f32(S, R, D)
     return call(
-        k_finish, (out, out), to_owner(line, "cluster"), signed, from_next, from_prev, *across, x, r, d1
+        k_finish, (out, out), to_owner(line, CLUSTER), signed, from_next, from_prev, *across, x, r, d1
     )
 
 
 def solution(mesh):
-    both = ("cluster", "sub")
+    n_y, n_z = 8, 12
+    torus = Mesh(mesh.devices.reshape(n_y, n_z, NSUB), ("y", "z", "sub"))
+    both = ("y", "z", "sub")
     in_specs = (
         P(both, None, None),
         P(both, None, None),
@@ -550,8 +596,8 @@
         P(both, None, None),
         P(both, None, None),
         P(both, None),
-        P("cluster", "sub", None),
+        P(CLUSTER, "sub", None),
         P("sub", None),
     )
     out_specs = (P(both, None, None), P(both, None, None))
-    return jax.shard_map(local, mesh=mesh, in_specs=in_specs, out_specs=out_specs, check_vma=False)
+    return jax.shard_map(local, mesh=torus, in_specs=in_specs, out_specs=out_specs, check_vma=False)

time: 195 us -> 165 us (0.85)
  blocking collectives: 127 us -> 86.9 us
  starting transfers between devices: 43.1 us -> 50 us
  waiting for transfers between devices: 9.54 us -> 13.1 us
  local copies, waits for them, and re-layouts: 6.75 us -> 4.2 us
    all_to_all x7, blocking collectives: 127 us -> 86.9 us  [to_owner(): return lax.all_to_all(x, axis, 0, 0, tiled=True)]
    all_to_all x1 -> x3, starting transfers between devices: 7.38 us -> 21.8 us  [to_owner(): return lax.all_to_all(x, axis, 0, 0, tiled=True)]
    ppermute x2, starting transfers between devices: 15 us -> 7.04 us  [exchange(): from_next = lax.ppermute(down, 'sub', back(n_sub))]
    all_to_all x1 -> x3, waiting for transfers between devices: 6.99 us -> 11.6 us  [to_owner(): return lax.all_to_all(x, axis, 0, 0, tiled=True)]
    unnamed x22, local copies, waits for them, and re-layouts: 6.75 us -> 4.2 us
    pallas_call x11 -> x15, Pallas kernels: 7.55 us -> 8.79 us  [call(): pl.pallas_call(body, out_shape=out_shape, in_specs=specs, out_specs=tuple...]
  transfers between devices with their start and end apart: 11 -> 13, of which waited for: 4 -> 4; matrix products, arithmetic and copies ran while one was open for 0% -> 0% of each run, Pallas kernels for 0% -> 2%
where the time goes in v4:
time: 165 us; the launch traced here: 164 us
  blocking collectives  86.9 us (53%)
  starting transfers between devices  50 us (30%)
  waiting for transfers between devices  13.1 us (8%)
  Pallas kernels  8.79 us (5%)
  local copies, waits for them, and re-layouts  4.2 us (3%)
    all_to_all x7, blocking collectives, to_owner(): return lax.all_to_all(x, axis, 0, 0, tiled=True)  86.9 us
    all_to_all x3, starting transfers between devices, to_owner(): return lax.all_to_all(x, axis, 0, 0, tiled=True)  21.8 us
    ppermute x3, starting transfers between devices, exchange_across(): even_in = lax.ppermute(even, CLUSTER, ahead(n_cl))  12.3 us
    all_to_all x3, waiting for transfers between devices, to_owner(): return lax.all_to_all(x, axis, 0, 0, tiled=True)  11.6 us
    pallas_call x15, Pallas kernels, call(): pl.pallas_call(body, out_shape=out_shape, in_specs=specs, out_specs=tuple...  8.79 us
    ppermute x2, starting transfers between devices, exchange(): from_next = lax.ppermute(down, 'sub', back(n_sub))  7.04 us
    ppermute x2, starting transfers between devices, exchange(): from_prev = lax.ppermute(up, 'sub', ahead(n_sub))  5.03 us
    unnamed x22, local copies, waits for them, and re-layouts  4.2 us
  transfers between devices with their start and end apart: 13, of which 4 were waited for; matrix products, arithmetic and copies ran while one was open for 0% of the time, Pallas kernels for 2%

profile of v4, /device:TPU:1, one launch (start us, length us, event | category | flops | bytes accessed | tf_op | source)
XLA Modules:
  0.0 163.9 jit_solution(10644939718076390633)
XLA Ops:
  0.6 0.0 copy-start.2
  0.7 1.0 copy-done.2
  1.7 0.9 copy-done.4
  2.6 0.8 copy-done.5
  3.4 0.7 copy-done.6
  4.2 0.7 copy-done.7
  4.8 1.1 k_coefs.1
  5.9 17.8 %all_to_all.50.recv = f32[8,4,640]{2,1,0:T(4,128)S(1)} all-to-all(f32[8,4,640]{2,1,0:T(4,128)S(1)} %get-tuple-element.49), channel_id=1, replica_groups=mesh['y'=8,'z'=12,'sub'=8] {'sub'}, dimensions={0} | all-to-all | bytes 163840 | tf_op jit(solution)/shard_map/all_to_all | solution.py:492
  23.7 0.1 k_first_rows.1
  23.8 9.7 %all_to_all.51.recv = f32[8,4,512]{2,1,0:T(4,128)S(1)} all-to-all(f32[8,4,512]{2,1,0:T(4,128)S(1)} %get-tuple-element.50), channel_id=1, replica_groups=mesh['y'=8,'z'=12,'sub'=8] {'y'}, dimensions={0} | all-to-all | bytes 131072 | tf_op jit(solution)/shard_map/all_to_all | solution.py:492
  33.4 0.7 k_pass.2
  34.1 11.8 %all-to-all-start.2 = ((f32[12,4,768]{2,1,0:T(4,128)}), f32[12,4,768]{2,1,0:T(4,128)S(1)}, u32[]{:S(2)}, u32[]{:S(2)}) async-start(f32[12,4,768]{2,1,0:T(4,128)} %k_pass.2), calls=%async_computation.2 | async-start | bytes 294912 | tf_op jit(solution)/shard_map/all_to_all | solution.py:492
  45.9 1.0 k_send_static.1
  46.9 4.4 %collective-permute-start = (f32[144,128]{1,0:T(8,128)}, f32[144,128]{1,0:T(8,128)S(1)}, u32[]{:S(2)}, u32[]{:S(2)}) collective-permute-start(f32[144,128]{1,0:T(8,128)} %get-tuple-element.59), channel_id=1, source_target_pairs={{1,0},{2,1},{3,2},{4,3},{5,4},{6,5},{7,6},{9,8},{10,9},{11,10},{12... | collective-permute-start | bytes 221192 | tf_op jit(solution)/shard_map/ppermute | solution.py:523
  51.3 2.1 %collective-permute-start.1 = (f32[144,128]{1,0:T(8,128)}, f32[144,128]{1,0:T(8,128)S(1)}, u32[]{:S(2)}, u32[]{:S(2)}) collective-permute-start(f32[144,128]{1,0:T(8,128)} %get-tuple-element.60), channel_id=1, source_target_pairs={{0,1},{1,2},{2,3},{3,4},{4,5},{5,6},{6,7},{8,9},{9,10},{10,11},{11... | collective-permute-start | bytes 221192 | tf_op jit(solution)/shard_map/ppermute | solution.py:522
  53.4 1.3 collective-permute-start.2
  54.7 4.2 %collective-permute-start.3 = (f32[72,128]{1,0:T(8,128)}, f32[72,128]{1,0:T(8,128)S(1)}, u32[]{:S(2)}, u32[]{:S(2)}) collective-permute-start(f32[72,128]{1,0:T(8,128)} %get-tuple-element.62), channel_id=1, source_target_pairs={{0,8},{8,16},{16,24},{24,32},{32,40},{40,48},{48,56},{56,64},{64,7... | collective-permute-start | bytes 110600 | tf_op jit(solution)/shard_map/ppermute | solution.py:516
  58.9 0.5 k_own_columns.1
  59.4 0.0 copy-start.1
  59.4 0.0 all-to-all-done.2.recv
  59.4 1.4 k_first_global.1
  60.8 4.2 %all-to-all-start.3 = ((f32[8,4,128]{2,1,0:T(4,128)}), f32[8,4,128]{2,1,0:T(4,128)S(1)}, u32[]{:S(2)}, u32[]{:S(2)}) async-start(f32[8,4,128]{2,1,0:T(4,128)} %get-tuple-element.54), calls=%async_computation.3 | async-start | bytes 32768 | tf_op jit(solution)/shard_map/all_to_all | solution.py:492
  65.0 0.0 collective-permute-done.2.odd_in
  65.0 0.0 collective-permute-done.from_next
  65.1 4.6 %all-to-all-done.3.recv = f32[8,4,128]{2,1,0:T(4,128)S(1)} async-done(((f32[8,4,128]{2,1,0:T(4,128)}), f32[8,4,128]{2,1,0:T(4,128)S(1)}, u32[]{:S(2)}, u32[]{:S(2)}) %all-to-all-start.3) | async-done | bytes 16416 | tf_op jit(solution)/shard_map/all_to_all | solution.py:492
  69.7 0.6 k_first_image.1
  70.3 2.6 %collective-permute-start.4 = (f32[16,128]{1,0:T(8,128)S(1)}, f32[16,128]{1,0:T(8,128)S(1)}, u32[]{:S(2)}, u32[]{:S(2)}) collective-permute-start(f32[16,128]{1,0:T(8,128)S(1)} %get-tuple-element.68), channel_id=1, source_target_pairs={{1,0},{2,1},{3,2},{4,3},{5,4},{6,5},{7,6},{9,8},{10,9},{11,10},{12... | collective-permute-start | bytes 24584 | tf_op jit(solution)/shard_map/ppermute | solution.py:523
  73.0 2.9 %collective-permute-start.5 = (f32[16,128]{1,0:T(8,128)S(1)}, f32[16,128]{1,0:T(8,128)S(1)}, u32[]{:S(2)}, u32[]{:S(2)}) collective-permute-start(f32[16,128]{1,0:T(8,128)S(1)} %get-tuple-element.69), channel_id=1, source_target_pairs={{0,1},{1,2},{2,3},{3,4},{4,5},{5,6},{6,7},{8,9},{9,10},{10,11},{11... | collective-permute-start | bytes 24584 | tf_op jit(solution)/shard_map/ppermute | solution.py:522
  75.9 1.3 collective-permute-start.6
  77.2 4.1 %collective-permute-start.7 = (f32[8,128]{1,0:T(8,128)S(1)}, f32[8,128]{1,0:T(8,128)S(1)}, u32[]{:S(2)}, u32[]{:S(2)}) collective-permute-start(f32[8,128]{1,0:T(8,128)S(1)} %get-tuple-element.71), channel_id=1, source_target_pairs={{0,8},{8,16},{16,24},{24,32},{32,40},{40,48},{48,56},{56,64},{64,7... | collective-permute-start | bytes 12296 | tf_op jit(solution)/shard_map/ppermute | solution.py:516
  81.3 0.0 collective-permute-done.6.oi
  81.3 0.7 collective-permute-done.7.ei
  82.1 1.1 k_product.1
  83.2 8.1 %all_to_all.52.recv = f32[8,4,640]{2,1,0:T(4,128)S(1)} all-to-all(f32[8,4,640]{2,1,0:T(4,128)S(1)} %get-tuple-element.73), channel_id=1, replica_groups=mesh['y'=8,'z'=12,'sub'=8] {'sub'}, dimensions={0} | all-to-all | bytes 163840 | tf_op jit(solution)/shard_map/all_to_all | solution.py:492
  91.2 20.3 %all_to_all.53.recv = f32[8,4,384]{2,1,0:T(4,128)S(1)} all-to-all(f32[8,4,384]{2,1,0:T(4,128)S(1)} %get-tuple-element.74), channel_id=1, replica_groups=mesh['y'=8,'z'=12,'sub'=8] {'y'}, dimensions={0} | all-to-all | bytes 98304 | tf_op jit(solution)/shard_map/all_to_all | solution.py:492
  111.6 12.5 %all_to_all.54.recv = f32[12,4,512]{2,1,0:T(4,128)S(1)} all-to-all(f32[12,4,512]{2,1,0:T(4,128)S(1)} %k_pass.3), channel_id=1, replica_groups=mesh['y'=8,'z'=12,'sub'=8] {'z'}, dimensions={0} | all-to-all | bytes 196608 | tf_op jit(solution)/shard_map/all_to_all | solution.py:492
  124.0 0.2 k_global.1
  124.3 10.6 %all_to_all.55.recv = f32[8,4,128]{2,1,0:T(4,128)S(1)} all-to-all(f32[8,4,128]{2,1,0:T(4,128)S(1)} %get-tuple-element.77), channel_id=1, replica_groups=mesh['y'=8,'z'=12,'sub'=8] {'sub'}, dimensions={0} | all-to-all | bytes 32768 | tf_op jit(solution)/shard_map/all_to_all | solution.py:492
  134.8 0.6 k_last_image.1
  135.5 8.1 %all_to_all.56.recv = f32[8,24,128]{2,1,0:T(8,128)S(1)} all-to-all(f32[8,24,128]{2,1,0:T(8,128)S(1)} %get-tuple-element.86), channel_id=1, replica_groups=mesh['y'=8,'z'=12,'sub'=8] {'sub'}, dimensions={0} | all-to-all | bytes 196608 | tf_op jit(solution)/shard_map/all_to_all | solution.py:492
  143.6 0.7 k_total.1
  144.2 5.9 %all-to-all-start.9 = ((f32[96,1,128]{2,1,0:T(1,128)}), f32[96,1,128]{2,1,0:T(1,128)S(1)}, u32[]{:S(2)}, u32[]{:S(2)}) async-start(f32[96,1,128]{2,1,0:T(1,128)} %get-tuple-element.87), calls=%async_computation.9 | async-start | bytes 98304 | tf_op jit(solution)/shard_map/all_to_all | solution.py:492
  150.1 1.3 collective-permute-start.8
  151.4 4.0 %collective-permute-start.9 = (f32[8,128]{1,0:T(8,128)S(1)}, f32[8,128]{1,0:T(8,128)S(1)}, u32[]{:S(2)}, u32[]{:S(2)}) collective-permute-start(f32[8,128]{1,0:T(8,128)S(1)} %get-tuple-element.92), channel_id=1, source_target_pairs={{0,8},{8,16},{16,24},{24,32},{32,40},{40,48},{48,56},{56,64},{64,7... | collective-permute-start | bytes 12296 | tf_op jit(solution)/shard_map/ppermute | solution.py:516
  155.4 0.0 collective-permute-done.8.oi
  155.4 0.7 collective-permute-done.9.ei
  156.1 7.0 %all-to-all-done.9.recv = f32[96,1,128]{2,1,0:T(1,128)S(1)} async-done(((f32[96,1,128]{2,1,0:T(1,128)}), f32[96,1,128]{2,1,0:T(1,128)S(1)}, u32[]{:S(2)}, u32[]{:S(2)}) %all-to-all-start.9) | async-done | bytes 49184 | tf_op jit(solution)/shard_map/all_to_all | solution.py:492
  163.1 0.8 k_finish.1
  (22 shorter events, 0.1 us)
Async XLA Ops:
  0.6 58.3 %copy-start = (f32[192,1536]{1,0:T(8,128)S(1)}, f32[192,1536]{1,0:T(8,128)}, u32[]{:S(2)}) copy-start(f32[192,1536]{1,0:T(8,128)} %gc.3) | copy-start | bytes 3538948
  0.6 1.1 copy-start.2
  1.7 0.9 copy-start.4
  2.6 0.8 copy-start.5
  3.4 0.7 copy-start.6
  4.1 0.7 copy-start.7
  4.8 41.1 %copy-start.9 = (s32[4,384]{1,0:T(4,128)S(1)}, s32[4,384]{1,0:T(4,128)}, u32[]{:S(2)}) copy-start(s32[4,384]{1,0:T(4,128)} %signs.1) | copy-start | bytes 18436
  4.8 41.1 %copy-start.10 = (s32[4,3,128]{2,0,1:T(4,128)S(1)}, s32[4,3,128]{2,0,1:T(4,128)}, u32[]{:S(2)}) copy-start(s32[4,3,128]{2,0,1:T(4,128)} %param.12) | copy-start | bytes 18436
  34.1 25.3 %all-to-all-start.2 = ((f32[12,4,768]{2,1,0:T(4,128)}), f32[12,4,768]{2,1,0:T(4,128)S(1)}, u32[]{:S(2)}, u32[]{:S(2)}) async-start(f32[12,4,768]{2,1,0:T(4,128)} %k_pass.2), calls=%async_computation.2 | async-start | bytes 294912 | tf_op jit(solution)/shard_map/all_to_all | solution.py:492
  46.9 18.2 %collective-permute-start = (f32[144,128]{1,0:T(8,128)}, f32[144,128]{1,0:T(8,128)S(1)}, u32[]{:S(2)}, u32[]{:S(2)}) collective-permute-start(f32[144,128]{1,0:T(8,128)} %get-tuple-element.59), channel_id=1, source_target_pairs={{1,0},{2,1},{3,2},{4,3},{5,4},{6,5},{7,6},{9,8},{10,9},{11,10},{12... | collective-permute-start | bytes 221192 | tf_op jit(solution)/shard_map/ppermute | solution.py:523
  51.3 13.8 %collective-permute-start.1 = (f32[144,128]{1,0:T(8,128)}, f32[144,128]{1,0:T(8,128)S(1)}, u32[]{:S(2)}, u32[]{:S(2)}) collective-permute-start(f32[144,128]{1,0:T(8,128)} %get-tuple-element.60), channel_id=1, source_target_pairs={{0,1},{1,2},{2,3},{3,4},{4,5},{5,6},{6,7},{8,9},{9,10},{10,11},{11... | collective-permute-start | bytes 221192 | tf_op jit(solution)/shard_map/ppermute | solution.py:522
  53.4 11.6 %collective-permute-start.2 = (f32[72,128]{1,0:T(8,128)}, f32[72,128]{1,0:T(8,128)S(1)}, u32[]{:S(2)}, u32[]{:S(2)}) collective-permute-start(f32[72,128]{1,0:T(8,128)} %get-tuple-element.61), channel_id=1, source_target_pairs={{8,0},{16,8},{24,16},{32,24},{40,32},{48,40},{56,48},{64,56},{72,6... | collective-permute-start | bytes 110600 | tf_op jit(solution)/shard_map/ppermute | solution.py:515
  54.7 10.3 %collective-permute-start.3 = (f32[72,128]{1,0:T(8,128)}, f32[72,128]{1,0:T(8,128)S(1)}, u32[]{:S(2)}, u32[]{:S(2)}) collective-permute-start(f32[72,128]{1,0:T(8,128)} %get-tuple-element.62), channel_id=1, source_target_pairs={{0,8},{8,16},{16,24},{24,32},{32,40},{40,48},{48,56},{56,64},{64,7... | collective-permute-start | bytes 110600 | tf_op jit(solution)/shard_map/ppermute | solution.py:516
  59.4 10.3 %copy-start.1 = (bf16[4,384,384]{2,1,0:T(8,128)(2,1)S(1)}, bf16[4,384,384]{2,1,0:T(8,128)(2,1)}, u32[]{:S(2)}) copy-start(bf16[4,384,384]{2,1,0:T(8,128)(2,1)} %ops.3) | copy-start | bytes 3538948
  60.8 21.2 %copy-start.3 = (f32[1,96,768]{2,1,0:T(8,128)S(1)}, f32[1,96,768]{2,1,0:T(8,128)}, u32[]{:S(2)}) copy-start(f32[1,96,768]{2,1,0:T(8,128)} %param.16) | copy-start | bytes 884740
  60.8 21.2 %copy-start.8 = (s32[4,8]{1,0:T(4,128)S(1)}, s32[4,8]{1,0:T(4,128)}, u32[]{:S(2)}) copy-start(s32[4,8]{1,0:T(4,128)} %ids.3) | copy-start | bytes 388
  60.8 8.9 %all-to-all-start.3 = ((f32[8,4,128]{2,1,0:T(4,128)}), f32[8,4,128]{2,1,0:T(4,128)S(1)}, u32[]{:S(2)}, u32[]{:S(2)}) async-start(f32[8,4,128]{2,1,0:T(4,128)} %get-tuple-element.54), calls=%async_computation.3 | async-start | bytes 32768 | tf_op jit(solution)/shard_map/all_to_all | solution.py:492
  70.3 11.7 %collective-permute-start.4 = (f32[16,128]{1,0:T(8,128)S(1)}, f32[16,128]{1,0:T(8,128)S(1)}, u32[]{:S(2)}, u32[]{:S(2)}) collective-permute-start(f32[16,128]{1,0:T(8,128)S(1)} %get-tuple-element.68), channel_id=1, source_target_pairs={{1,0},{2,1},{3,2},{4,3},{5,4},{6,5},{7,6},{9,8},{10,9},{11,10},{12... | collective-permute-start | bytes 24584 | tf_op jit(solution)/shard_map/ppermute | solution.py:523
  73.0 9.1 %collective-permute-start.5 = (f32[16,128]{1,0:T(8,128)S(1)}, f32[16,128]{1,0:T(8,128)S(1)}, u32[]{:S(2)}, u32[]{:S(2)}) collective-permute-start(f32[16,128]{1,0:T(8,128)S(1)} %get-tuple-element.69), channel_id=1, source_target_pairs={{0,1},{1,2},{2,3},{3,4},{4,5},{5,6},{6,7},{8,9},{9,10},{10,11},{11... | collective-permute-start | bytes 24584 | tf_op jit(solution)/shard_map/ppermute | solution.py:522
  75.9 5.4 %collective-permute-start.6 = (f32[8,128]{1,0:T(8,128)S(1)}, f32[8,128]{1,0:T(8,128)S(1)}, u32[]{:S(2)}, u32[]{:S(2)}) collective-permute-start(f32[8,128]{1,0:T(8,128)S(1)} %get-tuple-element.70), channel_id=1, source_target_pairs={{8,0},{16,8},{24,16},{32,24},{40,32},{48,40},{56,48},{64,56},{72,6... | collective-permute-start | bytes 12296 | tf_op jit(solution)/shard_map/ppermute | solution.py:515
  77.2 4.8 %collective-permute-start.7 = (f32[8,128]{1,0:T(8,128)S(1)}, f32[8,128]{1,0:T(8,128)S(1)}, u32[]{:S(2)}, u32[]{:S(2)}) collective-permute-start(f32[8,128]{1,0:T(8,128)S(1)} %get-tuple-element.71), channel_id=1, source_target_pairs={{0,8},{8,16},{16,24},{24,32},{32,40},{40,48},{48,56},{56,64},{64,7... | collective-permute-start | bytes 12296 | tf_op jit(solution)/shard_map/ppermute | solution.py:516
  144.2 18.9 %all-to-all-start.9 = ((f32[96,1,128]{2,1,0:T(1,128)}), f32[96,1,128]{2,1,0:T(1,128)S(1)}, u32[]{:S(2)}, u32[]{:S(2)}) async-start(f32[96,1,128]{2,1,0:T(1,128)} %get-tuple-element.87), calls=%async_computation.9 | async-start | bytes 98304 | tf_op jit(solution)/shard_map/all_to_all | solution.py:492
  150.1 5.3 %collective-permute-start.8 = (f32[8,128]{1,0:T(8,128)S(1)}, f32[8,128]{1,0:T(8,128)S(1)}, u32[]{:S(2)}, u32[]{:S(2)}) collective-permute-start(f32[8,128]{1,0:T(8,128)S(1)} %get-tuple-element.91), channel_id=1, source_target_pairs={{8,0},{16,8},{24,16},{32,24},{40,32},{48,40},{56,48},{64,56},{72,6... | collective-permute-start | bytes 12296 | tf_op jit(solution)/shard_map/ppermute | solution.py:515
  151.4 4.7 %collective-permute-start.9 = (f32[8,128]{1,0:T(8,128)S(1)}, f32[8,128]{1,0:T(8,128)S(1)}, u32[]{:S(2)}, u32[]{:S(2)}) collective-permute-start(f32[8,128]{1,0:T(8,128)S(1)} %get-tuple-element.92), channel_id=1, source_target_pairs={{0,8},{8,16},{16,24},{24,32},{32,40},{40,48},{48,56},{56,64},{64,7... | collective-permute-start | bytes 12296 | tf_op jit(solution)/shard_map/ppermute | solution.py:516

commit v5 on v4

--- a/solution.py
+++ b/solution.py
@@ -25,6 +25,18 @@
 
 def iota(shape, dim):
     return lax.broadcasted_iota(I32, shape, dim)
+
+
+def pick(flag, a, b):
+    return jnp.where(jnp.full(a.shape, flag.astype(I32), I32) == 1, a, b)
+
+
+def even_member():
+    return lax.axis_index("sub") % 2 == 0
+
+
+def even_cluster():
+    return (lax.axis_index("y") * lax.axis_size("z") + lax.axis_index("z")) % 2 == 0
 
 
 def split(x):
@@ -140,19 +152,16 @@
 PACK = 72
 
 
-def k_coefs(ids, rhs, cb, kb, cc, msg, w_out, v_out):
+def k_coefs(ids, rhs, w, cc, msg, v_out):
     for s in range(S):
         v_out[R * s : R * s + R, :] = rhs[s]
-        w_out[KC * s : KC * s + KC, :] = cb[s]
-        w_out[NCL + 8 * s : NCL + 8 * s + 8, :] = kb[s]
     v = v_out[...]
-    write_message(msg, coefs(v, w_out[...]), cc, ids, [row_dot(v, v)[:8]])
-
-
-def k_send_static(after, w, v, signs, links, up, down, even, odd, sg_out, idx_out):
+    write_message(msg, coefs(v, w[...]), cc, ids, [row_dot(v, v)[:8]])
+
+
+def k_tables(after, signs, links, sg_out, idx_out):
     del after
     pos = iota((8, B), 1).astype(BF16)
-    moves = []
     for s in range(S):
         sg_out[R * s : R * s + R, :] = jnp.broadcast_to(signs[s : s + 1, :].astype(F32), (R, D))
         for b in range(3):
@@ -161,35 +170,90 @@
                 hot = jnp.where(iota((B, B), 0) == q, 1.0, 0.0).astype(BF16)
                 q = mm_t(pos, hot)[:1].astype(I32)
             idx_out[b, R * s : R * s + R, :] = jnp.broadcast_to(q, (R, B))
-            moves.append(q)
-
-    def moved(at, n, s, b):
-        q = jnp.broadcast_to(moves[3 * s + b], (n, B))
-        return jnp.take_along_axis(w[at : at + n, b * B : (b + 1) * B], q, axis=1)
+
+
+def static_blocks(w, v, idx, b):
+    lanes = pl.ds(pl.multiple_of(b * B, B), B)
+
+    def moved(x, q):
+        return jnp.take_along_axis(x, jnp.broadcast_to(q, x.shape), axis=1)
 
     for s in range(S):
-        h = s // 2
-        side = odd if s % 2 else even
-        for at, n, to in ((KC * s, KC, KC * h), (NCL + 8 * s, 8, 2 * KC + 8 * h)):
-            up[at : at + n, :] = moved(at, n, s, 0)
-            down[at : at + n, :] = moved(at, n, s, 1)
-            side[to : to + n, :] = moved(at, n, s, 2)
-    write_moved(v[...], idx_out, up, down, even, odd, NB, 2 * KC + 16)
-
-
-def write_moved(v, idx, up, down, even, odd, at=0, pack_at=0):
-    def moved(b):
-        return jnp.take_along_axis(v[:, b * B : (b + 1) * B], idx[b], axis=1)
-
-    up[at : at + ROWS, :] = moved(0)
-    down[at : at + ROWS, :] = moved(1)
-    across = moved(2)
+        q = idx[b, R * s : R * s + 1, :]
+        for at, n in ((KC * s, KC), (NCL + 8 * s, 8)):
+            yield s, at, moved(w[at : at + n, lanes], q)
+    yield None, NB, moved(v[:, lanes], idx[b])
+
+
+def send_within(w, v, idx, out, b):
+    for _, at, x in static_blocks(w, v, idx, b):
+        out[at : at + x.shape[0], :] = x
+
+
+def k_send_first(after, signs, links, w, v, sg_out, idx_out, out):
+    k_tables(after, signs, links, sg_out, idx_out)
+    send_within(w, v, idx_out, out, lax.axis_index("sub") % 2)
+
+
+def k_send_second(after, w, v, idx, out):
+    del after
+    send_within(w, v, idx, out, 1 - lax.axis_index("sub") % 2)
+
+
+def k_send_across(after, w, v, idx, first, second):
+    del after
+    flag = even_cluster()
+    blocks = {(s, at): x for s, at, x in static_blocks(w, v, idx, 2)}
+
+    def put(to, even, odd):
+        n = even.shape[0]
+        first[to : to + n, :] = pick(flag, even, odd)
+        second[to : to + n, :] = pick(flag, odd, even)
+
     for h in range(2):
-        even[pack_at + R * h : pack_at + R * h + R, :] = across[8 * h : 8 * h + 4]
-        odd[pack_at + R * h : pack_at + R * h + R, :] = across[8 * h + 4 : 8 * h + 8]
-
-
-def k_take_static(from_next, from_prev, odd_in, even_in, pw_out, pv_out):
+        s = 2 * h
+        put(KC * h, blocks[s, KC * s], blocks[s + 1, KC * (s + 1)])
+        put(2 * KC + 8 * h, blocks[s, NCL + 8 * s], blocks[s + 1, NCL + 8 * s + 8])
+        x = blocks[None, NB][8 * h : 8 * h + 8]
+        put(2 * KC + 16 + R * h, x[:R], x[R:])
+
+
+def moved_blocks(v, idx):
+    up, down, across = (
+        jnp.take_along_axis(v[:, b * B : (b + 1) * B], idx[b], axis=1) for b in range(3)
+    )
+    even = jnp.concatenate([across[0:R], across[8 : 8 + R]], axis=0)
+    odd = jnp.concatenate([across[R:8], across[8 + R :]], axis=0)
+    return up, down, even, odd
+
+
+def write_across(even, odd, first, second):
+    flag = even_cluster()
+    first[...] = pick(flag, even, odd)
+    second[...] = pick(flag, odd, even)
+
+
+def write_moved(v, idx, in1, in2, out1, out2):
+    up, down, even, odd = moved_blocks(v, idx)
+    flag = even_member()
+    in1[...] = pick(flag, up, down)
+    in2[...] = pick(flag, down, up)
+    write_across(even, odd, out1, out2)
+
+
+def across_of(out1, out2):
+    flag = even_cluster()
+    return pick(flag, out1, out2), pick(flag, out2, out1)
+
+
+def within_of(in1, in2):
+    flag = even_member()
+    return pick(flag, in1, in2), pick(flag, in2, in1)
+
+
+def take_static(in1, in2, out1, out2, pw_out, pv_out):
+    from_next, from_prev = within_of(in1[...], in2[...])
+    odd_in, even_in = across_of(out1[...], out2[...])
     pw_out[:, 0:B] = from_next[0:NB, :]
     pw_out[:, B : 2 * B] = from_prev[0:NB, :]
     for s in range(S):
@@ -251,6 +315,11 @@
     out[...] = jnp.broadcast_to(x[None], (n_z, *x.shape))
 
 
+def k_first_pass(recv, after, out):
+    del after
+    k_pass(recv, out)
+
+
 def neighbours(recv, at, wrapped_at):
     z = lax.axis_index("z")
     n_z = recv.shape[0]
@@ -313,7 +382,8 @@
     cacross[...] = jnp.where(lane < NCL, both, 0.0)[:R]
 
 
-def k_first_global(recv, gc, gh, gl, msg, scal, cacross, ah, al):
+def k_first_global(recv, gc, gh, gl, odd_after, even_after, msg, scal, cacross, ah, al):
+    del odd_after, even_after
     after, before = neighbours(recv, 3 * B, 5 * B)
     lane = iota((8, B), 1)
     after = pltpu.roll(after, B - 8, 1)
@@ -346,11 +416,10 @@
     return own, jnp.concatenate(pi, axis=1)
 
 
-def received(from_next, from_prev, odd_in, even_in):
-    across = jnp.concatenate(
-        [odd_in[0:R, :], even_in[0:R, :], odd_in[R : 2 * R, :], even_in[R : 2 * R, :]], axis=0
-    )
-    return jnp.concatenate([from_next[...], from_prev[...], across], axis=1)
+def received(from_next, from_prev, out1, out2):
+    odd_in, even_in = across_of(out1[...], out2[...])
+    across = jnp.concatenate([odd_in[0:R], even_in[0:R], odd_in[R:], even_in[R:]], axis=0)
+    return jnp.concatenate([from_next, from_prev, across], axis=1)
 
 
 def paired(n_cl):
@@ -375,9 +444,10 @@
 
 
 def k_first_image(
-    recv, csol, cacross, w, pw, v, pv, sg, ops, idx,
-    d_out, pd_out, signed_out, curv, up, down, even, odd,
+    recv, csol, cacross, in1, in2, out1, out2, w, v, sg, ops, idx,
+    pw, pv, d_out, pd_out, signed_out, curv, *outs,
 ):
+    take_static(in1, in2, out1, out2, pw, pv)
     fix, pfix = corrections(recv, csol, cacross, w, pw)
     d = v[...] - fix
     pd = pv[...] - pfix
@@ -386,12 +456,12 @@
     signed, c = image_of(d, pd, sg[...], ops)
     signed_out[...] = signed
     curv[...] = jnp.broadcast_to(c[:8], (8, B))
-    write_moved(signed, idx, up, down, even, odd)
+    write_moved(signed, idx, *outs)
 
 
 def make_product(n_cl):
-    def k_product(ids, signed, fn, fp, oi, ei, v, w, cc, curv, ap_out, pap_out, msg):
-        pi = received(fn, fp, oi, ei)
+    def k_product(ids, signed, in1, in2, out1, out2, v, w, cc, curv, ap_out, pap_out, msg):
+        pi = received(*within_of(in1[...], in2[...]), out1, out2)
         u = signed[...]
         ap = u + pi
         ap_out[...] = ap
@@ -411,7 +481,7 @@
 
 def k_last_image(
     recv, csol, cacross, scal0, scal1, w, pw, v, d, pd, ap, pap, sg, ops, idx,
-    r_out, x_out, d_out, signed_out, msg, even, odd, up, down,
+    r_out, x_out, d_out, signed_out, msg, out1, out2,
 ):
     fix, pfix = corrections(recv, csol, cacross, w, pw)
     rho = scalar_at(scal0[...], 0)
@@ -435,13 +505,14 @@
     row = iota((8, B), 0)
     both = jnp.where(lane == row, c[:8], jnp.where(lane == row + R, sq[:8], 0.0))
     both = jnp.where(row < R, both, 0.0)
-    write_moved(signed, idx, up, down, even, odd)
+    up, down, even, odd = moved_blocks(signed, idx)
+    write_across(even, odd, out1, out2)
     msg[...] = jnp.zeros(msg.shape, F32)
     for k in range(NSUB):
         msg[k, ROWS:LAST, :] = both
     k = lax.axis_index("sub")
-    msg[jnp.minimum(k + 1, NSUB - 1), 0:ROWS, :] = up[...]
-    msg[jnp.maximum(k - 1, 0), 0:ROWS, :] = down[...]
+    msg[jnp.minimum(k + 1, NSUB - 1), 0:ROWS, :] = up
+    msg[jnp.maximum(k - 1, 0), 0:ROWS, :] = down
 
 
 def k_total(recv, out, from_next, from_prev):
@@ -457,7 +528,7 @@
     from_prev[...] = jnp.where(jnp.full((ROWS, B), k, I32) > 0, before, 0.0)
 
 
-def k_finish(recv, signed, fn, fp, oi, ei, x, r, d, x_out, r_out):
+def k_finish(recv, signed, fn, fp, out1, out2, x, r, d, x_out, r_out):
     line = jnp.broadcast_to(jnp.sum(recv[...], axis=0), (ROWS, B))
     lane = iota((ROWS, B), 1)
     row = iota((ROWS, B), 0) % R
@@ -465,7 +536,7 @@
     rho = jnp.sum(jnp.where(lane == row + R, line, 0.0), axis=1, keepdims=True)
     step = rho / curv
     xn = x[...] + step * d[...]
-    rn = r[...] - step * (signed[...] + received(fn, fp, oi, ei))
+    rn = r[...] - step * (signed[...] + received(fn[...], fp[...], out1, out2))
     for s in range(S):
         x_out[s] = xn[R * s : R * s + R]
         r_out[s] = rn[R * s : R * s + R]
@@ -499,29 +570,21 @@
 FIELD = f32(ROWS, D)
 
 
-def sends(rows, pack):
-    return (f32(rows, B), f32(rows, B), f32(pack, B), f32(pack, B))
-
-
-def ahead(n):
-    return [(i, i + 1) for i in range(n - 1)]
-
-
-def back(n):
-    return [(i + 1, i) for i in range(n - 1)]
-
-
-def exchange_across(even, odd, n_cl):
-    odd_in = lax.ppermute(odd, CLUSTER, back(n_cl))
-    even_in = lax.ppermute(even, CLUSTER, ahead(n_cl))
-    return odd_in, even_in
-
-
-def exchange(up, down, even, odd, n_sub, n_cl):
-    across = exchange_across(even, odd, n_cl)
-    from_prev = lax.ppermute(up, "sub", ahead(n_sub))
-    from_next = lax.ppermute(down, "sub", back(n_sub))
-    return from_next, from_prev, *across
+SENDS = (f32(ROWS, B), f32(ROWS, B), f32(2 * R, B), f32(2 * R, B))
+
+
+def swap(x, axis, n, first):
+    low = range(0 if first else 1, n - 1, 2)
+    return lax.ppermute(x, axis, [p for i in low for p in ((i, i + 1), (i + 1, i))])
+
+
+def exchange_across(first, second, n_cl):
+    return swap(first, CLUSTER, n_cl, True), swap(second, CLUSTER, n_cl, False)
+
+
+def exchange(in1, in2, out1, out2, n_sub, n_cl):
+    across = exchange_across(out1, out2, n_cl)
+    return swap(in1, "sub", n_sub, True), swap(in2, "sub", n_sub, False), *across
 
 
 def local(rhs, operators, signs, links, cb, kb, ids, cluster_coarse, gc):
@@ -534,29 +597,33 @@
     picked = ((2 * B, 2 * B), BF16)
     answer = (f32(NSUB, R, B), f32(ROWS, B), f32(R, B))
 
-    msg, w, v = call(
-        k_coefs, (message, f32(NB, D), FIELD), ids, rhs, cb, kb, cc, smem=(0,)
-    )
+    w = jnp.concatenate([cb.reshape(NCL, D), kb.reshape(NB - NCL, D)], axis=0)
+    msg, v = call(k_coefs, (message, FIELD), ids, rhs, w, cc, smem=(0,))
     recv = to_owner(msg, "sub")
     rows, csol, all_ids = call(
         k_first_rows, (f32(n_y, R, 4 * B), f32(3, R, B), f32(8, B)), recv
     )
-    *out, sg, idx = call(
-        k_send_static,
-        (*sends(STATIC, PACK), FIELD, ((3, ROWS, B), I32)),
-        all_ids, w, v, signs, links.transpose(1, 0, 2),
-    )
-    got = exchange(*out, n_sub, n_cl)
-    pw, pv = call(k_take_static, (f32(NB, D), FIELD), *got)
+    sg, idx, in1 = call(
+        k_send_first,
+        (FIELD, ((3, ROWS, B), I32), f32(STATIC, B)),
+        all_ids, signs, links.transpose(1, 0, 2), w, v,
+    )
+    in1 = swap(in1, "sub", n_sub, True)
+    recv = to_owner(rows, "y")
+    (rows,) = call(k_first_pass, (f32(n_z, R, 6 * B),), recv, in1)
+    out = call(k_send_across, (f32(PACK, B), f32(PACK, B)), recv, w, v, idx)
+    across = exchange_across(*out, n_cl)
     gh, gl = call(k_own_columns, (picked, picked), all_ids, gc)
-    (rows,) = call(k_pass, (f32(n_z, R, 6 * B),), to_owner(rows, "y"))
     to_all, scal0, cacross, ah, al = call(
-        k_first_global, (*answer, picked, picked), to_owner(rows, "z"), gc, gh, gl
-    )
-    d, pd, signed, curv, *out = call(
+        k_first_global, (*answer, picked, picked), to_owner(rows, "z"), gc, gh, gl, *across
+    )
+    (in2,) = call(k_send_second, (f32(STATIC, B),), to_all, w, v, idx)
+    in2 = swap(in2, "sub", n_sub, False)
+    pw, pv, d, pd, signed, curv, *out = call(
         k_first_image,
-        (FIELD, FIELD, FIELD, f32(8, B), *sends(ROWS, 2 * R)),
-        to_owner(to_all, "sub"), csol, cacross, w, pw, v, pv, sg, operators, idx,
+        (f32(NB, D), FIELD, FIELD, FIELD, FIELD, f32(8, B), *SENDS),
+        to_owner(to_all, "sub"), csol, cacross, in1, in2, *across,
+        w, v, sg, operators, idx,
     )
     got = exchange(*out, n_sub, n_cl)
     ap, pap, msg = call(
@@ -567,17 +634,16 @@
     rows, csol = call(k_rows, (f32(n_y, R, D), f32(3, R, B)), to_owner(msg, "sub"))
     (rows,) = call(k_pass, (f32(n_z, R, 4 * B),), to_owner(rows, "y"))
     to_all, scal1, cacross = call(k_global, answer, to_owner(rows, "z"), gh, gl, ah, al)
-    r, x, d1, signed, msg, even, odd = call(
+    r, x, d1, signed, msg, *out = call(
         k_last_image,
         (FIELD, FIELD, FIELD, FIELD, f32(NSUB, LAST, B), f32(2 * R, B), f32(2 * R, B)),
         to_owner(to_all, "sub"), csol, cacross, scal0, scal1,
         w, pw, v, d, pd, ap, pap, sg, operators, idx,
-        scratch=(pltpu.VMEM((ROWS, B), F32), pltpu.VMEM((ROWS, B), F32)),
     )
     line, from_next, from_prev = call(
         k_total, (f32(n_cl, 1, B), f32(ROWS, B), f32(ROWS, B)), to_owner(msg, "sub")
     )
-    across = exchange_across(even, odd, n_cl)
+    across = exchange_across(*out, n_cl)
     out = f32(S, R, D)
     return call(
         k_finish, (out, out), to_owner(line, CLUSTER), signed, from_next, from_prev, *across, x, r, d1

time: 165 us -> 164 us (level)
  waiting for transfers between devices: 13.1 us -> 19.8 us
  starting transfers between devices: 50 us -> 44 us
  blocking collectives: 86.9 us -> 84.7 us
    ppermute x10, starting transfers between devices: 28.2 us -> 23.6 us  [swap(): lax.ppermute(x, axis, [p for i in low for p in ((i, i + 1), (i + 1, i))])]
    all_to_all x3, waiting for transfers between devices: 11.6 us -> 15.7 us  [to_owner(): return lax.all_to_all(x, axis, 0, 0, tiled=True)]
    ppermute x10, waiting for transfers between devices: 1.47 us -> 4.06 us  [swap(): lax.ppermute(x, axis, [p for i in low for p in ((i, i + 1), (i + 1, i))])]
    all_to_all x7, blocking collectives: 86.9 us -> 84.7 us  [to_owner(): return lax.all_to_all(x, axis, 0, 0, tiled=True)]
    unnamed x22 -> x18, local copies, waits for them, and re-layouts: 4.2 us -> 3.77 us
    pallas_call x15 -> x16, Pallas kernels: 8.79 us -> 8.79 us  [call(): pl.pallas_call(body, out_shape=out_shape, in_specs=specs, out_specs=tuple...]
  transfers between devices with their start and end apart: 13 -> 13, of which waited for: 4 -> 7; matrix products, arithmetic and copies ran while one was open for 0% -> 0% of each run, Pallas kernels for 2% -> 1%
where the time goes in v5:
time: 164 us; the launch traced here: 163 us
  blocking collectives  84.7 us (52%)
  starting transfers between devices  44 us (27%)
  waiting for transfers between devices  19.8 us (12%)
  Pallas kernels  8.79 us (5%)
  local copies, waits for them, and re-layouts  3.77 us (2%)
    all_to_all x7, blocking collectives, to_owner(): return lax.all_to_all(x, axis, 0, 0, tiled=True)  84.7 us
    ppermute x10, starting transfers between devices, swap(): lax.ppermute(x, axis, [p for i in low for p in ((i, i + 1), (i + 1, i))])  23.6 us
    all_to_all x3, starting transfers between devices, to_owner(): return lax.all_to_all(x, axis, 0, 0, tiled=True)  20.3 us
    all_to_all x3, waiting for transfers between devices, to_owner(): return lax.all_to_all(x, axis, 0, 0, tiled=True)  15.7 us
    pallas_call x16, Pallas kernels, call(): pl.pallas_call(body, out_shape=out_shape, in_specs=specs, out_specs=tuple...  8.79 us
    ppermute x10, waiting for transfers between devices, swap(): lax.ppermute(x, axis, [p for i in low for p in ((i, i + 1), (i + 1, i))])  4.06 us
    unnamed x18, local copies, waits for them, and re-layouts  3.77 us
  transfers between devices with their start and end apart: 13, of which 7 were waited for; matrix products, arithmetic and copies ran while one was open for 0% of the time, Pallas kernels for 1%

profile of v5, /device:TPU:1, one launch (start us, length us, event | category | flops | bytes accessed | tf_op | source)
XLA Modules:
  0.0 163.0 jit_solution(1004591814326914365)
XLA Ops:
  0.6 1.0 pad_maximum_fusion.w
  1.7 0.0 copy-start.2
  1.7 1.0 copy-done.2
  2.7 0.7 copy-done.4
  3.4 0.7 copy-done.5
  4.1 1.1 k_coefs.1
  5.1 17.8 %all_to_all.50.recv = f32[8,4,640]{2,1,0:T(4,128)S(1)} all-to-all(f32[8,4,640]{2,1,0:T(4,128)S(1)} %get-tuple-element.46), channel_id=1, replica_groups=mesh['y'=8,'z'=12,'sub'=8] {'sub'}, dimensions={0} | all-to-all | bytes 163840 | tf_op jit(solution)/shard_map/all_to_all | solution.py:563
  22.9 0.7 k_first_rows.1
  23.6 3.3 %all-to-all-start.1 = ((f32[8,4,512]{2,1,0:T(4,128)}), f32[8,4,512]{2,1,0:T(4,128)S(1)}, u32[]{:S(2)}, u32[]{:S(2)}) async-start(f32[8,4,512]{2,1,0:T(4,128)} %get-tuple-element.47), calls=%async_computation.1 | async-start | bytes 131072 | tf_op jit(solution)/shard_map/all_to_all | solution.py:563
  27.0 0.7 copy-done.7
  27.7 0.7 copy-done.8
  28.4 0.3 k_send_first.1
  28.7 2.7 %collective-permute-start = (f32[144,128]{1,0:T(8,128)S(1)}, f32[144,128]{1,0:T(8,128)S(1)}, u32[]{:S(2)}, u32[]{:S(2)}) collective-permute-start(f32[144,128]{1,0:T(8,128)S(1)} %get-tuple-element.50), channel_id=1, source_target_pairs={{0,1},{1,0},{2,3},{3,2},{4,5},{5,4},{6,7},{7,6},{8,9},{9,8},{10,11... | collective-permute-start | bytes 221192 | tf_op jit(solution)/shard_map/ppermute | solution.py:578
  31.4 0.9 collective-permute-done.after.in1
  32.3 1.9 %all-to-all-done.1.recv.after = f32[8,4,512]{2,1,0:T(4,128)S(1)} async-done(((f32[8,4,512]{2,1,0:T(4,128)}), f32[8,4,512]{2,1,0:T(4,128)S(1)}, u32[]{:S(2)}, u32[]{:S(2)}) %all-to-all-start.1) | async-done | bytes 65568 | tf_op jit(solution)/shard_map/all_to_all | solution.py:563
  34.2 0.7 k_first_pass.1
  34.9 11.1 %all-to-all-start.2 = ((f32[12,4,768]{2,1,0:T(4,128)}), f32[12,4,768]{2,1,0:T(4,128)S(1)}, u32[]{:S(2)}, u32[]{:S(2)}) async-start(f32[12,4,768]{2,1,0:T(4,128)} %k_first_pass.1), calls=%async_computation.2 | async-start | bytes 294912 | tf_op jit(solution)/shard_map/all_to_all | solution.py:563
  46.0 0.1 k_send_across.1
  46.1 3.3 %collective-permute-start.1 = (f32[72,128]{1,0:T(8,128)S(1)}, f32[72,128]{1,0:T(8,128)S(1)}, u32[]{:S(2)}, u32[]{:S(2)}) collective-permute-start(f32[72,128]{1,0:T(8,128)S(1)} %get-tuple-element.54), channel_id=1, source_target_pairs={{0,8},{8,0},{16,24},{24,16},{32,40},{40,32},{48,56},{56,48},{64,72... | collective-permute-start | bytes 110600 | tf_op jit(solution)/shard_map/ppermute | solution.py:578
  49.4 0.7 collective-permute-start.2
  50.1 0.5 k_own_columns.1
  50.6 0.7 collective-permute-done.1.odd_after.out1
  51.3 5.4 %all-to-all-done.2.recv = f32[12,4,768]{2,1,0:T(4,128)S(1)} async-done(((f32[12,4,768]{2,1,0:T(4,128)}), f32[12,4,768]{2,1,0:T(4,128)S(1)}, u32[]{:S(2)}, u32[]{:S(2)}) %all-to-all-start.2) | async-done | bytes 147488 | tf_op jit(solution)/shard_map/all_to_all | solution.py:563
  56.7 0.8 k_first_global.1
  57.5 0.1 k_send_second.1
  57.6 5.7 %collective-permute-start.3 = (f32[144,128]{1,0:T(8,128)S(1)}, f32[144,128]{1,0:T(8,128)S(1)}, u32[]{:S(2)}, u32[]{:S(2)}) collective-permute-start(f32[144,128]{1,0:T(8,128)S(1)} %k_send_second.1), channel_id=1, source_target_pairs={{1,2},{2,1},{3,4},{4,3},{5,6},{6,5},{9,10},{10,9},{11,12},{12,11},... | collective-permute-start | bytes 221192 | tf_op jit(solution)/shard_map/ppermute | solution.py:578
  63.3 7.9 %all_to_all.51.recv = f32[8,4,128]{2,1,0:T(4,128)S(1)} all-to-all(f32[8,4,128]{2,1,0:T(4,128)S(1)} %get-tuple-element.56.after), channel_id=1, replica_groups=mesh['y'=8,'z'=12,'sub'=8] {'sub'}, dimensions={0} | all-to-all | bytes 32768 | tf_op jit(solution)/shard_map/all_to_all | solution.py:563
  71.2 1.1 k_first_image.1
  72.3 2.6 %collective-permute-start.4 = (f32[16,128]{1,0:T(8,128)S(1)}, f32[16,128]{1,0:T(8,128)S(1)}, u32[]{:S(2)}, u32[]{:S(2)}) collective-permute-start(f32[16,128]{1,0:T(8,128)S(1)} %get-tuple-element.61), channel_id=1, source_target_pairs={{0,1},{1,0},{2,3},{3,2},{4,5},{5,4},{6,7},{7,6},{8,9},{9,8},{10,11... | collective-permute-start | bytes 24584 | tf_op jit(solution)/shard_map/ppermute | solution.py:578
  74.9 2.1 %collective-permute-start.5 = (f32[16,128]{1,0:T(8,128)S(1)}, f32[16,128]{1,0:T(8,128)S(1)}, u32[]{:S(2)}, u32[]{:S(2)}) collective-permute-start(f32[16,128]{1,0:T(8,128)S(1)} %get-tuple-element.62), channel_id=1, source_target_pairs={{1,2},{2,1},{3,4},{4,3},{5,6},{6,5},{9,10},{10,9},{11,12},{12,11},... | collective-permute-start | bytes 24584 | tf_op jit(solution)/shard_map/ppermute | solution.py:578
  77.0 2.6 %collective-permute-start.6 = (f32[8,128]{1,0:T(8,128)S(1)}, f32[8,128]{1,0:T(8,128)S(1)}, u32[]{:S(2)}, u32[]{:S(2)}) collective-permute-start(f32[8,128]{1,0:T(8,128)S(1)} %get-tuple-element.63), channel_id=1, source_target_pairs={{0,8},{8,0},{16,24},{24,16},{32,40},{40,32},{48,56},{56,48},{64,72... | collective-permute-start | bytes 12296 | tf_op jit(solution)/shard_map/ppermute | solution.py:578
  79.7 0.7 collective-permute-start.7
  80.3 1.0 collective-permute-done.6.out1
  81.4 1.1 k_product.1
  82.5 9.7 %all_to_all.52.recv = f32[8,4,640]{2,1,0:T(4,128)S(1)} all-to-all(f32[8,4,640]{2,1,0:T(4,128)S(1)} %get-tuple-element.66), channel_id=1, replica_groups=mesh['y'=8,'z'=12,'sub'=8] {'sub'}, dimensions={0} | all-to-all | bytes 163840 | tf_op jit(solution)/shard_map/all_to_all | solution.py:563
  92.2 18.1 %all_to_all.53.recv = f32[8,4,384]{2,1,0:T(4,128)S(1)} all-to-all(f32[8,4,384]{2,1,0:T(4,128)S(1)} %get-tuple-element.67), channel_id=1, replica_groups=mesh['y'=8,'z'=12,'sub'=8] {'y'}, dimensions={0} | all-to-all | bytes 98304 | tf_op jit(solution)/shard_map/all_to_all | solution.py:563
  110.4 12.5 %all_to_all.54.recv = f32[12,4,512]{2,1,0:T(4,128)S(1)} all-to-all(f32[12,4,512]{2,1,0:T(4,128)S(1)} %k_pass.1), channel_id=1, replica_groups=mesh['y'=8,'z'=12,'sub'=8] {'z'}, dimensions={0} | all-to-all | bytes 196608 | tf_op jit(solution)/shard_map/all_to_all | solution.py:563
  122.9 0.2 k_global.1
  123.1 10.6 %all_to_all.55.recv = f32[8,4,128]{2,1,0:T(4,128)S(1)} all-to-all(f32[8,4,128]{2,1,0:T(4,128)S(1)} %get-tuple-element.70), channel_id=1, replica_groups=mesh['y'=8,'z'=12,'sub'=8] {'sub'}, dimensions={0} | all-to-all | bytes 32768 | tf_op jit(solution)/shard_map/all_to_all | solution.py:563
  133.7 0.6 k_last_image.1
  134.4 8.1 %all_to_all.56.recv = f32[8,24,128]{2,1,0:T(8,128)S(1)} all-to-all(f32[8,24,128]{2,1,0:T(8,128)S(1)} %get-tuple-element.80), channel_id=1, replica_groups=mesh['y'=8,'z'=12,'sub'=8] {'sub'}, dimensions={0} | all-to-all | bytes 196608 | tf_op jit(solution)/shard_map/all_to_all | solution.py:563
  142.5 0.7 k_total.1
  143.1 5.9 %all-to-all-start.9 = ((f32[96,1,128]{2,1,0:T(1,128)}), f32[96,1,128]{2,1,0:T(1,128)S(1)}, u32[]{:S(2)}, u32[]{:S(2)}) async-start(f32[96,1,128]{2,1,0:T(1,128)} %get-tuple-element.81), calls=%async_computation.9 | async-start | bytes 98304 | tf_op jit(solution)/shard_map/all_to_all | solution.py:563
  149.1 2.6 %collective-permute-start.8 = (f32[8,128]{1,0:T(8,128)S(1)}, f32[8,128]{1,0:T(8,128)S(1)}, u32[]{:S(2)}, u32[]{:S(2)}) collective-permute-start(f32[8,128]{1,0:T(8,128)S(1)} %get-tuple-element.85), channel_id=1, source_target_pairs={{0,8},{8,0},{16,24},{24,16},{32,40},{40,32},{48,56},{56,48},{64,72... | collective-permute-start | bytes 12296 | tf_op jit(solution)/shard_map/ppermute | solution.py:578
  151.7 0.7 collective-permute-start.9
  152.3 1.4 collective-permute-done.8.out1
  153.8 8.4 %all-to-all-done.9.recv = f32[96,1,128]{2,1,0:T(1,128)S(1)} async-done(((f32[96,1,128]{2,1,0:T(1,128)}), f32[96,1,128]{2,1,0:T(1,128)S(1)}, u32[]{:S(2)}, u32[]{:S(2)}) %all-to-all-start.9) | async-done | bytes 49184 | tf_op jit(solution)/shard_map/all_to_all | solution.py:563
  162.1 0.8 k_finish.1
  (20 shorter events, 0.1 us)
Async XLA Ops:
  0.6 49.5 %copy-start = (f32[192,1536]{1,0:T(8,128)S(1)}, f32[192,1536]{1,0:T(8,128)}, u32[]{:S(2)}) copy-start(f32[192,1536]{1,0:T(8,128)} %gc.3) | copy-start | bytes 3538948
  1.7 1.0 copy-start.2
  2.7 0.7 copy-start.4
  3.4 0.7 copy-start.5
  23.6 10.6 %all-to-all-start.1 = ((f32[8,4,512]{2,1,0:T(4,128)}), f32[8,4,512]{2,1,0:T(4,128)S(1)}, u32[]{:S(2)}, u32[]{:S(2)}) async-start(f32[8,4,512]{2,1,0:T(4,128)} %get-tuple-element.47), calls=%async_computation.1 | async-start | bytes 131072 | tf_op jit(solution)/shard_map/all_to_all | solution.py:563
  27.0 0.7 copy-start.7
  27.7 0.7 copy-start.8
  28.7 3.6 %collective-permute-start = (f32[144,128]{1,0:T(8,128)S(1)}, f32[144,128]{1,0:T(8,128)S(1)}, u32[]{:S(2)}, u32[]{:S(2)}) collective-permute-start(f32[144,128]{1,0:T(8,128)S(1)} %get-tuple-element.50), channel_id=1, source_target_pairs={{0,1},{1,0},{2,3},{3,2},{4,5},{5,4},{6,7},{7,6},{8,9},{9,8},{10,11... | collective-permute-start | bytes 221192 | tf_op jit(solution)/shard_map/ppermute | solution.py:578
  34.9 21.8 %all-to-all-start.2 = ((f32[12,4,768]{2,1,0:T(4,128)}), f32[12,4,768]{2,1,0:T(4,128)S(1)}, u32[]{:S(2)}, u32[]{:S(2)}) async-start(f32[12,4,768]{2,1,0:T(4,128)} %k_first_pass.1), calls=%async_computation.2 | async-start | bytes 294912 | tf_op jit(solution)/shard_map/all_to_all | solution.py:563
  46.1 5.2 %collective-permute-start.1 = (f32[72,128]{1,0:T(8,128)S(1)}, f32[72,128]{1,0:T(8,128)S(1)}, u32[]{:S(2)}, u32[]{:S(2)}) collective-permute-start(f32[72,128]{1,0:T(8,128)S(1)} %get-tuple-element.54), channel_id=1, source_target_pairs={{0,8},{8,0},{16,24},{24,16},{32,40},{40,32},{48,56},{56,48},{64,72... | collective-permute-start | bytes 110600 | tf_op jit(solution)/shard_map/ppermute | solution.py:578
  49.4 1.9 %collective-permute-start.2 = (f32[72,128]{1,0:T(8,128)S(1)}, f32[72,128]{1,0:T(8,128)S(1)}, u32[]{:S(2)}, u32[]{:S(2)}) collective-permute-start(f32[72,128]{1,0:T(8,128)S(1)} %get-tuple-element.55), channel_id=1, source_target_pairs={{8,16},{16,8},{24,32},{32,24},{40,48},{48,40},{56,64},{64,56},{72,... | collective-permute-start | bytes 110600 | tf_op jit(solution)/shard_map/ppermute | solution.py:578
  50.6 20.6 %copy-start.1 = (bf16[4,384,384]{2,1,0:T(8,128)(2,1)S(1)}, bf16[4,384,384]{2,1,0:T(8,128)(2,1)}, u32[]{:S(2)}) copy-start(bf16[4,384,384]{2,1,0:T(8,128)(2,1)} %ops.3) | copy-start | bytes 3538948
  57.5 23.9 %copy-start.3 = (f32[1,96,768]{2,1,0:T(8,128)S(1)}, f32[1,96,768]{2,1,0:T(8,128)}, u32[]{:S(2)}) copy-start(f32[1,96,768]{2,1,0:T(8,128)} %param.16) | copy-start | bytes 884740
  57.5 23.9 %copy-start.6 = (s32[4,8]{1,0:T(4,128)S(1)}, s32[4,8]{1,0:T(4,128)}, u32[]{:S(2)}) copy-start(s32[4,8]{1,0:T(4,128)} %ids.3) | copy-start | bytes 388
  57.6 13.6 %collective-permute-start.3 = (f32[144,128]{1,0:T(8,128)S(1)}, f32[144,128]{1,0:T(8,128)S(1)}, u32[]{:S(2)}, u32[]{:S(2)}) collective-permute-start(f32[144,128]{1,0:T(8,128)S(1)} %k_send_second.1), channel_id=1, source_target_pairs={{1,2},{2,1},{3,4},{4,3},{5,6},{6,5},{9,10},{10,9},{11,12},{12,11},... | collective-permute-start | bytes 221192 | tf_op jit(solution)/shard_map/ppermute | solution.py:578
  72.3 9.1 %collective-permute-start.4 = (f32[16,128]{1,0:T(8,128)S(1)}, f32[16,128]{1,0:T(8,128)S(1)}, u32[]{:S(2)}, u32[]{:S(2)}) collective-permute-start(f32[16,128]{1,0:T(8,128)S(1)} %get-tuple-element.61), channel_id=1, source_target_pairs={{0,1},{1,0},{2,3},{3,2},{4,5},{5,4},{6,7},{7,6},{8,9},{9,8},{10,11... | collective-permute-start | bytes 24584 | tf_op jit(solution)/shard_map/ppermute | solution.py:578
  74.9 6.5 %collective-permute-start.5 = (f32[16,128]{1,0:T(8,128)S(1)}, f32[16,128]{1,0:T(8,128)S(1)}, u32[]{:S(2)}, u32[]{:S(2)}) collective-permute-start(f32[16,128]{1,0:T(8,128)S(1)} %get-tuple-element.62), channel_id=1, source_target_pairs={{1,2},{2,1},{3,4},{4,3},{5,6},{6,5},{9,10},{10,9},{11,12},{12,11},... | collective-permute-start | bytes 24584 | tf_op jit(solution)/shard_map/ppermute | solution.py:578
  77.0 4.4 %collective-permute-start.6 = (f32[8,128]{1,0:T(8,128)S(1)}, f32[8,128]{1,0:T(8,128)S(1)}, u32[]{:S(2)}, u32[]{:S(2)}) collective-permute-start(f32[8,128]{1,0:T(8,128)S(1)} %get-tuple-element.63), channel_id=1, source_target_pairs={{0,8},{8,0},{16,24},{24,16},{32,40},{40,32},{48,56},{56,48},{64,72... | collective-permute-start | bytes 12296 | tf_op jit(solution)/shard_map/ppermute | solution.py:578
  79.7 1.7 %collective-permute-start.7 = (f32[8,128]{1,0:T(8,128)S(1)}, f32[8,128]{1,0:T(8,128)S(1)}, u32[]{:S(2)}, u32[]{:S(2)}) collective-permute-start(f32[8,128]{1,0:T(8,128)S(1)} %get-tuple-element.64), channel_id=1, source_target_pairs={{8,16},{16,8},{24,32},{32,24},{40,48},{48,40},{56,64},{64,56},{72,... | collective-permute-start | bytes 12296 | tf_op jit(solution)/shard_map/ppermute | solution.py:578
  143.1 19.0 %all-to-all-start.9 = ((f32[96,1,128]{2,1,0:T(1,128)}), f32[96,1,128]{2,1,0:T(1,128)S(1)}, u32[]{:S(2)}, u32[]{:S(2)}) async-start(f32[96,1,128]{2,1,0:T(1,128)} %get-tuple-element.81), calls=%async_computation.9 | async-start | bytes 98304 | tf_op jit(solution)/shard_map/all_to_all | solution.py:563
  149.1 4.7 %collective-permute-start.8 = (f32[8,128]{1,0:T(8,128)S(1)}, f32[8,128]{1,0:T(8,128)S(1)}, u32[]{:S(2)}, u32[]{:S(2)}) collective-permute-start(f32[8,128]{1,0:T(8,128)S(1)} %get-tuple-element.85), channel_id=1, source_target_pairs={{0,8},{8,0},{16,24},{24,16},{32,40},{40,32},{48,56},{56,48},{64,72... | collective-permute-start | bytes 12296 | tf_op jit(solution)/shard_map/ppermute | solution.py:578
  151.7 2.1 %collective-permute-start.9 = (f32[8,128]{1,0:T(8,128)S(1)}, f32[8,128]{1,0:T(8,128)S(1)}, u32[]{:S(2)}, u32[]{:S(2)}) collective-permute-start(f32[8,128]{1,0:T(8,128)S(1)} %get-tuple-element.86), channel_id=1, source_target_pairs={{8,16},{16,8},{24,32},{32,24},{40,48},{48,40},{56,64},{64,56},{72,... | collective-permute-start | bytes 12296 | tf_op jit(solution)/shard_map/ppermute | solution.py:578

commit v6 on v5

--- a/solution.py
+++ b/solution.py
@@ -5,6 +5,7 @@
 from jax.experimental.pallas import tpu as pltpu
 from jax.sharding import Mesh
 from jax.sharding import PartitionSpec as P
+
 
 F32 = jnp.float32
 BF16 = jnp.bfloat16
@@ -554,7 +555,6 @@
         in_specs=specs,
         out_specs=tuple(pl.BlockSpec(memory_space=pltpu.VMEM) for _ in outs),
         scratch_shapes=scratch,
-        name=body.__name__,
         compiler_params=pltpu.CompilerParams(vmem_limit_bytes=VMEM_LIMIT),
     )(*args)
 
@@ -579,15 +579,19 @@
 
 
 def exchange_across(first, second, n_cl):
-    return swap(first, CLUSTER, n_cl, True), swap(second, CLUSTER, n_cl, False)
+    first = swap(first, CLUSTER, n_cl, True)
+    second = swap(second, CLUSTER, n_cl, False)
+    return first, second
 
 
 def exchange(in1, in2, out1, out2, n_sub, n_cl):
     across = exchange_across(out1, out2, n_cl)
-    return swap(in1, "sub", n_sub, True), swap(in2, "sub", n_sub, False), *across
-
-
-def local(rhs, operators, signs, links, cb, kb, ids, cluster_coarse, gc):
+    in2 = swap(in2, "sub", n_sub, False)
+    in1 = swap(in1, "sub", n_sub, True)
+    return in1, in2, *across
+
+
+def solve_all(rhs, operators, signs, links, cb, kb, ids, cluster_coarse, gc):
     n_sub = lax.axis_size("sub")
     n_y = lax.axis_size("y")
     n_z = lax.axis_size("z")
@@ -619,10 +623,11 @@
     )
     (in2,) = call(k_send_second, (f32(STATIC, B),), to_all, w, v, idx)
     in2 = swap(in2, "sub", n_sub, False)
+    to_all = to_owner(to_all, "sub")
     pw, pv, d, pd, signed, curv, *out = call(
         k_first_image,
         (f32(NB, D), FIELD, FIELD, FIELD, FIELD, f32(8, B), *SENDS),
-        to_owner(to_all, "sub"), csol, cacross, in1, in2, *across,
+        to_all, csol, cacross, in1, in2, *across,
         w, v, sg, operators, idx,
     )
     got = exchange(*out, n_sub, n_cl)
@@ -666,4 +671,4 @@
         P("sub", None),
     )
     out_specs = (P(both, None, None), P(both, None, None))
-    return jax.shard_map(local, mesh=torus, in_specs=in_specs, out_specs=out_specs, check_vma=False)
+    return jax.shard_map(solve_all, mesh=torus, in_specs=in_specs, out_specs=out_specs, check_vma=False)

time: 164 us -> 164 us (level)
  no operation moved by 1% of the time
where the time goes in v6:
time: 164 us; the launch traced here: 163 us
  blocking collectives  84.7 us (52%)
  starting transfers between devices  44 us (27%)
  waiting for transfers between devices  19.8 us (12%)
  Pallas kernels  8.79 us (5%)
  local copies, waits for them, and re-layouts  3.77 us (2%)
    all_to_all x7, blocking collectives, to_owner(): return lax.all_to_all(x, axis, 0, 0, tiled=True)  84.7 us
    ppermute x10, starting transfers between devices, swap(): lax.ppermute(x, axis, [p for i in low for p in ((i, i + 1), (i + 1, i))])  23.6 us
    all_to_all x3, starting transfers between devices, to_owner(): return lax.all_to_all(x, axis, 0, 0, tiled=True)  20.3 us
    all_to_all x3, waiting for transfers between devices, to_owner(): return lax.all_to_all(x, axis, 0, 0, tiled=True)  15.7 us
    pallas_call x16, Pallas kernels, call(): pl.pallas_call(body, out_shape=out_shape, in_specs=specs, out_specs=tuple...  8.79 us
    ppermute x10, waiting for transfers between devices, swap(): lax.ppermute(x, axis, [p for i in low for p in ((i, i + 1), (i + 1, i))])  4.06 us
    unnamed x18, local copies, waits for them, and re-layouts  3.77 us
  transfers between devices with their start and end apart: 13, of which 7 were waited for; matrix products, arithmetic and copies ran while one was open for 0% of the time, Pallas kernels for 1%

profile of v6, /device:TPU:1, one launch (start us, length us, event | category | flops | bytes accessed | tf_op | source)
XLA Modules:
  0.0 163.0 jit_solution(1004591814326914365)
XLA Ops:
  0.6 1.0 pad_maximum_fusion.w
  1.7 0.0 copy-start.2
  1.7 1.0 copy-done.2
  2.7 0.7 copy-done.4
  3.4 0.7 copy-done.5
  4.1 1.1 shard_map.104
  5.1 17.8 %all_to_all.50.recv = f32[8,4,640]{2,1,0:T(4,128)S(1)} all-to-all(f32[8,4,640]{2,1,0:T(4,128)S(1)} %get-tuple-element.46), channel_id=1, replica_groups=mesh['y'=8,'z'=12,'sub'=8] {'sub'}, dimensions={0} | all-to-all | bytes 163840 | tf_op jit(solution)/shard_map/all_to_all | solution.py:563
  22.9 0.7 shard_map.105
  23.6 3.3 %all-to-all-start.1 = ((f32[8,4,512]{2,1,0:T(4,128)}), f32[8,4,512]{2,1,0:T(4,128)S(1)}, u32[]{:S(2)}, u32[]{:S(2)}) async-start(f32[8,4,512]{2,1,0:T(4,128)} %get-tuple-element.47), calls=%async_computation.1 | async-start | bytes 131072 | tf_op jit(solution)/shard_map/all_to_all | solution.py:563
  27.0 0.7 copy-done.7
  27.7 0.7 copy-done.8
  28.4 0.3 shard_map.106
  28.7 2.7 %collective-permute-start = (f32[144,128]{1,0:T(8,128)S(1)}, f32[144,128]{1,0:T(8,128)S(1)}, u32[]{:S(2)}, u32[]{:S(2)}) collective-permute-start(f32[144,128]{1,0:T(8,128)S(1)} %get-tuple-element.50), channel_id=1, source_target_pairs={{0,1},{1,0},{2,3},{3,2},{4,5},{5,4},{6,7},{7,6},{8,9},{9,8},{10,11... | collective-permute-start | bytes 221192 | tf_op jit(solution)/shard_map/ppermute | solution.py:578
  31.4 0.9 collective-permute-done.after.in1
  32.3 1.9 %all-to-all-done.1.recv.after = f32[8,4,512]{2,1,0:T(4,128)S(1)} async-done(((f32[8,4,512]{2,1,0:T(4,128)}), f32[8,4,512]{2,1,0:T(4,128)S(1)}, u32[]{:S(2)}, u32[]{:S(2)}) %all-to-all-start.1) | async-done | bytes 65568 | tf_op jit(solution)/shard_map/all_to_all | solution.py:563
  34.2 0.7 shard_map.107
  34.9 11.1 %all-to-all-start.2 = ((f32[12,4,768]{2,1,0:T(4,128)}), f32[12,4,768]{2,1,0:T(4,128)S(1)}, u32[]{:S(2)}, u32[]{:S(2)}) async-start(f32[12,4,768]{2,1,0:T(4,128)} %shard_map.107), calls=%async_computation.2 | async-start | bytes 294912 | tf_op jit(solution)/shard_map/all_to_all | solution.py:563
  46.0 0.1 shard_map.109
  46.1 3.3 %collective-permute-start.1 = (f32[72,128]{1,0:T(8,128)S(1)}, f32[72,128]{1,0:T(8,128)S(1)}, u32[]{:S(2)}, u32[]{:S(2)}) collective-permute-start(f32[72,128]{1,0:T(8,128)S(1)} %get-tuple-element.54), channel_id=1, source_target_pairs={{0,8},{8,0},{16,24},{24,16},{32,40},{40,32},{48,56},{56,48},{64,72... | collective-permute-start | bytes 110600 | tf_op jit(solution)/shard_map/ppermute | solution.py:578
  49.4 0.7 collective-permute-start.2
  50.1 0.5 shard_map.108
  50.6 0.7 collective-permute-done.1.odd_after.out1
  51.3 5.4 %all-to-all-done.2.recv = f32[12,4,768]{2,1,0:T(4,128)S(1)} async-done(((f32[12,4,768]{2,1,0:T(4,128)}), f32[12,4,768]{2,1,0:T(4,128)S(1)}, u32[]{:S(2)}, u32[]{:S(2)}) %all-to-all-start.2) | async-done | bytes 147488 | tf_op jit(solution)/shard_map/all_to_all | solution.py:563
  56.7 0.8 shard_map.110
  57.5 0.1 shard_map.111
  57.6 5.7 %collective-permute-start.3 = (f32[144,128]{1,0:T(8,128)S(1)}, f32[144,128]{1,0:T(8,128)S(1)}, u32[]{:S(2)}, u32[]{:S(2)}) collective-permute-start(f32[144,128]{1,0:T(8,128)S(1)} %shard_map.111), channel_id=1, source_target_pairs={{1,2},{2,1},{3,4},{4,3},{5,6},{6,5},{9,10},{10,9},{11,12},{12,11},... | collective-permute-start | bytes 221192 | tf_op jit(solution)/shard_map/ppermute | solution.py:578
  63.3 7.9 %all_to_all.51.recv = f32[8,4,128]{2,1,0:T(4,128)S(1)} all-to-all(f32[8,4,128]{2,1,0:T(4,128)S(1)} %get-tuple-element.56.after), channel_id=1, replica_groups=mesh['y'=8,'z'=12,'sub'=8] {'sub'}, dimensions={0} | all-to-all | bytes 32768 | tf_op jit(solution)/shard_map/all_to_all | solution.py:563
  71.2 1.1 shard_map.112
  72.3 2.6 %collective-permute-start.4 = (f32[16,128]{1,0:T(8,128)S(1)}, f32[16,128]{1,0:T(8,128)S(1)}, u32[]{:S(2)}, u32[]{:S(2)}) collective-permute-start(f32[16,128]{1,0:T(8,128)S(1)} %get-tuple-element.61), channel_id=1, source_target_pairs={{0,1},{1,0},{2,3},{3,2},{4,5},{5,4},{6,7},{7,6},{8,9},{9,8},{10,11... | collective-permute-start | bytes 24584 | tf_op jit(solution)/shard_map/ppermute | solution.py:578
  74.9 2.1 %collective-permute-start.5 = (f32[16,128]{1,0:T(8,128)S(1)}, f32[16,128]{1,0:T(8,128)S(1)}, u32[]{:S(2)}, u32[]{:S(2)}) collective-permute-start(f32[16,128]{1,0:T(8,128)S(1)} %get-tuple-element.62), channel_id=1, source_target_pairs={{1,2},{2,1},{3,4},{4,3},{5,6},{6,5},{9,10},{10,9},{11,12},{12,11},... | collective-permute-start | bytes 24584 | tf_op jit(solution)/shard_map/ppermute | solution.py:578
  77.0 2.6 %collective-permute-start.6 = (f32[8,128]{1,0:T(8,128)S(1)}, f32[8,128]{1,0:T(8,128)S(1)}, u32[]{:S(2)}, u32[]{:S(2)}) collective-permute-start(f32[8,128]{1,0:T(8,128)S(1)} %get-tuple-element.63), channel_id=1, source_target_pairs={{0,8},{8,0},{16,24},{24,16},{32,40},{40,32},{48,56},{56,48},{64,72... | collective-permute-start | bytes 12296 | tf_op jit(solution)/shard_map/ppermute | solution.py:578
  79.7 0.7 collective-permute-start.7
  80.3 1.0 collective-permute-done.6.out1
  81.4 1.1 shard_map.113
  82.5 9.7 %all_to_all.52.recv = f32[8,4,640]{2,1,0:T(4,128)S(1)} all-to-all(f32[8,4,640]{2,1,0:T(4,128)S(1)} %get-tuple-element.66), channel_id=1, replica_groups=mesh['y'=8,'z'=12,'sub'=8] {'sub'}, dimensions={0} | all-to-all | bytes 163840 | tf_op jit(solution)/shard_map/all_to_all | solution.py:563
  92.2 18.1 %all_to_all.53.recv = f32[8,4,384]{2,1,0:T(4,128)S(1)} all-to-all(f32[8,4,384]{2,1,0:T(4,128)S(1)} %get-tuple-element.67), channel_id=1, replica_groups=mesh['y'=8,'z'=12,'sub'=8] {'y'}, dimensions={0} | all-to-all | bytes 98304 | tf_op jit(solution)/shard_map/all_to_all | solution.py:563
  110.4 12.5 %all_to_all.54.recv = f32[12,4,512]{2,1,0:T(4,128)S(1)} all-to-all(f32[12,4,512]{2,1,0:T(4,128)S(1)} %shard_map.115), channel_id=1, replica_groups=mesh['y'=8,'z'=12,'sub'=8] {'z'}, dimensions={0} | all-to-all | bytes 196608 | tf_op jit(solution)/shard_map/all_to_all | solution.py:563
  122.9 0.2 shard_map.116
  123.1 10.6 %all_to_all.55.recv = f32[8,4,128]{2,1,0:T(4,128)S(1)} all-to-all(f32[8,4,128]{2,1,0:T(4,128)S(1)} %get-tuple-element.70), channel_id=1, replica_groups=mesh['y'=8,'z'=12,'sub'=8] {'sub'}, dimensions={0} | all-to-all | bytes 32768 | tf_op jit(solution)/shard_map/all_to_all | solution.py:563
  133.7 0.6 shard_map.117
  134.4 8.1 %all_to_all.56.recv = f32[8,24,128]{2,1,0:T(8,128)S(1)} all-to-all(f32[8,24,128]{2,1,0:T(8,128)S(1)} %get-tuple-element.80), channel_id=1, replica_groups=mesh['y'=8,'z'=12,'sub'=8] {'sub'}, dimensions={0} | all-to-all | bytes 196608 | tf_op jit(solution)/shard_map/all_to_all | solution.py:563
  142.5 0.7 shard_map.118
  143.1 5.9 %all-to-all-start.9 = ((f32[96,1,128]{2,1,0:T(1,128)}), f32[96,1,128]{2,1,0:T(1,128)S(1)}, u32[]{:S(2)}, u32[]{:S(2)}) async-start(f32[96,1,128]{2,1,0:T(1,128)} %get-tuple-element.81), calls=%async_computation.9 | async-start | bytes 98304 | tf_op jit(solution)/shard_map/all_to_all | solution.py:563
  149.1 2.6 %collective-permute-start.8 = (f32[8,128]{1,0:T(8,128)S(1)}, f32[8,128]{1,0:T(8,128)S(1)}, u32[]{:S(2)}, u32[]{:S(2)}) collective-permute-start(f32[8,128]{1,0:T(8,128)S(1)} %get-tuple-element.85), channel_id=1, source_target_pairs={{0,8},{8,0},{16,24},{24,16},{32,40},{40,32},{48,56},{56,48},{64,72... | collective-permute-start | bytes 12296 | tf_op jit(solution)/shard_map/ppermute | solution.py:578
  151.7 0.7 collective-permute-start.9
  152.3 1.4 collective-permute-done.8.out1
  153.8 8.4 %all-to-all-done.9.recv = f32[96,1,128]{2,1,0:T(1,128)S(1)} async-done(((f32[96,1,128]{2,1,0:T(1,128)}), f32[96,1,128]{2,1,0:T(1,128)S(1)}, u32[]{:S(2)}, u32[]{:S(2)}) %all-to-all-start.9) | async-done | bytes 49184 | tf_op jit(solution)/shard_map/all_to_all | solution.py:563
  162.1 0.8 shard_map.119
  (20 shorter events, 0.1 us)
Async XLA Ops:
  0.6 49.5 %copy-start = (f32[192,1536]{1,0:T(8,128)S(1)}, f32[192,1536]{1,0:T(8,128)}, u32[]{:S(2)}) copy-start(f32[192,1536]{1,0:T(8,128)} %gc.3) | copy-start | bytes 3538948
  1.7 1.0 copy-start.2
  2.7 0.7 copy-start.4
  3.4 0.7 copy-start.5
  23.6 10.6 %all-to-all-start.1 = ((f32[8,4,512]{2,1,0:T(4,128)}), f32[8,4,512]{2,1,0:T(4,128)S(1)}, u32[]{:S(2)}, u32[]{:S(2)}) async-start(f32[8,4,512]{2,1,0:T(4,128)} %get-tuple-element.47), calls=%async_computation.1 | async-start | bytes 131072 | tf_op jit(solution)/shard_map/all_to_all | solution.py:563
  27.0 0.7 copy-start.7
  27.7 0.7 copy-start.8
  28.7 3.6 %collective-permute-start = (f32[144,128]{1,0:T(8,128)S(1)}, f32[144,128]{1,0:T(8,128)S(1)}, u32[]{:S(2)}, u32[]{:S(2)}) collective-permute-start(f32[144,128]{1,0:T(8,128)S(1)} %get-tuple-element.50), channel_id=1, source_target_pairs={{0,1},{1,0},{2,3},{3,2},{4,5},{5,4},{6,7},{7,6},{8,9},{9,8},{10,11... | collective-permute-start | bytes 221192 | tf_op jit(solution)/shard_map/ppermute | solution.py:578
  34.9 21.8 %all-to-all-start.2 = ((f32[12,4,768]{2,1,0:T(4,128)}), f32[12,4,768]{2,1,0:T(4,128)S(1)}, u32[]{:S(2)}, u32[]{:S(2)}) async-start(f32[12,4,768]{2,1,0:T(4,128)} %shard_map.107), calls=%async_computation.2 | async-start | bytes 294912 | tf_op jit(solution)/shard_map/all_to_all | solution.py:563
  46.1 5.2 %collective-permute-start.1 = (f32[72,128]{1,0:T(8,128)S(1)}, f32[72,128]{1,0:T(8,128)S(1)}, u32[]{:S(2)}, u32[]{:S(2)}) collective-permute-start(f32[72,128]{1,0:T(8,128)S(1)} %get-tuple-element.54), channel_id=1, source_target_pairs={{0,8},{8,0},{16,24},{24,16},{32,40},{40,32},{48,56},{56,48},{64,72... | collective-permute-start | bytes 110600 | tf_op jit(solution)/shard_map/ppermute | solution.py:578
  49.4 1.9 %collective-permute-start.2 = (f32[72,128]{1,0:T(8,128)S(1)}, f32[72,128]{1,0:T(8,128)S(1)}, u32[]{:S(2)}, u32[]{:S(2)}) collective-permute-start(f32[72,128]{1,0:T(8,128)S(1)} %get-tuple-element.55), channel_id=1, source_target_pairs={{8,16},{16,8},{24,32},{32,24},{40,48},{48,40},{56,64},{64,56},{72,... | collective-permute-start | bytes 110600 | tf_op jit(solution)/shard_map/ppermute | solution.py:578
  50.6 20.6 %copy-start.1 = (bf16[4,384,384]{2,1,0:T(8,128)(2,1)S(1)}, bf16[4,384,384]{2,1,0:T(8,128)(2,1)}, u32[]{:S(2)}) copy-start(bf16[4,384,384]{2,1,0:T(8,128)(2,1)} %ops.3) | copy-start | bytes 3538948
  57.5 23.9 %copy-start.3 = (f32[1,96,768]{2,1,0:T(8,128)S(1)}, f32[1,96,768]{2,1,0:T(8,128)}, u32[]{:S(2)}) copy-start(f32[1,96,768]{2,1,0:T(8,128)} %param.16) | copy-start | bytes 884740
  57.5 23.9 %copy-start.6 = (s32[4,8]{1,0:T(4,128)S(1)}, s32[4,8]{1,0:T(4,128)}, u32[]{:S(2)}) copy-start(s32[4,8]{1,0:T(4,128)} %ids.3) | copy-start | bytes 388
  57.6 13.6 %collective-permute-start.3 = (f32[144,128]{1,0:T(8,128)S(1)}, f32[144,128]{1,0:T(8,128)S(1)}, u32[]{:S(2)}, u32[]{:S(2)}) collective-permute-start(f32[144,128]{1,0:T(8,128)S(1)} %shard_map.111), channel_id=1, source_target_pairs={{1,2},{2,1},{3,4},{4,3},{5,6},{6,5},{9,10},{10,9},{11,12},{12,11},... | collective-permute-start | bytes 221192 | tf_op jit(solution)/shard_map/ppermute | solution.py:578
  72.3 9.1 %collective-permute-start.4 = (f32[16,128]{1,0:T(8,128)S(1)}, f32[16,128]{1,0:T(8,128)S(1)}, u32[]{:S(2)}, u32[]{:S(2)}) collective-permute-start(f32[16,128]{1,0:T(8,128)S(1)} %get-tuple-element.61), channel_id=1, source_target_pairs={{0,1},{1,0},{2,3},{3,2},{4,5},{5,4},{6,7},{7,6},{8,9},{9,8},{10,11... | collective-permute-start | bytes 24584 | tf_op jit(solution)/shard_map/ppermute | solution.py:578
  74.9 6.5 %collective-permute-start.5 = (f32[16,128]{1,0:T(8,128)S(1)}, f32[16,128]{1,0:T(8,128)S(1)}, u32[]{:S(2)}, u32[]{:S(2)}) collective-permute-start(f32[16,128]{1,0:T(8,128)S(1)} %get-tuple-element.62), channel_id=1, source_target_pairs={{1,2},{2,1},{3,4},{4,3},{5,6},{6,5},{9,10},{10,9},{11,12},{12,11},... | collective-permute-start | bytes 24584 | tf_op jit(solution)/shard_map/ppermute | solution.py:578
  77.0 4.4 %collective-permute-start.6 = (f32[8,128]{1,0:T(8,128)S(1)}, f32[8,128]{1,0:T(8,128)S(1)}, u32[]{:S(2)}, u32[]{:S(2)}) collective-permute-start(f32[8,128]{1,0:T(8,128)S(1)} %get-tuple-element.63), channel_id=1, source_target_pairs={{0,8},{8,0},{16,24},{24,16},{32,40},{40,32},{48,56},{56,48},{64,72... | collective-permute-start | bytes 12296 | tf_op jit(solution)/shard_map/ppermute | solution.py:578
  79.7 1.7 %collective-permute-start.7 = (f32[8,128]{1,0:T(8,128)S(1)}, f32[8,128]{1,0:T(8,128)S(1)}, u32[]{:S(2)}, u32[]{:S(2)}) collective-permute-start(f32[8,128]{1,0:T(8,128)S(1)} %get-tuple-element.64), channel_id=1, source_target_pairs={{8,16},{16,8},{24,32},{32,24},{40,48},{48,40},{56,64},{64,56},{72,... | collective-permute-start | bytes 12296 | tf_op jit(solution)/shard_map/ppermute | solution.py:578
  143.1 19.0 %all-to-all-start.9 = ((f32[96,1,128]{2,1,0:T(1,128)}), f32[96,1,128]{2,1,0:T(1,128)S(1)}, u32[]{:S(2)}, u32[]{:S(2)}) async-start(f32[96,1,128]{2,1,0:T(1,128)} %get-tuple-element.81), calls=%async_computation.9 | async-start | bytes 98304 | tf_op jit(solution)/shard_map/all_to_all | solution.py:563
  149.1 4.7 %collective-permute-start.8 = (f32[8,128]{1,0:T(8,128)S(1)}, f32[8,128]{1,0:T(8,128)S(1)}, u32[]{:S(2)}, u32[]{:S(2)}) collective-permute-start(f32[8,128]{1,0:T(8,128)S(1)} %get-tuple-element.85), channel_id=1, source_target_pairs={{0,8},{8,0},{16,24},{24,16},{32,40},{40,32},{48,56},{56,48},{64,72... | collective-permute-start | bytes 12296 | tf_op jit(solution)/shard_map/ppermute | solution.py:578
  151.7 2.1 %collective-permute-start.9 = (f32[8,128]{1,0:T(8,128)S(1)}, f32[8,128]{1,0:T(8,128)S(1)}, u32[]{:S(2)}, u32[]{:S(2)}) collective-permute-start(f32[8,128]{1,0:T(8,128)S(1)} %get-tuple-element.86), channel_id=1, source_target_pairs={{8,16},{16,8},{24,32},{32,24},{40,48},{48,40},{56,64},{64,56},{72,... | collective-permute-start | bytes 12296 | tf_op jit(solution)/shard_map/ppermute | solution.py:578

commit v7 on v6

--- a/solution.py
+++ b/solution.py
@@ -316,11 +316,6 @@
     out[...] = jnp.broadcast_to(x[None], (n_z, *x.shape))
 
 
-def k_first_pass(recv, after, out):
-    del after
-    k_pass(recv, out)
-
-
 def neighbours(recv, at, wrapped_at):
     z = lax.axis_index("z")
     n_z = recv.shape[0]
@@ -383,8 +378,7 @@
     cacross[...] = jnp.where(lane < NCL, both, 0.0)[:R]
 
 
-def k_first_global(recv, gc, gh, gl, odd_after, even_after, msg, scal, cacross, ah, al):
-    del odd_after, even_after
+def k_first_global(recv, gc, gh, gl, msg, scal, cacross, ah, al):
     after, before = neighbours(recv, 3 * B, 5 * B)
     lane = iota((8, B), 1)
     after = pltpu.roll(after, B - 8, 1)
@@ -477,12 +471,9 @@
     return jnp.sum(jnp.where(iota((ROWS, B), 1) == 64 + j, scal, 0.0), axis=1, keepdims=True)
 
 
-LAST = ROWS + 8
-
-
 def k_last_image(
     recv, csol, cacross, scal0, scal1, w, pw, v, d, pd, ap, pap, sg, ops, idx,
-    r_out, x_out, d_out, signed_out, msg, out1, out2,
+    r_out, x_out, d_out, signed_out, msg, *outs,
 ):
     fix, pfix = corrections(recv, csol, cacross, w, pw)
     rho = scalar_at(scal0[...], 0)
@@ -505,31 +496,16 @@
     lane = iota((8, B), 1)
     row = iota((8, B), 0)
     both = jnp.where(lane == row, c[:8], jnp.where(lane == row + R, sq[:8], 0.0))
-    both = jnp.where(row < R, both, 0.0)
-    up, down, even, odd = moved_blocks(signed, idx)
-    write_across(even, odd, out1, out2)
-    msg[...] = jnp.zeros(msg.shape, F32)
-    for k in range(NSUB):
-        msg[k, ROWS:LAST, :] = both
-    k = lax.axis_index("sub")
-    msg[jnp.minimum(k + 1, NSUB - 1), 0:ROWS, :] = up
-    msg[jnp.maximum(k - 1, 0), 0:ROWS, :] = down
-
-
-def k_total(recv, out, from_next, from_prev):
-    total = recv[0, ROWS:LAST, :]
-    for j in range(1, NSUB):
-        total = total + recv[j, ROWS:LAST, :]
-    line = jnp.sum(total, axis=0, keepdims=True)
-    out[...] = jnp.broadcast_to(line[None], out.shape)
-    k = lax.axis_index("sub")
-    after = recv[jnp.minimum(k + 1, NSUB - 1), 0:ROWS, :]
-    before = recv[jnp.maximum(k - 1, 0), 0:ROWS, :]
-    from_next[...] = jnp.where(jnp.full((ROWS, B), k, I32) < NSUB - 1, after, 0.0)
-    from_prev[...] = jnp.where(jnp.full((ROWS, B), k, I32) > 0, before, 0.0)
-
-
-def k_finish(recv, signed, fn, fp, out1, out2, x, r, d, x_out, r_out):
+    line = jnp.sum(jnp.where(row < R, both, 0.0), axis=0, keepdims=True)
+    msg[...] = jnp.broadcast_to(line[None], msg.shape)
+    write_moved(signed, idx, *outs)
+
+
+def k_total(recv, out):
+    out[...] = jnp.broadcast_to(jnp.sum(recv[...], axis=0, keepdims=True), out.shape)
+
+
+def k_finish(recv, signed, in1, in2, out1, out2, x, r, d, x_out, r_out):
     line = jnp.broadcast_to(jnp.sum(recv[...], axis=0), (ROWS, B))
     lane = iota((ROWS, B), 1)
     row = iota((ROWS, B), 0) % R
@@ -537,7 +513,8 @@
     rho = jnp.sum(jnp.where(lane == row + R, line, 0.0), axis=1, keepdims=True)
     step = rho / curv
     xn = x[...] + step * d[...]
-    rn = r[...] - step * (signed[...] + received(fn[...], fp[...], out1, out2))
+    pi = received(*within_of(in1[...], in2[...]), out1, out2)
+    rn = r[...] - step * (signed[...] + pi)
     for s in range(S):
         x_out[s] = xn[R * s : R * s + R]
         r_out[s] = rn[R * s : R * s + R]
@@ -612,14 +589,15 @@
         (FIELD, ((3, ROWS, B), I32), f32(STATIC, B)),
         all_ids, signs, links.transpose(1, 0, 2), w, v,
     )
+    recv = to_owner(rows, "y")
     in1 = swap(in1, "sub", n_sub, True)
-    recv = to_owner(rows, "y")
-    (rows,) = call(k_first_pass, (f32(n_z, R, 6 * B),), recv, in1)
+    (rows,) = call(k_pass, (f32(n_z, R, 6 * B),), recv)
+    recv_z = to_owner(rows, "z")
     out = call(k_send_across, (f32(PACK, B), f32(PACK, B)), recv, w, v, idx)
     across = exchange_across(*out, n_cl)
     gh, gl = call(k_own_columns, (picked, picked), all_ids, gc)
     to_all, scal0, cacross, ah, al = call(
-        k_first_global, (*answer, picked, picked), to_owner(rows, "z"), gc, gh, gl, *across
+        k_first_global, (*answer, picked, picked), recv_z, gc, gh, gl
     )
     (in2,) = call(k_send_second, (f32(STATIC, B),), to_all, w, v, idx)
     in2 = swap(in2, "sub", n_sub, False)
@@ -639,20 +617,18 @@
     rows, csol = call(k_rows, (f32(n_y, R, D), f32(3, R, B)), to_owner(msg, "sub"))
     (rows,) = call(k_pass, (f32(n_z, R, 4 * B),), to_owner(rows, "y"))
     to_all, scal1, cacross = call(k_global, answer, to_owner(rows, "z"), gh, gl, ah, al)
-    r, x, d1, signed, msg, *out = call(
+    r, x, d1, signed, line, *out = call(
         k_last_image,
-        (FIELD, FIELD, FIELD, FIELD, f32(NSUB, LAST, B), f32(2 * R, B), f32(2 * R, B)),
+        (FIELD, FIELD, FIELD, FIELD, f32(n_y * n_sub, 1, B), *SENDS),
         to_owner(to_all, "sub"), csol, cacross, scal0, scal1,
         w, pw, v, d, pd, ap, pap, sg, operators, idx,
     )
-    line, from_next, from_prev = call(
-        k_total, (f32(n_cl, 1, B), f32(ROWS, B), f32(ROWS, B)), to_owner(msg, "sub")
-    )
-    across = exchange_across(*out, n_cl)
+    line = to_owner(line, ("y", "sub"))
+    (line,) = call(k_total, (f32(n_z, 1, B),), line)
+    line = to_owner(line, "z")
+    got = exchange(*out, n_sub, n_cl)
     out = f32(S, R, D)
-    return call(
-        k_finish, (out, out), to_owner(line, CLUSTER), signed, from_next, from_prev, *across, x, r, d1
-    )
+    return call(k_finish, (out, out), line, signed, *got, x, r, d1)
 
 
 def solution(mesh):

time: 164 us -> 171 us (1.043)
  the two profiles are of different devices: /device:TPU:1 before, /device:TPU:10 now
where the time goes in v7:
time: 171 us; the launch traced here: 170 us
  blocking collectives  80.9 us (47%)
  starting transfers between devices  57.1 us (33%)
  waiting for transfers between devices  18.1 us (11%)
  Pallas kernels  9.5 us (6%)
  local copies, waits for them, and re-layouts  2.4 us (1%)
    all_to_all x7, blocking collectives, to_owner(): return lax.all_to_all(x, axis, 0, 0, tiled=True)  80.9 us
    ppermute x12, starting transfers between devices, swap(): lax.ppermute(x, axis, [p for i in low for p in ((i, i + 1), (i + 1, i))])  36.7 us
    all_to_all x3, starting transfers between devices, to_owner(): return lax.all_to_all(x, axis, 0, 0, tiled=True)  20.4 us
    all_to_all x3, waiting for transfers between devices, to_owner(): return lax.all_to_all(x, axis, 0, 0, tiled=True)  13 us
    pallas_call x16, Pallas kernels, call(): pl.pallas_call(body, out_shape=out_shape, in_specs=specs, out_specs=tuple...  9.5 us
    ppermute x12, waiting for transfers between devices, swap(): lax.ppermute(x, axis, [p for i in low for p in ((i, i + 1), (i + 1, i))])  5.18 us
  transfers between devices with their start and end apart: 15, of which 5 were waited for; matrix products, arithmetic and copies ran while one was open for 0% of the time, Pallas kernels for 2%

profile of v7, /device:TPU:10, one launch (start us, length us, event | category | flops | bytes accessed | tf_op | source)
XLA Modules:
  0.0 170.0 jit_solution(5094859750717224269)
XLA Ops:
  0.6 1.0 pad_maximum_fusion.w
  1.7 0.0 copy-start.2
  1.7 1.0 copy-done.2
  2.7 0.7 copy-done.4
  3.4 0.7 copy-done.5
  4.1 1.1 shard_map.104
  5.1 8.9 %all_to_all.50.recv = f32[8,4,640]{2,1,0:T(4,128)S(1)} all-to-all(f32[8,4,640]{2,1,0:T(4,128)S(1)} %get-tuple-element.45), channel_id=1, replica_groups=mesh['y'=8,'z'=12,'sub'=8] {'sub'}, dimensions={0} | all-to-all | bytes 163840 | tf_op jit(solution)/shard_map/all_to_all | solution.py:540
  14.0 0.1 shard_map.105
  14.1 17.0 %all_to_all.51.recv.after = f32[8,4,512]{2,1,0:T(4,128)S(1)} all-to-all(f32[8,4,512]{2,1,0:T(4,128)S(1)} %get-tuple-element.46), channel_id=1, replica_groups=mesh['y'=8,'z'=12,'sub'=8] {'y'}, dimensions={0} | all-to-all | bytes 131072 | tf_op jit(solution)/shard_map/all_to_all | solution.py:540
  31.1 0.7 shard_map.106
  31.8 12.4 %all-to-all-start.2 = ((f32[12,4,768]{2,1,0:T(4,128)}), f32[12,4,768]{2,1,0:T(4,128)S(1)}, u32[]{:S(2)}, u32[]{:S(2)}) async-start(f32[12,4,768]{2,1,0:T(4,128)} %shard_map.106), calls=%async_computation.2 | async-start | bytes 294912 | tf_op jit(solution)/shard_map/all_to_all | solution.py:540
  44.2 0.3 shard_map.109
  44.5 1.9 %collective-permute-start = (f32[144,128]{1,0:T(8,128)S(1)}, f32[144,128]{1,0:T(8,128)S(1)}, u32[]{:S(2)}, u32[]{:S(2)}) collective-permute-start(f32[144,128]{1,0:T(8,128)S(1)} %get-tuple-element.54), channel_id=1, source_target_pairs={{0,1},{1,0},{2,3},{3,2},{4,5},{5,4},{6,7},{7,6},{8,9},{9,8},{10,11... | collective-permute-start | bytes 221192 | tf_op jit(solution)/shard_map/ppermute | solution.py:555
  46.5 0.5 shard_map.107
  47.0 0.0 copy-start.1
  47.0 9.1 %all-to-all-done.2.recv = f32[12,4,768]{2,1,0:T(4,128)S(1)} async-done(((f32[12,4,768]{2,1,0:T(4,128)}), f32[12,4,768]{2,1,0:T(4,128)S(1)}, u32[]{:S(2)}, u32[]{:S(2)}) %all-to-all-start.2) | async-done | bytes 147488 | tf_op jit(solution)/shard_map/all_to_all | solution.py:540
  56.1 1.4 shard_map.108
  57.5 0.8 shard_map.110
  58.3 1.9 %collective-permute-start.1 = (f32[144,128]{1,0:T(8,128)S(1)}, f32[144,128]{1,0:T(8,128)S(1)}, u32[]{:S(2)}, u32[]{:S(2)}) collective-permute-start(f32[144,128]{1,0:T(8,128)S(1)} %shard_map.110), channel_id=1, source_target_pairs={{1,2},{2,1},{3,4},{4,3},{5,6},{6,5},{9,10},{10,9},{11,12},{12,11},... | collective-permute-start | bytes 221192 | tf_op jit(solution)/shard_map/ppermute | solution.py:555
  60.3 0.1 shard_map.111
  60.4 3.0 %collective-permute-start.2 = (f32[72,128]{1,0:T(8,128)S(1)}, f32[72,128]{1,0:T(8,128)S(1)}, u32[]{:S(2)}, u32[]{:S(2)}) collective-permute-start(f32[72,128]{1,0:T(8,128)S(1)} %get-tuple-element.56), channel_id=1, source_target_pairs={{0,8},{8,0},{16,24},{24,16},{32,40},{40,32},{48,56},{56,48},{64,72... | collective-permute-start | bytes 110600 | tf_op jit(solution)/shard_map/ppermute | solution.py:555
  63.4 3.4 %collective-permute-start.3 = (f32[72,128]{1,0:T(8,128)S(1)}, f32[72,128]{1,0:T(8,128)S(1)}, u32[]{:S(2)}, u32[]{:S(2)}) collective-permute-start(f32[72,128]{1,0:T(8,128)S(1)} %get-tuple-element.57), channel_id=1, source_target_pairs={{8,16},{16,8},{24,32},{32,24},{40,48},{48,40},{56,64},{64,56},{72,... | collective-permute-start | bytes 110600 | tf_op jit(solution)/shard_map/ppermute | solution.py:555
  66.7 4.5 %all-to-all-start.3 = ((f32[8,4,128]{2,1,0:T(4,128)}), f32[8,4,128]{2,1,0:T(4,128)S(1)}, u32[]{:S(2)}, u32[]{:S(2)}) async-start(f32[8,4,128]{2,1,0:T(4,128)} %get-tuple-element.50.after), calls=%async_computation.3 | async-start | bytes 32768 | tf_op jit(solution)/shard_map/all_to_all | solution.py:540
  71.3 0.0 collective-permute-done.in1
  71.3 0.1 collective-permute-done.3.out2
  71.3 3.8 %all-to-all-done.3.recv = f32[8,4,128]{2,1,0:T(4,128)S(1)} async-done(((f32[8,4,128]{2,1,0:T(4,128)}), f32[8,4,128]{2,1,0:T(4,128)S(1)}, u32[]{:S(2)}, u32[]{:S(2)}) %all-to-all-start.3) | async-done | bytes 16416 | tf_op jit(solution)/shard_map/all_to_all | solution.py:540
  75.2 1.1 shard_map.112
  76.3 1.9 %collective-permute-start.4 = (f32[16,128]{1,0:T(8,128)S(1)}, f32[16,128]{1,0:T(8,128)S(1)}, u32[]{:S(2)}, u32[]{:S(2)}) collective-permute-start(f32[16,128]{1,0:T(8,128)S(1)} %get-tuple-element.60), channel_id=1, source_target_pairs={{0,1},{1,0},{2,3},{3,2},{4,5},{5,4},{6,7},{7,6},{8,9},{9,8},{10,11... | collective-permute-start | bytes 24584 | tf_op jit(solution)/shard_map/ppermute | solution.py:555
  78.2 3.5 %collective-permute-start.5 = (f32[16,128]{1,0:T(8,128)S(1)}, f32[16,128]{1,0:T(8,128)S(1)}, u32[]{:S(2)}, u32[]{:S(2)}) collective-permute-start(f32[16,128]{1,0:T(8,128)S(1)} %get-tuple-element.61), channel_id=1, source_target_pairs={{1,2},{2,1},{3,4},{4,3},{5,6},{6,5},{9,10},{10,9},{11,12},{12,11},... | collective-permute-start | bytes 24584 | tf_op jit(solution)/shard_map/ppermute | solution.py:555
  81.7 1.9 %collective-permute-start.6 = (f32[8,128]{1,0:T(8,128)S(1)}, f32[8,128]{1,0:T(8,128)S(1)}, u32[]{:S(2)}, u32[]{:S(2)}) collective-permute-start(f32[8,128]{1,0:T(8,128)S(1)} %get-tuple-element.62), channel_id=1, source_target_pairs={{0,8},{8,0},{16,24},{24,16},{32,40},{40,32},{48,56},{56,48},{64,72... | collective-permute-start | bytes 12296 | tf_op jit(solution)/shard_map/ppermute | solution.py:555
  83.6 4.6 %collective-permute-start.7 = (f32[8,128]{1,0:T(8,128)S(1)}, f32[8,128]{1,0:T(8,128)S(1)}, u32[]{:S(2)}, u32[]{:S(2)}) collective-permute-start(f32[8,128]{1,0:T(8,128)S(1)} %get-tuple-element.63), channel_id=1, source_target_pairs={{8,16},{16,8},{24,32},{32,24},{40,48},{48,40},{56,64},{64,56},{72,... | collective-permute-start | bytes 12296 | tf_op jit(solution)/shard_map/ppermute | solution.py:555
  88.2 3.0 %collective-permute-done.7.out2 = f32[8,128]{1,0:T(8,128)S(1)} collective-permute-done((f32[8,128]{1,0:T(8,128)S(1)}, f32[8,128]{1,0:T(8,128)S(1)}, u32[]{:S(2)}, u32[]{:S(2)}) %collective-permute-start.7) | collective-permute-done | bytes 4128 | tf_op jit(solution)/shard_map/ppermute | solution.py:555
  91.3 1.1 shard_map.113
  92.4 8.0 %all_to_all.52.recv = f32[8,4,640]{2,1,0:T(4,128)S(1)} all-to-all(f32[8,4,640]{2,1,0:T(4,128)S(1)} %get-tuple-element.65), channel_id=1, replica_groups=mesh['y'=8,'z'=12,'sub'=8] {'sub'}, dimensions={0} | all-to-all | bytes 163840 | tf_op jit(solution)/shard_map/all_to_all | solution.py:540
  100.3 12.1 %all_to_all.53.recv = f32[8,4,384]{2,1,0:T(4,128)S(1)} all-to-all(f32[8,4,384]{2,1,0:T(4,128)S(1)} %get-tuple-element.66), channel_id=1, replica_groups=mesh['y'=8,'z'=12,'sub'=8] {'y'}, dimensions={0} | all-to-all | bytes 98304 | tf_op jit(solution)/shard_map/all_to_all | solution.py:540
  112.5 13.8 %all_to_all.54.recv = f32[12,4,512]{2,1,0:T(4,128)S(1)} all-to-all(f32[12,4,512]{2,1,0:T(4,128)S(1)} %shard_map.115), channel_id=1, replica_groups=mesh['y'=8,'z'=12,'sub'=8] {'z'}, dimensions={0} | all-to-all | bytes 196608 | tf_op jit(solution)/shard_map/all_to_all | solution.py:540
  126.2 0.2 shard_map.116
  126.5 7.7 %all_to_all.55.recv = f32[8,4,128]{2,1,0:T(4,128)S(1)} all-to-all(f32[8,4,128]{2,1,0:T(4,128)S(1)} %get-tuple-element.69), channel_id=1, replica_groups=mesh['y'=8,'z'=12,'sub'=8] {'sub'}, dimensions={0} | all-to-all | bytes 32768 | tf_op jit(solution)/shard_map/all_to_all | solution.py:540
  134.2 0.7 shard_map.117
  134.9 13.5 %all_to_all.56.recv = f32[64,1,128]{2,1,0:T(1,128)S(1)} all-to-all(f32[64,1,128]{2,1,0:T(1,128)S(1)} %get-tuple-element.79), channel_id=1, replica_groups=mesh['y'=8,'z'=12,'sub'=8] {'y','sub'}, dimensions={0} | all-to-all | bytes 65536 | tf_op jit(solution)/shard_map/all_to_all | solution.py:540
  148.4 0.7 shard_map.118
  149.1 3.5 %all-to-all-start.9 = ((f32[12,1,128]{2,1,0:T(1,128)}), f32[12,1,128]{2,1,0:T(1,128)S(1)}, u32[]{:S(2)}, u32[]{:S(2)}) async-start(f32[12,1,128]{2,1,0:T(1,128)} %shard_map.118), calls=%async_computation.9 | async-start | bytes 12288 | tf_op jit(solution)/shard_map/all_to_all | solution.py:540
  152.5 1.9 %collective-permute-start.8 = (f32[16,128]{1,0:T(8,128)S(1)}, f32[16,128]{1,0:T(8,128)S(1)}, u32[]{:S(2)}, u32[]{:S(2)}) collective-permute-start(f32[16,128]{1,0:T(8,128)S(1)} %get-tuple-element.81), channel_id=1, source_target_pairs={{0,1},{1,0},{2,3},{3,2},{4,5},{5,4},{6,7},{7,6},{8,9},{9,8},{10,11... | collective-permute-start | bytes 24584 | tf_op jit(solution)/shard_map/ppermute | solution.py:555
  154.5 3.5 %collective-permute-start.9 = (f32[16,128]{1,0:T(8,128)S(1)}, f32[16,128]{1,0:T(8,128)S(1)}, u32[]{:S(2)}, u32[]{:S(2)}) collective-permute-start(f32[16,128]{1,0:T(8,128)S(1)} %get-tuple-element.82), channel_id=1, source_target_pairs={{1,2},{2,1},{3,4},{4,3},{5,6},{6,5},{9,10},{10,9},{11,12},{12,11},... | collective-permute-start | bytes 24584 | tf_op jit(solution)/shard_map/ppermute | solution.py:555
  157.9 3.8 %collective-permute-start.10 = (f32[8,128]{1,0:T(8,128)S(1)}, f32[8,128]{1,0:T(8,128)S(1)}, u32[]{:S(2)}, u32[]{:S(2)}) collective-permute-start(f32[8,128]{1,0:T(8,128)S(1)} %get-tuple-element.83), channel_id=1, source_target_pairs={{0,8},{8,0},{16,24},{24,16},{32,40},{40,32},{48,56},{56,48},{64,72... | collective-permute-start | bytes 12296 | tf_op jit(solution)/shard_map/ppermute | solution.py:555
  161.7 5.5 %collective-permute-start.11 = (f32[8,128]{1,0:T(8,128)S(1)}, f32[8,128]{1,0:T(8,128)S(1)}, u32[]{:S(2)}, u32[]{:S(2)}) collective-permute-start(f32[8,128]{1,0:T(8,128)S(1)} %get-tuple-element.84), channel_id=1, source_target_pairs={{8,16},{16,8},{24,32},{32,24},{40,48},{48,40},{56,64},{64,56},{72,... | collective-permute-start | bytes 12296 | tf_op jit(solution)/shard_map/ppermute | solution.py:555
  167.2 2.1 %collective-permute-done.11.out2 = f32[8,128]{1,0:T(8,128)S(1)} collective-permute-done((f32[8,128]{1,0:T(8,128)S(1)}, f32[8,128]{1,0:T(8,128)S(1)}, u32[]{:S(2)}, u32[]{:S(2)}) %collective-permute-start.11) | collective-permute-done | bytes 4128 | tf_op jit(solution)/shard_map/ppermute | solution.py:555
  169.3 0.7 shard_map.119
  (24 shorter events, 0.1 us)
Async XLA Ops:
  0.6 45.8 %copy-start = (f32[192,1536]{1,0:T(8,128)S(1)}, f32[192,1536]{1,0:T(8,128)}, u32[]{:S(2)}) copy-start(f32[192,1536]{1,0:T(8,128)} %gc.3) | copy-start | bytes 3538948
  1.7 1.0 copy-start.2
  2.7 0.7 copy-start.4
  3.4 0.7 copy-start.5
  4.1 40.1 %copy-start.7 = (s32[4,384]{1,0:T(4,128)S(1)}, s32[4,384]{1,0:T(4,128)}, u32[]{:S(2)}) copy-start(s32[4,384]{1,0:T(4,128)} %signs.1) | copy-start | bytes 18436
  4.1 40.1 %copy-start.8 = (s32[4,3,128]{2,0,1:T(4,128)S(1)}, s32[4,3,128]{2,0,1:T(4,128)}, u32[]{:S(2)}) copy-start(s32[4,3,128]{2,0,1:T(4,128)} %param.12) | copy-start | bytes 18436
  31.8 24.3 %all-to-all-start.2 = ((f32[12,4,768]{2,1,0:T(4,128)}), f32[12,4,768]{2,1,0:T(4,128)S(1)}, u32[]{:S(2)}, u32[]{:S(2)}) async-start(f32[12,4,768]{2,1,0:T(4,128)} %shard_map.106), calls=%async_computation.2 | async-start | bytes 294912 | tf_op jit(solution)/shard_map/all_to_all | solution.py:540
  44.5 26.8 %collective-permute-start = (f32[144,128]{1,0:T(8,128)S(1)}, f32[144,128]{1,0:T(8,128)S(1)}, u32[]{:S(2)}, u32[]{:S(2)}) collective-permute-start(f32[144,128]{1,0:T(8,128)S(1)} %get-tuple-element.54), channel_id=1, source_target_pairs={{0,1},{1,0},{2,3},{3,2},{4,5},{5,4},{6,7},{7,6},{8,9},{9,8},{10,11... | collective-permute-start | bytes 221192 | tf_op jit(solution)/shard_map/ppermute | solution.py:555
  47.0 28.2 %copy-start.1 = (bf16[4,384,384]{2,1,0:T(8,128)(2,1)S(1)}, bf16[4,384,384]{2,1,0:T(8,128)(2,1)}, u32[]{:S(2)}) copy-start(bf16[4,384,384]{2,1,0:T(8,128)(2,1)} %ops.3) | copy-start | bytes 3538948
  57.5 33.8 %copy-start.3 = (f32[1,96,768]{2,1,0:T(8,128)S(1)}, f32[1,96,768]{2,1,0:T(8,128)}, u32[]{:S(2)}) copy-start(f32[1,96,768]{2,1,0:T(8,128)} %param.16) | copy-start | bytes 884740
  57.5 33.8 %copy-start.6 = (s32[4,8]{1,0:T(4,128)S(1)}, s32[4,8]{1,0:T(4,128)}, u32[]{:S(2)}) copy-start(s32[4,8]{1,0:T(4,128)} %ids.3) | copy-start | bytes 388
  58.3 16.8 %collective-permute-start.1 = (f32[144,128]{1,0:T(8,128)S(1)}, f32[144,128]{1,0:T(8,128)S(1)}, u32[]{:S(2)}, u32[]{:S(2)}) collective-permute-start(f32[144,128]{1,0:T(8,128)S(1)} %shard_map.110), channel_id=1, source_target_pairs={{1,2},{2,1},{3,4},{4,3},{5,6},{6,5},{9,10},{10,9},{11,12},{12,11},... | collective-permute-start | bytes 221192 | tf_op jit(solution)/shard_map/ppermute | solution.py:555
  60.4 10.9 %collective-permute-start.2 = (f32[72,128]{1,0:T(8,128)S(1)}, f32[72,128]{1,0:T(8,128)S(1)}, u32[]{:S(2)}, u32[]{:S(2)}) collective-permute-start(f32[72,128]{1,0:T(8,128)S(1)} %get-tuple-element.56), channel_id=1, source_target_pairs={{0,8},{8,0},{16,24},{24,16},{32,40},{40,32},{48,56},{56,48},{64,72... | collective-permute-start | bytes 110600 | tf_op jit(solution)/shard_map/ppermute | solution.py:555
  63.4 8.0 %collective-permute-start.3 = (f32[72,128]{1,0:T(8,128)S(1)}, f32[72,128]{1,0:T(8,128)S(1)}, u32[]{:S(2)}, u32[]{:S(2)}) collective-permute-start(f32[72,128]{1,0:T(8,128)S(1)} %get-tuple-element.57), channel_id=1, source_target_pairs={{8,16},{16,8},{24,32},{32,24},{40,48},{48,40},{56,64},{64,56},{72,... | collective-permute-start | bytes 110600 | tf_op jit(solution)/shard_map/ppermute | solution.py:555
  66.7 8.4 %all-to-all-start.3 = ((f32[8,4,128]{2,1,0:T(4,128)}), f32[8,4,128]{2,1,0:T(4,128)S(1)}, u32[]{:S(2)}, u32[]{:S(2)}) async-start(f32[8,4,128]{2,1,0:T(4,128)} %get-tuple-element.50.after), calls=%async_computation.3 | async-start | bytes 32768 | tf_op jit(solution)/shard_map/all_to_all | solution.py:540
  76.3 14.9 %collective-permute-start.4 = (f32[16,128]{1,0:T(8,128)S(1)}, f32[16,128]{1,0:T(8,128)S(1)}, u32[]{:S(2)}, u32[]{:S(2)}) collective-permute-start(f32[16,128]{1,0:T(8,128)S(1)} %get-tuple-element.60), channel_id=1, source_target_pairs={{0,1},{1,0},{2,3},{3,2},{4,5},{5,4},{6,7},{7,6},{8,9},{9,8},{10,11... | collective-permute-start | bytes 24584 | tf_op jit(solution)/shard_map/ppermute | solution.py:555
  78.2 13.0 %collective-permute-start.5 = (f32[16,128]{1,0:T(8,128)S(1)}, f32[16,128]{1,0:T(8,128)S(1)}, u32[]{:S(2)}, u32[]{:S(2)}) collective-permute-start(f32[16,128]{1,0:T(8,128)S(1)} %get-tuple-element.61), channel_id=1, source_target_pairs={{1,2},{2,1},{3,4},{4,3},{5,6},{6,5},{9,10},{10,9},{11,12},{12,11},... | collective-permute-start | bytes 24584 | tf_op jit(solution)/shard_map/ppermute | solution.py:555
  81.7 6.5 %collective-permute-start.6 = (f32[8,128]{1,0:T(8,128)S(1)}, f32[8,128]{1,0:T(8,128)S(1)}, u32[]{:S(2)}, u32[]{:S(2)}) collective-permute-start(f32[8,128]{1,0:T(8,128)S(1)} %get-tuple-element.62), channel_id=1, source_target_pairs={{0,8},{8,0},{16,24},{24,16},{32,40},{40,32},{48,56},{56,48},{64,72... | collective-permute-start | bytes 12296 | tf_op jit(solution)/shard_map/ppermute | solution.py:555
  83.6 7.6 %collective-permute-start.7 = (f32[8,128]{1,0:T(8,128)S(1)}, f32[8,128]{1,0:T(8,128)S(1)}, u32[]{:S(2)}, u32[]{:S(2)}) collective-permute-start(f32[8,128]{1,0:T(8,128)S(1)} %get-tuple-element.63), channel_id=1, source_target_pairs={{8,16},{16,8},{24,32},{32,24},{40,48},{48,40},{56,64},{64,56},{72,... | collective-permute-start | bytes 12296 | tf_op jit(solution)/shard_map/ppermute | solution.py:555
  149.1 20.3 %all-to-all-start.9 = ((f32[12,1,128]{2,1,0:T(1,128)}), f32[12,1,128]{2,1,0:T(1,128)S(1)}, u32[]{:S(2)}, u32[]{:S(2)}) async-start(f32[12,1,128]{2,1,0:T(1,128)} %shard_map.118), calls=%async_computation.9 | async-start | bytes 12288 | tf_op jit(solution)/shard_map/all_to_all | solution.py:540
  152.5 16.8 %collective-permute-start.8 = (f32[16,128]{1,0:T(8,128)S(1)}, f32[16,128]{1,0:T(8,128)S(1)}, u32[]{:S(2)}, u32[]{:S(2)}) collective-permute-start(f32[16,128]{1,0:T(8,128)S(1)} %get-tuple-element.81), channel_id=1, source_target_pairs={{0,1},{1,0},{2,3},{3,2},{4,5},{5,4},{6,7},{7,6},{8,9},{9,8},{10,11... | collective-permute-start | bytes 24584 | tf_op jit(solution)/shard_map/ppermute | solution.py:555
  154.5 14.9 %collective-permute-start.9 = (f32[16,128]{1,0:T(8,128)S(1)}, f32[16,128]{1,0:T(8,128)S(1)}, u32[]{:S(2)}, u32[]{:S(2)}) collective-permute-start(f32[16,128]{1,0:T(8,128)S(1)} %get-tuple-element.82), channel_id=1, source_target_pairs={{1,2},{2,1},{3,4},{4,3},{5,6},{6,5},{9,10},{10,9},{11,12},{12,11},... | collective-permute-start | bytes 24584 | tf_op jit(solution)/shard_map/ppermute | solution.py:555
  157.9 9.3 %collective-permute-start.10 = (f32[8,128]{1,0:T(8,128)S(1)}, f32[8,128]{1,0:T(8,128)S(1)}, u32[]{:S(2)}, u32[]{:S(2)}) collective-permute-start(f32[8,128]{1,0:T(8,128)S(1)} %get-tuple-element.83), channel_id=1, source_target_pairs={{0,8},{8,0},{16,24},{24,16},{32,40},{40,32},{48,56},{56,48},{64,72... | collective-permute-start | bytes 12296 | tf_op jit(solution)/shard_map/ppermute | solution.py:555
  161.7 7.6 %collective-permute-start.11 = (f32[8,128]{1,0:T(8,128)S(1)}, f32[8,128]{1,0:T(8,128)S(1)}, u32[]{:S(2)}, u32[]{:S(2)}) collective-permute-start(f32[8,128]{1,0:T(8,128)S(1)} %get-tuple-element.84), channel_id=1, source_target_pairs={{8,16},{16,8},{24,32},{32,24},{40,48},{48,40},{56,64},{64,56},{72,... | collective-permute-start | bytes 12296 | tf_op jit(solution)/shard_map/ppermute | solution.py:555

commit v8 on v7

--- a/solution.py
+++ b/solution.py
@@ -115,18 +115,25 @@
 MSG = 5 * B
 
 
-def write_message(msg, coef, cc, ids, scalars):
-    row = ids_row(ids).astype(F32)
-    col = to_column(row).astype(I32)
-    c4 = coef[:8]
-    hi, lo = split(c4)
-    low = (c4 - hi.astype(F32) - lo.astype(F32)).astype(BF16)
-    parts = jnp.concatenate([hi, lo, low], axis=0)
-    ccp = dot2(jnp.where(iota((8, NB), 1) < NCL, c4, 0.0)[:, :NCL], cc[...])
+def clustered(c4, cc):
+    return dot2(jnp.where(iota((8, NB), 1) < NCL, c4, 0.0)[:, :NCL], cc)
+
+
+def marked(scalars):
     lane = iota((8, B), 1)
     extra = jnp.zeros((8, B), F32)
     for j, val in enumerate(scalars):
         extra = jnp.where(lane == 64 + j, val, extra)
+    return extra
+
+
+def write_message(msg, c4, ccp, row, scalars=()):
+    col = to_column(row).astype(I32)
+    hi, lo = split(c4)
+    low = (c4 - hi.astype(F32) - lo.astype(F32)).astype(BF16)
+    parts = jnp.concatenate([hi, lo, low], axis=0)
+    lane = iota((8, B), 1)
+    extra = marked(scalars)
     none = jnp.zeros((8, B), F32)
     cluster = [jnp.where(lane < NCL, window(ccp, NCL * k, NCL), 0.0) for k in range(NSUB)]
     for k in range(NSUB):
@@ -150,6 +157,7 @@
 
 
 STATIC = NB + ROWS
+WITHIN = STATIC + NCL * 6
 PACK = 72
 
 
@@ -157,7 +165,9 @@
     for s in range(S):
         v_out[R * s : R * s + R, :] = rhs[s]
     v = v_out[...]
-    write_message(msg, coefs(v, w[...]), cc, ids, [row_dot(v, v)[:8]])
+    c4 = coefs(v, w[...])[:8]
+    row = ids_row(ids).astype(F32)
+    write_message(msg, c4, clustered(c4, cc[...]), row, [row_dot(v, v)[:8]])
 
 
 def k_tables(after, signs, links, sg_out, idx_out):
@@ -186,23 +196,25 @@
     yield None, NB, moved(v[:, lanes], idx[b])
 
 
-def send_within(w, v, idx, out, b):
+def send_within(w, v, cc, idx, out, b):
     for _, at, x in static_blocks(w, v, idx, b):
         out[at : at + x.shape[0], :] = x
-
-
-def k_send_first(after, signs, links, w, v, sg_out, idx_out, out):
+    for j in range(6):
+        out[STATIC + NCL * j : STATIC + NCL * j + NCL, :] = cc[:, j * B : (j + 1) * B]
+
+
+def coarse_rows(x):
+    return jnp.concatenate([x[STATIC + NCL * j : STATIC + NCL * j + NCL, :] for j in range(6)], axis=1)
+
+
+def k_send_first(after, signs, links, w, v, cc, sg_out, idx_out, out):
     k_tables(after, signs, links, sg_out, idx_out)
-    send_within(w, v, idx_out, out, lax.axis_index("sub") % 2)
-
-
-def k_send_second(after, w, v, idx, out):
+    send_within(w, v, cc, idx_out, out, lax.axis_index("sub") % 2)
+
+
+def k_send_rest(after, w, v, cc, idx, first, second, within):
     del after
-    send_within(w, v, idx, out, 1 - lax.axis_index("sub") % 2)
-
-
-def k_send_across(after, w, v, idx, first, second):
-    del after
+    send_within(w, v, cc, idx, within, 1 - lax.axis_index("sub") % 2)
     flag = even_cluster()
     blocks = {(s, at): x for s, at, x in static_blocks(w, v, idx, 2)}
 
@@ -253,7 +265,7 @@
 
 
 def take_static(in1, in2, out1, out2, pw_out, pv_out):
-    from_next, from_prev = within_of(in1[...], in2[...])
+    from_next, from_prev = within_of(in1[0:STATIC, :], in2[0:STATIC, :])
     odd_in, even_in = across_of(out1[...], out2[...])
     pw_out[:, 0:B] = from_next[0:NB, :]
     pw_out[:, B : 2 * B] = from_prev[0:NB, :]
@@ -276,13 +288,16 @@
     return total
 
 
-def k_rows(recv, out, csol):
-    total = member_sum(recv)
+def k_rows(recv, out, csol, scalars=()):
+    total = recv[0, :, 0:MSG]
+    for k in range(1, NSUB):
+        total = total + recv[k, :, 0:MSG]
     own = jnp.where(iota((R, B), 1) < NCL, total[:, 2 * B : 3 * B], 0.0)
     csol[0] = own
     csol[1] = total[:, 3 * B : 4 * B]
     csol[2] = total[:, 4 * B : 5 * B]
-    x = jnp.concatenate([total[:, : 2 * B], own], axis=1)
+    second = total[:, B : 2 * B] + marked(scalars)[:R]
+    x = jnp.concatenate([total[:, :B], second, own], axis=1)
     out[:, :, 0:D] = jnp.broadcast_to(x[None], (out.shape[0], R, D))
 
 
@@ -360,16 +375,18 @@
         y = mm(jnp.concatenate([xh, xl], axis=0), gh[...])
         ys.append(y[:8] + y[8:] + mm(xh, gl[...]))
 
-    def pick(kind, k, to):
+    def picked(kind, k, to):
         at = 32 * k
         return pltpu.roll(ys[kind][:, at // B * B : at // B * B + B], (to - at) % B, 1)
 
     none = jnp.zeros((8, B), F32)
     for k in range(NSUB):
-        after = pick(0, k + 1, 32) if k + 1 < NSUB else none
-        before = pick(0, k - 1, 64) if k > 0 else none
-        here = jnp.where(lane < 32, pick(0, k, 0), jnp.where(lane < 64, after, before))
-        msg[k] = jnp.where(lane < 96, here, pick(1, k, 96))[:R]
+        after = picked(0, k + 1, 32) if k + 1 < NSUB else none
+        before = picked(0, k - 1, 64) if k > 0 else none
+        here = jnp.where(lane < 32, picked(0, k, 0), jnp.where(lane < 64, after, before))
+        msg[k, :, 0:B] = jnp.where(lane < 96, here, picked(1, k, 96))[:R]
+        if msg.shape[2] > B:
+            msg[k, :, B : 2 * B] = second[:R]
     scal[...] = jnp.concatenate([second, second], axis=0)
     after, before = neighbours(recv, 2 * B, 2 * B + stride)
     after = pltpu.roll(after, B - KC, 1)
@@ -398,7 +415,7 @@
 
 
 def corrections(recv, csol, cacross, w, pw):
-    picks = four_times(member_sum(recv))
+    picks = four_times(member_sum(recv)[:, :B])
     tail = iota((ROWS, B), 1) >= NCL
 
     def sol(cluster, turn):
@@ -411,10 +428,13 @@
     return own, jnp.concatenate(pi, axis=1)
 
 
+def across_received(out1, out2):
+    odd_in, even_in = across_of(out1[...], out2[...])
+    return jnp.concatenate([odd_in[0:R], even_in[0:R], odd_in[R:], even_in[R:]], axis=0)
+
+
 def received(from_next, from_prev, out1, out2):
-    odd_in, even_in = across_of(out1[...], out2[...])
-    across = jnp.concatenate([odd_in[0:R], even_in[0:R], odd_in[R:], even_in[R:]], axis=0)
-    return jnp.concatenate([from_next, from_prev, across], axis=1)
+    return jnp.concatenate([from_next, from_prev, across_received(out1, out2)], axis=1)
 
 
 def paired(n_cl):
@@ -440,7 +460,7 @@
 
 def k_first_image(
     recv, csol, cacross, in1, in2, out1, out2, w, v, sg, ops, idx,
-    pw, pv, d_out, pd_out, signed_out, curv, *outs,
+    pw, pv, d_out, pd_out, signed_out, curv, up_out, down_out, *outs,
 ):
     take_static(in1, in2, out1, out2, pw, pv)
     fix, pfix = corrections(recv, csol, cacross, w, pw)
@@ -451,20 +471,85 @@
     signed, c = image_of(d, pd, sg[...], ops)
     signed_out[...] = signed
     curv[...] = jnp.broadcast_to(c[:8], (8, B))
-    write_moved(signed, idx, *outs)
-
-
-def make_product(n_cl):
-    def k_product(ids, signed, in1, in2, out1, out2, v, w, cc, curv, ap_out, pap_out, msg):
-        pi = received(*within_of(in1[...], in2[...]), out1, out2)
+    up, down, even, odd = moved_blocks(signed, idx)
+    up_out[...] = up
+    down_out[...] = down
+    write_across(even, odd, *outs)
+
+
+def member_ids(all_ids, member, to):
+    row = jnp.zeros((8, B), F32)
+    which = jnp.full((8, B), member, I32)
+    for j in range(NSUB):
+        x = jnp.broadcast_to(all_ids[j // 4 : j // 4 + 1, :], (8, B))
+        row = jnp.where(which == j, pltpu.roll(x, (to - 32 * (j % 4)) % B, 1), row)
+    return row
+
+
+def k_product(
+    ids, signed, up, down, out1, out2, static1, static2, w, pw, cc, all_ids, across_out, msg
+):
+    k = lax.axis_index("sub")
+    odd_k = k % 2
+    across = across_received(out1, out2)
+    across_out[...] = across
+    u = signed[...]
+    known = jnp.concatenate([u[:, : 2 * B], u[:, 2 * B :] + across], axis=1)
+    own = coefs(known, w[...])[:8]
+
+    def towards(b):
+        lanes = pl.ds(pl.multiple_of(b * B, B), B)
+        return coefs(signed[:, lanes], pw[:, lanes])[:8]
+
+    first, second = towards(odd_k), towards(1 - odd_k)
+    ccp = (
+        clustered(own, cc[...])
+        + clustered(first, coarse_rows(static1))
+        + clustered(second, coarse_rows(static2))
+    )
+    lane = iota((8, B), 1)
+    other = jnp.clip(k - 1 + 2 * odd_k, 0, NSUB - 1)
+
+    def lanes_of(c96, c64, c32, rest):
+        return jnp.where(
+            lane >= 96, c96, jnp.where(lane >= 64, c64, jnp.where(lane >= 32, c32, rest))
+        )
+
+    c4 = lanes_of(own, pltpu.roll(first, B - 32, 1), pltpu.roll(second, B - 64, 1), 0.0)
+    row = lanes_of(
+        ids_row(ids).astype(F32),
+        member_ids(all_ids, k + 1 - 2 * odd_k, 64),
+        member_ids(all_ids, other, 32),
+        -1.0,
+    )
+    write_message(msg, c4, ccp, row)
+    after, before = jnp.minimum(k + 1, NSUB - 1), jnp.maximum(k - 1, 0)
+    for s in range(S):
+        at = MSG + B * s
+        msg[after, :, at : at + B] = up[R * s : R * s + R, :]
+        msg[before, :, at : at + B] = down[R * s : R * s + R, :]
+
+
+def make_joined(n_cl):
+    def k_joined(recv, signed, across, curv, v, out, csol, ap_out, pap_out):
+        k = lax.axis_index("sub")
+
+        def block(member, there):
+            x = [recv[member, :, MSG + B * s : MSG + B * s + B] for s in range(S)]
+            x = jnp.concatenate(x, axis=0)
+            return pick(there, x, jnp.zeros_like(x))
+
+        from_next = block(jnp.minimum(k + 1, NSUB - 1), k < NSUB - 1)
+        from_prev = block(jnp.maximum(k - 1, 0), k > 0)
         u = signed[...]
+        pi = jnp.concatenate([from_next, from_prev, across[...]], axis=1)
         ap = u + pi
         ap_out[...] = ap
         pap_out[...] = pi + paired(n_cl) * u
         scalars = [curv[...][:, :1], row_dot(v[...], ap)[:8], row_dot(ap, ap)[:8]]
-        write_message(msg, coefs(ap, w[...]), cc, ids, scalars)
-
-    return k_product
+        k_rows(recv, out, csol, scalars)
+
+    return k_joined
 
 
 def scalar_at(scal, j):
@@ -472,12 +557,12 @@
 
 
 def k_last_image(
-    recv, csol, cacross, scal0, scal1, w, pw, v, d, pd, ap, pap, sg, ops, idx,
+    recv, csol, cacross, scal0, w, pw, v, d, pd, ap, pap, sg, ops, idx,
     r_out, x_out, d_out, signed_out, msg, *outs,
 ):
     fix, pfix = corrections(recv, csol, cacross, w, pw)
     rho = scalar_at(scal0[...], 0)
-    s1 = scal1[...]
+    s1 = four_times(member_sum(recv)[:, B : 2 * B])
     step = rho / scalar_at(s1, 0)
     rho_new = rho - 2.0 * step * scalar_at(s1, 1) + step * step * scalar_at(s1, 2)
     beta = rho_new / rho
@@ -586,41 +671,48 @@
     )
     sg, idx, in1 = call(
         k_send_first,
-        (FIELD, ((3, ROWS, B), I32), f32(STATIC, B)),
-        all_ids, signs, links.transpose(1, 0, 2), w, v,
+        (FIELD, ((3, ROWS, B), I32), f32(WITHIN, B)),
+        all_ids, signs, links.transpose(1, 0, 2), w, v, cc,
     )
     recv = to_owner(rows, "y")
     in1 = swap(in1, "sub", n_sub, True)
     (rows,) = call(k_pass, (f32(n_z, R, 6 * B),), recv)
     recv_z = to_owner(rows, "z")
-    out = call(k_send_across, (f32(PACK, B), f32(PACK, B)), recv, w, v, idx)
+    *out, in2 = call(k_send_rest, (f32(PACK, B), f32(PACK, B), f32(WITHIN, B)), recv, w, v, cc, idx)
     across = exchange_across(*out, n_cl)
+    in2 = swap(in2, "sub", n_sub, False)
     gh, gl = call(k_own_columns, (picked, picked), all_ids, gc)
     to_all, scal0, cacross, ah, al = call(
         k_first_global, (*answer, picked, picked), recv_z, gc, gh, gl
     )
-    (in2,) = call(k_send_second, (f32(STATIC, B),), to_all, w, v, idx)
-    in2 = swap(in2, "sub", n_sub, False)
     to_all = to_owner(to_all, "sub")
-    pw, pv, d, pd, signed, curv, *out = call(
+    pw, pv, d, pd, signed, curv, up, down, *out = call(
         k_first_image,
         (f32(NB, D), FIELD, FIELD, FIELD, FIELD, f32(8, B), *SENDS),
         to_all, csol, cacross, in1, in2, *across,
         w, v, sg, operators, idx,
     )
-    got = exchange(*out, n_sub, n_cl)
-    ap, pap, msg = call(
-        make_product(n_cl),
-        (FIELD, FIELD, message),
-        ids, signed, *got, v, w, cc, curv, smem=(0,),
-    )
-    rows, csol = call(k_rows, (f32(n_y, R, D), f32(3, R, B)), to_owner(msg, "sub"))
+    got = exchange_across(*out, n_cl)
+    across, msg = call(
+        k_product,
+        (f32(ROWS, B), f32(NSUB, R, MSG + S * B)),
+        ids, signed, up, down, *got, in1, in2, w, pw, cc, all_ids, smem=(0,),
+    )
+    rows, csol, ap, pap = call(
+        make_joined(n_cl),
+        (f32(n_y, R, D), f32(3, R, B), FIELD, FIELD),
+        to_owner(msg, "sub"), signed, across, curv, v,
+    )
     (rows,) = call(k_pass, (f32(n_z, R, 4 * B),), to_owner(rows, "y"))
-    to_all, scal1, cacross = call(k_global, answer, to_owner(rows, "z"), gh, gl, ah, al)
+    to_all, _, cacross = call(
+        k_global,
+        (f32(NSUB, R, 2 * B), f32(ROWS, B), f32(R, B)),
+        to_owner(rows, "z"), gh, gl, ah, al,
+    )
     r, x, d1, signed, line, *out = call(
         k_last_image,
         (FIELD, FIELD, FIELD, FIELD, f32(n_y * n_sub, 1, B), *SENDS),
-        to_owner(to_all, "sub"), csol, cacross, scal0, scal1,
+        to_owner(to_all, "sub"), csol, cacross, scal0,
         w, pw, v, d, pd, ap, pap, sg, operators, idx,
     )
     line = to_owner(line, ("y", "sub"))

time: 171 us -> 170 us (level)
  waiting for transfers between devices: 18.1 us -> 8.75 us
  local copies, waits for them, and re-layouts: 2.4 us -> 7.94 us
  Pallas kernels: 9.5 us -> 11.6 us
    all_to_all x3, waiting for transfers between devices: 13 us -> 3.88 us  [to_owner(): return lax.all_to_all(x, axis, 0, 0, tiled=True)]
    unnamed x18 -> x48, local copies, waits for them, and re-layouts: 2.4 us -> 7.94 us
    pallas_call x16 -> x15, Pallas kernels: 9.5 us -> 11.6 us  [call(): pl.pallas_call(body, out_shape=out_shape, in_specs=specs, out_specs=tuple...]
    ppermute x12 -> x10, starting transfers between devices: 36.7 us -> 36.2 us  [swap(): lax.ppermute(x, axis, [p for i in low for p in ((i, i + 1), (i + 1, i))])]
    ppermute x12 -> x10, waiting for transfers between devices: 5.18 us -> 4.87 us  [swap(): lax.ppermute(x, axis, [p for i in low for p in ((i, i + 1), (i + 1, i))])]
  transfers between devices with their start and end apart: 15 -> 13, of which waited for: 5 -> 3; matrix products, arithmetic and copies ran while one was open for 0% -> 0% of each run, Pallas kernels for 2% -> 2%
where the time goes in v8:
time: 170 us; the launch traced here: 169 us
  blocking collectives  82.4 us (48%)
  starting transfers between devices  56.2 us (33%)
  Pallas kernels  11.6 us (7%)
  waiting for transfers between devices  8.75 us (5%)
  local copies, waits for them, and re-layouts  7.94 us (5%)
    all_to_all x7, blocking collectives, to_owner(): return lax.all_to_all(x, axis, 0, 0, tiled=True)  82.4 us
    ppermute x10, starting transfers between devices, swap(): lax.ppermute(x, axis, [p for i in low for p in ((i, i + 1), (i + 1, i))])  36.2 us
    all_to_all x3, starting transfers between devices, to_owner(): return lax.all_to_all(x, axis, 0, 0, tiled=True)  19.9 us
    pallas_call x15, Pallas kernels, call(): pl.pallas_call(body, out_shape=out_shape, in_specs=specs, out_specs=tuple...  11.6 us
    unnamed x48, local copies, waits for them, and re-layouts  7.94 us
    ppermute x10, waiting for transfers between devices, swap(): lax.ppermute(x, axis, [p for i in low for p in ((i, i + 1), (i + 1, i))])  4.87 us
    all_to_all x3, waiting for transfers between devices, to_owner(): return lax.all_to_all(x, axis, 0, 0, tiled=True)  3.88 us
  transfers between devices with their start and end apart: 13, of which 3 were waited for; matrix products, arithmetic and copies ran while one was open for 0% of the time, Pallas kernels for 2%

profile of v8, /device:TPU:10, one launch (start us, length us, event | category | flops | bytes accessed | tf_op | source)
XLA Modules:
  0.0 168.7 jit_solution(14737816234141327172)
XLA Ops:
  0.7 1.0 pad_maximum_fusion.w
  1.7 1.0 copy-done.2
  2.6 0.7 copy-done.14
  3.4 0.7 copy-done.18
  4.0 1.1 shard_map.104
  5.1 8.9 %all_to_all.50.recv = f32[8,4,640]{2,1,0:T(4,128)S(1)} all-to-all(f32[8,4,640]{2,1,0:T(4,128)S(1)} %get-tuple-element.46), channel_id=1, replica_groups=mesh['y'=8,'z'=12,'sub'=8] {'sub'}, dimensions={0} | all-to-all | bytes 163840 | tf_op jit(solution)/shard_map/all_to_all | solution.py:625
  14.1 17.0 %all_to_all.51.recv.after = f32[8,4,512]{2,1,0:T(4,128)S(1)} all-to-all(f32[8,4,512]{2,1,0:T(4,128)S(1)} %get-tuple-element.47), channel_id=1, replica_groups=mesh['y'=8,'z'=12,'sub'=8] {'y'}, dimensions={0} | all-to-all | bytes 131072 | tf_op jit(solution)/shard_map/all_to_all | solution.py:625
  31.1 0.7 shard_map.106
  31.8 12.4 %all-to-all-start.2 = ((f32[12,4,768]{2,1,0:T(4,128)}), f32[12,4,768]{2,1,0:T(4,128)S(1)}, u32[]{:S(2)}, u32[]{:S(2)}) async-start(f32[12,4,768]{2,1,0:T(4,128)} %shard_map.106), calls=%async_computation.2 | async-start | bytes 294912 | tf_op jit(solution)/shard_map/all_to_all | solution.py:625
  44.2 1.1 shard_map.109
  45.3 1.9 %collective-permute-start = (f32[720,128]{1,0:T(8,128)}, f32[720,128]{1,0:T(8,128)S(1)}, u32[]{:S(2)}, u32[]{:S(2)}) collective-permute-start(f32[720,128]{1,0:T(8,128)} %get-tuple-element.55), channel_id=1, source_target_pairs={{0,1},{1,0},{2,3},{3,2},{4,5},{5,4},{6,7},{7,6},{8,9},{9,8},{10,11... | collective-permute-start | bytes 1105928 | tf_op jit(solution)/shard_map/ppermute | solution.py:640
  47.2 0.9 shard_map.110
  48.2 3.5 %collective-permute-start.1 = (f32[720,128]{1,0:T(8,128)}, f32[720,128]{1,0:T(8,128)}, u32[]{:S(2)}, u32[]{:S(2)}) collective-permute-start(f32[720,128]{1,0:T(8,128)} %get-tuple-element.57), channel_id=1, source_target_pairs={{1,2},{2,1},{3,4},{4,3},{5,6},{6,5},{9,10},{10,9},{11,12},{12,11},... | collective-permute-start | bytes 1105928 | tf_op jit(solution)/shard_map/ppermute | solution.py:640
  51.6 3.9 %collective-permute-start.2 = (f32[72,128]{1,0:T(8,128)}, f32[72,128]{1,0:T(8,128)}, u32[]{:S(2)}, u32[]{:S(2)}) collective-permute-start(f32[72,128]{1,0:T(8,128)} %get-tuple-element.58), channel_id=1, source_target_pairs={{0,8},{8,0},{16,24},{24,16},{32,40},{40,32},{48,56},{56,48},{64,72... | collective-permute-start | bytes 110600 | tf_op jit(solution)/shard_map/ppermute | solution.py:640
  55.6 5.6 %collective-permute-start.3 = (f32[72,128]{1,0:T(8,128)}, f32[72,128]{1,0:T(8,128)}, u32[]{:S(2)}, u32[]{:S(2)}) collective-permute-start(f32[72,128]{1,0:T(8,128)} %get-tuple-element.59), channel_id=1, source_target_pairs={{8,16},{16,8},{24,32},{32,24},{40,48},{48,40},{56,64},{64,56},{72,... | collective-permute-start | bytes 110600 | tf_op jit(solution)/shard_map/ppermute | solution.py:640
  61.2 0.5 shard_map.107
  61.7 0.6 copy-done.4
  62.3 0.9 copy-done.5
  63.3 0.8 shard_map.108
  64.0 0.7 copy-done.7
  64.7 0.6 copy-done.9
  65.4 0.6 copy-done.15
  66.0 0.6 copy-done.16
  66.6 4.0 %all-to-all-start.3 = ((f32[8,4,128]{2,1,0:T(4,128)}), f32[8,4,128]{2,1,0:T(4,128)S(1)}, u32[]{:S(2)}, u32[]{:S(2)}) async-start(f32[8,4,128]{2,1,0:T(4,128)} %copy-done.15), calls=%async_computation.3 | async-start | bytes 32768 | tf_op jit(solution)/shard_map/all_to_all | solution.py:625
  70.6 3.9 %all-to-all-done.3.recv = f32[8,4,128]{2,1,0:T(4,128)S(1)} async-done(((f32[8,4,128]{2,1,0:T(4,128)}), f32[8,4,128]{2,1,0:T(4,128)S(1)}, u32[]{:S(2)}, u32[]{:S(2)}) %all-to-all-start.3) | async-done | bytes 16416 | tf_op jit(solution)/shard_map/all_to_all | solution.py:625
  74.5 0.7 copy-done.12
  75.2 0.7 copy-done.23
  75.9 1.8 %shard_map.111 = (f32[128,384]{1,0:T(8,128)S(1)}, f32[16,384]{1,0:T(8,128)}, f32[16,384]{1,0:T(8,128)S(1)}, f32[16,384]{1,0:T(8,128)S(1)}, f32[16,384]{1,0:T(8,1...) custom-call(f32[8,4,128]{2,1,0:T(4,128)S(1)} %all-to-all-done.3.recv, ...), custom_call_target="tpu_custom_call" | custom-call | tf_op jit(solution)/shard_map/pallas_call | solution.py:614
  77.7 1.9 %collective-permute-start.4 = (f32[8,128]{1,0:T(8,128)S(1)}, f32[8,128]{1,0:T(8,128)S(1)}, u32[]{:S(2)}, u32[]{:S(2)}) collective-permute-start(f32[8,128]{1,0:T(8,128)S(1)} %get-tuple-element.64), channel_id=1, source_target_pairs={{0,8},{8,0},{16,24},{24,16},{32,40},{40,32},{48,56},{56,48},{64,72... | collective-permute-start | bytes 12296 | tf_op jit(solution)/shard_map/ppermute | solution.py:640
  79.6 4.8 %collective-permute-start.5 = (f32[8,128]{1,0:T(8,128)S(1)}, f32[8,128]{1,0:T(8,128)S(1)}, u32[]{:S(2)}, u32[]{:S(2)}) collective-permute-start(f32[8,128]{1,0:T(8,128)S(1)} %get-tuple-element.65), channel_id=1, source_target_pairs={{8,16},{16,8},{24,32},{32,24},{40,48},{48,40},{56,64},{64,56},{72,... | collective-permute-start | bytes 12296 | tf_op jit(solution)/shard_map/ppermute | solution.py:640
  84.5 2.8 %collective-permute-done.5.out2 = f32[8,128]{1,0:T(8,128)S(1)} collective-permute-done((f32[8,128]{1,0:T(8,128)S(1)}, f32[8,128]{1,0:T(8,128)S(1)}, u32[]{:S(2)}, u32[]{:S(2)}) %collective-permute-start.5) | collective-permute-done | bytes 4128 | tf_op jit(solution)/shard_map/ppermute | solution.py:640
  87.2 1.6 shard_map.112
  88.9 8.7 %all_to_all.52.recv = f32[8,4,1152]{2,1,0:T(4,128)S(1)} all-to-all(f32[8,4,1152]{2,1,0:T(4,128)S(1)} %get-tuple-element.67), channel_id=1, replica_groups=mesh['y'=8,'z'=12,'sub'=8] {'sub'}, dimensions={0} | all-to-all | bytes 294912 | tf_op jit(solution)/shard_map/all_to_all | solution.py:625
  97.6 0.2 shard_map.113
  97.8 12.1 %all_to_all.53.recv = f32[8,4,384]{2,1,0:T(4,128)S(1)} all-to-all(f32[8,4,384]{2,1,0:T(4,128)S(1)} %get-tuple-element.70), channel_id=1, replica_groups=mesh['y'=8,'z'=12,'sub'=8] {'y'}, dimensions={0} | all-to-all | bytes 98304 | tf_op jit(solution)/shard_map/all_to_all | solution.py:625
  109.9 14.4 %all_to_all.54.recv = f32[12,4,512]{2,1,0:T(4,128)S(1)} all-to-all(f32[12,4,512]{2,1,0:T(4,128)S(1)} %shard_map.114), channel_id=1, replica_groups=mesh['y'=8,'z'=12,'sub'=8] {'z'}, dimensions={0} | all-to-all | bytes 196608 | tf_op jit(solution)/shard_map/all_to_all | solution.py:625
  124.3 0.8 shard_map.115
  125.1 7.8 %all_to_all.55.recv = f32[8,4,256]{2,1,0:T(4,128)S(1)} all-to-all(f32[8,4,256]{2,1,0:T(4,128)S(1)} %get-tuple-element.73), channel_id=1, replica_groups=mesh['y'=8,'z'=12,'sub'=8] {'sub'}, dimensions={0} | all-to-all | bytes 65536 | tf_op jit(solution)/shard_map/all_to_all | solution.py:625
  132.9 0.7 shard_map.116
  133.6 13.5 %all_to_all.56.recv = f32[64,1,128]{2,1,0:T(1,128)S(1)} all-to-all(f32[64,1,128]{2,1,0:T(1,128)S(1)} %get-tuple-element.81), channel_id=1, replica_groups=mesh['y'=8,'z'=12,'sub'=8] {'y','sub'}, dimensions={0} | all-to-all | bytes 65536 | tf_op jit(solution)/shard_map/all_to_all | solution.py:625
  147.0 0.7 shard_map.117
  147.7 3.5 %all-to-all-start.9 = ((f32[12,1,128]{2,1,0:T(1,128)}), f32[12,1,128]{2,1,0:T(1,128)S(1)}, u32[]{:S(2)}, u32[]{:S(2)}) async-start(f32[12,1,128]{2,1,0:T(1,128)} %shard_map.117), calls=%async_computation.9 | async-start | bytes 12288 | tf_op jit(solution)/shard_map/all_to_all | solution.py:625
  151.2 1.9 %collective-permute-start.6 = (f32[16,128]{1,0:T(8,128)S(1)}, f32[16,128]{1,0:T(8,128)S(1)}, u32[]{:S(2)}, u32[]{:S(2)}) collective-permute-start(f32[16,128]{1,0:T(8,128)S(1)} %get-tuple-element.83), channel_id=1, source_target_pairs={{0,1},{1,0},{2,3},{3,2},{4,5},{5,4},{6,7},{7,6},{8,9},{9,8},{10,11... | collective-permute-start | bytes 24584 | tf_op jit(solution)/shard_map/ppermute | solution.py:640
  153.1 3.5 %collective-permute-start.7 = (f32[16,128]{1,0:T(8,128)S(1)}, f32[16,128]{1,0:T(8,128)S(1)}, u32[]{:S(2)}, u32[]{:S(2)}) collective-permute-start(f32[16,128]{1,0:T(8,128)S(1)} %get-tuple-element.84), channel_id=1, source_target_pairs={{1,2},{2,1},{3,4},{4,3},{5,6},{6,5},{9,10},{10,9},{11,12},{12,11},... | collective-permute-start | bytes 24584 | tf_op jit(solution)/shard_map/ppermute | solution.py:640
  156.6 3.8 %collective-permute-start.8 = (f32[8,128]{1,0:T(8,128)S(1)}, f32[8,128]{1,0:T(8,128)S(1)}, u32[]{:S(2)}, u32[]{:S(2)}) collective-permute-start(f32[8,128]{1,0:T(8,128)S(1)} %get-tuple-element.85), channel_id=1, source_target_pairs={{0,8},{8,0},{16,24},{24,16},{32,40},{40,32},{48,56},{56,48},{64,72... | collective-permute-start | bytes 12296 | tf_op jit(solution)/shard_map/ppermute | solution.py:640
  160.4 5.5 %collective-permute-start.9 = (f32[8,128]{1,0:T(8,128)S(1)}, f32[8,128]{1,0:T(8,128)S(1)}, u32[]{:S(2)}, u32[]{:S(2)}) collective-permute-start(f32[8,128]{1,0:T(8,128)S(1)} %get-tuple-element.86), channel_id=1, source_target_pairs={{8,16},{16,8},{24,32},{32,24},{40,48},{48,40},{56,64},{64,56},{72,... | collective-permute-start | bytes 12296 | tf_op jit(solution)/shard_map/ppermute | solution.py:640
  165.9 2.1 %collective-permute-done.9.out2 = f32[8,128]{1,0:T(8,128)S(1)} collective-permute-done((f32[8,128]{1,0:T(8,128)S(1)}, f32[8,128]{1,0:T(8,128)S(1)}, u32[]{:S(2)}, u32[]{:S(2)}) %collective-permute-start.9) | collective-permute-done | bytes 4128 | tf_op jit(solution)/shard_map/ppermute | solution.py:640
  168.0 0.7 shard_map.118
  (49 shorter events, 0.2 us)
Async XLA Ops:
  0.6 43.6 %copy-start.3 = (f32[1,96,768]{2,1,0:T(8,128)S(1)}, f32[1,96,768]{2,1,0:T(8,128)}, u32[]{:S(2)}) copy-start(f32[1,96,768]{2,1,0:T(8,128)} %param.16) | copy-start | bytes 884740
  0.6 43.6 %copy-start.21 = (s32[4,3,128]{2,0,1:T(4,128)S(1)}, s32[4,3,128]{2,0,1:T(4,128)}, u32[]{:S(2)}) copy-start(s32[4,3,128]{2,0,1:T(4,128)} %param.12) | copy-start | bytes 18436
  0.7 43.6 %copy-start.20 = (s32[4,384]{1,0:T(4,128)S(1)}, s32[4,384]{1,0:T(4,128)}, u32[]{:S(2)}) copy-start(s32[4,384]{1,0:T(4,128)} %signs.1) | copy-start | bytes 18436
  1.7 1.0 copy-start.2
  2.6 0.7 copy-start.14
  3.4 0.7 copy-start.18
  4.0 57.1 %copy-start = (f32[192,1536]{1,0:T(8,128)S(1)}, f32[192,1536]{1,0:T(8,128)}, u32[]{:S(2)}) copy-start(f32[192,1536]{1,0:T(8,128)} %gc.3) | copy-start | bytes 3538948
  14.1 30.1 %copy-start.22 = (f32[3,4,128]{2,1,0:T(4,128)}, f32[3,4,128]{2,1,0:T(4,128)S(1)}, u32[]{:S(2)}) copy-start(f32[3,4,128]{2,1,0:T(4,128)S(1)} %get-tuple-element.52.csol) | copy-start | bytes 18436
  31.8 30.6 %all-to-all-start.2 = ((f32[12,4,768]{2,1,0:T(4,128)}), f32[12,4,768]{2,1,0:T(4,128)S(1)}, u32[]{:S(2)}, u32[]{:S(2)}) async-start(f32[12,4,768]{2,1,0:T(4,128)} %shard_map.106), calls=%async_computation.2 | async-start | bytes 294912 | tf_op jit(solution)/shard_map/all_to_all | solution.py:625
  45.3 15.9 %copy-start.11 = (f32[16,384]{1,0:T(8,128)}, f32[16,384]{1,0:T(8,128)S(1)}, u32[]{:S(2)}) copy-start(f32[16,384]{1,0:T(8,128)S(1)} %get-tuple-element.60.sg) | copy-start | bytes 73732
  45.3 25.3 %collective-permute-start = (f32[720,128]{1,0:T(8,128)}, f32[720,128]{1,0:T(8,128)S(1)}, u32[]{:S(2)}, u32[]{:S(2)}) collective-permute-start(f32[720,128]{1,0:T(8,128)} %get-tuple-element.55), channel_id=1, source_target_pairs={{0,1},{1,0},{2,3},{3,2},{4,5},{5,4},{6,7},{7,6},{8,9},{9,8},{10,11... | collective-permute-start | bytes 1105928 | tf_op jit(solution)/shard_map/ppermute | solution.py:640
  48.2 22.4 %collective-permute-start.1 = (f32[720,128]{1,0:T(8,128)}, f32[720,128]{1,0:T(8,128)}, u32[]{:S(2)}, u32[]{:S(2)}) collective-permute-start(f32[720,128]{1,0:T(8,128)} %get-tuple-element.57), channel_id=1, source_target_pairs={{1,2},{2,1},{3,4},{4,3},{5,6},{6,5},{9,10},{10,9},{11,12},{12,11},... | collective-permute-start | bytes 1105928 | tf_op jit(solution)/shard_map/ppermute | solution.py:640
  51.6 19.0 %collective-permute-start.2 = (f32[72,128]{1,0:T(8,128)}, f32[72,128]{1,0:T(8,128)}, u32[]{:S(2)}, u32[]{:S(2)}) collective-permute-start(f32[72,128]{1,0:T(8,128)} %get-tuple-element.58), channel_id=1, source_target_pairs={{0,8},{8,0},{16,24},{24,16},{32,40},{40,32},{48,56},{56,48},{64,72... | collective-permute-start | bytes 110600 | tf_op jit(solution)/shard_map/ppermute | solution.py:640
  55.5 19.0 %copy-start.1 = (bf16[4,384,384]{2,1,0:T(8,128)(2,1)S(1)}, bf16[4,384,384]{2,1,0:T(8,128)(2,1)}, u32[]{:S(2)}) copy-start(bf16[4,384,384]{2,1,0:T(8,128)(2,1)} %ops.3) | copy-start | bytes 3538948
  55.6 15.1 %collective-permute-start.3 = (f32[72,128]{1,0:T(8,128)}, f32[72,128]{1,0:T(8,128)}, u32[]{:S(2)}, u32[]{:S(2)}) collective-permute-start(f32[72,128]{1,0:T(8,128)} %get-tuple-element.59), channel_id=1, source_target_pairs={{8,16},{16,8},{24,32},{32,24},{40,48},{48,40},{56,64},{64,56},{72,... | collective-permute-start | bytes 110600 | tf_op jit(solution)/shard_map/ppermute | solution.py:640
  61.7 0.7 copy-start.4
  62.3 0.9 copy-start.5
  64.0 0.7 copy-start.7
  64.7 0.7 copy-start.9
  65.4 0.6 copy-start.15
  66.0 0.6 copy-start.16
  66.6 20.7 %copy-start.19 = (s32[4,8]{1,0:T(4,128)S(1)}, s32[4,8]{1,0:T(4,128)}, u32[]{:S(2)}) copy-start(s32[4,8]{1,0:T(4,128)} %ids.3) | copy-start | bytes 388
  66.6 7.9 %all-to-all-start.3 = ((f32[8,4,128]{2,1,0:T(4,128)}), f32[8,4,128]{2,1,0:T(4,128)S(1)}, u32[]{:S(2)}, u32[]{:S(2)}) async-start(f32[8,4,128]{2,1,0:T(4,128)} %copy-done.15), calls=%async_computation.3 | async-start | bytes 32768 | tf_op jit(solution)/shard_map/all_to_all | solution.py:625
  74.5 0.7 copy-start.12
  75.2 0.7 copy-start.23
  77.7 6.8 %collective-permute-start.4 = (f32[8,128]{1,0:T(8,128)S(1)}, f32[8,128]{1,0:T(8,128)S(1)}, u32[]{:S(2)}, u32[]{:S(2)}) collective-permute-start(f32[8,128]{1,0:T(8,128)S(1)} %get-tuple-element.64), channel_id=1, source_target_pairs={{0,8},{8,0},{16,24},{24,16},{32,40},{40,32},{48,56},{56,48},{64,72... | collective-permute-start | bytes 12296 | tf_op jit(solution)/shard_map/ppermute | solution.py:640
  79.6 7.6 %collective-permute-start.5 = (f32[8,128]{1,0:T(8,128)S(1)}, f32[8,128]{1,0:T(8,128)S(1)}, u32[]{:S(2)}, u32[]{:S(2)}) collective-permute-start(f32[8,128]{1,0:T(8,128)S(1)} %get-tuple-element.65), channel_id=1, source_target_pairs={{8,16},{16,8},{24,32},{32,24},{40,48},{48,40},{56,64},{64,56},{72,... | collective-permute-start | bytes 12296 | tf_op jit(solution)/shard_map/ppermute | solution.py:640
  87.2 37.1 %copy-start.6 = (bf16[256,256]{1,0:T(8,128)(2,1)S(1)}, bf16[256,256]{1,0:T(8,128)(2,1)}, u32[]{:S(2)}) copy-start(bf16[256,256]{1,0:T(8,128)(2,1)} %copy-done.4) | copy-start | bytes 393220
  87.2 37.1 %copy-start.8 = (bf16[256,256]{1,0:T(8,128)(2,1)S(1)}, bf16[256,256]{1,0:T(8,128)(2,1)}, u32[]{:S(2)}) copy-start(bf16[256,256]{1,0:T(8,128)(2,1)} %copy-done.7) | copy-start | bytes 393220
  87.2 37.1 %copy-start.10 = (bf16[256,256]{1,0:T(8,128)(2,1)S(1)}, bf16[256,256]{1,0:T(8,128)(2,1)}, u32[]{:S(2)}) copy-start(bf16[256,256]{1,0:T(8,128)(2,1)} %copy-done.9) | copy-start | bytes 393220
  88.9 44.0 %copy-start.13 = (f32[16,384]{1,0:T(8,128)S(1)}, f32[16,384]{1,0:T(8,128)}, u32[]{:S(2)}) copy-start(f32[16,384]{1,0:T(8,128)} %copy-done.11) | copy-start | bytes 73732
  88.9 44.0 %copy-start.17 = (f32[16,128]{1,0:T(8,128)S(1)}, f32[16,128]{1,0:T(8,128)}, u32[]{:S(2)}) copy-start(f32[16,128]{1,0:T(8,128)} %copy-done.16) | copy-start | bytes 24580
  147.7 20.3 %all-to-all-start.9 = ((f32[12,1,128]{2,1,0:T(1,128)}), f32[12,1,128]{2,1,0:T(1,128)S(1)}, u32[]{:S(2)}, u32[]{:S(2)}) async-start(f32[12,1,128]{2,1,0:T(1,128)} %shard_map.117), calls=%async_computation.9 | async-start | bytes 12288 | tf_op jit(solution)/shard_map/all_to_all | solution.py:625
  151.2 16.8 %collective-permute-start.6 = (f32[16,128]{1,0:T(8,128)S(1)}, f32[16,128]{1,0:T(8,128)S(1)}, u32[]{:S(2)}, u32[]{:S(2)}) collective-permute-start(f32[16,128]{1,0:T(8,128)S(1)} %get-tuple-element.83), channel_id=1, source_target_pairs={{0,1},{1,0},{2,3},{3,2},{4,5},{5,4},{6,7},{7,6},{8,9},{9,8},{10,11... | collective-permute-start | bytes 24584 | tf_op jit(solution)/shard_map/ppermute | solution.py:640
  153.1 14.9 %collective-permute-start.7 = (f32[16,128]{1,0:T(8,128)S(1)}, f32[16,128]{1,0:T(8,128)S(1)}, u32[]{:S(2)}, u32[]{:S(2)}) collective-permute-start(f32[16,128]{1,0:T(8,128)S(1)} %get-tuple-element.84), channel_id=1, source_target_pairs={{1,2},{2,1},{3,4},{4,3},{5,6},{6,5},{9,10},{10,9},{11,12},{12,11},... | collective-permute-start | bytes 24584 | tf_op jit(solution)/shard_map/ppermute | solution.py:640
  156.6 9.3 %collective-permute-start.8 = (f32[8,128]{1,0:T(8,128)S(1)}, f32[8,128]{1,0:T(8,128)S(1)}, u32[]{:S(2)}, u32[]{:S(2)}) collective-permute-start(f32[8,128]{1,0:T(8,128)S(1)} %get-tuple-element.85), channel_id=1, source_target_pairs={{0,8},{8,0},{16,24},{24,16},{32,40},{40,32},{48,56},{56,48},{64,72... | collective-permute-start | bytes 12296 | tf_op jit(solution)/shard_map/ppermute | solution.py:640
  160.4 7.6 %collective-permute-start.9 = (f32[8,128]{1,0:T(8,128)S(1)}, f32[8,128]{1,0:T(8,128)S(1)}, u32[]{:S(2)}, u32[]{:S(2)}) collective-permute-start(f32[8,128]{1,0:T(8,128)S(1)} %get-tuple-element.86), channel_id=1, source_target_pairs={{8,16},{16,8},{24,32},{32,24},{40,48},{48,40},{56,64},{64,56},{72,... | collective-permute-start | bytes 12296 | tf_op jit(solution)/shard_map/ppermute | solution.py:640

commit v9 on v8

--- a/solution.py
+++ b/solution.py
@@ -207,14 +207,15 @@
     return jnp.concatenate([x[STATIC + NCL * j : STATIC + NCL * j + NCL, :] for j in range(6)], axis=1)
 
 
-def k_send_first(after, signs, links, w, v, cc, sg_out, idx_out, out):
+def k_send_first(after, signs, links, w, v, cc, sg_out, idx_out, first, second):
     k_tables(after, signs, links, sg_out, idx_out)
-    send_within(w, v, cc, idx_out, out, lax.axis_index("sub") % 2)
-
-
-def k_send_rest(after, w, v, cc, idx, first, second, within):
+    odd = lax.axis_index("sub") % 2
+    send_within(w, v, cc, idx_out, first, odd)
+    send_within(w, v, cc, idx_out, second, 1 - odd)
+
+
+def k_send_across(after, w, v, idx, first, second):
     del after
-    send_within(w, v, cc, idx, within, 1 - lax.axis_index("sub") % 2)
     flag = even_cluster()
     blocks = {(s, at): x for s, at, x in static_blocks(w, v, idx, 2)}
 
@@ -359,10 +360,6 @@
     lo_out[CHUNK : 2 * B, :] = zero
 
 
-def k_own_columns(ids, gc, hi_out, lo_out):
-    picked_columns(gc, [ids[0:1, :], ids[1:2, :]], hi_out, lo_out)
-
-
 def solve(recv, parts, msg, scal, cacross, stride):
     total = jnp.sum(recv[:, :, 0 : 2 * B], axis=0)
     total = jnp.concatenate([total, total], axis=0)
@@ -395,7 +392,8 @@
     cacross[...] = jnp.where(lane < NCL, both, 0.0)[:R]
 
 
-def k_first_global(recv, gc, gh, gl, msg, scal, cacross, ah, al):
+def k_first_global(recv, own, gc, msg, scal, cacross, gh, gl, ah, al):
+    picked_columns(gc, [own[0:1, :], own[1:2, :]], gh, gl)
     after, before = neighbours(recv, 3 * B, 5 * B)
     lane = iota((8, B), 1)
     after = pltpu.roll(after, B - 8, 1)
@@ -669,21 +667,20 @@
     rows, csol, all_ids = call(
         k_first_rows, (f32(n_y, R, 4 * B), f32(3, R, B), f32(8, B)), recv
     )
-    sg, idx, in1 = call(
+    sg, idx, in1, in2 = call(
         k_send_first,
-        (FIELD, ((3, ROWS, B), I32), f32(WITHIN, B)),
+        (FIELD, ((3, ROWS, B), I32), f32(WITHIN, B), f32(WITHIN, B)),
         all_ids, signs, links.transpose(1, 0, 2), w, v, cc,
     )
     recv = to_owner(rows, "y")
     in1 = swap(in1, "sub", n_sub, True)
+    in2 = swap(in2, "sub", n_sub, False)
     (rows,) = call(k_pass, (f32(n_z, R, 6 * B),), recv)
     recv_z = to_owner(rows, "z")
-    *out, in2 = call(k_send_rest, (f32(PACK, B), f32(PACK, B), f32(WITHIN, B)), recv, w, v, cc, idx)
+    out = call(k_send_across, (f32(PACK, B), f32(PACK, B)), recv, w, v, idx)
     across = exchange_across(*out, n_cl)
-    in2 = swap(in2, "sub", n_sub, False)
-    gh, gl = call(k_own_columns, (picked, picked), all_ids, gc)
-    to_all, scal0, cacross, ah, al = call(
-        k_first_global, (*answer, picked, picked), recv_z, gc, gh, gl
+    to_all, scal0, cacross, gh, gl, ah, al = call(
+        k_first_global, (*answer, picked, picked, picked, picked), recv_z, all_ids, gc
     )
     to_all = to_owner(to_all, "sub")
     pw, pv, d, pd, signed, curv, up, down, *out = call(

time: 170 us -> 163 us (0.959)
  local copies, waits for them, and re-layouts: 7.94 us -> 3.67 us
  Pallas kernels: 11.6 us -> 9.68 us
    unnamed x48 -> x18, local copies, waits for them, and re-layouts: 7.94 us -> 3.67 us
    pallas_call x15 -> x14, Pallas kernels: 11.6 us -> 9.68 us  [call(): pl.pallas_call(body, out_shape=out_shape, in_specs=specs, out_specs=tuple...]
where the time goes in v9:
time: 163 us; the launch traced here: 162 us
  blocking collectives  82.3 us (50%)
  starting transfers between devices  56 us (34%)
  Pallas kernels  9.68 us (6%)
  waiting for transfers between devices  8.77 us (5%)
  local copies, waits for them, and re-layouts  3.67 us (2%)
    all_to_all x7, blocking collectives, to_owner(): return lax.all_to_all(x, axis, 0, 0, tiled=True)  82.3 us
    ppermute x10, starting transfers between devices, swap(): lax.ppermute(x, axis, [p for i in low for p in ((i, i + 1), (i + 1, i))])  36.1 us
    all_to_all x3, starting transfers between devices, to_owner(): return lax.all_to_all(x, axis, 0, 0, tiled=True)  19.9 us
    pallas_call x14, Pallas kernels, call(): pl.pallas_call(body, out_shape=out_shape, in_specs=specs, out_specs=tuple...  9.68 us
    ppermute x10, waiting for transfers between devices, swap(): lax.ppermute(x, axis, [p for i in low for p in ((i, i + 1), (i + 1, i))])  4.89 us
    all_to_all x3, waiting for transfers between devices, to_owner(): return lax.all_to_all(x, axis, 0, 0, tiled=True)  3.88 us
    unnamed x18, local copies, waits for them, and re-layouts  3.67 us
  transfers between devices with their start and end apart: 13, of which 3 were waited for; matrix products, arithmetic and copies ran while one was open for 0% of the time, Pallas kernels for 2%

profile of v9, /device:TPU:10, one launch (start us, length us, event | category | flops | bytes accessed | tf_op | source)
XLA Modules:
  0.0 162.4 jit_solution(15361062948915940907)
XLA Ops:
  0.6 0.0 copy-start.2
  0.7 1.0 pad_maximum_fusion.w
  1.7 0.0 copy-start.1
  1.7 1.0 copy-done.1
  2.6 0.7 copy-done.4
  3.4 0.7 copy-done.5
  4.0 1.1 shard_map.104
  5.1 8.9 %all_to_all.50.recv = f32[8,4,640]{2,1,0:T(4,128)S(1)} all-to-all(f32[8,4,640]{2,1,0:T(4,128)S(1)} %get-tuple-element.46), channel_id=1, replica_groups=mesh['y'=8,'z'=12,'sub'=8] {'sub'}, dimensions={0} | all-to-all | bytes 163840 | tf_op jit(solution)/shard_map/all_to_all | solution.py:623
  14.0 0.1 shard_map.105
  14.1 17.0 %all_to_all.51.recv.after = f32[8,4,512]{2,1,0:T(4,128)S(1)} all-to-all(f32[8,4,512]{2,1,0:T(4,128)S(1)} %get-tuple-element.47), channel_id=1, replica_groups=mesh['y'=8,'z'=12,'sub'=8] {'y'}, dimensions={0} | all-to-all | bytes 131072 | tf_op jit(solution)/shard_map/all_to_all | solution.py:623
  31.1 0.7 shard_map.106
  31.8 12.4 %all-to-all-start.2 = ((f32[12,4,768]{2,1,0:T(4,128)}), f32[12,4,768]{2,1,0:T(4,128)S(1)}, u32[]{:S(2)}, u32[]{:S(2)}) async-start(f32[12,4,768]{2,1,0:T(4,128)} %shard_map.106), calls=%async_computation.2 | async-start | bytes 294912 | tf_op jit(solution)/shard_map/all_to_all | solution.py:623
  44.2 0.0 copy-start
  44.2 1.2 shard_map.108
  45.4 1.9 %collective-permute-start = (f32[720,128]{1,0:T(8,128)}, f32[720,128]{1,0:T(8,128)S(1)}, u32[]{:S(2)}, u32[]{:S(2)}) collective-permute-start(f32[720,128]{1,0:T(8,128)} %get-tuple-element.53), channel_id=1, source_target_pairs={{0,1},{1,0},{2,3},{3,2},{4,5},{5,4},{6,7},{7,6},{8,9},{9,8},{10,11... | collective-permute-start | bytes 1105928 | tf_op jit(solution)/shard_map/ppermute | solution.py:638
  47.3 3.5 %collective-permute-start.1 = (f32[720,128]{1,0:T(8,128)}, f32[720,128]{1,0:T(8,128)S(1)}, u32[]{:S(2)}, u32[]{:S(2)}) collective-permute-start(f32[720,128]{1,0:T(8,128)} %get-tuple-element.54), channel_id=1, source_target_pairs={{1,2},{2,1},{3,4},{4,3},{5,6},{6,5},{9,10},{10,9},{11,12},{12,11},... | collective-permute-start | bytes 1105928 | tf_op jit(solution)/shard_map/ppermute | solution.py:638
  50.8 0.1 shard_map.109
  50.9 3.9 %collective-permute-start.2 = (f32[72,128]{1,0:T(8,128)S(1)}, f32[72,128]{1,0:T(8,128)S(1)}, u32[]{:S(2)}, u32[]{:S(2)}) collective-permute-start(f32[72,128]{1,0:T(8,128)S(1)} %get-tuple-element.56), channel_id=1, source_target_pairs={{0,8},{8,0},{16,24},{24,16},{32,40},{40,32},{48,56},{56,48},{64,72... | collective-permute-start | bytes 110600 | tf_op jit(solution)/shard_map/ppermute | solution.py:638
  54.8 5.5 %collective-permute-start.3 = (f32[72,128]{1,0:T(8,128)S(1)}, f32[72,128]{1,0:T(8,128)S(1)}, u32[]{:S(2)}, u32[]{:S(2)}) collective-permute-start(f32[72,128]{1,0:T(8,128)S(1)} %get-tuple-element.57), channel_id=1, source_target_pairs={{8,16},{16,8},{24,32},{32,24},{40,48},{48,40},{56,64},{64,56},{72,... | collective-permute-start | bytes 110600 | tf_op jit(solution)/shard_map/ppermute | solution.py:638
  60.3 0.0 copy-start.3
  60.3 1.3 copy-done.3
  61.6 1.6 shard_map.107
  63.2 4.0 %all-to-all-start.3 = ((f32[8,4,128]{2,1,0:T(4,128)}), f32[8,4,128]{2,1,0:T(4,128)S(1)}, u32[]{:S(2)}, u32[]{:S(2)}) async-start(f32[8,4,128]{2,1,0:T(4,128)} %get-tuple-element.49), calls=%async_computation.3 | async-start | bytes 32768 | tf_op jit(solution)/shard_map/all_to_all | solution.py:623
  67.2 0.0 collective-permute-done.2.out1
  67.2 0.0 collective-permute-done.3.out2
  67.3 0.0 collective-permute-done.1.in2.static2
  67.3 3.9 %all-to-all-done.3.recv = f32[8,4,128]{2,1,0:T(4,128)S(1)} async-done(((f32[8,4,128]{2,1,0:T(4,128)}), f32[8,4,128]{2,1,0:T(4,128)S(1)}, u32[]{:S(2)}, u32[]{:S(2)}) %all-to-all-start.3) | async-done | bytes 16416 | tf_op jit(solution)/shard_map/all_to_all | solution.py:623
  71.1 0.8 shard_map.110
  71.9 1.9 %collective-permute-start.4 = (f32[8,128]{1,0:T(8,128)S(1)}, f32[8,128]{1,0:T(8,128)S(1)}, u32[]{:S(2)}, u32[]{:S(2)}) collective-permute-start(f32[8,128]{1,0:T(8,128)S(1)} %get-tuple-element.62), channel_id=1, source_target_pairs={{0,8},{8,0},{16,24},{24,16},{32,40},{40,32},{48,56},{56,48},{64,72... | collective-permute-start | bytes 12296 | tf_op jit(solution)/shard_map/ppermute | solution.py:638
  73.8 4.8 %collective-permute-start.5 = (f32[8,128]{1,0:T(8,128)S(1)}, f32[8,128]{1,0:T(8,128)S(1)}, u32[]{:S(2)}, u32[]{:S(2)}) collective-permute-start(f32[8,128]{1,0:T(8,128)S(1)} %get-tuple-element.63), channel_id=1, source_target_pairs={{8,16},{16,8},{24,32},{32,24},{40,48},{48,40},{56,64},{64,56},{72,... | collective-permute-start | bytes 12296 | tf_op jit(solution)/shard_map/ppermute | solution.py:638
  78.7 2.8 %collective-permute-done.5.out2 = f32[8,128]{1,0:T(8,128)S(1)} collective-permute-done((f32[8,128]{1,0:T(8,128)S(1)}, f32[8,128]{1,0:T(8,128)S(1)}, u32[]{:S(2)}, u32[]{:S(2)}) %collective-permute-start.5) | collective-permute-done | bytes 4128 | tf_op jit(solution)/shard_map/ppermute | solution.py:638
  81.4 1.2 shard_map.111
  82.6 8.7 %all_to_all.52.recv = f32[8,4,1152]{2,1,0:T(4,128)S(1)} all-to-all(f32[8,4,1152]{2,1,0:T(4,128)S(1)} %get-tuple-element.65), channel_id=1, replica_groups=mesh['y'=8,'z'=12,'sub'=8] {'sub'}, dimensions={0} | all-to-all | bytes 294912 | tf_op jit(solution)/shard_map/all_to_all | solution.py:623
  91.3 0.2 shard_map.112
  91.5 12.1 %all_to_all.53.recv = f32[8,4,384]{2,1,0:T(4,128)S(1)} all-to-all(f32[8,4,384]{2,1,0:T(4,128)S(1)} %get-tuple-element.68), channel_id=1, replica_groups=mesh['y'=8,'z'=12,'sub'=8] {'y'}, dimensions={0} | all-to-all | bytes 98304 | tf_op jit(solution)/shard_map/all_to_all | solution.py:623
  103.6 14.4 %all_to_all.54.recv = f32[12,4,512]{2,1,0:T(4,128)S(1)} all-to-all(f32[12,4,512]{2,1,0:T(4,128)S(1)} %shard_map.113), channel_id=1, replica_groups=mesh['y'=8,'z'=12,'sub'=8] {'z'}, dimensions={0} | all-to-all | bytes 196608 | tf_op jit(solution)/shard_map/all_to_all | solution.py:623
  118.0 0.7 shard_map.114
  118.7 7.8 %all_to_all.55.recv = f32[8,4,256]{2,1,0:T(4,128)S(1)} all-to-all(f32[8,4,256]{2,1,0:T(4,128)S(1)} %get-tuple-element.73), channel_id=1, replica_groups=mesh['y'=8,'z'=12,'sub'=8] {'sub'}, dimensions={0} | all-to-all | bytes 65536 | tf_op jit(solution)/shard_map/all_to_all | solution.py:623
  126.5 0.7 shard_map.115
  127.2 13.5 %all_to_all.56.recv = f32[64,1,128]{2,1,0:T(1,128)S(1)} all-to-all(f32[64,1,128]{2,1,0:T(1,128)S(1)} %get-tuple-element.81), channel_id=1, replica_groups=mesh['y'=8,'z'=12,'sub'=8] {'y','sub'}, dimensions={0} | all-to-all | bytes 65536 | tf_op jit(solution)/shard_map/all_to_all | solution.py:623
  140.7 0.7 shard_map.116
  141.4 3.5 %all-to-all-start.9 = ((f32[12,1,128]{2,1,0:T(1,128)}), f32[12,1,128]{2,1,0:T(1,128)S(1)}, u32[]{:S(2)}, u32[]{:S(2)}) async-start(f32[12,1,128]{2,1,0:T(1,128)} %shard_map.116), calls=%async_computation.9 | async-start | bytes 12288 | tf_op jit(solution)/shard_map/all_to_all | solution.py:623
  144.9 1.9 %collective-permute-start.6 = (f32[16,128]{1,0:T(8,128)S(1)}, f32[16,128]{1,0:T(8,128)S(1)}, u32[]{:S(2)}, u32[]{:S(2)}) collective-permute-start(f32[16,128]{1,0:T(8,128)S(1)} %get-tuple-element.83), channel_id=1, source_target_pairs={{0,1},{1,0},{2,3},{3,2},{4,5},{5,4},{6,7},{7,6},{8,9},{9,8},{10,11... | collective-permute-start | bytes 24584 | tf_op jit(solution)/shard_map/ppermute | solution.py:638
  146.8 3.5 %collective-permute-start.7 = (f32[16,128]{1,0:T(8,128)S(1)}, f32[16,128]{1,0:T(8,128)S(1)}, u32[]{:S(2)}, u32[]{:S(2)}) collective-permute-start(f32[16,128]{1,0:T(8,128)S(1)} %get-tuple-element.84), channel_id=1, source_target_pairs={{1,2},{2,1},{3,4},{4,3},{5,6},{6,5},{9,10},{10,9},{11,12},{12,11},... | collective-permute-start | bytes 24584 | tf_op jit(solution)/shard_map/ppermute | solution.py:638
  150.3 3.8 %collective-permute-start.8 = (f32[8,128]{1,0:T(8,128)S(1)}, f32[8,128]{1,0:T(8,128)S(1)}, u32[]{:S(2)}, u32[]{:S(2)}) collective-permute-start(f32[8,128]{1,0:T(8,128)S(1)} %get-tuple-element.85), channel_id=1, source_target_pairs={{0,8},{8,0},{16,24},{24,16},{32,40},{40,32},{48,56},{56,48},{64,72... | collective-permute-start | bytes 12296 | tf_op jit(solution)/shard_map/ppermute | solution.py:638
  154.0 5.5 %collective-permute-start.9 = (f32[8,128]{1,0:T(8,128)S(1)}, f32[8,128]{1,0:T(8,128)S(1)}, u32[]{:S(2)}, u32[]{:S(2)}) collective-permute-start(f32[8,128]{1,0:T(8,128)S(1)} %get-tuple-element.86), channel_id=1, source_target_pairs={{8,16},{16,8},{24,32},{32,24},{40,48},{48,40},{56,64},{64,56},{72,... | collective-permute-start | bytes 12296 | tf_op jit(solution)/shard_map/ppermute | solution.py:638
  159.5 2.1 %collective-permute-done.9.out2 = f32[8,128]{1,0:T(8,128)S(1)} collective-permute-done((f32[8,128]{1,0:T(8,128)S(1)}, f32[8,128]{1,0:T(8,128)S(1)}, u32[]{:S(2)}, u32[]{:S(2)}) %collective-permute-start.9) | collective-permute-done | bytes 4128 | tf_op jit(solution)/shard_map/ppermute | solution.py:638
  161.6 0.7 shard_map.117
  (18 shorter events, 0.1 us)
Async XLA Ops:
  0.6 43.6 %copy-start.2 = (f32[1,96,768]{2,1,0:T(8,128)S(1)}, f32[1,96,768]{2,1,0:T(8,128)}, u32[]{:S(2)}) copy-start(f32[1,96,768]{2,1,0:T(8,128)} %param.16) | copy-start | bytes 884740
  0.6 43.6 %copy-start.8 = (s32[4,3,128]{2,0,1:T(4,128)S(1)}, s32[4,3,128]{2,0,1:T(4,128)}, u32[]{:S(2)}) copy-start(s32[4,3,128]{2,0,1:T(4,128)} %param.12) | copy-start | bytes 18436
  0.7 43.6 %copy-start.7 = (s32[4,384]{1,0:T(4,128)S(1)}, s32[4,384]{1,0:T(4,128)}, u32[]{:S(2)}) copy-start(s32[4,384]{1,0:T(4,128)} %signs.1) | copy-start | bytes 18436
  1.7 1.0 copy-start.1
  2.6 0.7 copy-start.4
  3.4 0.7 copy-start.5
  31.8 28.6 %all-to-all-start.2 = ((f32[12,4,768]{2,1,0:T(4,128)}), f32[12,4,768]{2,1,0:T(4,128)S(1)}, u32[]{:S(2)}, u32[]{:S(2)}) async-start(f32[12,4,768]{2,1,0:T(4,128)} %shard_map.106), calls=%async_computation.2 | async-start | bytes 294912 | tf_op jit(solution)/shard_map/all_to_all | solution.py:623
  44.2 27.0 %copy-start = (bf16[4,384,384]{2,1,0:T(8,128)(2,1)S(1)}, bf16[4,384,384]{2,1,0:T(8,128)(2,1)}, u32[]{:S(2)}) copy-start(bf16[4,384,384]{2,1,0:T(8,128)(2,1)} %ops.3) | copy-start | bytes 3538948
  45.4 21.8 %collective-permute-start = (f32[720,128]{1,0:T(8,128)}, f32[720,128]{1,0:T(8,128)S(1)}, u32[]{:S(2)}, u32[]{:S(2)}) collective-permute-start(f32[720,128]{1,0:T(8,128)} %get-tuple-element.53), channel_id=1, source_target_pairs={{0,1},{1,0},{2,3},{3,2},{4,5},{5,4},{6,7},{7,6},{8,9},{9,8},{10,11... | collective-permute-start | bytes 1105928 | tf_op jit(solution)/shard_map/ppermute | solution.py:638
  47.3 19.9 %collective-permute-start.1 = (f32[720,128]{1,0:T(8,128)}, f32[720,128]{1,0:T(8,128)S(1)}, u32[]{:S(2)}, u32[]{:S(2)}) collective-permute-start(f32[720,128]{1,0:T(8,128)} %get-tuple-element.54), channel_id=1, source_target_pairs={{1,2},{2,1},{3,4},{4,3},{5,6},{6,5},{9,10},{10,9},{11,12},{12,11},... | collective-permute-start | bytes 1105928 | tf_op jit(solution)/shard_map/ppermute | solution.py:638
  50.9 16.3 %collective-permute-start.2 = (f32[72,128]{1,0:T(8,128)S(1)}, f32[72,128]{1,0:T(8,128)S(1)}, u32[]{:S(2)}, u32[]{:S(2)}) collective-permute-start(f32[72,128]{1,0:T(8,128)S(1)} %get-tuple-element.56), channel_id=1, source_target_pairs={{0,8},{8,0},{16,24},{24,16},{32,40},{40,32},{48,56},{56,48},{64,72... | collective-permute-start | bytes 110600 | tf_op jit(solution)/shard_map/ppermute | solution.py:638
  54.8 12.4 %collective-permute-start.3 = (f32[72,128]{1,0:T(8,128)S(1)}, f32[72,128]{1,0:T(8,128)S(1)}, u32[]{:S(2)}, u32[]{:S(2)}) collective-permute-start(f32[72,128]{1,0:T(8,128)S(1)} %get-tuple-element.57), channel_id=1, source_target_pairs={{8,16},{16,8},{24,32},{32,24},{40,48},{48,40},{56,64},{64,56},{72,... | collective-permute-start | bytes 110600 | tf_op jit(solution)/shard_map/ppermute | solution.py:638
  60.3 1.3 copy-start.3
  63.2 18.2 %copy-start.6 = (s32[4,8]{1,0:T(4,128)S(1)}, s32[4,8]{1,0:T(4,128)}, u32[]{:S(2)}) copy-start(s32[4,8]{1,0:T(4,128)} %ids.3) | copy-start | bytes 388
  63.2 7.9 %all-to-all-start.3 = ((f32[8,4,128]{2,1,0:T(4,128)}), f32[8,4,128]{2,1,0:T(4,128)S(1)}, u32[]{:S(2)}, u32[]{:S(2)}) async-start(f32[8,4,128]{2,1,0:T(4,128)} %get-tuple-element.49), calls=%async_computation.3 | async-start | bytes 32768 | tf_op jit(solution)/shard_map/all_to_all | solution.py:623
  71.9 6.7 %collective-permute-start.4 = (f32[8,128]{1,0:T(8,128)S(1)}, f32[8,128]{1,0:T(8,128)S(1)}, u32[]{:S(2)}, u32[]{:S(2)}) collective-permute-start(f32[8,128]{1,0:T(8,128)S(1)} %get-tuple-element.62), channel_id=1, source_target_pairs={{0,8},{8,0},{16,24},{24,16},{32,40},{40,32},{48,56},{56,48},{64,72... | collective-permute-start | bytes 12296 | tf_op jit(solution)/shard_map/ppermute | solution.py:638
  73.8 7.6 %collective-permute-start.5 = (f32[8,128]{1,0:T(8,128)S(1)}, f32[8,128]{1,0:T(8,128)S(1)}, u32[]{:S(2)}, u32[]{:S(2)}) collective-permute-start(f32[8,128]{1,0:T(8,128)S(1)} %get-tuple-element.63), channel_id=1, source_target_pairs={{8,16},{16,8},{24,32},{32,24},{40,48},{48,40},{56,64},{64,56},{72,... | collective-permute-start | bytes 12296 | tf_op jit(solution)/shard_map/ppermute | solution.py:638
  141.4 20.3 %all-to-all-start.9 = ((f32[12,1,128]{2,1,0:T(1,128)}), f32[12,1,128]{2,1,0:T(1,128)S(1)}, u32[]{:S(2)}, u32[]{:S(2)}) async-start(f32[12,1,128]{2,1,0:T(1,128)} %shard_map.116), calls=%async_computation.9 | async-start | bytes 12288 | tf_op jit(solution)/shard_map/all_to_all | solution.py:623
  144.9 16.8 %collective-permute-start.6 = (f32[16,128]{1,0:T(8,128)S(1)}, f32[16,128]{1,0:T(8,128)S(1)}, u32[]{:S(2)}, u32[]{:S(2)}) collective-permute-start(f32[16,128]{1,0:T(8,128)S(1)} %get-tuple-element.83), channel_id=1, source_target_pairs={{0,1},{1,0},{2,3},{3,2},{4,5},{5,4},{6,7},{7,6},{8,9},{9,8},{10,11... | collective-permute-start | bytes 24584 | tf_op jit(solution)/shard_map/ppermute | solution.py:638
  146.8 14.9 %collective-permute-start.7 = (f32[16,128]{1,0:T(8,128)S(1)}, f32[16,128]{1,0:T(8,128)S(1)}, u32[]{:S(2)}, u32[]{:S(2)}) collective-permute-start(f32[16,128]{1,0:T(8,128)S(1)} %get-tuple-element.84), channel_id=1, source_target_pairs={{1,2},{2,1},{3,4},{4,3},{5,6},{6,5},{9,10},{10,9},{11,12},{12,11},... | collective-permute-start | bytes 24584 | tf_op jit(solution)/shard_map/ppermute | solution.py:638
  150.3 9.3 %collective-permute-start.8 = (f32[8,128]{1,0:T(8,128)S(1)}, f32[8,128]{1,0:T(8,128)S(1)}, u32[]{:S(2)}, u32[]{:S(2)}) collective-permute-start(f32[8,128]{1,0:T(8,128)S(1)} %get-tuple-element.85), channel_id=1, source_target_pairs={{0,8},{8,0},{16,24},{24,16},{32,40},{40,32},{48,56},{56,48},{64,72... | collective-permute-start | bytes 12296 | tf_op jit(solution)/shard_map/ppermute | solution.py:638
  154.0 7.6 %collective-permute-start.9 = (f32[8,128]{1,0:T(8,128)S(1)}, f32[8,128]{1,0:T(8,128)S(1)}, u32[]{:S(2)}, u32[]{:S(2)}) collective-permute-start(f32[8,128]{1,0:T(8,128)S(1)} %get-tuple-element.86), channel_id=1, source_target_pairs={{8,16},{16,8},{24,32},{32,24},{40,48},{48,40},{56,64},{64,56},{72,... | collective-permute-start | bytes 12296 | tf_op jit(solution)/shard_map/ppermute | solution.py:638

commit v10 on v9

--- a/solution.py
+++ b/solution.py
@@ -207,15 +207,18 @@
     return jnp.concatenate([x[STATIC + NCL * j : STATIC + NCL * j + NCL, :] for j in range(6)], axis=1)
 
 
-def k_send_first(after, signs, links, w, v, cc, sg_out, idx_out, first, second):
+def k_send_static(after, signs, links, w, v, cc, sg_out, idx_out, within, out1, out2):
     k_tables(after, signs, links, sg_out, idx_out)
-    odd = lax.axis_index("sub") % 2
-    send_within(w, v, cc, idx_out, first, odd)
-    send_within(w, v, cc, idx_out, second, 1 - odd)
-
-
-def k_send_across(after, w, v, idx, first, second):
+    send_within(w, v, cc, idx_out, within, 1 - lax.axis_index("sub") % 2)
+    send_across(w, v, idx_out, out1, out2)
+
+
+def k_send_chip(after, w, v, cc, idx, within):
     del after
+    send_within(w, v, cc, idx, within, lax.axis_index("sub") % 2)
+
+
+def send_across(w, v, idx, first, second):
     flag = even_cluster()
     blocks = {(s, at): x for s, at, x in static_blocks(w, v, idx, 2)}
 
@@ -360,7 +363,7 @@
     lo_out[CHUNK : 2 * B, :] = zero
 
 
-def solve(recv, parts, msg, scal, cacross, stride):
+def solve(recv, parts, msg, cacross, stride):
     total = jnp.sum(recv[:, :, 0 : 2 * B], axis=0)
     total = jnp.concatenate([total, total], axis=0)
     second = total[:, B:]
@@ -384,12 +387,12 @@
         msg[k, :, 0:B] = jnp.where(lane < 96, here, picked(1, k, 96))[:R]
         if msg.shape[2] > B:
             msg[k, :, B : 2 * B] = second[:R]
-    scal[...] = jnp.concatenate([second, second], axis=0)
     after, before = neighbours(recv, 2 * B, 2 * B + stride)
     after = pltpu.roll(after, B - KC, 1)
     before = pltpu.roll(before, KC, 1)
     both = jnp.where(lane // KC % 2 == 0, after, before)
     cacross[...] = jnp.where(lane < NCL, both, 0.0)[:R]
+    return second
 
 
 def k_first_global(recv, own, gc, msg, scal, cacross, gh, gl, ah, al):
@@ -400,11 +403,12 @@
     before = pltpu.roll(before, 8, 1)
     ids = jnp.where(lane // 8 % 2 == 0, after, before)
     picked_columns(gc, [ids[0:1], ids[1:2]], ah, al)
-    solve(recv, ((gh, gl), (ah, al)), msg, scal, cacross, 2 * B)
-
-
-def k_global(recv, gh, gl, ah, al, msg, scal, cacross):
-    solve(recv, ((gh, gl), (ah, al)), msg, scal, cacross, B)
+    second = solve(recv, ((gh, gl), (ah, al)), msg, cacross, 2 * B)
+    scal[...] = jnp.concatenate([second, second], axis=0)
+
+
+def k_global(recv, gh, gl, ah, al, msg, cacross):
+    solve(recv, ((gh, gl), (ah, al)), msg, cacross, B)
 
 
 def four_times(x):
@@ -667,18 +671,20 @@
     rows, csol, all_ids = call(
         k_first_rows, (f32(n_y, R, 4 * B), f32(3, R, B), f32(8, B)), recv
     )
-    sg, idx, in1, in2 = call(
-        k_send_first,
-        (FIELD, ((3, ROWS, B), I32), f32(WITHIN, B), f32(WITHIN, B)),
-        all_ids, signs, links.transpose(1, 0, 2), w, v, cc,
-    )
     recv = to_owner(rows, "y")
-    in1 = swap(in1, "sub", n_sub, True)
-    in2 = swap(in2, "sub", n_sub, False)
     (rows,) = call(k_pass, (f32(n_z, R, 6 * B),), recv)
     recv_z = to_owner(rows, "z")
-    out = call(k_send_across, (f32(PACK, B), f32(PACK, B)), recv, w, v, idx)
+    sg, idx, in2, *out = call(
+        k_send_static,
+        (
+            FIELD, ((3, ROWS, B), I32), f32(WITHIN, B), f32(PACK, B), f32(PACK, B),
+        ),
+        recv, signs, links.transpose(1, 0, 2), w, v, cc,
+    )
     across = exchange_across(*out, n_cl)
+    in2 = swap(in2, "sub", n_sub, False)
+    (in1,) = call(k_send_chip, (f32(WITHIN, B),), recv_z, w, v, cc, idx)
+    in1 = swap(in1, "sub", n_sub, True)
     to_all, scal0, cacross, gh, gl, ah, al = call(
         k_first_global, (*answer, picked, picked, picked, picked), recv_z, all_ids, gc
     )
@@ -701,9 +707,9 @@
         to_owner(msg, "sub"), signed, across, curv, v,
     )
     (rows,) = call(k_pass, (f32(n_z, R, 4 * B),), to_owner(rows, "y"))
-    to_all, _, cacross = call(
+    to_all, cacross = call(
         k_global,
-        (f32(NSUB, R, 2 * B), f32(ROWS, B), f32(R, B)),
+        (f32(NSUB, R, 2 * B), f32(R, B)),
         to_owner(rows, "z"), gh, gl, ah, al,
     )
     r, x, d1, signed, line, *out = call(

time: 163 us -> 168 us (1.031)
  waiting for transfers between devices: 8.77 us -> 17.9 us
  starting transfers between devices: 56 us -> 52.2 us
    all_to_all x3, waiting for transfers between devices: 3.88 us -> 12.8 us  [to_owner(): return lax.all_to_all(x, axis, 0, 0, tiled=True)]
    ppermute x10, starting transfers between devices: 36.1 us -> 31.5 us  [swap(): lax.ppermute(x, axis, [p for i in low for p in ((i, i + 1), (i + 1, i))])]
  transfers between devices with their start and end apart: 13 -> 13, of which waited for: 3 -> 4; matrix products, arithmetic and copies ran while one was open for 0% -> 0% of each run, Pallas kernels for 2% -> 2%
where the time goes in v10:
time: 168 us; the launch traced here: 167 us
  blocking collectives  81.7 us (49%)
  starting transfers between devices  52.2 us (31%)
  waiting for transfers between devices  17.9 us (11%)
  Pallas kernels  9.83 us (6%)
  local copies, waits for them, and re-layouts  3.66 us (2%)
    all_to_all x7, blocking collectives, to_owner(): return lax.all_to_all(x, axis, 0, 0, tiled=True)  81.7 us
    ppermute x10, starting transfers between devices, swap(): lax.ppermute(x, axis, [p for i in low for p in ((i, i + 1), (i + 1, i))])  31.5 us
    all_to_all x3, starting transfers between devices, to_owner(): return lax.all_to_all(x, axis, 0, 0, tiled=True)  20.7 us
    all_to_all x3, waiting for transfers between devices, to_owner(): return lax.all_to_all(x, axis, 0, 0, tiled=True)  12.8 us
    pallas_call x14, Pallas kernels, call(): pl.pallas_call(body, out_shape=out_shape, in_specs=specs, out_specs=tuple...  9.83 us
    ppermute x10, waiting for transfers between devices, swap(): lax.ppermute(x, axis, [p for i in low for p in ((i, i + 1), (i + 1, i))])  5.12 us
    unnamed x18, local copies, waits for them, and re-layouts  3.66 us
  transfers between devices with their start and end apart: 13, of which 4 were waited for; matrix products, arithmetic and copies ran while one was open for 0% of the time, Pallas kernels for 2%

profile of v10, /device:TPU:10, one launch (start us, length us, event | category | flops | bytes accessed | tf_op | source)
XLA Modules:
  0.0 167.2 jit_solution(8611697782377192806)
XLA Ops:
  0.6 0.0 copy-start.2
  0.7 1.0 pad_maximum_fusion.w
  1.7 0.0 copy-start.1
  1.7 1.0 copy-done.1
  2.6 0.7 copy-done.4
  3.4 0.7 copy-done.5
  4.0 1.1 shard_map.104
  5.1 8.9 %all_to_all.50.recv = f32[8,4,640]{2,1,0:T(4,128)S(1)} all-to-all(f32[8,4,640]{2,1,0:T(4,128)S(1)} %get-tuple-element.45), channel_id=1, replica_groups=mesh['y'=8,'z'=12,'sub'=8] {'sub'}, dimensions={0} | all-to-all | bytes 163840 | tf_op jit(solution)/shard_map/all_to_all | solution.py:627
  14.0 0.1 shard_map.105
  14.1 17.0 %all_to_all.51.recv.after = f32[8,4,512]{2,1,0:T(4,128)S(1)} all-to-all(f32[8,4,512]{2,1,0:T(4,128)S(1)} %get-tuple-element.46), channel_id=1, replica_groups=mesh['y'=8,'z'=12,'sub'=8] {'y'}, dimensions={0} | all-to-all | bytes 131072 | tf_op jit(solution)/shard_map/all_to_all | solution.py:627
  31.1 0.7 shard_map.106
  31.8 12.4 %all-to-all-start.2 = ((f32[12,4,768]{2,1,0:T(4,128)}), f32[12,4,768]{2,1,0:T(4,128)S(1)}, u32[]{:S(2)}, u32[]{:S(2)}) async-start(f32[12,4,768]{2,1,0:T(4,128)} %shard_map.106), calls=%async_computation.2 | async-start | bytes 294912 | tf_op jit(solution)/shard_map/all_to_all | solution.py:627
  44.2 1.1 shard_map.108
  45.3 1.9 %collective-permute-start.1 = (f32[720,128]{1,0:T(8,128)}, f32[720,128]{1,0:T(8,128)S(1)}, u32[]{:S(2)}, u32[]{:S(2)}) collective-permute-start(f32[720,128]{1,0:T(8,128)} %get-tuple-element.53), channel_id=1, source_target_pairs={{1,2},{2,1},{3,4},{4,3},{5,6},{6,5},{9,10},{10,9},{11,12},{12,11},... | collective-permute-start | bytes 1105928 | tf_op jit(solution)/shard_map/ppermute | solution.py:642
  47.2 8.9 %all-to-all-done.2.recv.after = f32[12,4,768]{2,1,0:T(4,128)S(1)} async-done(((f32[12,4,768]{2,1,0:T(4,128)}), f32[12,4,768]{2,1,0:T(4,128)S(1)}, u32[]{:S(2)}, u32[]{:S(2)}) %all-to-all-start.2) | async-done | bytes 147488 | tf_op jit(solution)/shard_map/all_to_all | solution.py:627
  56.1 0.1 shard_map.109
  56.2 2.1 %collective-permute-start = (f32[720,128]{1,0:T(8,128)S(1)}, f32[720,128]{1,0:T(8,128)S(1)}, u32[]{:S(2)}, u32[]{:S(2)}) collective-permute-start(f32[720,128]{1,0:T(8,128)S(1)} %shard_map.109), channel_id=1, source_target_pairs={{0,1},{1,0},{2,3},{3,2},{4,5},{5,4},{6,7},{7,6},{8,9},{9,8},{10,11... | collective-permute-start | bytes 1105928 | tf_op jit(solution)/shard_map/ppermute | solution.py:642
  58.2 3.0 %collective-permute-start.2 = (f32[72,128]{1,0:T(8,128)}, f32[72,128]{1,0:T(8,128)}, u32[]{:S(2)}, u32[]{:S(2)}) collective-permute-start(f32[72,128]{1,0:T(8,128)} %get-tuple-element.54), channel_id=1, source_target_pairs={{0,8},{8,0},{16,24},{24,16},{32,40},{40,32},{48,56},{56,48},{64,72... | collective-permute-start | bytes 110600 | tf_op jit(solution)/shard_map/ppermute | solution.py:642
  61.2 3.4 %collective-permute-start.3 = (f32[72,128]{1,0:T(8,128)}, f32[72,128]{1,0:T(8,128)}, u32[]{:S(2)}, u32[]{:S(2)}) collective-permute-start(f32[72,128]{1,0:T(8,128)} %get-tuple-element.55), channel_id=1, source_target_pairs={{8,16},{16,8},{24,32},{32,24},{40,48},{48,40},{56,64},{64,56},{72,... | collective-permute-start | bytes 110600 | tf_op jit(solution)/shard_map/ppermute | solution.py:642
  64.6 0.0 copy-start.3
  64.6 1.3 copy-done.3
  65.9 1.6 shard_map.107
  67.5 4.8 %all-to-all-start.3 = ((f32[8,4,128]{2,1,0:T(4,128)}), f32[8,4,128]{2,1,0:T(4,128)S(1)}, u32[]{:S(2)}, u32[]{:S(2)}) async-start(f32[8,4,128]{2,1,0:T(4,128)} %get-tuple-element.48), calls=%async_computation.3 | async-start | bytes 32768 | tf_op jit(solution)/shard_map/all_to_all | solution.py:627
  72.3 0.0 collective-permute-done.2.out1
  72.3 0.0 collective-permute-done.3.out2
  72.4 3.9 %all-to-all-done.3.recv = f32[8,4,128]{2,1,0:T(4,128)S(1)} async-done(((f32[8,4,128]{2,1,0:T(4,128)}), f32[8,4,128]{2,1,0:T(4,128)S(1)}, u32[]{:S(2)}, u32[]{:S(2)}) %all-to-all-start.3) | async-done | bytes 16416 | tf_op jit(solution)/shard_map/all_to_all | solution.py:627
  76.3 0.0 collective-permute-done.in1.static1
  76.3 1.5 shard_map.110
  77.8 1.9 %collective-permute-start.4 = (f32[8,128]{1,0:T(8,128)S(1)}, f32[8,128]{1,0:T(8,128)S(1)}, u32[]{:S(2)}, u32[]{:S(2)}) collective-permute-start(f32[8,128]{1,0:T(8,128)S(1)} %get-tuple-element.60), channel_id=1, source_target_pairs={{0,8},{8,0},{16,24},{24,16},{32,40},{40,32},{48,56},{56,48},{64,72... | collective-permute-start | bytes 12296 | tf_op jit(solution)/shard_map/ppermute | solution.py:642
  79.7 4.6 %collective-permute-start.5 = (f32[8,128]{1,0:T(8,128)S(1)}, f32[8,128]{1,0:T(8,128)S(1)}, u32[]{:S(2)}, u32[]{:S(2)}) collective-permute-start(f32[8,128]{1,0:T(8,128)S(1)} %get-tuple-element.61), channel_id=1, source_target_pairs={{8,16},{16,8},{24,32},{32,24},{40,48},{48,40},{56,64},{64,56},{72,... | collective-permute-start | bytes 12296 | tf_op jit(solution)/shard_map/ppermute | solution.py:642
  84.3 3.0 %collective-permute-done.5.out2 = f32[8,128]{1,0:T(8,128)S(1)} collective-permute-done((f32[8,128]{1,0:T(8,128)S(1)}, f32[8,128]{1,0:T(8,128)S(1)}, u32[]{:S(2)}, u32[]{:S(2)}) %collective-permute-start.5) | collective-permute-done | bytes 4128 | tf_op jit(solution)/shard_map/ppermute | solution.py:642
  87.3 1.2 shard_map.111
  88.5 8.7 %all_to_all.52.recv = f32[8,4,1152]{2,1,0:T(4,128)S(1)} all-to-all(f32[8,4,1152]{2,1,0:T(4,128)S(1)} %get-tuple-element.63), channel_id=1, replica_groups=mesh['y'=8,'z'=12,'sub'=8] {'sub'}, dimensions={0} | all-to-all | bytes 294912 | tf_op jit(solution)/shard_map/all_to_all | solution.py:627
  97.2 0.2 shard_map.112
  97.3 12.1 %all_to_all.53.recv = f32[8,4,384]{2,1,0:T(4,128)S(1)} all-to-all(f32[8,4,384]{2,1,0:T(4,128)S(1)} %get-tuple-element.66), channel_id=1, replica_groups=mesh['y'=8,'z'=12,'sub'=8] {'y'}, dimensions={0} | all-to-all | bytes 98304 | tf_op jit(solution)/shard_map/all_to_all | solution.py:627
  109.5 13.8 %all_to_all.54.recv = f32[12,4,512]{2,1,0:T(4,128)S(1)} all-to-all(f32[12,4,512]{2,1,0:T(4,128)S(1)} %shard_map.113), channel_id=1, replica_groups=mesh['y'=8,'z'=12,'sub'=8] {'z'}, dimensions={0} | all-to-all | bytes 196608 | tf_op jit(solution)/shard_map/all_to_all | solution.py:627
  123.3 0.2 shard_map.114
  123.5 7.8 %all_to_all.55.recv = f32[8,4,256]{2,1,0:T(4,128)S(1)} all-to-all(f32[8,4,256]{2,1,0:T(4,128)S(1)} %get-tuple-element.71), channel_id=1, replica_groups=mesh['y'=8,'z'=12,'sub'=8] {'sub'}, dimensions={0} | all-to-all | bytes 65536 | tf_op jit(solution)/shard_map/all_to_all | solution.py:627
  131.3 0.7 shard_map.115
  132.0 13.5 %all_to_all.56.recv = f32[64,1,128]{2,1,0:T(1,128)S(1)} all-to-all(f32[64,1,128]{2,1,0:T(1,128)S(1)} %get-tuple-element.79), channel_id=1, replica_groups=mesh['y'=8,'z'=12,'sub'=8] {'y','sub'}, dimensions={0} | all-to-all | bytes 65536 | tf_op jit(solution)/shard_map/all_to_all | solution.py:627
  145.5 0.7 shard_map.116
  146.2 3.5 %all-to-all-start.9 = ((f32[12,1,128]{2,1,0:T(1,128)}), f32[12,1,128]{2,1,0:T(1,128)S(1)}, u32[]{:S(2)}, u32[]{:S(2)}) async-start(f32[12,1,128]{2,1,0:T(1,128)} %shard_map.116), calls=%async_computation.9 | async-start | bytes 12288 | tf_op jit(solution)/shard_map/all_to_all | solution.py:627
  149.7 1.9 %collective-permute-start.6 = (f32[16,128]{1,0:T(8,128)S(1)}, f32[16,128]{1,0:T(8,128)S(1)}, u32[]{:S(2)}, u32[]{:S(2)}) collective-permute-start(f32[16,128]{1,0:T(8,128)S(1)} %get-tuple-element.81), channel_id=1, source_target_pairs={{0,1},{1,0},{2,3},{3,2},{4,5},{5,4},{6,7},{7,6},{8,9},{9,8},{10,11... | collective-permute-start | bytes 24584 | tf_op jit(solution)/shard_map/ppermute | solution.py:642
  151.6 3.5 %collective-permute-start.7 = (f32[16,128]{1,0:T(8,128)S(1)}, f32[16,128]{1,0:T(8,128)S(1)}, u32[]{:S(2)}, u32[]{:S(2)}) collective-permute-start(f32[16,128]{1,0:T(8,128)S(1)} %get-tuple-element.82), channel_id=1, source_target_pairs={{1,2},{2,1},{3,4},{4,3},{5,6},{6,5},{9,10},{10,9},{11,12},{12,11},... | collective-permute-start | bytes 24584 | tf_op jit(solution)/shard_map/ppermute | solution.py:642
  155.0 3.8 %collective-permute-start.8 = (f32[8,128]{1,0:T(8,128)S(1)}, f32[8,128]{1,0:T(8,128)S(1)}, u32[]{:S(2)}, u32[]{:S(2)}) collective-permute-start(f32[8,128]{1,0:T(8,128)S(1)} %get-tuple-element.83), channel_id=1, source_target_pairs={{0,8},{8,0},{16,24},{24,16},{32,40},{40,32},{48,56},{56,48},{64,72... | collective-permute-start | bytes 12296 | tf_op jit(solution)/shard_map/ppermute | solution.py:642
  158.8 5.5 %collective-permute-start.9 = (f32[8,128]{1,0:T(8,128)S(1)}, f32[8,128]{1,0:T(8,128)S(1)}, u32[]{:S(2)}, u32[]{:S(2)}) collective-permute-start(f32[8,128]{1,0:T(8,128)S(1)} %get-tuple-element.84), channel_id=1, source_target_pairs={{8,16},{16,8},{24,32},{32,24},{40,48},{48,40},{56,64},{64,56},{72,... | collective-permute-start | bytes 12296 | tf_op jit(solution)/shard_map/ppermute | solution.py:642
  164.3 2.1 %collective-permute-done.9.out2 = f32[8,128]{1,0:T(8,128)S(1)} collective-permute-done((f32[8,128]{1,0:T(8,128)S(1)}, f32[8,128]{1,0:T(8,128)S(1)}, u32[]{:S(2)}, u32[]{:S(2)}) %collective-permute-start.9) | collective-permute-done | bytes 4128 | tf_op jit(solution)/shard_map/ppermute | solution.py:642
  166.4 0.7 shard_map.117
  (18 shorter events, 0.1 us)
Async XLA Ops:
  0.6 43.5 %copy-start.2 = (f32[1,96,768]{2,1,0:T(8,128)S(1)}, f32[1,96,768]{2,1,0:T(8,128)}, u32[]{:S(2)}) copy-start(f32[1,96,768]{2,1,0:T(8,128)} %param.16) | copy-start | bytes 884740
  0.6 43.5 %copy-start.8 = (s32[4,3,128]{2,0,1:T(4,128)S(1)}, s32[4,3,128]{2,0,1:T(4,128)}, u32[]{:S(2)}) copy-start(s32[4,3,128]{2,0,1:T(4,128)} %param.12) | copy-start | bytes 18436
  0.7 43.5 %copy-start.7 = (s32[4,384]{1,0:T(4,128)S(1)}, s32[4,384]{1,0:T(4,128)}, u32[]{:S(2)}) copy-start(s32[4,384]{1,0:T(4,128)} %signs.1) | copy-start | bytes 18436
  1.7 1.0 copy-start.1
  2.6 0.7 copy-start.4
  3.4 0.7 copy-start.5
  31.8 24.3 %all-to-all-start.2 = ((f32[12,4,768]{2,1,0:T(4,128)}), f32[12,4,768]{2,1,0:T(4,128)S(1)}, u32[]{:S(2)}, u32[]{:S(2)}) async-start(f32[12,4,768]{2,1,0:T(4,128)} %shard_map.106), calls=%async_computation.2 | async-start | bytes 294912 | tf_op jit(solution)/shard_map/all_to_all | solution.py:627
  45.3 27.1 %collective-permute-start.1 = (f32[720,128]{1,0:T(8,128)}, f32[720,128]{1,0:T(8,128)S(1)}, u32[]{:S(2)}, u32[]{:S(2)}) collective-permute-start(f32[720,128]{1,0:T(8,128)} %get-tuple-element.53), channel_id=1, source_target_pairs={{1,2},{2,1},{3,4},{4,3},{5,6},{6,5},{9,10},{10,9},{11,12},{12,11},... | collective-permute-start | bytes 1105928 | tf_op jit(solution)/shard_map/ppermute | solution.py:642
  56.1 20.2 %copy-start = (bf16[4,384,384]{2,1,0:T(8,128)(2,1)S(1)}, bf16[4,384,384]{2,1,0:T(8,128)(2,1)}, u32[]{:S(2)}) copy-start(bf16[4,384,384]{2,1,0:T(8,128)(2,1)} %ops.3) | copy-start | bytes 3538948
  56.2 20.1 %collective-permute-start = (f32[720,128]{1,0:T(8,128)S(1)}, f32[720,128]{1,0:T(8,128)S(1)}, u32[]{:S(2)}, u32[]{:S(2)}) collective-permute-start(f32[720,128]{1,0:T(8,128)S(1)} %shard_map.109), channel_id=1, source_target_pairs={{0,1},{1,0},{2,3},{3,2},{4,5},{5,4},{6,7},{7,6},{8,9},{9,8},{10,11... | collective-permute-start | bytes 1105928 | tf_op jit(solution)/shard_map/ppermute | solution.py:642
  58.2 14.1 %collective-permute-start.2 = (f32[72,128]{1,0:T(8,128)}, f32[72,128]{1,0:T(8,128)}, u32[]{:S(2)}, u32[]{:S(2)}) collective-permute-start(f32[72,128]{1,0:T(8,128)} %get-tuple-element.54), channel_id=1, source_target_pairs={{0,8},{8,0},{16,24},{24,16},{32,40},{40,32},{48,56},{56,48},{64,72... | collective-permute-start | bytes 110600 | tf_op jit(solution)/shard_map/ppermute | solution.py:642
  61.2 11.1 %collective-permute-start.3 = (f32[72,128]{1,0:T(8,128)}, f32[72,128]{1,0:T(8,128)}, u32[]{:S(2)}, u32[]{:S(2)}) collective-permute-start(f32[72,128]{1,0:T(8,128)} %get-tuple-element.55), channel_id=1, source_target_pairs={{8,16},{16,8},{24,32},{32,24},{40,48},{48,40},{56,64},{64,56},{72,... | collective-permute-start | bytes 110600 | tf_op jit(solution)/shard_map/ppermute | solution.py:642
  64.6 1.3 copy-start.3
  67.5 19.8 %copy-start.6 = (s32[4,8]{1,0:T(4,128)S(1)}, s32[4,8]{1,0:T(4,128)}, u32[]{:S(2)}) copy-start(s32[4,8]{1,0:T(4,128)} %ids.3) | copy-start | bytes 388
  67.5 8.8 %all-to-all-start.3 = ((f32[8,4,128]{2,1,0:T(4,128)}), f32[8,4,128]{2,1,0:T(4,128)S(1)}, u32[]{:S(2)}, u32[]{:S(2)}) async-start(f32[8,4,128]{2,1,0:T(4,128)} %get-tuple-element.48), calls=%async_computation.3 | async-start | bytes 32768 | tf_op jit(solution)/shard_map/all_to_all | solution.py:627
  77.8 6.5 %collective-permute-start.4 = (f32[8,128]{1,0:T(8,128)S(1)}, f32[8,128]{1,0:T(8,128)S(1)}, u32[]{:S(2)}, u32[]{:S(2)}) collective-permute-start(f32[8,128]{1,0:T(8,128)S(1)} %get-tuple-element.60), channel_id=1, source_target_pairs={{0,8},{8,0},{16,24},{24,16},{32,40},{40,32},{48,56},{56,48},{64,72... | collective-permute-start | bytes 12296 | tf_op jit(solution)/shard_map/ppermute | solution.py:642
  79.7 7.6 %collective-permute-start.5 = (f32[8,128]{1,0:T(8,128)S(1)}, f32[8,128]{1,0:T(8,128)S(1)}, u32[]{:S(2)}, u32[]{:S(2)}) collective-permute-start(f32[8,128]{1,0:T(8,128)S(1)} %get-tuple-element.61), channel_id=1, source_target_pairs={{8,16},{16,8},{24,32},{32,24},{40,48},{48,40},{56,64},{64,56},{72,... | collective-permute-start | bytes 12296 | tf_op jit(solution)/shard_map/ppermute | solution.py:642
  146.2 20.3 %all-to-all-start.9 = ((f32[12,1,128]{2,1,0:T(1,128)}), f32[12,1,128]{2,1,0:T(1,128)S(1)}, u32[]{:S(2)}, u32[]{:S(2)}) async-start(f32[12,1,128]{2,1,0:T(1,128)} %shard_map.116), calls=%async_computation.9 | async-start | bytes 12288 | tf_op jit(solution)/shard_map/all_to_all | solution.py:627
  149.7 16.8 %collective-permute-start.6 = (f32[16,128]{1,0:T(8,128)S(1)}, f32[16,128]{1,0:T(8,128)S(1)}, u32[]{:S(2)}, u32[]{:S(2)}) collective-permute-start(f32[16,128]{1,0:T(8,128)S(1)} %get-tuple-element.81), channel_id=1, source_target_pairs={{0,1},{1,0},{2,3},{3,2},{4,5},{5,4},{6,7},{7,6},{8,9},{9,8},{10,11... | collective-permute-start | bytes 24584 | tf_op jit(solution)/shard_map/ppermute | solution.py:642
  151.6 14.9 %collective-permute-start.7 = (f32[16,128]{1,0:T(8,128)S(1)}, f32[16,128]{1,0:T(8,128)S(1)}, u32[]{:S(2)}, u32[]{:S(2)}) collective-permute-start(f32[16,128]{1,0:T(8,128)S(1)} %get-tuple-element.82), channel_id=1, source_target_pairs={{1,2},{2,1},{3,4},{4,3},{5,6},{6,5},{9,10},{10,9},{11,12},{12,11},... | collective-permute-start | bytes 24584 | tf_op jit(solution)/shard_map/ppermute | solution.py:642
  155.0 9.3 %collective-permute-start.8 = (f32[8,128]{1,0:T(8,128)S(1)}, f32[8,128]{1,0:T(8,128)S(1)}, u32[]{:S(2)}, u32[]{:S(2)}) collective-permute-start(f32[8,128]{1,0:T(8,128)S(1)} %get-tuple-element.83), channel_id=1, source_target_pairs={{0,8},{8,0},{16,24},{24,16},{32,40},{40,32},{48,56},{56,48},{64,72... | collective-permute-start | bytes 12296 | tf_op jit(solution)/shard_map/ppermute | solution.py:642
  158.8 7.6 %collective-permute-start.9 = (f32[8,128]{1,0:T(8,128)S(1)}, f32[8,128]{1,0:T(8,128)S(1)}, u32[]{:S(2)}, u32[]{:S(2)}) collective-permute-start(f32[8,128]{1,0:T(8,128)S(1)} %get-tuple-element.84), channel_id=1, source_target_pairs={{8,16},{16,8},{24,32},{32,24},{40,48},{48,40},{56,64},{64,56},{72,... | collective-permute-start | bytes 12296 | tf_op jit(solution)/shard_map/ppermute | solution.py:642

commit v11 on v10

--- a/solution.py
+++ b/solution.py
@@ -207,15 +207,14 @@
     return jnp.concatenate([x[STATIC + NCL * j : STATIC + NCL * j + NCL, :] for j in range(6)], axis=1)
 
 
-def k_send_static(after, signs, links, w, v, cc, sg_out, idx_out, within, out1, out2):
+def k_send_static(
+    after, signs, links, w, v, cc, sg_out, idx_out, first, second, out1, out2
+):
     k_tables(after, signs, links, sg_out, idx_out)
-    send_within(w, v, cc, idx_out, within, 1 - lax.axis_index("sub") % 2)
+    odd = lax.axis_index("sub") % 2
+    send_within(w, v, cc, idx_out, first, odd)
+    send_within(w, v, cc, idx_out, second, 1 - odd)
     send_across(w, v, idx_out, out1, out2)
-
-
-def k_send_chip(after, w, v, cc, idx, within):
-    del after
-    send_within(w, v, cc, idx, within, lax.axis_index("sub") % 2)
 
 
 def send_across(w, v, idx, first, second):
@@ -674,16 +673,16 @@
     recv = to_owner(rows, "y")
     (rows,) = call(k_pass, (f32(n_z, R, 6 * B),), recv)
     recv_z = to_owner(rows, "z")
-    sg, idx, in2, *out = call(
+    sg, idx, in1, in2, *out = call(
         k_send_static,
         (
-            FIELD, ((3, ROWS, B), I32), f32(WITHIN, B), f32(PACK, B), f32(PACK, B),
+            FIELD, ((3, ROWS, B), I32), f32(WITHIN, B), f32(WITHIN, B),
+            f32(PACK, B), f32(PACK, B),
         ),
         recv, signs, links.transpose(1, 0, 2), w, v, cc,
     )
     across = exchange_across(*out, n_cl)
     in2 = swap(in2, "sub", n_sub, False)
-    (in1,) = call(k_send_chip, (f32(WITHIN, B),), recv_z, w, v, cc, idx)
     in1 = swap(in1, "sub", n_sub, True)
     to_all, scal0, cacross, gh, gl, ah, al = call(
         k_first_global, (*answer, picked, picked, picked, picked), recv_z, all_ids, gc

time: 168 us -> 163 us (0.970)
  waiting for transfers between devices: 17.9 us -> 8.76 us
  starting transfers between devices: 52.2 us -> 56.2 us
    all_to_all x3, waiting for transfers between devices: 12.8 us -> 3.88 us  [to_owner(): return lax.all_to_all(x, axis, 0, 0, tiled=True)]
    ppermute x10, starting transfers between devices: 31.5 us -> 36.1 us  [swap(): lax.ppermute(x, axis, [p for i in low for p in ((i, i + 1), (i + 1, i))])]
    pallas_call x14 -> x13, Pallas kernels: 9.83 us -> 9.08 us  [call(): pl.pallas_call(body, out_shape=out_shape, in_specs=specs, out_specs=tuple...]
  transfers between devices with their start and end apart: 13 -> 13, of which waited for: 4 -> 3; matrix products, arithmetic and copies ran while one was open for 0% -> 0% of each run, Pallas kernels for 2% -> 2%
where the time goes in v11:
time: 163 us; the launch traced here: 162 us
  blocking collectives  82.4 us (51%)
  starting transfers between devices  56.2 us (34%)
  Pallas kernels  9.08 us (6%)
  waiting for transfers between devices  8.76 us (5%)
  local copies, waits for them, and re-layouts  3.66 us (2%)
    all_to_all x7, blocking collectives, to_owner(): return lax.all_to_all(x, axis, 0, 0, tiled=True)  82.4 us
    ppermute x10, starting transfers between devices, swap(): lax.ppermute(x, axis, [p for i in low for p in ((i, i + 1), (i + 1, i))])  36.1 us
    all_to_all x3, starting transfers between devices, to_owner(): return lax.all_to_all(x, axis, 0, 0, tiled=True)  20 us
    pallas_call x13, Pallas kernels, call(): pl.pallas_call(body, out_shape=out_shape, in_specs=specs, out_specs=tuple...  9.08 us
    ppermute x10, waiting for transfers between devices, swap(): lax.ppermute(x, axis, [p for i in low for p in ((i, i + 1), (i + 1, i))])  4.88 us
    all_to_all x3, waiting for transfers between devices, to_owner(): return lax.all_to_all(x, axis, 0, 0, tiled=True)  3.88 us
    unnamed x18, local copies, waits for them, and re-layouts  3.66 us
  transfers between devices with their start and end apart: 13, of which 3 were waited for; matrix products, arithmetic and copies ran while one was open for 0% of the time, Pallas kernels for 2%

profile of v11, /device:TPU:10, one launch (start us, length us, event | category | flops | bytes accessed | tf_op | source)
XLA Modules:
  0.0 161.9 jit_solution(2852409842709978304)
XLA Ops:
  0.6 0.0 copy-start.2
  0.7 1.0 pad_maximum_fusion.w
  1.7 0.0 copy-start.1
  1.7 1.0 copy-done.1
  2.6 0.7 copy-done.4
  3.4 0.7 copy-done.5
  4.0 1.1 shard_map.104
  5.1 8.9 %all_to_all.50.recv = f32[8,4,640]{2,1,0:T(4,128)S(1)} all-to-all(f32[8,4,640]{2,1,0:T(4,128)S(1)} %get-tuple-element.46), channel_id=1, replica_groups=mesh['y'=8,'z'=12,'sub'=8] {'sub'}, dimensions={0} | all-to-all | bytes 163840 | tf_op jit(solution)/shard_map/all_to_all | solution.py:626
  14.0 0.1 shard_map.105
  14.1 17.0 %all_to_all.51.recv.after = f32[8,4,512]{2,1,0:T(4,128)S(1)} all-to-all(f32[8,4,512]{2,1,0:T(4,128)S(1)} %get-tuple-element.47), channel_id=1, replica_groups=mesh['y'=8,'z'=12,'sub'=8] {'y'}, dimensions={0} | all-to-all | bytes 131072 | tf_op jit(solution)/shard_map/all_to_all | solution.py:626
  31.1 0.7 shard_map.106
  31.8 12.5 %all-to-all-start.2 = ((f32[12,4,768]{2,1,0:T(4,128)}), f32[12,4,768]{2,1,0:T(4,128)S(1)}, u32[]{:S(2)}, u32[]{:S(2)}) async-start(f32[12,4,768]{2,1,0:T(4,128)} %shard_map.106), calls=%async_computation.2 | async-start | bytes 294912 | tf_op jit(solution)/shard_map/all_to_all | solution.py:626
  44.3 1.2 shard_map.108
  45.5 1.9 %collective-permute-start = (f32[720,128]{1,0:T(8,128)}, f32[720,128]{1,0:T(8,128)S(1)}, u32[]{:S(2)}, u32[]{:S(2)}) collective-permute-start(f32[720,128]{1,0:T(8,128)} %get-tuple-element.53), channel_id=1, source_target_pairs={{0,1},{1,0},{2,3},{3,2},{4,5},{5,4},{6,7},{7,6},{8,9},{9,8},{10,11... | collective-permute-start | bytes 1105928 | tf_op jit(solution)/shard_map/ppermute | solution.py:641
  47.5 3.5 %collective-permute-start.1 = (f32[720,128]{1,0:T(8,128)}, f32[720,128]{1,0:T(8,128)S(1)}, u32[]{:S(2)}, u32[]{:S(2)}) collective-permute-start(f32[720,128]{1,0:T(8,128)} %get-tuple-element.54), channel_id=1, source_target_pairs={{1,2},{2,1},{3,4},{4,3},{5,6},{6,5},{9,10},{10,9},{11,12},{12,11},... | collective-permute-start | bytes 1105928 | tf_op jit(solution)/shard_map/ppermute | solution.py:641
  50.9 3.9 %collective-permute-start.2 = (f32[72,128]{1,0:T(8,128)S(1)}, f32[72,128]{1,0:T(8,128)S(1)}, u32[]{:S(2)}, u32[]{:S(2)}) collective-permute-start(f32[72,128]{1,0:T(8,128)S(1)} %get-tuple-element.55), channel_id=1, source_target_pairs={{0,8},{8,0},{16,24},{24,16},{32,40},{40,32},{48,56},{56,48},{64,72... | collective-permute-start | bytes 110600 | tf_op jit(solution)/shard_map/ppermute | solution.py:641
  54.8 5.5 %collective-permute-start.3 = (f32[72,128]{1,0:T(8,128)S(1)}, f32[72,128]{1,0:T(8,128)S(1)}, u32[]{:S(2)}, u32[]{:S(2)}) collective-permute-start(f32[72,128]{1,0:T(8,128)S(1)} %get-tuple-element.56), channel_id=1, source_target_pairs={{8,16},{16,8},{24,32},{32,24},{40,48},{48,40},{56,64},{64,56},{72,... | collective-permute-start | bytes 110600 | tf_op jit(solution)/shard_map/ppermute | solution.py:641
  60.3 0.0 all-to-all-done.2.recv
  60.3 0.0 copy-start.3
  60.3 1.3 copy-done.3
  61.6 1.6 shard_map.107
  63.2 4.0 %all-to-all-start.3 = ((f32[8,4,128]{2,1,0:T(4,128)}), f32[8,4,128]{2,1,0:T(4,128)S(1)}, u32[]{:S(2)}, u32[]{:S(2)}) async-start(f32[8,4,128]{2,1,0:T(4,128)} %get-tuple-element.49), calls=%async_computation.3 | async-start | bytes 32768 | tf_op jit(solution)/shard_map/all_to_all | solution.py:626
  67.3 0.0 collective-permute-done.3.out2
  67.3 0.0 collective-permute-done.1.in2.static2
  67.3 3.9 %all-to-all-done.3.recv = f32[8,4,128]{2,1,0:T(4,128)S(1)} async-done(((f32[8,4,128]{2,1,0:T(4,128)}), f32[8,4,128]{2,1,0:T(4,128)S(1)}, u32[]{:S(2)}, u32[]{:S(2)}) %all-to-all-start.3) | async-done | bytes 16416 | tf_op jit(solution)/shard_map/all_to_all | solution.py:626
  71.2 0.8 shard_map.109
  71.9 1.9 %collective-permute-start.4 = (f32[8,128]{1,0:T(8,128)S(1)}, f32[8,128]{1,0:T(8,128)S(1)}, u32[]{:S(2)}, u32[]{:S(2)}) collective-permute-start(f32[8,128]{1,0:T(8,128)S(1)} %get-tuple-element.62), channel_id=1, source_target_pairs={{0,8},{8,0},{16,24},{24,16},{32,40},{40,32},{48,56},{56,48},{64,72... | collective-permute-start | bytes 12296 | tf_op jit(solution)/shard_map/ppermute | solution.py:641
  73.8 4.8 %collective-permute-start.5 = (f32[8,128]{1,0:T(8,128)S(1)}, f32[8,128]{1,0:T(8,128)S(1)}, u32[]{:S(2)}, u32[]{:S(2)}) collective-permute-start(f32[8,128]{1,0:T(8,128)S(1)} %get-tuple-element.63), channel_id=1, source_target_pairs={{8,16},{16,8},{24,32},{32,24},{40,48},{48,40},{56,64},{64,56},{72,... | collective-permute-start | bytes 12296 | tf_op jit(solution)/shard_map/ppermute | solution.py:641
  78.7 0.0 collective-permute-done.4.out1
  78.7 2.8 %collective-permute-done.5.out2 = f32[8,128]{1,0:T(8,128)S(1)} collective-permute-done((f32[8,128]{1,0:T(8,128)S(1)}, f32[8,128]{1,0:T(8,128)S(1)}, u32[]{:S(2)}, u32[]{:S(2)}) %collective-permute-start.5) | collective-permute-done | bytes 4128 | tf_op jit(solution)/shard_map/ppermute | solution.py:641
  81.4 1.2 shard_map.110
  82.6 8.7 %all_to_all.52.recv = f32[8,4,1152]{2,1,0:T(4,128)S(1)} all-to-all(f32[8,4,1152]{2,1,0:T(4,128)S(1)} %get-tuple-element.65), channel_id=1, replica_groups=mesh['y'=8,'z'=12,'sub'=8] {'sub'}, dimensions={0} | all-to-all | bytes 294912 | tf_op jit(solution)/shard_map/all_to_all | solution.py:626
  91.3 0.2 shard_map.111
  91.5 12.1 %all_to_all.53.recv = f32[8,4,384]{2,1,0:T(4,128)S(1)} all-to-all(f32[8,4,384]{2,1,0:T(4,128)S(1)} %get-tuple-element.68), channel_id=1, replica_groups=mesh['y'=8,'z'=12,'sub'=8] {'y'}, dimensions={0} | all-to-all | bytes 98304 | tf_op jit(solution)/shard_map/all_to_all | solution.py:626
  103.6 14.4 %all_to_all.54.recv = f32[12,4,512]{2,1,0:T(4,128)S(1)} all-to-all(f32[12,4,512]{2,1,0:T(4,128)S(1)} %shard_map.112), channel_id=1, replica_groups=mesh['y'=8,'z'=12,'sub'=8] {'z'}, dimensions={0} | all-to-all | bytes 196608 | tf_op jit(solution)/shard_map/all_to_all | solution.py:626
  118.0 0.2 shard_map.113
  118.2 7.8 %all_to_all.55.recv = f32[8,4,256]{2,1,0:T(4,128)S(1)} all-to-all(f32[8,4,256]{2,1,0:T(4,128)S(1)} %get-tuple-element.73), channel_id=1, replica_groups=mesh['y'=8,'z'=12,'sub'=8] {'sub'}, dimensions={0} | all-to-all | bytes 65536 | tf_op jit(solution)/shard_map/all_to_all | solution.py:626
  126.1 0.7 shard_map.114
  126.8 13.5 %all_to_all.56.recv = f32[64,1,128]{2,1,0:T(1,128)S(1)} all-to-all(f32[64,1,128]{2,1,0:T(1,128)S(1)} %get-tuple-element.81), channel_id=1, replica_groups=mesh['y'=8,'z'=12,'sub'=8] {'y','sub'}, dimensions={0} | all-to-all | bytes 65536 | tf_op jit(solution)/shard_map/all_to_all | solution.py:626
  140.3 0.7 shard_map.115
  140.9 3.5 %all-to-all-start.9 = ((f32[12,1,128]{2,1,0:T(1,128)}), f32[12,1,128]{2,1,0:T(1,128)S(1)}, u32[]{:S(2)}, u32[]{:S(2)}) async-start(f32[12,1,128]{2,1,0:T(1,128)} %shard_map.115), calls=%async_computation.9 | async-start | bytes 12288 | tf_op jit(solution)/shard_map/all_to_all | solution.py:626
  144.4 1.9 %collective-permute-start.6 = (f32[16,128]{1,0:T(8,128)S(1)}, f32[16,128]{1,0:T(8,128)S(1)}, u32[]{:S(2)}, u32[]{:S(2)}) collective-permute-start(f32[16,128]{1,0:T(8,128)S(1)} %get-tuple-element.83), channel_id=1, source_target_pairs={{0,1},{1,0},{2,3},{3,2},{4,5},{5,4},{6,7},{7,6},{8,9},{9,8},{10,11... | collective-permute-start | bytes 24584 | tf_op jit(solution)/shard_map/ppermute | solution.py:641
  146.3 3.5 %collective-permute-start.7 = (f32[16,128]{1,0:T(8,128)S(1)}, f32[16,128]{1,0:T(8,128)S(1)}, u32[]{:S(2)}, u32[]{:S(2)}) collective-permute-start(f32[16,128]{1,0:T(8,128)S(1)} %get-tuple-element.84), channel_id=1, source_target_pairs={{1,2},{2,1},{3,4},{4,3},{5,6},{6,5},{9,10},{10,9},{11,12},{12,11},... | collective-permute-start | bytes 24584 | tf_op jit(solution)/shard_map/ppermute | solution.py:641
  149.8 3.8 %collective-permute-start.8 = (f32[8,128]{1,0:T(8,128)S(1)}, f32[8,128]{1,0:T(8,128)S(1)}, u32[]{:S(2)}, u32[]{:S(2)}) collective-permute-start(f32[8,128]{1,0:T(8,128)S(1)} %get-tuple-element.85), channel_id=1, source_target_pairs={{0,8},{8,0},{16,24},{24,16},{32,40},{40,32},{48,56},{56,48},{64,72... | collective-permute-start | bytes 12296 | tf_op jit(solution)/shard_map/ppermute | solution.py:641
  153.6 5.5 %collective-permute-start.9 = (f32[8,128]{1,0:T(8,128)S(1)}, f32[8,128]{1,0:T(8,128)S(1)}, u32[]{:S(2)}, u32[]{:S(2)}) collective-permute-start(f32[8,128]{1,0:T(8,128)S(1)} %get-tuple-element.86), channel_id=1, source_target_pairs={{8,16},{16,8},{24,32},{32,24},{40,48},{48,40},{56,64},{64,56},{72,... | collective-permute-start | bytes 12296 | tf_op jit(solution)/shard_map/ppermute | solution.py:641
  159.1 2.1 %collective-permute-done.9.out2 = f32[8,128]{1,0:T(8,128)S(1)} collective-permute-done((f32[8,128]{1,0:T(8,128)S(1)}, f32[8,128]{1,0:T(8,128)S(1)}, u32[]{:S(2)}, u32[]{:S(2)}) %collective-permute-start.9) | collective-permute-done | bytes 4128 | tf_op jit(solution)/shard_map/ppermute | solution.py:641
  161.2 0.0 collective-permute-done.6.in1
  161.2 0.7 shard_map.116
  (17 shorter events, 0.1 us)
Async XLA Ops:
  0.6 43.7 %copy-start.2 = (f32[1,96,768]{2,1,0:T(8,128)S(1)}, f32[1,96,768]{2,1,0:T(8,128)}, u32[]{:S(2)}) copy-start(f32[1,96,768]{2,1,0:T(8,128)} %param.16) | copy-start | bytes 884740
  0.6 43.7 %copy-start.8 = (s32[4,3,128]{2,0,1:T(4,128)S(1)}, s32[4,3,128]{2,0,1:T(4,128)}, u32[]{:S(2)}) copy-start(s32[4,3,128]{2,0,1:T(4,128)} %param.12) | copy-start | bytes 18436
  0.7 43.7 %copy-start.7 = (s32[4,384]{1,0:T(4,128)S(1)}, s32[4,384]{1,0:T(4,128)}, u32[]{:S(2)}) copy-start(s32[4,384]{1,0:T(4,128)} %signs.1) | copy-start | bytes 18436
  1.7 1.0 copy-start.1
  2.6 0.7 copy-start.4
  3.4 0.7 copy-start.5
  31.8 39.4 %copy-start = (bf16[4,384,384]{2,1,0:T(8,128)(2,1)S(1)}, bf16[4,384,384]{2,1,0:T(8,128)(2,1)}, u32[]{:S(2)}) copy-start(bf16[4,384,384]{2,1,0:T(8,128)(2,1)} %ops.3) | copy-start | bytes 3538948
  31.8 28.6 %all-to-all-start.2 = ((f32[12,4,768]{2,1,0:T(4,128)}), f32[12,4,768]{2,1,0:T(4,128)S(1)}, u32[]{:S(2)}, u32[]{:S(2)}) async-start(f32[12,4,768]{2,1,0:T(4,128)} %shard_map.106), calls=%async_computation.2 | async-start | bytes 294912 | tf_op jit(solution)/shard_map/all_to_all | solution.py:626
  45.5 21.7 %collective-permute-start = (f32[720,128]{1,0:T(8,128)}, f32[720,128]{1,0:T(8,128)S(1)}, u32[]{:S(2)}, u32[]{:S(2)}) collective-permute-start(f32[720,128]{1,0:T(8,128)} %get-tuple-element.53), channel_id=1, source_target_pairs={{0,1},{1,0},{2,3},{3,2},{4,5},{5,4},{6,7},{7,6},{8,9},{9,8},{10,11... | collective-permute-start | bytes 1105928 | tf_op jit(solution)/shard_map/ppermute | solution.py:641
  47.5 19.8 %collective-permute-start.1 = (f32[720,128]{1,0:T(8,128)}, f32[720,128]{1,0:T(8,128)S(1)}, u32[]{:S(2)}, u32[]{:S(2)}) collective-permute-start(f32[720,128]{1,0:T(8,128)} %get-tuple-element.54), channel_id=1, source_target_pairs={{1,2},{2,1},{3,4},{4,3},{5,6},{6,5},{9,10},{10,9},{11,12},{12,11},... | collective-permute-start | bytes 1105928 | tf_op jit(solution)/shard_map/ppermute | solution.py:641
  50.9 16.3 %collective-permute-start.2 = (f32[72,128]{1,0:T(8,128)S(1)}, f32[72,128]{1,0:T(8,128)S(1)}, u32[]{:S(2)}, u32[]{:S(2)}) collective-permute-start(f32[72,128]{1,0:T(8,128)S(1)} %get-tuple-element.55), channel_id=1, source_target_pairs={{0,8},{8,0},{16,24},{24,16},{32,40},{40,32},{48,56},{56,48},{64,72... | collective-permute-start | bytes 110600 | tf_op jit(solution)/shard_map/ppermute | solution.py:641
  54.8 12.4 %collective-permute-start.3 = (f32[72,128]{1,0:T(8,128)S(1)}, f32[72,128]{1,0:T(8,128)S(1)}, u32[]{:S(2)}, u32[]{:S(2)}) collective-permute-start(f32[72,128]{1,0:T(8,128)S(1)} %get-tuple-element.56), channel_id=1, source_target_pairs={{8,16},{16,8},{24,32},{32,24},{40,48},{48,40},{56,64},{64,56},{72,... | collective-permute-start | bytes 110600 | tf_op jit(solution)/shard_map/ppermute | solution.py:641
  60.3 1.3 copy-start.3
  63.2 18.2 %copy-start.6 = (s32[4,8]{1,0:T(4,128)S(1)}, s32[4,8]{1,0:T(4,128)}, u32[]{:S(2)}) copy-start(s32[4,8]{1,0:T(4,128)} %ids.3) | copy-start | bytes 388
  63.2 7.9 %all-to-all-start.3 = ((f32[8,4,128]{2,1,0:T(4,128)}), f32[8,4,128]{2,1,0:T(4,128)S(1)}, u32[]{:S(2)}, u32[]{:S(2)}) async-start(f32[8,4,128]{2,1,0:T(4,128)} %get-tuple-element.49), calls=%async_computation.3 | async-start | bytes 32768 | tf_op jit(solution)/shard_map/all_to_all | solution.py:626
  71.9 6.7 %collective-permute-start.4 = (f32[8,128]{1,0:T(8,128)S(1)}, f32[8,128]{1,0:T(8,128)S(1)}, u32[]{:S(2)}, u32[]{:S(2)}) collective-permute-start(f32[8,128]{1,0:T(8,128)S(1)} %get-tuple-element.62), channel_id=1, source_target_pairs={{0,8},{8,0},{16,24},{24,16},{32,40},{40,32},{48,56},{56,48},{64,72... | collective-permute-start | bytes 12296 | tf_op jit(solution)/shard_map/ppermute | solution.py:641
  73.8 7.6 %collective-permute-start.5 = (f32[8,128]{1,0:T(8,128)S(1)}, f32[8,128]{1,0:T(8,128)S(1)}, u32[]{:S(2)}, u32[]{:S(2)}) collective-permute-start(f32[8,128]{1,0:T(8,128)S(1)} %get-tuple-element.63), channel_id=1, source_target_pairs={{8,16},{16,8},{24,32},{32,24},{40,48},{48,40},{56,64},{64,56},{72,... | collective-permute-start | bytes 12296 | tf_op jit(solution)/shard_map/ppermute | solution.py:641
  140.9 20.3 %all-to-all-start.9 = ((f32[12,1,128]{2,1,0:T(1,128)}), f32[12,1,128]{2,1,0:T(1,128)S(1)}, u32[]{:S(2)}, u32[]{:S(2)}) async-start(f32[12,1,128]{2,1,0:T(1,128)} %shard_map.115), calls=%async_computation.9 | async-start | bytes 12288 | tf_op jit(solution)/shard_map/all_to_all | solution.py:626
  144.4 16.8 %collective-permute-start.6 = (f32[16,128]{1,0:T(8,128)S(1)}, f32[16,128]{1,0:T(8,128)S(1)}, u32[]{:S(2)}, u32[]{:S(2)}) collective-permute-start(f32[16,128]{1,0:T(8,128)S(1)} %get-tuple-element.83), channel_id=1, source_target_pairs={{0,1},{1,0},{2,3},{3,2},{4,5},{5,4},{6,7},{7,6},{8,9},{9,8},{10,11... | collective-permute-start | bytes 24584 | tf_op jit(solution)/shard_map/ppermute | solution.py:641
  146.3 14.9 %collective-permute-start.7 = (f32[16,128]{1,0:T(8,128)S(1)}, f32[16,128]{1,0:T(8,128)S(1)}, u32[]{:S(2)}, u32[]{:S(2)}) collective-permute-start(f32[16,128]{1,0:T(8,128)S(1)} %get-tuple-element.84), channel_id=1, source_target_pairs={{1,2},{2,1},{3,4},{4,3},{5,6},{6,5},{9,10},{10,9},{11,12},{12,11},... | collective-permute-start | bytes 24584 | tf_op jit(solution)/shard_map/ppermute | solution.py:641
  149.8 9.3 %collective-permute-start.8 = (f32[8,128]{1,0:T(8,128)S(1)}, f32[8,128]{1,0:T(8,128)S(1)}, u32[]{:S(2)}, u32[]{:S(2)}) collective-permute-start(f32[8,128]{1,0:T(8,128)S(1)} %get-tuple-element.85), channel_id=1, source_target_pairs={{0,8},{8,0},{16,24},{24,16},{32,40},{40,32},{48,56},{56,48},{64,72... | collective-permute-start | bytes 12296 | tf_op jit(solution)/shard_map/ppermute | solution.py:641
  153.6 7.6 %collective-permute-start.9 = (f32[8,128]{1,0:T(8,128)S(1)}, f32[8,128]{1,0:T(8,128)S(1)}, u32[]{:S(2)}, u32[]{:S(2)}) collective-permute-start(f32[8,128]{1,0:T(8,128)S(1)} %get-tuple-element.86), channel_id=1, source_target_pairs={{8,16},{16,8},{24,32},{32,24},{40,48},{48,40},{56,64},{64,56},{72,... | collective-permute-start | bytes 12296 | tf_op jit(solution)/shard_map/ppermute | solution.py:641

commit v12 on v9

--- a/solution.py
+++ b/solution.py
@@ -360,7 +360,7 @@
     lo_out[CHUNK : 2 * B, :] = zero
 
 
-def solve(recv, parts, msg, scal, cacross, stride):
+def solve(recv, parts, msg, cacross, stride):
     total = jnp.sum(recv[:, :, 0 : 2 * B], axis=0)
     total = jnp.concatenate([total, total], axis=0)
     second = total[:, B:]
@@ -384,12 +384,12 @@
         msg[k, :, 0:B] = jnp.where(lane < 96, here, picked(1, k, 96))[:R]
         if msg.shape[2] > B:
             msg[k, :, B : 2 * B] = second[:R]
-    scal[...] = jnp.concatenate([second, second], axis=0)
     after, before = neighbours(recv, 2 * B, 2 * B + stride)
     after = pltpu.roll(after, B - KC, 1)
     before = pltpu.roll(before, KC, 1)
     both = jnp.where(lane // KC % 2 == 0, after, before)
     cacross[...] = jnp.where(lane < NCL, both, 0.0)[:R]
+    return second
 
 
 def k_first_global(recv, own, gc, msg, scal, cacross, gh, gl, ah, al):
@@ -400,11 +400,12 @@
     before = pltpu.roll(before, 8, 1)
     ids = jnp.where(lane // 8 % 2 == 0, after, before)
     picked_columns(gc, [ids[0:1], ids[1:2]], ah, al)
-    solve(recv, ((gh, gl), (ah, al)), msg, scal, cacross, 2 * B)
-
-
-def k_global(recv, gh, gl, ah, al, msg, scal, cacross):
-    solve(recv, ((gh, gl), (ah, al)), msg, scal, cacross, B)
+    second = solve(recv, ((gh, gl), (ah, al)), msg, cacross, 2 * B)
+    scal[...] = jnp.concatenate([second, second], axis=0)
+
+
+def k_global(recv, gh, gl, ah, al, msg, cacross):
+    solve(recv, ((gh, gl), (ah, al)), msg, cacross, B)
 
 
 def four_times(x):
@@ -701,9 +702,9 @@
         to_owner(msg, "sub"), signed, across, curv, v,
     )
     (rows,) = call(k_pass, (f32(n_z, R, 4 * B),), to_owner(rows, "y"))
-    to_all, _, cacross = call(
+    to_all, cacross = call(
         k_global,
-        (f32(NSUB, R, 2 * B), f32(ROWS, B), f32(R, B)),
+        (f32(NSUB, R, 2 * B), f32(R, B)),
         to_owner(rows, "z"), gh, gl, ah, al,
     )
     r, x, d1, signed, line, *out = call(

time: 163 us -> 163 us (level)
  no operation moved by 1% of the time
where the time goes in v12:
time: 163 us; the launch traced here: 162 us
  blocking collectives  82.4 us (51%)
  starting transfers between devices  56 us (34%)
  Pallas kernels  9.18 us (6%)
  waiting for transfers between devices  8.77 us (5%)
  local copies, waits for them, and re-layouts  3.67 us (2%)
    all_to_all x7, blocking collectives, to_owner(): return lax.all_to_all(x, axis, 0, 0, tiled=True)  82.4 us
    ppermute x10, starting transfers between devices, swap(): lax.ppermute(x, axis, [p for i in low for p in ((i, i + 1), (i + 1, i))])  36.1 us
    all_to_all x3, starting transfers between devices, to_owner(): return lax.all_to_all(x, axis, 0, 0, tiled=True)  19.9 us
    pallas_call x14, Pallas kernels, call(): pl.pallas_call(body, out_shape=out_shape, in_specs=specs, out_specs=tuple...  9.18 us
    ppermute x10, waiting for transfers between devices, swap(): lax.ppermute(x, axis, [p for i in low for p in ((i, i + 1), (i + 1, i))])  4.89 us
    all_to_all x3, waiting for transfers between devices, to_owner(): return lax.all_to_all(x, axis, 0, 0, tiled=True)  3.88 us
    unnamed x18, local copies, waits for them, and re-layouts  3.67 us
  transfers between devices with their start and end apart: 13, of which 3 were waited for; matrix products, arithmetic and copies ran while one was open for 0% of the time, Pallas kernels for 2%

profile of v12, /device:TPU:10, one launch (start us, length us, event | category | flops | bytes accessed | tf_op | source)
XLA Modules:
  0.0 161.9 jit_solution(1865820269918792417)
XLA Ops:
  0.6 0.0 copy-start.2
  0.7 1.0 pad_maximum_fusion.w
  1.7 0.0 copy-start.1
  1.7 1.0 copy-done.1
  2.6 0.7 copy-done.4
  3.4 0.7 copy-done.5
  4.0 1.1 shard_map.104
  5.1 8.9 %all_to_all.50.recv = f32[8,4,640]{2,1,0:T(4,128)S(1)} all-to-all(f32[8,4,640]{2,1,0:T(4,128)S(1)} %get-tuple-element.46), channel_id=1, replica_groups=mesh['y'=8,'z'=12,'sub'=8] {'sub'}, dimensions={0} | all-to-all | bytes 163840 | tf_op jit(solution)/shard_map/all_to_all | solution.py:624
  14.0 0.1 shard_map.105
  14.1 17.0 %all_to_all.51.recv.after = f32[8,4,512]{2,1,0:T(4,128)S(1)} all-to-all(f32[8,4,512]{2,1,0:T(4,128)S(1)} %get-tuple-element.47), channel_id=1, replica_groups=mesh['y'=8,'z'=12,'sub'=8] {'y'}, dimensions={0} | all-to-all | bytes 131072 | tf_op jit(solution)/shard_map/all_to_all | solution.py:624
  31.1 0.7 shard_map.106
  31.8 12.4 %all-to-all-start.2 = ((f32[12,4,768]{2,1,0:T(4,128)}), f32[12,4,768]{2,1,0:T(4,128)S(1)}, u32[]{:S(2)}, u32[]{:S(2)}) async-start(f32[12,4,768]{2,1,0:T(4,128)} %shard_map.106), calls=%async_computation.2 | async-start | bytes 294912 | tf_op jit(solution)/shard_map/all_to_all | solution.py:624
  44.2 0.0 copy-start
  44.2 1.2 shard_map.108
  45.4 1.9 %collective-permute-start = (f32[720,128]{1,0:T(8,128)}, f32[720,128]{1,0:T(8,128)S(1)}, u32[]{:S(2)}, u32[]{:S(2)}) collective-permute-start(f32[720,128]{1,0:T(8,128)} %get-tuple-element.53), channel_id=1, source_target_pairs={{0,1},{1,0},{2,3},{3,2},{4,5},{5,4},{6,7},{7,6},{8,9},{9,8},{10,11... | collective-permute-start | bytes 1105928 | tf_op jit(solution)/shard_map/ppermute | solution.py:639
  47.3 3.5 %collective-permute-start.1 = (f32[720,128]{1,0:T(8,128)}, f32[720,128]{1,0:T(8,128)S(1)}, u32[]{:S(2)}, u32[]{:S(2)}) collective-permute-start(f32[720,128]{1,0:T(8,128)} %get-tuple-element.54), channel_id=1, source_target_pairs={{1,2},{2,1},{3,4},{4,3},{5,6},{6,5},{9,10},{10,9},{11,12},{12,11},... | collective-permute-start | bytes 1105928 | tf_op jit(solution)/shard_map/ppermute | solution.py:639
  50.8 0.1 shard_map.109
  50.9 3.9 %collective-permute-start.2 = (f32[72,128]{1,0:T(8,128)S(1)}, f32[72,128]{1,0:T(8,128)S(1)}, u32[]{:S(2)}, u32[]{:S(2)}) collective-permute-start(f32[72,128]{1,0:T(8,128)S(1)} %get-tuple-element.56), channel_id=1, source_target_pairs={{0,8},{8,0},{16,24},{24,16},{32,40},{40,32},{48,56},{56,48},{64,72... | collective-permute-start | bytes 110600 | tf_op jit(solution)/shard_map/ppermute | solution.py:639
  54.8 5.5 %collective-permute-start.3 = (f32[72,128]{1,0:T(8,128)S(1)}, f32[72,128]{1,0:T(8,128)S(1)}, u32[]{:S(2)}, u32[]{:S(2)}) collective-permute-start(f32[72,128]{1,0:T(8,128)S(1)} %get-tuple-element.57), channel_id=1, source_target_pairs={{8,16},{16,8},{24,32},{32,24},{40,48},{48,40},{56,64},{64,56},{72,... | collective-permute-start | bytes 110600 | tf_op jit(solution)/shard_map/ppermute | solution.py:639
  60.3 0.0 copy-start.3
  60.3 1.3 copy-done.3
  61.6 1.6 shard_map.107
  63.2 4.0 %all-to-all-start.3 = ((f32[8,4,128]{2,1,0:T(4,128)}), f32[8,4,128]{2,1,0:T(4,128)S(1)}, u32[]{:S(2)}, u32[]{:S(2)}) async-start(f32[8,4,128]{2,1,0:T(4,128)} %get-tuple-element.49), calls=%async_computation.3 | async-start | bytes 32768 | tf_op jit(solution)/shard_map/all_to_all | solution.py:624
  67.2 0.0 collective-permute-done.2.out1
  67.2 0.0 collective-permute-done.3.out2
  67.3 0.0 collective-permute-done.1.in2.static2
  67.3 3.9 %all-to-all-done.3.recv = f32[8,4,128]{2,1,0:T(4,128)S(1)} async-done(((f32[8,4,128]{2,1,0:T(4,128)}), f32[8,4,128]{2,1,0:T(4,128)S(1)}, u32[]{:S(2)}, u32[]{:S(2)}) %all-to-all-start.3) | async-done | bytes 16416 | tf_op jit(solution)/shard_map/all_to_all | solution.py:624
  71.1 0.8 shard_map.110
  71.9 1.9 %collective-permute-start.4 = (f32[8,128]{1,0:T(8,128)S(1)}, f32[8,128]{1,0:T(8,128)S(1)}, u32[]{:S(2)}, u32[]{:S(2)}) collective-permute-start(f32[8,128]{1,0:T(8,128)S(1)} %get-tuple-element.62), channel_id=1, source_target_pairs={{0,8},{8,0},{16,24},{24,16},{32,40},{40,32},{48,56},{56,48},{64,72... | collective-permute-start | bytes 12296 | tf_op jit(solution)/shard_map/ppermute | solution.py:639
  73.8 4.8 %collective-permute-start.5 = (f32[8,128]{1,0:T(8,128)S(1)}, f32[8,128]{1,0:T(8,128)S(1)}, u32[]{:S(2)}, u32[]{:S(2)}) collective-permute-start(f32[8,128]{1,0:T(8,128)S(1)} %get-tuple-element.63), channel_id=1, source_target_pairs={{8,16},{16,8},{24,32},{32,24},{40,48},{48,40},{56,64},{64,56},{72,... | collective-permute-start | bytes 12296 | tf_op jit(solution)/shard_map/ppermute | solution.py:639
  78.7 2.8 %collective-permute-done.5.out2 = f32[8,128]{1,0:T(8,128)S(1)} collective-permute-done((f32[8,128]{1,0:T(8,128)S(1)}, f32[8,128]{1,0:T(8,128)S(1)}, u32[]{:S(2)}, u32[]{:S(2)}) %collective-permute-start.5) | collective-permute-done | bytes 4128 | tf_op jit(solution)/shard_map/ppermute | solution.py:639
  81.4 1.2 shard_map.111
  82.6 8.7 %all_to_all.52.recv = f32[8,4,1152]{2,1,0:T(4,128)S(1)} all-to-all(f32[8,4,1152]{2,1,0:T(4,128)S(1)} %get-tuple-element.65), channel_id=1, replica_groups=mesh['y'=8,'z'=12,'sub'=8] {'sub'}, dimensions={0} | all-to-all | bytes 294912 | tf_op jit(solution)/shard_map/all_to_all | solution.py:624
  91.3 0.2 shard_map.112
  91.5 12.1 %all_to_all.53.recv = f32[8,4,384]{2,1,0:T(4,128)S(1)} all-to-all(f32[8,4,384]{2,1,0:T(4,128)S(1)} %get-tuple-element.68), channel_id=1, replica_groups=mesh['y'=8,'z'=12,'sub'=8] {'y'}, dimensions={0} | all-to-all | bytes 98304 | tf_op jit(solution)/shard_map/all_to_all | solution.py:624
  103.6 14.4 %all_to_all.54.recv = f32[12,4,512]{2,1,0:T(4,128)S(1)} all-to-all(f32[12,4,512]{2,1,0:T(4,128)S(1)} %shard_map.113), channel_id=1, replica_groups=mesh['y'=8,'z'=12,'sub'=8] {'z'}, dimensions={0} | all-to-all | bytes 196608 | tf_op jit(solution)/shard_map/all_to_all | solution.py:624
  118.0 0.2 shard_map.114
  118.2 7.8 %all_to_all.55.recv = f32[8,4,256]{2,1,0:T(4,128)S(1)} all-to-all(f32[8,4,256]{2,1,0:T(4,128)S(1)} %get-tuple-element.73), channel_id=1, replica_groups=mesh['y'=8,'z'=12,'sub'=8] {'sub'}, dimensions={0} | all-to-all | bytes 65536 | tf_op jit(solution)/shard_map/all_to_all | solution.py:624
  126.1 0.7 shard_map.115
  126.8 13.5 %all_to_all.56.recv = f32[64,1,128]{2,1,0:T(1,128)S(1)} all-to-all(f32[64,1,128]{2,1,0:T(1,128)S(1)} %get-tuple-element.81), channel_id=1, replica_groups=mesh['y'=8,'z'=12,'sub'=8] {'y','sub'}, dimensions={0} | all-to-all | bytes 65536 | tf_op jit(solution)/shard_map/all_to_all | solution.py:624
  140.2 0.7 shard_map.116
  140.9 3.5 %all-to-all-start.9 = ((f32[12,1,128]{2,1,0:T(1,128)}), f32[12,1,128]{2,1,0:T(1,128)S(1)}, u32[]{:S(2)}, u32[]{:S(2)}) async-start(f32[12,1,128]{2,1,0:T(1,128)} %shard_map.116), calls=%async_computation.9 | async-start | bytes 12288 | tf_op jit(solution)/shard_map/all_to_all | solution.py:624
  144.4 1.9 %collective-permute-start.6 = (f32[16,128]{1,0:T(8,128)S(1)}, f32[16,128]{1,0:T(8,128)S(1)}, u32[]{:S(2)}, u32[]{:S(2)}) collective-permute-start(f32[16,128]{1,0:T(8,128)S(1)} %get-tuple-element.83), channel_id=1, source_target_pairs={{0,1},{1,0},{2,3},{3,2},{4,5},{5,4},{6,7},{7,6},{8,9},{9,8},{10,11... | collective-permute-start | bytes 24584 | tf_op jit(solution)/shard_map/ppermute | solution.py:639
  146.3 3.5 %collective-permute-start.7 = (f32[16,128]{1,0:T(8,128)S(1)}, f32[16,128]{1,0:T(8,128)S(1)}, u32[]{:S(2)}, u32[]{:S(2)}) collective-permute-start(f32[16,128]{1,0:T(8,128)S(1)} %get-tuple-element.84), channel_id=1, source_target_pairs={{1,2},{2,1},{3,4},{4,3},{5,6},{6,5},{9,10},{10,9},{11,12},{12,11},... | collective-permute-start | bytes 24584 | tf_op jit(solution)/shard_map/ppermute | solution.py:639
  149.8 3.8 %collective-permute-start.8 = (f32[8,128]{1,0:T(8,128)S(1)}, f32[8,128]{1,0:T(8,128)S(1)}, u32[]{:S(2)}, u32[]{:S(2)}) collective-permute-start(f32[8,128]{1,0:T(8,128)S(1)} %get-tuple-element.85), channel_id=1, source_target_pairs={{0,8},{8,0},{16,24},{24,16},{32,40},{40,32},{48,56},{56,48},{64,72... | collective-permute-start | bytes 12296 | tf_op jit(solution)/shard_map/ppermute | solution.py:639
  153.5 5.5 %collective-permute-start.9 = (f32[8,128]{1,0:T(8,128)S(1)}, f32[8,128]{1,0:T(8,128)S(1)}, u32[]{:S(2)}, u32[]{:S(2)}) collective-permute-start(f32[8,128]{1,0:T(8,128)S(1)} %get-tuple-element.86), channel_id=1, source_target_pairs={{8,16},{16,8},{24,32},{32,24},{40,48},{48,40},{56,64},{64,56},{72,... | collective-permute-start | bytes 12296 | tf_op jit(solution)/shard_map/ppermute | solution.py:639
  159.1 2.1 %collective-permute-done.9.out2 = f32[8,128]{1,0:T(8,128)S(1)} collective-permute-done((f32[8,128]{1,0:T(8,128)S(1)}, f32[8,128]{1,0:T(8,128)S(1)}, u32[]{:S(2)}, u32[]{:S(2)}) %collective-permute-start.9) | collective-permute-done | bytes 4128 | tf_op jit(solution)/shard_map/ppermute | solution.py:639
  161.2 0.7 shard_map.117
  (18 shorter events, 0.1 us)
Async XLA Ops:
  0.6 43.6 %copy-start.2 = (f32[1,96,768]{2,1,0:T(8,128)S(1)}, f32[1,96,768]{2,1,0:T(8,128)}, u32[]{:S(2)}) copy-start(f32[1,96,768]{2,1,0:T(8,128)} %param.16) | copy-start | bytes 884740
  0.6 43.6 %copy-start.8 = (s32[4,3,128]{2,0,1:T(4,128)S(1)}, s32[4,3,128]{2,0,1:T(4,128)}, u32[]{:S(2)}) copy-start(s32[4,3,128]{2,0,1:T(4,128)} %param.12) | copy-start | bytes 18436
  0.7 43.6 %copy-start.7 = (s32[4,384]{1,0:T(4,128)S(1)}, s32[4,384]{1,0:T(4,128)}, u32[]{:S(2)}) copy-start(s32[4,384]{1,0:T(4,128)} %signs.1) | copy-start | bytes 18436
  1.7 1.0 copy-start.1
  2.6 0.7 copy-start.4
  3.4 0.7 copy-start.5
  31.8 28.6 %all-to-all-start.2 = ((f32[12,4,768]{2,1,0:T(4,128)}), f32[12,4,768]{2,1,0:T(4,128)S(1)}, u32[]{:S(2)}, u32[]{:S(2)}) async-start(f32[12,4,768]{2,1,0:T(4,128)} %shard_map.106), calls=%async_computation.2 | async-start | bytes 294912 | tf_op jit(solution)/shard_map/all_to_all | solution.py:624
  44.2 27.0 %copy-start = (bf16[4,384,384]{2,1,0:T(8,128)(2,1)S(1)}, bf16[4,384,384]{2,1,0:T(8,128)(2,1)}, u32[]{:S(2)}) copy-start(bf16[4,384,384]{2,1,0:T(8,128)(2,1)} %ops.3) | copy-start | bytes 3538948
  45.4 21.8 %collective-permute-start = (f32[720,128]{1,0:T(8,128)}, f32[720,128]{1,0:T(8,128)S(1)}, u32[]{:S(2)}, u32[]{:S(2)}) collective-permute-start(f32[720,128]{1,0:T(8,128)} %get-tuple-element.53), channel_id=1, source_target_pairs={{0,1},{1,0},{2,3},{3,2},{4,5},{5,4},{6,7},{7,6},{8,9},{9,8},{10,11... | collective-permute-start | bytes 1105928 | tf_op jit(solution)/shard_map/ppermute | solution.py:639
  47.3 19.9 %collective-permute-start.1 = (f32[720,128]{1,0:T(8,128)}, f32[720,128]{1,0:T(8,128)S(1)}, u32[]{:S(2)}, u32[]{:S(2)}) collective-permute-start(f32[720,128]{1,0:T(8,128)} %get-tuple-element.54), channel_id=1, source_target_pairs={{1,2},{2,1},{3,4},{4,3},{5,6},{6,5},{9,10},{10,9},{11,12},{12,11},... | collective-permute-start | bytes 1105928 | tf_op jit(solution)/shard_map/ppermute | solution.py:639
  50.9 16.3 %collective-permute-start.2 = (f32[72,128]{1,0:T(8,128)S(1)}, f32[72,128]{1,0:T(8,128)S(1)}, u32[]{:S(2)}, u32[]{:S(2)}) collective-permute-start(f32[72,128]{1,0:T(8,128)S(1)} %get-tuple-element.56), channel_id=1, source_target_pairs={{0,8},{8,0},{16,24},{24,16},{32,40},{40,32},{48,56},{56,48},{64,72... | collective-permute-start | bytes 110600 | tf_op jit(solution)/shard_map/ppermute | solution.py:639
  54.8 12.4 %collective-permute-start.3 = (f32[72,128]{1,0:T(8,128)S(1)}, f32[72,128]{1,0:T(8,128)S(1)}, u32[]{:S(2)}, u32[]{:S(2)}) collective-permute-start(f32[72,128]{1,0:T(8,128)S(1)} %get-tuple-element.57), channel_id=1, source_target_pairs={{8,16},{16,8},{24,32},{32,24},{40,48},{48,40},{56,64},{64,56},{72,... | collective-permute-start | bytes 110600 | tf_op jit(solution)/shard_map/ppermute | solution.py:639
  60.3 1.3 copy-start.3
  63.2 18.2 %copy-start.6 = (s32[4,8]{1,0:T(4,128)S(1)}, s32[4,8]{1,0:T(4,128)}, u32[]{:S(2)}) copy-start(s32[4,8]{1,0:T(4,128)} %ids.3) | copy-start | bytes 388
  63.2 7.9 %all-to-all-start.3 = ((f32[8,4,128]{2,1,0:T(4,128)}), f32[8,4,128]{2,1,0:T(4,128)S(1)}, u32[]{:S(2)}, u32[]{:S(2)}) async-start(f32[8,4,128]{2,1,0:T(4,128)} %get-tuple-element.49), calls=%async_computation.3 | async-start | bytes 32768 | tf_op jit(solution)/shard_map/all_to_all | solution.py:624
  71.9 6.7 %collective-permute-start.4 = (f32[8,128]{1,0:T(8,128)S(1)}, f32[8,128]{1,0:T(8,128)S(1)}, u32[]{:S(2)}, u32[]{:S(2)}) collective-permute-start(f32[8,128]{1,0:T(8,128)S(1)} %get-tuple-element.62), channel_id=1, source_target_pairs={{0,8},{8,0},{16,24},{24,16},{32,40},{40,32},{48,56},{56,48},{64,72... | collective-permute-start | bytes 12296 | tf_op jit(solution)/shard_map/ppermute | solution.py:639
  73.8 7.6 %collective-permute-start.5 = (f32[8,128]{1,0:T(8,128)S(1)}, f32[8,128]{1,0:T(8,128)S(1)}, u32[]{:S(2)}, u32[]{:S(2)}) collective-permute-start(f32[8,128]{1,0:T(8,128)S(1)} %get-tuple-element.63), channel_id=1, source_target_pairs={{8,16},{16,8},{24,32},{32,24},{40,48},{48,40},{56,64},{64,56},{72,... | collective-permute-start | bytes 12296 | tf_op jit(solution)/shard_map/ppermute | solution.py:639
  140.9 20.3 %all-to-all-start.9 = ((f32[12,1,128]{2,1,0:T(1,128)}), f32[12,1,128]{2,1,0:T(1,128)S(1)}, u32[]{:S(2)}, u32[]{:S(2)}) async-start(f32[12,1,128]{2,1,0:T(1,128)} %shard_map.116), calls=%async_computation.9 | async-start | bytes 12288 | tf_op jit(solution)/shard_map/all_to_all | solution.py:624
  144.4 16.8 %collective-permute-start.6 = (f32[16,128]{1,0:T(8,128)S(1)}, f32[16,128]{1,0:T(8,128)S(1)}, u32[]{:S(2)}, u32[]{:S(2)}) collective-permute-start(f32[16,128]{1,0:T(8,128)S(1)} %get-tuple-element.83), channel_id=1, source_target_pairs={{0,1},{1,0},{2,3},{3,2},{4,5},{5,4},{6,7},{7,6},{8,9},{9,8},{10,11... | collective-permute-start | bytes 24584 | tf_op jit(solution)/shard_map/ppermute | solution.py:639
  146.3 14.9 %collective-permute-start.7 = (f32[16,128]{1,0:T(8,128)S(1)}, f32[16,128]{1,0:T(8,128)S(1)}, u32[]{:S(2)}, u32[]{:S(2)}) collective-permute-start(f32[16,128]{1,0:T(8,128)S(1)} %get-tuple-element.84), channel_id=1, source_target_pairs={{1,2},{2,1},{3,4},{4,3},{5,6},{6,5},{9,10},{10,9},{11,12},{12,11},... | collective-permute-start | bytes 24584 | tf_op jit(solution)/shard_map/ppermute | solution.py:639
  149.8 9.3 %collective-permute-start.8 = (f32[8,128]{1,0:T(8,128)S(1)}, f32[8,128]{1,0:T(8,128)S(1)}, u32[]{:S(2)}, u32[]{:S(2)}) collective-permute-start(f32[8,128]{1,0:T(8,128)S(1)} %get-tuple-element.85), channel_id=1, source_target_pairs={{0,8},{8,0},{16,24},{24,16},{32,40},{40,32},{48,56},{56,48},{64,72... | collective-permute-start | bytes 12296 | tf_op jit(solution)/shard_map/ppermute | solution.py:639
  153.5 7.6 %collective-permute-start.9 = (f32[8,128]{1,0:T(8,128)S(1)}, f32[8,128]{1,0:T(8,128)S(1)}, u32[]{:S(2)}, u32[]{:S(2)}) collective-permute-start(f32[8,128]{1,0:T(8,128)S(1)} %get-tuple-element.86), channel_id=1, source_target_pairs={{8,16},{16,8},{24,32},{32,24},{40,48},{48,40},{56,64},{64,56},{72,... | collective-permute-start | bytes 12296 | tf_op jit(solution)/shard_map/ppermute | solution.py:639
